TPU v7x, 32 devices: a whole 2x2x4 slice. The times are simulated.
32 devices in a mesh: fsdp: 8 (over z, y), context: 2 (over x), tensor: 2 (over core).
Axes of the slice: x: 2, y: 2, z: 4, core: 2. Of those that a mesh axis runs over, the one named last changes fastest.
Arguments:
- tokens: bfloat16 [4096, 2048], P(('fsdp', 'context')), may hold values from -6 to 6
- cont_lengths: int32 [8, 4], P('fsdp'), may hold values from 1 to 128, 256 in all within a row
- w_query: bfloat16 [2048, 2048], P('fsdp', 'tensor'), may hold values from -0.125 to 0.125
- w_key: bfloat16 [2048, 2048], P('fsdp', 'tensor'), may hold values from -0.125 to 0.125
- w_value: bfloat16 [2048, 2048], P('fsdp', 'tensor'), may hold values from -0.125 to 0.125
- w_output: bfloat16 [2048, 2048], P('tensor', 'fsdp'), may hold values from -0.125 to 0.125
- query_gain: bfloat16 [16, 128], P('tensor', 'fsdp'), may hold values from 0.099609375 to 1.8984375
- key_gain: bfloat16 [16, 128], P('tensor', 'fsdp'), may hold values from 0.099609375 to 1.8984375
- attn_gain: bfloat16 [2048], P('fsdp'), may hold values from 0.099609375 to 1.8984375
- w_gate: bfloat16 [2048, 8192], P('fsdp', 'tensor'), may hold values from -0.125 to 0.125
- w_up: bfloat16 [2048, 8192], P('fsdp', 'tensor'), may hold values from -0.125 to 0.125
- w_down: bfloat16 [8192, 2048], P('tensor', 'fsdp'), may hold values from -0.0625 to 0.0625
- mlp_gain: bfloat16 [2048], P('fsdp'), may hold values from 0.099609375 to 1.8984375
- cotangent: bfloat16 [4096, 2048], P(('fsdp', 'context')), may hold values from -6 to 6
Outputs:
- outputs: bfloat16 [4096, 2048], P(('fsdp', 'context'))
- input_grad: float32 [4096, 2048], P(('fsdp', 'context'))
- grad_query: float32 [2048, 2048], P('fsdp', 'tensor')
- grad_key: float32 [2048, 2048], P('fsdp', 'tensor')
- grad_value: float32 [2048, 2048], P('fsdp', 'tensor')
- grad_output: float32 [2048, 2048], P('tensor', 'fsdp')
- grad_query_gain: float32 [16, 128], P('tensor', 'fsdp')
- grad_key_gain: float32 [16, 128], P('tensor', 'fsdp')
- grad_attn_gain: float32 [2048], P('fsdp')
- grad_gate: float32 [2048, 8192], P('fsdp', 'tensor')
- grad_up: float32 [2048, 8192], P('fsdp', 'tensor')
- grad_down: float32 [8192, 2048], P('tensor', 'fsdp')
- grad_mlp_gain: float32 [2048], P('fsdp')
Inputs may be any that keep to these rules, and one draw needn't show every extreme that they name: `cont_lengths`: a group's 4 lengths sum to 256; in every group the longest is exactly 128.
All inputs are finite; a program needn't handle non-finite values.
Results may differ from a plain program's by a relative error of at most 0.017.
Values may be sent and summed in bfloat16 or wider, within the bound.
A program may use at most 320 MiB of HBM per device.

v0:
```python
import math

import jax
import jax.numpy as jnp
from jax import lax
from jax.sharding import PartitionSpec as P

EPS = 1e-06
THETA = 500000.0


def from_behind(value, axis, steps):
    count = lax.axis_size(axis)
    first, last = (max(0, -steps), min(count, count - steps))
    return lax.ppermute(value, axis, [(source, source + steps) for source in range(first, last)])


def product(left, right):
    return jnp.dot(left, right, preferred_element_type=jnp.float32)


def product_left(left, right):
    return jnp.einsum("rd,rf->df", left, right, preferred_element_type=jnp.float32)


def product_right(left, right):
    return jnp.einsum("rf,df->rd", left, right, preferred_element_type=jnp.float32)


def rotary_tables(positions, head_size):
    half = head_size // 2
    inverse = jnp.exp(-(2.0 * jnp.arange(half, dtype=jnp.float32) / head_size) * math.log(THETA))
    angles = positions.astype(jnp.float32)[:, None] * inverse[None, :]
    angles = jnp.concatenate([angles, angles], axis=1)
    return (jnp.cos(angles), jnp.sin(angles))


def rotate(values, cosine, sine):
    half = values.shape[-1] // 2
    turned = jnp.concatenate([-values[..., half:], values[..., :half]], axis=-1)
    return values * cosine[:, None, :] + turned * sine[:, None, :]


def rotate_back(grads, cosine, sine):
    half = grads.shape[-1] // 2
    scaled = grads * sine[:, None, :]
    turned = jnp.concatenate([scaled[..., half:], -scaled[..., :half]], axis=-1)
    return grads * cosine[:, None, :] + turned


def norm_back(values, scale, gain, grads, total, width):
    return scale * gain * grads - values * scale * scale * scale * (total / width)[:, None]


def layout(lengths, rows):
    segment_ends = jnp.cumsum(lengths)
    segment_starts = segment_ends - lengths
    row_index = jnp.arange(rows, dtype=jnp.int32)
    segment = jnp.sum((row_index[:, None] >= segment_ends[None, :]).astype(jnp.int32), axis=1)
    chosen = segment[:, None] == jnp.arange(lengths.shape[0], dtype=jnp.int32)[None, :]
    offset = row_index - jnp.sum(jnp.where(chosen, segment_starts[None, :], 0), axis=1)
    return (segment, offset)


def local(
    tokens,
    cont_lengths,
    w_query,
    w_key,
    w_value,
    w_output,
    query_gain,
    key_gain,
    attn_gain,
    w_gate,
    w_up,
    w_down,
    mlp_gain,
    cotangent,
):
    rows = tokens.shape[0]
    width = tokens.shape[1]
    later = lax.axis_index("context") == 1
    segment, offset = layout(cont_lengths[0], rows)
    row_index = jnp.arange(rows, dtype=jnp.int32)
    positions = jnp.where(later, rows + offset, row_index)
    own_segment = jnp.where(later, segment, -1)
    attn_weights = (
        lax.all_gather(w_query, "fsdp", axis=0, tiled=True),
        lax.all_gather(w_key, "fsdp", axis=0, tiled=True),
        lax.all_gather(w_value, "fsdp", axis=0, tiled=True),
        lax.all_gather(w_output, "fsdp", axis=1, tiled=True),
        lax.all_gather(query_gain, "fsdp", axis=1, tiled=True),
        lax.all_gather(key_gain, "fsdp", axis=1, tiled=True),
        lax.all_gather(attn_gain, "fsdp", axis=0, tiled=True),
    )
    full_query, full_key, full_value, full_output, gain_query, gain_key, gain_attn = attn_weights
    local_heads = gain_query.shape[0]
    head_size = gain_query.shape[1]
    local_width = local_heads * head_size
    cosine, sine = rotary_tables(positions, head_size)
    query_raw = product(tokens, full_query)
    key_raw = product(tokens, full_key)
    value_raw = product(tokens, full_value)
    sum_query, sum_key = lax.psum(
        (jnp.sum(query_raw * query_raw, axis=1), jnp.sum(key_raw * key_raw, axis=1)), "tensor"
    )
    scale_query = lax.rsqrt(sum_query / width + EPS)[:, None]
    scale_key = lax.rsqrt(sum_key / width + EPS)[:, None]
    query_norm = query_raw * scale_query * gain_query.reshape(-1)
    key_norm = key_raw * scale_key * gain_key.reshape(-1)
    query_low = rotate(query_norm.reshape(rows, local_heads, head_size), cosine, sine).astype(
        jnp.bfloat16
    )
    key_low = rotate(key_norm.reshape(rows, local_heads, head_size), cosine, sine).astype(
        jnp.bfloat16
    )
    value_low = value_raw.reshape(rows, local_heads, head_size).astype(jnp.bfloat16)
    sent_key, sent_value = from_behind((key_low, value_low), "context", 1)
    keys_all = jnp.concatenate([sent_key, key_low], axis=0)
    values_all = jnp.concatenate([sent_value, value_low], axis=0)
    key_segment = jnp.concatenate([jnp.full((rows,), -2, jnp.int32), own_segment])
    key_index = jnp.arange(2 * rows, dtype=jnp.int32)
    scale = 1.0 / math.sqrt(head_size)

    def block_scores(query_block, start):
        count = query_block.shape[0]
        block_rows = start + jnp.arange(count, dtype=jnp.int32)
        remote = (key_index < rows)[None, :] & later
        own_keys = (
            (key_index >= rows)[None, :]
            & (key_index[None, :] - rows <= block_rows[:, None])
            & (key_segment[None, :] == own_segment[:, None])
        )
        allowed = remote | own_keys
        products = (
            jnp.einsum("qhd,khd->hqk", query_block, keys_all, preferred_element_type=jnp.float32)
            * scale
        )
        return jnp.where(allowed[None], products, -1e30)

    block = min(rows, 512)
    blocks = rows // block
    starts = jnp.arange(blocks, dtype=jnp.int32) * block
    query_blocks = query_low.reshape(blocks, block, local_heads, head_size)

    def attend(packed):
        query_block, start = packed
        scores = block_scores(query_block, start)
        highest = jnp.max(scores, axis=-1, keepdims=True)
        weights = jnp.exp(scores - highest)
        totals = jnp.sum(weights, axis=-1, keepdims=True)
        probs = (weights / totals).astype(jnp.bfloat16)
        mixed = jnp.einsum("hqk,khd->qhd", probs, values_all, preferred_element_type=jnp.float32)
        return (mixed, highest[..., 0] + jnp.log(totals[..., 0]))

    mixed, logsum = lax.map(attend, (query_blocks, starts))
    attended_low = mixed.reshape(rows, local_width).astype(jnp.bfloat16)
    attn_sum = lax.psum(product(attended_low, full_output), "tensor")
    attn_scale = lax.rsqrt(jnp.mean(attn_sum * attn_sum, axis=1, keepdims=True) + EPS)
    hidden = tokens.astype(jnp.float32) + attn_sum * attn_scale * gain_attn
    hidden_low = hidden.astype(jnp.bfloat16)
    mlp_weights = (
        lax.all_gather(w_gate, "fsdp", axis=0, tiled=True),
        lax.all_gather(w_up, "fsdp", axis=0, tiled=True),
        lax.all_gather(w_down, "fsdp", axis=1, tiled=True),
        lax.all_gather(mlp_gain, "fsdp", axis=0, tiled=True),
    )
    full_gate, full_up, full_down, gain_mlp = mlp_weights
    gate = product(hidden_low, full_gate)
    upward = product(hidden_low, full_up)
    inner_low = (jax.nn.silu(gate) * upward).astype(jnp.bfloat16)
    mlp_sum = lax.psum(product(inner_low, full_down), "tensor")
    mlp_scale = lax.rsqrt(jnp.mean(mlp_sum * mlp_sum, axis=1, keepdims=True) + EPS)
    outputs = (hidden + mlp_sum * mlp_scale * gain_mlp).astype(jnp.bfloat16)
    grad_out = cotangent.astype(jnp.float32)
    mlp_back = (
        lax.all_gather(w_gate, "fsdp", axis=0, tiled=True),
        lax.all_gather(w_up, "fsdp", axis=0, tiled=True),
        lax.all_gather(w_down, "fsdp", axis=1, tiled=True),
        lax.all_gather(mlp_gain, "fsdp", axis=0, tiled=True),
    )
    back_gate, back_up, back_down, back_mlp_gain = mlp_back
    grad_mlp_gain = jnp.sum(grad_out * mlp_sum * mlp_scale, axis=0)
    grad_mlp_low = norm_back(
        mlp_sum,
        mlp_scale,
        back_mlp_gain,
        grad_out,
        jnp.sum(mlp_sum * back_mlp_gain * grad_out, axis=1),
        width,
    ).astype(jnp.bfloat16)
    grad_down = product_left(inner_low, grad_mlp_low)
    grad_inner = product_right(grad_mlp_low, back_down)
    sigma = jax.nn.sigmoid(gate)
    grad_gate_low = (grad_inner * upward * sigma * (1.0 + gate * (1.0 - sigma))).astype(
        jnp.bfloat16
    )
    grad_up_low = (grad_inner * jax.nn.silu(gate)).astype(jnp.bfloat16)
    grad_w_gate = product_left(hidden_low, grad_gate_low)
    grad_w_up = product_left(hidden_low, grad_up_low)
    mlp_terms = product_right(grad_gate_low, back_gate) + product_right(grad_up_low, back_up)
    grad_hidden = grad_out + lax.psum(mlp_terms, "tensor")
    attn_back = (
        lax.all_gather(w_query, "fsdp", axis=0, tiled=True),
        lax.all_gather(w_key, "fsdp", axis=0, tiled=True),
        lax.all_gather(w_value, "fsdp", axis=0, tiled=True),
        lax.all_gather(w_output, "fsdp", axis=1, tiled=True),
        lax.all_gather(query_gain, "fsdp", axis=1, tiled=True),
        lax.all_gather(key_gain, "fsdp", axis=1, tiled=True),
        lax.all_gather(attn_gain, "fsdp", axis=0, tiled=True),
    )
    (
        back_query,
        back_key,
        back_value,
        back_output,
        back_query_gain,
        back_key_gain,
        back_attn_gain,
    ) = attn_back
    flat_query = back_query_gain.reshape(-1)
    flat_key = back_key_gain.reshape(-1)
    grad_attn_gain = jnp.sum(grad_hidden * attn_sum * attn_scale, axis=0)
    grad_branch_low = norm_back(
        attn_sum,
        attn_scale,
        back_attn_gain,
        grad_hidden,
        jnp.sum(attn_sum * back_attn_gain * grad_hidden, axis=1),
        width,
    ).astype(jnp.bfloat16)
    grad_w_output = product_left(attended_low, grad_branch_low)
    grad_attended_low = product_right(grad_branch_low, back_output).astype(jnp.bfloat16)
    grad_blocks = grad_attended_low.reshape(blocks, block, local_heads, head_size)

    def attend_back(carry, packed):
        grad_keys, grad_values = carry
        query_block, start, grad_block, logsum_block = packed
        scores = block_scores(query_block, start)
        probs = jnp.exp(scores - logsum_block[..., None])
        probs_low = probs.astype(jnp.bfloat16)
        grad_probs = jnp.einsum(
            "qhd,khd->hqk", grad_block, values_all, preferred_element_type=jnp.float32
        )
        centre = jnp.sum(probs * grad_probs, axis=-1, keepdims=True)
        grad_scores = (probs * (grad_probs - centre)).astype(jnp.bfloat16)
        grad_query_block = (
            jnp.einsum("hqk,khd->qhd", grad_scores, keys_all, preferred_element_type=jnp.float32)
            * scale
        )
        grad_keys = (
            grad_keys
            + jnp.einsum(
                "hqk,qhd->khd", grad_scores, query_block, preferred_element_type=jnp.float32
            )
            * scale
        )
        grad_values = grad_values + jnp.einsum(
            "hqk,qhd->khd", probs_low, grad_block, preferred_element_type=jnp.float32
        )
        return ((grad_keys, grad_values), grad_query_block)

    zeros_keys = jnp.zeros((2 * rows, local_heads, head_size), jnp.float32)
    (grad_keys, grad_values), grad_query_rot = lax.scan(
        attend_back, (zeros_keys, zeros_keys), (query_blocks, starts, grad_blocks, logsum)
    )
    back_keys, back_values = (
        from_behind(grad_keys[:rows].astype(jnp.bfloat16), "context", -1).astype(jnp.float32),
        from_behind(grad_values[:rows].astype(jnp.bfloat16), "context", -1).astype(jnp.float32),
    )
    grad_key_rot = grad_keys[rows:] + back_keys
    grad_value_low = (
        (grad_values[rows:] + back_values).reshape(rows, local_width).astype(jnp.bfloat16)
    )
    grad_query_norm = rotate_back(
        grad_query_rot.reshape(rows, local_heads, head_size), cosine, sine
    ).reshape(rows, local_width)
    grad_key_norm = rotate_back(grad_key_rot, cosine, sine).reshape(rows, local_width)
    grad_query_gain = jnp.sum(grad_query_norm * query_raw * scale_query, axis=0).reshape(
        local_heads, head_size
    )
    grad_key_gain = jnp.sum(grad_key_norm * key_raw * scale_key, axis=0).reshape(
        local_heads, head_size
    )
    total_query, total_key = lax.psum(
        (
            jnp.sum(query_raw * flat_query * grad_query_norm, axis=1),
            jnp.sum(key_raw * flat_key * grad_key_norm, axis=1),
        ),
        "tensor",
    )
    grad_query_low = norm_back(
        query_raw, scale_query, flat_query, grad_query_norm, total_query, width
    ).astype(jnp.bfloat16)
    grad_key_low = norm_back(key_raw, scale_key, flat_key, grad_key_norm, total_key, width).astype(
        jnp.bfloat16
    )
    grad_w_query = product_left(tokens, grad_query_low)
    grad_w_key = product_left(tokens, grad_key_low)
    grad_w_value = product_left(tokens, grad_value_low)
    back_terms = (
        product_right(grad_query_low, back_query)
        + product_right(grad_key_low, back_key)
        + product_right(grad_value_low, back_value)
    )
    input_grad = grad_hidden + lax.psum(back_terms.astype(jnp.bfloat16), "tensor").astype(
        jnp.float32
    )
    shards = (
        lax.psum_scatter(grad_w_query, "fsdp", scatter_dimension=0, tiled=True),
        lax.psum_scatter(grad_w_key, "fsdp", scatter_dimension=0, tiled=True),
        lax.psum_scatter(grad_w_value, "fsdp", scatter_dimension=0, tiled=True),
        lax.psum_scatter(grad_w_output, "fsdp", scatter_dimension=1, tiled=True),
        lax.psum_scatter(grad_query_gain, "fsdp", scatter_dimension=1, tiled=True),
        lax.psum_scatter(grad_key_gain, "fsdp", scatter_dimension=1, tiled=True),
        lax.psum_scatter(grad_attn_gain, "fsdp", scatter_dimension=0, tiled=True),
        lax.psum_scatter(grad_w_gate, "fsdp", scatter_dimension=0, tiled=True),
        lax.psum_scatter(grad_w_up, "fsdp", scatter_dimension=0, tiled=True),
        lax.psum_scatter(grad_down, "fsdp", scatter_dimension=1, tiled=True),
        lax.psum_scatter(grad_mlp_gain, "fsdp", scatter_dimension=0, tiled=True),
    )
    totals = lax.psum(
        (
            shards[0],
            shards[1],
            shards[2],
            shards[3],
            shards[4],
            shards[5],
            shards[6],
            shards[7],
            shards[8],
            shards[9],
            shards[10],
        ),
        "context",
    )
    return (
        outputs,
        input_grad,
        totals[0],
        totals[1],
        totals[2],
        totals[3],
        totals[4],
        totals[5],
        totals[6],
        totals[7],
        totals[8],
        totals[9],
        totals[10],
    )


def solution(mesh):
    return jax.shard_map(
        local,
        mesh=mesh,
        in_specs=(
            P(("fsdp", "context"), None),
            P("fsdp", None),
            P("fsdp", "tensor"),
            P("fsdp", "tensor"),
            P("fsdp", "tensor"),
            P("tensor", "fsdp"),
            P("tensor", "fsdp"),
            P("tensor", "fsdp"),
            P("fsdp"),
            P("fsdp", "tensor"),
            P("fsdp", "tensor"),
            P("tensor", "fsdp"),
            P("fsdp"),
            P(("fsdp", "context"), None),
        ),
        out_specs=(
            P(("fsdp", "context"), None),
            P(("fsdp", "context"), None),
            P("fsdp", "tensor"),
            P("fsdp", "tensor"),
            P("fsdp", "tensor"),
            P("tensor", "fsdp"),
            P("tensor", "fsdp"),
            P("tensor", "fsdp"),
            P("fsdp"),
            P("fsdp", "tensor"),
            P("fsdp", "tensor"),
            P("tensor", "fsdp"),
            P("fsdp"),
        ),
        check_vma=False,
    )
```

profile of v0, /device:TPU:16, one launch (start us, length us, event | category | flops | bytes accessed | tf_op | source)
XLA Modules:
  0.0 3909.7 jit_solution(6971893191242168918)
XLA Ops:
  10.1 24.3 all-gather
  34.4 26.9 all-gather.1
  64.3 19.6 all-gather.16.cloned.1.call-done
  83.8 4.1 multiply_reduce_fusion.7
  87.9 69.4 %all-gather.14.cloned.1.call-done = bf16[2048,1024]{1,0:T(8,128)(2,1)} async-done(((bf16[256,1024]{1,0:T(8,128)(2,1)}), bf16[2048,1024]{1,0:T(8,128)(2,1)}) %all-gather.14.cloned.1.call-update) | async-done | bytes 4194320 | tf_op jit(solution)/shard_map/all_gather | solution.py:89
  157.3 4.1 multiply_reduce_fusion.8
  161.4 3.1 all-reduce.5
  168.2 3.4 collective-permute-start.1
  172.5 58.4 %all-gather.12.cloned.1.call-done = bf16[2048,1024]{1,0:T(8,128)(2,1)} async-done(((bf16[256,1024]{1,0:T(8,128)(2,1)}), bf16[2048,1024]{1,0:T(8,128)(2,1)}) %all-gather.12.cloned.1.call-update) | async-done | bytes 4194320 | tf_op jit(solution)/shard_map/all_gather | solution.py:91
  230.8 3.4 convolution_convert_fusion.1
  234.5 3.4 collective-permute-start
  237.9 2.2 fusion.44
  241.2 6.8 collective-permute-done
  249.6 56.0 %all-gather.18.cloned.1.call-done = bf16[1024,2048]{1,0:T(8,128)(2,1)} async-done(((bf16[1024,256]{1,0:T(8,128)(2,1)}), bf16[1024,2048]{1,0:T(8,128)(2,1)}) %all-gather.18.cloned.1.call-update) | async-done | bytes 4194320 | tf_op jit(solution)/shard_map/all_gather | solution.py:92
  305.6 4.8 fusion.48
  312.5 14.3 all-gather.2
  326.9 4.3 all-reduce.14.cloned.1.call-done
  335.1 225.4 %all-gather.20.cloned.1.call-done = bf16[2048,4096]{1,0:T(8,128)(2,1)} async-done(((bf16[256,4096]{1,0:T(8,128)(2,1)}), bf16[2048,4096]{1,0:T(8,128)(2,1)}) %all-gather.20.cloned.1.call-update) | async-done | bytes 16777232 | tf_op jit(solution)/shard_map/all_gather | solution.py:164
  560.5 12.6 fusion.49
  573.1 215.0 %all-gather.22.cloned.1.call-done = bf16[2048,4096]{1,0:T(8,128)(2,1)} async-done(((bf16[256,4096]{1,0:T(8,128)(2,1)}), bf16[2048,4096]{1,0:T(8,128)(2,1)}) %all-gather.22.cloned.1.call-update) | async-done | bytes 16777232 | tf_op jit(solution)/shard_map/all_gather | solution.py:165
  788.1 14.8 multiply_convert_fusion.3
  802.9 212.7 %all-gather.24.cloned.1.call-done = bf16[4096,2048]{1,0:T(8,128)(2,1)} async-done(((bf16[4096,256]{1,0:T(8,128)(2,1)}), bf16[4096,2048]{1,0:T(8,128)(2,1)}) %all-gather.24.cloned.1.call-update) | async-done | bytes 16777232 | tf_op jit(solution)/shard_map/all_gather | solution.py:166
  1015.7 12.2 fusion.50
  1028.6 14.5 all-gather.3
  1043.1 5.7 all-reduce.16.cloned.1.call-done
  1050.9 2.4 fusion.10
  1053.9 13.6 multiply_convert_fusion.1
  1067.5 12.2 fusion.51
  1079.7 12.8 convolution_add_fusion.2
  1092.8 22.4 all-reduce.18.cloned.1.call-done
  1115.2 3.2 multiply_reduce_fusion.1
  1121.6 4.6 fusion.53
  1127.5 3.5 convolution_convert_fusion
  1131.1 3.1 fusion.13
  1135.6 14.7 collective-permute-done.3
  1151.3 4.5 convolution_bitcast_fusion
  1157.7 3.2 multiply_reduce_fusion
  1172.5 8.3 collective-permute-done.2
  1185.1 2.7 all-reduce.4
  1187.8 2.8 fusion.19
  1191.4 4.6 convolution_bitcast_fusion.1
  1198.4 4.5 convolution_bitcast_fusion.2
  1204.8 15.6 fusion.45
  1221.5 14.8 fusion.55
  1236.4 15.4 fusion.54
  1253.8 3.7 fusion.52
  1259.9 2.3 fusion.3
  1262.3 12.0 reduce-scatter.20.cloned.1.call-done
  1274.3 150.5 %reduce-scatter.18.cloned.1.call-done = f32[256,1024]{0,1:T(8,128)} async-done(((f32[2048,1024]{0,1:T(8,128)}), f32[256,1024]{0,1:T(8,128)}) %reduce-scatter.18.cloned.1.call-update) | async-done | bytes 1048592 | tf_op jit(solution)/shard_map/reduce_scatter | solution.py:313
  1424.8 150.7 %reduce-scatter.16.cloned.1.call-done = f32[256,1024]{0,1:T(8,128)} async-done(((f32[2048,1024]{0,1:T(8,128)}), f32[256,1024]{0,1:T(8,128)}) %reduce-scatter.16.cloned.1.call-update) | async-done | bytes 1048592 | tf_op jit(solution)/shard_map/reduce_scatter | solution.py:312
  1575.5 150.5 %reduce-scatter.14.cloned.1.call-done = f32[256,1024]{0,1:T(8,128)} async-done(((f32[2048,1024]{0,1:T(8,128)}), f32[256,1024]{0,1:T(8,128)}) %reduce-scatter.14.cloned.1.call-update) | async-done | bytes 1048592 | tf_op jit(solution)/shard_map/reduce_scatter | solution.py:311
  1725.9 541.5 %reduce-scatter.26.cloned.1.call-done = f32[4096,256]{1,0:T(8,128)} async-done(((f32[4096,2048]{1,0:T(8,128)}), f32[4096,256]{1,0:T(8,128)}) %reduce-scatter.26.cloned.1.call-update) | async-done | bytes 4194320 | tf_op jit(solution)/shard_map/reduce_scatter | solution.py:320
  2267.5 541.2 %reduce-scatter.24.cloned.1.call-done = f32[256,4096]{1,0:T(8,128)} async-done(((f32[2048,4096]{1,0:T(8,128)}), f32[256,4096]{1,0:T(8,128)}) %reduce-scatter.24.cloned.1.call-update) | async-done | bytes 4194320 | tf_op jit(solution)/shard_map/reduce_scatter | solution.py:319
  2808.7 541.5 %reduce-scatter.22.cloned.1.call-done = f32[256,4096]{1,0:T(8,128)} async-done(((f32[2048,4096]{1,0:T(8,128)}), f32[256,4096]{1,0:T(8,128)}) %reduce-scatter.22.cloned.1.call-update) | async-done | bytes 4194320 | tf_op jit(solution)/shard_map/reduce_scatter | solution.py:318
  3352.2 30.7 all-reduce.3
  3383.0 32.6 reduce-scatter.28.cloned.1.call-done
  3416.3 64.7 %reduce-scatter.30.cloned.1.call-done = f32[16,8]{1,0:T(8,128)} async-done(((f32[128,8]{1,0:T(8,128)}), f32[16,8]{1,0:T(8,128)}) %reduce-scatter.30.cloned.1.call-update) | async-done | bytes 528
  3481.8 8.6 all-reduce.6
  3490.4 13.1 all-reduce.20.cloned.1.call-done
  3503.5 3.0 convert_add_fusion.1
  3506.5 379.1 %all-reduce.22.cloned.1.call-done = (f32[256,1024]{0,1:T(8,128)}, f32[256,1024]{0,1:T(8,128)}, f32[256,1024]{0,1:T(8,128)}, f32[1024,256]{1,0:T(8,128)}, f32[256...) async-done(((f32[256,1024]{0,1:T(8,128)}, f32[256,1024]{0,1:T(8,128)}, f32[256,1024]{0,1:T(8,128)}, f32[1024,256]{1,0:T(8,128)}, f32[256,4096]{1,0:T(8,128)}, ...) | async-done | bytes 16777232 | tf_op jit(solution)/shard_map/psum | solution.py:323
  3885.6 2.7 copy.114
  3891.9 4.8 copy.152
  3896.7 2.1 copy.153
  (271 shorter events, 67.8 us)
Async XLA Ops:
  7.2 2.9 copy-start.69
  7.2 27.2 copy-start.70
  7.2 54.3 %copy-start.74 = (s32[1,4]{1,0:T(1,128)S(1)}, s32[1,4]{1,0:T(1,128)}, u32[]{:S(2)}) copy-start(s32[1,4]{1,0:T(1,128)} %param.15) | copy-start | bytes 52
  7.2 76.6 %copy-start.6 = (bf16[256,2048]{1,0:T(8,128)(2,1)S(1)}, bf16[256,2048]{1,0:T(8,128)(2,1)}, u32[]{:S(2)}) copy-start(bf16[256,2048]{1,0:T(8,128)(2,1)} %param.14) | copy-start | bytes 3145732
  7.2 76.6 %all-gather.16.cloned.1.call-start = ((), (), s32[]{:S(2)}) async-start(), calls=%async_computation.11 | async-start | bytes 4718592 | tf_op jit(solution)/shard_map/all_gather | solution.py:90
  8.0 149.4 %all-gather.14.cloned.1.call-start = ((), (), s32[]{:S(2)}) async-start(), calls=%async_computation.10 | async-start | bytes 4718592 | tf_op jit(solution)/shard_map/all_gather | solution.py:89
  8.7 222.1 %all-gather.12.cloned.1.call-start = ((), (), s32[]{:S(2)}) async-start(), calls=%async_computation.9 | async-start | bytes 4718592 | tf_op jit(solution)/shard_map/all_gather | solution.py:91
  9.4 296.1 %all-gather.18.cloned.1.call-start = ((), (), s32[]{:S(2)}) async-start(), calls=%async_computation.12 | async-start | bytes 4718592 | tf_op jit(solution)/shard_map/all_gather | solution.py:92
  10.0 321.2 %all-reduce.14.cloned.1.call-start = ((), (), s32[]{:S(2)}) async-start(), calls=%async_computation.13 | async-start | bytes 4194304 | tf_op jit(solution)/shard_map/psum | solution.py:159
  34.4 131.9 %copy-start.48 = (f32[128,8]{0,1:T(8,128)}, f32[128,8]{0,1:T(8,128)S(1)}, u32[]{:S(2)}) copy-start(f32[128,8]{0,1:T(8,128)S(1)} %reshape.313) | copy-start | bytes 12292
  61.4 104.9 %copy-start.50 = (f32[128,8]{0,1:T(8,128)}, f32[128,8]{0,1:T(8,128)S(1)}, u32[]{:S(2)}) copy-start(f32[128,8]{0,1:T(8,128)S(1)} %reshape.314) | copy-start | bytes 12292
  87.9 78.4 %copy-start.13 = (f32[256,1024]{1,0:T(8,128)}, f32[256,1024]{1,0:T(8,128)S(1)}, u32[]{:S(2)}) copy-start(f32[256,1024]{1,0:T(8,128)S(1)} %get-tuple-element.180) | copy-start | bytes 3145732
  161.4 4.9 copy-start.11
  166.4 5.2 copy-start.67
  166.4 5.2 copy-start.71
  166.4 5.2 copy-start.72
  168.2 69.7 %collective-permute-start.1 = (bf16[256,8,128]{2,0,1:T(8,128)(2,1)}, bf16[256,8,128]{2,0,1:T(8,128)(2,1)S(1)}, u32[]{:S(2)}, u32[]{:S(2)}) collective-permute-start(bf16[256,8,128]{2,0,1:T(8,128)(2,1)} %get-tuple-element.171), channel_id=1, source_target_pairs={{0,2},{1,3},{4,6},{5,7},{8,10},{9,11},{12,14},{13,15},{16,18},{17,... | collective-permute-start | bytes 1572872 | tf_op jit(solution)/shard_map/ppermute | solution.py:15
  172.5 65.5 %copy-start.31 = (bf16[256,8,128]{2,0,1:T(8,128)(2,1)S(1)}, bf16[256,8,128]{2,0,1:T(8,128)(2,1)}, u32[]{:S(2)}) copy-start(bf16[256,8,128]{2,0,1:T(8,128)(2,1)} %get-tuple-element.172) | copy-start | bytes 1572868
  234.5 13.5 copy-start.33
  234.5 13.5 collective-permute-start
  240.1 7.9 copy-start
  240.1 7.9 copy-start.52
  241.2 8.3 copy-start.54
  249.6 60.8 %copy-start.40 = (bf16[8,128,256]{2,1,0:T(8,128)(2,1)}, bf16[8,128,256]{2,1,0:T(8,128)(2,1)S(1)}, u32[]{:S(2)}) copy-start(bf16[8,128,256]{2,1,0:T(8,128)(2,1)S(1)} %fusion.16) | copy-start | bytes 1572868
  310.4 250.1 %all-gather.20.cloned.1.call-start = ((), (), s32[]{:S(2)}) async-start(), calls=%async_computation.14 | async-start | bytes 18874368 | tf_op jit(solution)/shard_map/all_gather | solution.py:164
  311.0 477.1 %all-gather.22.cloned.1.call-start = ((), (), s32[]{:S(2)}) async-start(), calls=%async_computation.15 | async-start | bytes 18874368 | tf_op jit(solution)/shard_map/all_gather | solution.py:165
  311.7 703.9 %all-gather.24.cloned.1.call-start = ((), (), s32[]{:S(2)}) async-start(), calls=%async_computation.16 | async-start | bytes 18874368 | tf_op jit(solution)/shard_map/all_gather | solution.py:166
  312.5 736.3 %all-reduce.16.cloned.1.call-start = ((), (), s32[]{:S(2)}) async-start(), calls=%async_computation.17 | async-start | bytes 4194304 | tf_op jit(solution)/shard_map/psum | solution.py:173
  1027.9 87.3 %all-reduce.18.cloned.1.call-start = ((), (), s32[]{:S(2)}) async-start(), calls=%async_computation.18 | async-start | bytes 4194304 | tf_op jit(solution)/shard_map/psum | solution.py:203
  1092.5 181.8 %reduce-scatter.20.cloned.1.call-start = ((), (), s32[]{:S(2)}) async-start(), calls=%async_computation.23 | async-start | bytes 9437184 | tf_op jit(solution)/shard_map/reduce_scatter | solution.py:314
  1115.2 3.2 copy-start.4
  1115.2 3.2 copy-start.7
  1115.2 3.5 copy-start.9
  1115.2 3.5 copy-start.63
  1115.2 3.5 copy-start.66
  1118.7 3.0 copy-start.41
  1126.2 298.6 %reduce-scatter.18.cloned.1.call-start = ((), (), s32[]{:S(2)}) async-start(), calls=%async_computation.22 | async-start | bytes 9437184 | tf_op jit(solution)/shard_map/reduce_scatter | solution.py:313
  1134.3 16.0 collective-permute-start.3
  1155.9 419.6 %reduce-scatter.16.cloned.1.call-start = ((), (), s32[]{:S(2)}) async-start(), calls=%async_computation.21 | async-start | bytes 9437184 | tf_op jit(solution)/shard_map/reduce_scatter | solution.py:312
  1157.7 3.5 copy-start.1
  1162.2 4.3 copy-start.47
  1165.3 15.5 collective-permute-start.2
  1169.4 2.7 copy-start.12
  1169.4 2.7 copy-start.49
  1169.4 2.7 copy-start.59
  1172.1 8.7 copy-start.18
  1172.1 8.7 copy-start.16
  1182.4 2.7 copy-start.20
  1182.4 2.7 copy-start.21
  1196.0 529.9 %reduce-scatter.14.cloned.1.call-start = ((), (), s32[]{:S(2)}) async-start(), calls=%async_computation.20 | async-start | bytes 9437184 | tf_op jit(solution)/shard_map/reduce_scatter | solution.py:311
  1202.9 1064.5 %reduce-scatter.26.cloned.1.call-start = ((), (), s32[]{:S(2)}) async-start(), calls=%async_computation.26 | async-start | bytes 37748736 | tf_op jit(solution)/shard_map/reduce_scatter | solution.py:320
  1220.3 1588.4 %reduce-scatter.24.cloned.1.call-start = ((), (), s32[]{:S(2)}) async-start(), calls=%async_computation.25 | async-start | bytes 37748736 | tf_op jit(solution)/shard_map/reduce_scatter | solution.py:319
  1236.3 2113.9 %reduce-scatter.22.cloned.1.call-start = ((), (), s32[]{:S(2)}) async-start(), calls=%async_computation.24 | async-start | bytes 37748736 | tf_op jit(solution)/shard_map/reduce_scatter | solution.py:318
  1251.9 2163.7 %reduce-scatter.28.cloned.1.call-start = ((), (), s32[]{:S(2)}) async-start(), calls=%async_computation.27 | async-start | bytes 73728
  1252.7 2228.4 %reduce-scatter.30.cloned.1.call-start = ((), (), s32[]{:S(2)}) async-start(), calls=%async_computation.28 | async-start | bytes 73728
  1253.5 4.1 copy-start.23
  1253.5 2250.0 %all-reduce.20.cloned.1.call-start = ((), (), s32[]{:S(2)}) async-start(), calls=%async_computation.19 | async-start | bytes 2097152 | tf_op jit(solution)/shard_map/psum | solution.py:307
  1253.8 3.7 copy-start.26
  1262.2 2623.4 %all-reduce.22.cloned.1.call-start = ((), (), s32[]{:S(2)}) async-start(), calls=%async_computation.29 | async-start | bytes 33554432 | tf_op jit(solution)/shard_map/psum | solution.py:323
  3350.3 153.3 %copy-start.10 = (f32[256,2048]{1,0:T(8,128)S(1)}, f32[256,2048]{1,0:T(8,128)}, u32[]{:S(2)}) copy-start(f32[256,2048]{1,0:T(8,128)} %all-reduce.18.cloned.1.call-done) | copy-start | bytes 6291460
  3885.6 2.7 copy-start.39
  3885.6 4.0 copy-start.38
  3891.9 4.8 copy-start.28
  3896.7 3.7 copy-start.27
  (39 other events, 55.8 us)
Sparse Core Ops, SparseCore 0:
  10.2 73.6 all-gather.15
  86.0 71.3 all-gather.13
  159.5 71.3 all-gather.11
  232.7 72.7 all-gather.17
  310.5 20.6 all-reduce.13
  333.2 227.2 all-gather.19
  562.6 225.4 all-gather.21
  790.1 225.4 all-gather.23
  1028.0 20.6 all-reduce.15
  1092.7 22.4 all-reduce.17
  1126.3 147.9 reduce-scatter.19
  1277.8 146.9 reduce-scatter.17
  1428.4 146.9 reduce-scatter.15
  1579.0 146.9 reduce-scatter.13
  1729.5 537.8 reduce-scatter.25
  2271.1 537.5 reduce-scatter.23
  2812.3 537.8 reduce-scatter.21
  3354.1 61.4 reduce-scatter.27
  3419.5 61.4 reduce-scatter.29
  3483.8 19.6 all-reduce.19
  3506.6 378.9 all-reduce.21
where the time goes:
time: 3920 us; the launch traced here: 3910 us
  waiting for transfers between devices  3500 us (89%)
  matrix products  182 us (5%)
  blocking collectives  125 us (3%)
  local copies, waits for them, and re-layouts  40.8 us (1%)
    reduce_scatter x1, waiting for transfers between devices, local(): lax.psum_scatter(grad_w_gate, 'fsdp', scatter_dimension=0, tiled=True)  542 us
    reduce_scatter x1, waiting for transfers between devices, local(): lax.psum_scatter(grad_down, 'fsdp', scatter_dimension=1, tiled=True)  542 us
    reduce_scatter x1, waiting for transfers between devices, local(): lax.psum_scatter(grad_w_up, 'fsdp', scatter_dimension=0, tiled=True)  541 us
    psum x1, waiting for transfers between devices, local(): lax.psum((shards[0], shards[1], shards[2], shards[3], shards[4], shards[5...  379 us
    all_gather x1, waiting for transfers between devices, local(): lax.all_gather(w_gate, 'fsdp', axis=0, tiled=True)  225 us
    all_gather x1, waiting for transfers between devices, local(): lax.all_gather(w_up, 'fsdp', axis=0, tiled=True)  215 us
    all_gather x1, waiting for transfers between devices, local(): lax.all_gather(w_down, 'fsdp', axis=1, tiled=True)  213 us
    reduce_scatter x1, waiting for transfers between devices, local(): lax.psum_scatter(grad_w_key, 'fsdp', scatter_dimension=0, tiled=True)  151 us
  transfers between devices with their start and end apart: 25, of which 24 were waited for; matrix products, arithmetic and copies ran while one was open for 4% of the time, Pallas kernels for 0%

commit v1 on v0

v1 whole, which is shorter than its diff:
```python
import functools
import math

import jax
import jax.numpy as jnp
from jax import lax
from jax.experimental import pallas as pl
from jax.experimental.pallas import tpu as pltpu
from jax.sharding import PartitionSpec as P

EPS = 1e-06
THETA = 500000.0
BF = jnp.bfloat16
F32 = jnp.float32


def product(left, right):
    return jnp.dot(left, right, preferred_element_type=F32)


def product_left(left, right):
    return jnp.einsum("rd,rf->df", left, right, preferred_element_type=F32)


def product_right(left, right):
    return jnp.einsum("rf,df->rd", left, right, preferred_element_type=F32)


def rotary_tables(positions, head_size):
    half = head_size // 2
    inverse = jnp.exp(-(2.0 * jnp.arange(half, dtype=F32) / head_size) * math.log(THETA))
    angles = positions.astype(F32)[..., None] * inverse
    angles = jnp.concatenate([angles, angles], axis=-1)
    return (jnp.cos(angles), jnp.sin(angles))


def rotate(values, cosine, sine):
    half = values.shape[-1] // 2
    turned = jnp.concatenate([-values[..., half:], values[..., :half]], axis=-1)
    return values * cosine + turned * sine


def rotate_back(grads, cosine, sine):
    half = grads.shape[-1] // 2
    scaled = grads * sine
    turned = jnp.concatenate([scaled[..., half:], -scaled[..., :half]], axis=-1)
    return grads * cosine + turned


def norm_back(values, scale, gain, grads, total, width):
    return scale * gain * grads - values * scale * scale * scale * (total / width)


def layout(lengths, rows):
    segment_ends = jnp.cumsum(lengths)
    segment_starts = segment_ends - lengths
    row_index = jnp.arange(rows, dtype=jnp.int32)
    segment = jnp.sum((row_index[:, None] >= segment_ends[None, :]).astype(jnp.int32), axis=1)
    chosen = segment[:, None] == jnp.arange(lengths.shape[0], dtype=jnp.int32)[None, :]
    offset = row_index - jnp.sum(jnp.where(chosen, segment_starts[None, :], 0), axis=1)
    return (segment, offset)


LINE = 4
CHUNK = 16
MESH_ID = pl.DeviceIdType.MESH
HBM = pl.BlockSpec(memory_space=pl.ANY)
VMEM = pl.BlockSpec(memory_space=pltpu.VMEM)
DMA = pltpu.SemaphoreType.DMA


class Place:
    def __init__(self):
        device = lax.axis_index("fsdp")
        member = lax.rem(device, 2 * LINE)
        self.base = device - member
        self.z = member // 2
        self.y = lax.rem(member, 2)
        self.core = lax.axis_index("tensor")

    def at(self, z, y, core):
        return {"fsdp": self.base + 2 * z + y, "tensor": core}

    def near(self):
        yield None, self.at(self.z, self.y, 1 - self.core)
        yield None, self.at(self.z, 1 - self.y, self.core)
        yield self.z > 0, self.at(self.z - 1, self.y, self.core)
        yield self.z < LINE - 1, self.at(self.z + 1, self.y, self.core)

    def rows(self, z, y, core, count):
        start = ((2 * z + y) * 2 + core) * count
        return pl.ds(pl.multiple_of(start, count), count)


def guarded(condition, action):
    if condition is None:
        action()
    else:
        pl.when(condition)(action)


def greet(place):
    barrier = pltpu.get_barrier_semaphore()
    for condition, device in place.near():

        def signal(device=device):
            pl.semaphore_signal(barrier, inc=1, device_id=device, device_id_type=MESH_ID)

        guarded(condition, signal)
    inside = (place.z > 0) & (place.z < LINE - 1)
    pl.semaphore_wait(barrier, jnp.where(inside, 4, 3))


class Sender:
    def __init__(self):
        self.sent = []

    def __call__(self, condition, make):
        def start():
            make().start()

        guarded(condition, start)
        self.sent.append((condition, make))

    def drain(self):
        for condition, make in self.sent:

            def wait(make=make):
                make().wait_send()

            guarded(condition, wait)


def remote(source, target, send, receive, device):
    return pltpu.make_async_remote_copy(
        src_ref=source,
        dst_ref=target,
        send_sem=send,
        recv_sem=receive,
        device_id=device,
        device_id_type=MESH_ID,
    )


def by_rows(rows, body):
    def step(index, carry):
        body(pl.ds(pl.multiple_of(index * CHUNK, CHUNK), CHUNK))
        return carry

    lax.fori_loop(0, rows // CHUNK, step, 0)


def reduce_scratch(rows, width):
    return [
        pltpu.VMEM((2 * LINE, rows, width), BF),
        pltpu.VMEM((2 * LINE, rows, width), BF),
        pltpu.VMEM((LINE, rows, width), BF),
        pltpu.VMEM((LINE + 1, rows, width), BF),
        pltpu.VMEM((rows, width), F32),
        DMA((2 * LINE,)),
        DMA((2, 2 * LINE)),
        DMA((2, LINE)),
        DMA((2, LINE + 1)),
    ]


def reduce_phase(place, sender, partial, scratch):
    mine, core_in, y_in, line_in, total, local_sem, core_sem, y_sem, line_sem = scratch
    rows = total.shape[0]
    z, y, core = place.z, place.y, place.core
    low = z < LINE // 2
    order = []
    for k in range(LINE - 1):
        down = LINE - 1 - k
        down = jnp.where(down <= z, down - 1, down)
        up = jnp.where(k >= z, k + 1, k)
        order.append(jnp.where(low, down, up))
    order.append(z)

    def fetch(slot):
        half = lax.rem(slot, 2)
        return pltpu.make_async_copy(
            partial.at[place.rows(slot // 2, half, core, rows)], mine.at[slot], local_sem.at[slot]
        )

    def to_core(slot):
        half = lax.rem(slot, 2)
        return remote(
            partial.at[place.rows(slot // 2, half, 1 - core, rows)],
            core_in.at[slot],
            core_sem.at[0, slot],
            core_sem.at[1, slot],
            place.at(z, y, 1 - core),
        )

    def to_y(block):
        return remote(
            mine.at[2 * block + 1 - y],
            y_in.at[block],
            y_sem.at[0, block],
            y_sem.at[1, block],
            place.at(z, 1 - y, core),
        )

    def to_line(block):
        step = jnp.where(block > z, 1, -1)
        slot = jnp.where((step < 0) & (block == z - 1), LINE, block)
        return remote(
            mine.at[2 * block + y],
            line_in.at[slot],
            line_sem.at[0, block],
            line_sem.at[1, slot],
            place.at(z + step, y, core),
        )

    def from_line(slot):
        return remote(
            mine.at[0],
            line_in.at[slot],
            line_sem.at[0, 0],
            line_sem.at[1, slot],
            place.at(z, y, 1 - core),
        )

    for half in (1 - y, y):
        for block in order:
            sender(None, functools.partial(to_core, 2 * block + half))
            fetch(2 * block + half).start()

    for block in order:
        slot = 2 * block + 1 - y
        fetch(slot).wait()
        to_core(slot).wait_recv()

        def add(at, slot=slot):
            value = mine[slot, at].astype(F32) + core_in[slot, at].astype(F32)
            mine[slot, at] = value.astype(BF)

        by_rows(rows, add)
        sender(None, functools.partial(to_y, block))

    for block in order[:-1]:
        slot = 2 * block + y
        fetch(slot).wait()
        to_core(slot).wait_recv()
        to_y(block).wait_recv()
        inner = jnp.where(block > z, z > 0, z < LINE - 1)

        @pl.when(inner)
        def _(block=block, slot=slot):
            from_line(block).wait_recv()

            def add(at):
                value = mine[slot, at].astype(F32) + core_in[slot, at].astype(F32)
                value = value + y_in[block, at].astype(F32)
                mine[slot, at] = (value + line_in[block, at].astype(F32)).astype(BF)

            by_rows(rows, add)

        @pl.when(jnp.logical_not(inner))
        def _(block=block, slot=slot):
            def add(at):
                value = mine[slot, at].astype(F32) + core_in[slot, at].astype(F32)
                mine[slot, at] = (value + y_in[block, at].astype(F32)).astype(BF)

            by_rows(rows, add)

        sender(None, functools.partial(to_line, block))

    slot = 2 * z + y
    fetch(slot).wait()
    to_core(slot).wait_recv()
    to_y(z).wait_recv()

    def start(at):
        value = mine[slot, at].astype(F32) + core_in[slot, at].astype(F32)
        total[at] = value + y_in[z, at].astype(F32)

    by_rows(rows, start)
    for condition, source in ((z > 0, z), (z < LINE - 1, LINE)):

        @pl.when(condition)
        def _(source=source):
            from_line(source).wait_recv()

            def add(at):
                total[at] += line_in[source, at].astype(F32)

            by_rows(rows, add)


def gather_scratch(rows, width):
    return [
        pltpu.VMEM((rows, width), BF),
        DMA((1,)),
        DMA((2, 2 * LINE)),
        DMA((2, LINE)),
        DMA((2, LINE + 2)),
    ]


def gather_phase(place, sender, gathered, scratch):
    own, local_sem, core_sem, y_sem, line_sem = scratch
    rows = own.shape[0]
    z, y, core = place.z, place.y, place.core

    def spot(block, half):
        return gathered.at[place.rows(block, half, core, rows)]

    def to_core(source, block, half):
        return remote(
            source,
            spot(block, half),
            core_sem.at[0, 2 * block + half],
            core_sem.at[1, 2 * block + half],
            place.at(z, y, 1 - core),
        )

    def to_y(source, block):
        return remote(
            source,
            spot(block, y),
            y_sem.at[0, block],
            y_sem.at[1, block],
            place.at(z, 1 - y, core),
        )

    def to_line(source, block, step, index):
        return remote(
            source,
            spot(block, y),
            line_sem.at[0, index],
            line_sem.at[1, block],
            place.at(z + step, y, core),
        )

    keep = pltpu.make_async_copy(own, spot(z, y), local_sem.at[0])
    keep.start()
    sender(z < LINE - 1, functools.partial(to_line, own, z, 1, LINE))
    sender(z > 0, functools.partial(to_line, own, z, -1, LINE + 1))
    sender(None, functools.partial(to_y, own, z))
    sender(None, functools.partial(to_core, own, z, y))

    def took_y(block):
        remote(
            own,
            spot(block, 1 - y),
            y_sem.at[0, block],
            y_sem.at[1, block],
            place.at(z, 1 - y, core),
        ).wait_recv()

    def across(condition, block):
        guarded(condition, functools.partial(took_y, block))
        sender(condition, lambda: to_core(spot(block, 1 - y), block, 1 - y))

    def along(condition, block, step):
        def took():
            to_line(own, block, step, block).wait_recv()

        guarded(condition, took)
        onward = condition & ((z < LINE - 1) if step > 0 else (z > 0))
        sender(onward, lambda: to_line(spot(block, y), block, step, block))
        sender(condition, lambda: to_y(spot(block, y), block))
        sender(condition, lambda: to_core(spot(block, y), block, y))

    for distance in range(1, LINE + 1):
        if distance < LINE:
            along(z >= distance, z - distance, 1)
            along(z + distance < LINE, z + distance, -1)
        if distance == 1:
            across(None, z)
        else:
            across(z >= distance - 1, z - distance + 1)
            across(z + distance - 1 < LINE, z + distance - 1)

    keep.wait()
    for block in range(LINE):
        for half in range(2):
            remote(
                own,
                gathered.at[place.rows(block, half, 1 - core, rows)],
                core_sem.at[0, 2 * block + half],
                core_sem.at[1, 2 * block + half],
                place.at(z, y, 1 - core),
            ).wait_recv()


def pair_scratch():
    return [DMA((3,))]


def pair_phase(place, sender, own, pair, scratch):
    (sem,) = scratch
    rows = own.shape[0]
    spot = pair.at[pl.ds(pl.multiple_of(place.core * rows, rows), rows)]
    keep = pltpu.make_async_copy(own, spot, sem.at[0])
    keep.start()

    def send():
        return remote(
            own, spot, sem.at[1], sem.at[2], place.at(place.z, place.y, 1 - place.core)
        )

    sender(None, send)

    def finish():
        keep.wait()
        other = pair.at[pl.ds(pl.multiple_of((1 - place.core) * rows, rows), rows)]
        remote(
            own, other, sem.at[1], sem.at[2], place.at(place.z, place.y, 1 - place.core)
        ).wait_recv()

    return finish


REDUCE = 9
GATHER = 5


def first_kernel(own_ref, gathered, *scratch):
    place = Place()
    sender = Sender()
    own = scratch[0]
    own[...] = own_ref[...]
    greet(place)
    gather_phase(place, sender, gathered, scratch)
    sender.drain()


def hidden_kernel(partial, tokens, gain, gathered, branch, hidden, *scratch):
    place = Place()
    sender = Sender()
    greet(place)
    reduce_phase(place, sender, partial, scratch[:REDUCE])
    total, own = scratch[4], scratch[REDUCE]
    rows, width = total.shape

    def body(at):
        value = total[at]
        scale = lax.rsqrt(jnp.sum(value * value, axis=1, keepdims=True) / width + EPS)
        result = tokens[at].astype(F32) + value * scale * gain[...]
        branch[at] = value
        hidden[at] = result
        own[at] = result.astype(BF)

    by_rows(rows, body)
    gather_phase(place, sender, gathered, scratch[REDUCE:])
    sender.drain()


def turn_kernel(partial, hidden, cotangent, gain, gathered, outputs, gain_grad, *scratch):
    place = Place()
    sender = Sender()
    greet(place)
    reduce_phase(place, sender, partial, scratch[:REDUCE])
    total, own = scratch[4], scratch[REDUCE]
    out_own = scratch[REDUCE + GATHER]
    rows, width = total.shape
    gain_grad[...] = jnp.zeros_like(gain_grad)

    def body(at):
        value = total[at]
        scale = lax.rsqrt(jnp.sum(value * value, axis=1, keepdims=True) / width + EPS)
        grads = cotangent[at].astype(F32)
        normed = value * scale
        out_own[at] = (hidden[at] + normed * gain[...]).astype(BF)
        gain_grad[...] += jnp.sum(grads * normed, axis=0, keepdims=True)
        gained = gain[...] * grads
        inner = jnp.sum(normed * gained, axis=1, keepdims=True)
        own[at] = (scale * (gained - normed * (inner / width))).astype(BF)

    by_rows(rows, body)
    finish = pair_phase(place, sender, out_own, outputs, scratch[REDUCE + GATHER + 1 :])
    gather_phase(place, sender, gathered, scratch[REDUCE : REDUCE + GATHER])
    finish()
    sender.drain()


def branch_kernel(partial, branch, cotangent, gain, gathered, grad_hidden, gain_grad, *scratch):
    place = Place()
    sender = Sender()
    greet(place)
    reduce_phase(place, sender, partial, scratch[:REDUCE])
    total, own = scratch[4], scratch[REDUCE]
    rows, width = total.shape
    gain_grad[...] = jnp.zeros_like(gain_grad)

    def body(at):
        value = branch[at]
        scale = lax.rsqrt(jnp.sum(value * value, axis=1, keepdims=True) / width + EPS)
        grads = cotangent[at].astype(F32) + total[at]
        grad_hidden[at] = grads
        normed = value * scale
        gain_grad[...] += jnp.sum(grads * normed, axis=0, keepdims=True)
        gained = gain[...] * grads
        inner = jnp.sum(normed * gained, axis=1, keepdims=True)
        own[at] = (scale * (gained - normed * (inner / width))).astype(BF)

    by_rows(rows, body)
    gather_phase(place, sender, gathered, scratch[REDUCE:])
    sender.drain()


def last_kernel(partial, grad_hidden, result, *scratch):
    place = Place()
    sender = Sender()
    greet(place)
    reduce_phase(place, sender, partial, scratch[:REDUCE])
    total = scratch[4]

    def body(at):
        total[at] += grad_hidden[at]

    by_rows(total.shape[0], body)
    finish = pair_phase(place, sender, total, result, scratch[REDUCE:])
    finish()
    sender.drain()


def sum_kernel(value, result, core_in, y_in, held, line_in, sem):
    place = Place()
    sender = Sender()
    z, y, core = place.z, place.y, place.core
    barrier = pltpu.get_barrier_semaphore()
    others = [place.at(z, y, 1 - core), place.at(z, 1 - y, core)]
    others += [place.at(lax.rem(z + k, LINE), y, core) for k in range(1, LINE)]
    for device in others:
        pl.semaphore_signal(barrier, inc=1, device_id=device, device_id_type=MESH_ID)
    pl.semaphore_wait(barrier, len(others))
    first = remote(value, core_in, sem.at[0, 0], sem.at[1, 0], others[0])
    first.start()
    first.wait_recv()
    held[0] = value[...] + core_in[...]
    second = remote(held.at[0], y_in, sem.at[0, 1], sem.at[1, 1], others[1])
    second.start()
    second.wait_recv()
    held[1] = held[0] + y_in[...]
    sends = [
        remote(held.at[1], line_in.at[k - 1], sem.at[0, 1 + k], sem.at[1, 1 + k], others[1 + k])
        for k in range(1, LINE)
    ]
    for send in sends:
        send.start()
    line_in[LINE - 1] = held[1]
    for send in sends:
        send.wait_recv()
    added = jnp.zeros_like(value)
    for source in range(LINE):
        slot = lax.rem(z - source + 2 * LINE - 1, LINE)
        added = added + line_in[slot]
    result[...] = added
    first.wait_send()
    second.wait_send()
    for send in sends:
        send.wait_send()


def talk(kernel, which, shapes, specs, scratch, microseconds):
    def call(*operands):
        return pl.pallas_call(
            kernel,
            out_shape=shapes,
            in_specs=specs[0],
            out_specs=specs[1],
            scratch_shapes=scratch,
            compiler_params=pltpu.CompilerParams(
                collective_id=which, has_side_effects=True, vmem_limit_bytes=48 << 20
            ),
            cost_estimate=pl.CostEstimate(
                flops=0, bytes_accessed=int(microseconds * 3.0e6), transcendentals=0
            ),
            name=kernel.__name__,
        )(*operands)

    return call


class Team:
    def __init__(self, local_heads, rows, width):
        self.fsdp = lax.axis_size("fsdp")
        self.tensor = lax.axis_size("tensor")
        self.size = 2 * LINE
        self.teams = self.fsdp // self.size
        assert self.fsdp % self.size == 0 and self.tensor == 2 and local_heads % self.size == 0
        self.member = lax.rem(lax.axis_index("fsdp"), self.size)
        self.core = lax.axis_index("tensor")
        self.context = lax.axis_index("context")
        self.groups = None
        if self.teams > 1:
            self.groups = [
                [team * self.size + one for one in range(self.size)] for team in range(self.teams)
            ]
        self.rows = rows
        self.width = width
        self.all_low = jax.ShapeDtypeStruct((2 * self.size * rows, width), BF)
        self.own_wide = jax.ShapeDtypeStruct((rows, width), F32)
        self.line_wide = jax.ShapeDtypeStruct((1, width), F32)
        self.reduces = reduce_scratch(rows, width)
        self.gathers = gather_scratch(rows, width)

    def first(self, own):
        return talk(first_kernel, 0, self.all_low, ([VMEM], HBM), self.gathers, 50)(own)

    def hidden(self, partial, tokens, gain):
        return talk(
            hidden_kernel,
            1,
            (self.all_low, self.own_wide, self.own_wide),
            ([HBM, VMEM, VMEM], (HBM, VMEM, VMEM)),
            self.reduces + self.gathers,
            100,
        )(partial, tokens, gain)

    def turn(self, partial, hidden, cotangent, gain):
        pair = jax.ShapeDtypeStruct((2 * self.rows, self.width), BF)
        return talk(
            turn_kernel,
            2,
            (self.all_low, pair, self.line_wide),
            ([HBM, VMEM, VMEM, VMEM], (HBM, HBM, VMEM)),
            self.reduces + self.gathers + [pltpu.VMEM((self.rows, self.width), BF)] + pair_scratch(),
            100,
        )(partial, hidden, cotangent, gain)

    def branch(self, partial, branch, cotangent, gain):
        return talk(
            branch_kernel,
            3,
            (self.all_low, self.own_wide, self.line_wide),
            ([HBM, VMEM, VMEM, VMEM], (HBM, VMEM, VMEM)),
            self.reduces + self.gathers,
            100,
        )(partial, branch, cotangent, gain)

    def last(self, partial, grad_hidden):
        pair = jax.ShapeDtypeStruct((2 * self.rows, self.width), F32)
        return talk(
            last_kernel,
            4,
            pair,
            ([HBM, VMEM], HBM),
            self.reduces + pair_scratch(),
            50,
        )(partial, grad_hidden)

    def total(self, values):
        flat = values.reshape(-1, 128)
        shape = jax.ShapeDtypeStruct(flat.shape, F32)
        scratch = [pltpu.VMEM(flat.shape, F32)] * 2
        scratch += [pltpu.VMEM((2,) + flat.shape, F32), pltpu.VMEM((LINE,) + flat.shape, F32)]
        scratch += [DMA((2, LINE + 1))]
        which = 5 + self.sums
        self.sums += 1
        return talk(sum_kernel, which, shape, ([VMEM], VMEM), scratch, 10)(flat).reshape(
            values.shape
        )

    sums = 0

    def half(self, array, axis):
        count = array.shape[axis] // 2
        return lax.dynamic_slice_in_dim(array, self.context * count, count, axis)

    def swap(self, pieces):
        if self.teams > 1:
            pieces = jnp.concatenate([pieces] * self.teams, axis=0)
        return lax.all_to_all(pieces, "fsdp", split_axis=0, concat_axis=0, tiled=True)

    def columns_in(self, weights):
        pieces = []
        for weight in weights:
            rows, columns = weight.shape
            part = self.half(weight, 0).reshape(rows // 2, self.size, columns // self.size)
            pieces.append(part.transpose(1, 0, 2))
        came = self.swap(jnp.concatenate(pieces, axis=2))
        whole = lax.all_gather(came, "context", axis=1, tiled=True)
        return whole.reshape(self.fsdp * rows, whole.shape[2])

    def rows_in(self, weight):
        rows, columns = weight.shape
        pieces = self.half(weight.reshape(self.size, rows // self.size, columns), 1)
        came = self.swap(pieces).transpose(1, 0, 2)
        came = came.reshape(came.shape[0], self.fsdp * columns)
        return lax.all_gather(came, "context", axis=0, tiled=True)

    def back(self, pieces):
        pieces = lax.psum_scatter(
            pieces.astype(BF), "context", scatter_dimension=1, tiled=True
        )
        came = lax.all_to_all(pieces, "fsdp", split_axis=0, concat_axis=0, tiled=True)
        if self.teams > 1:
            came = came.reshape((self.teams, self.size) + came.shape[1:]).astype(F32)
            came = jnp.sum(came, axis=0).astype(BF)
        return lax.all_gather(came, "context", axis=1, tiled=True)

    def columns_out(self, grad, count):
        rows, columns = grad.shape
        came = self.back(grad.reshape(self.fsdp, rows // self.fsdp, columns))
        return [
            part.transpose(1, 0, 2).reshape(rows // self.fsdp, -1).astype(F32)
            for part in jnp.split(came, count, axis=2)
        ]

    def rows_out(self, grad):
        rows, columns = grad.shape
        came = self.back(grad.reshape(rows, self.fsdp, columns // self.fsdp).transpose(1, 0, 2))
        return came.reshape(self.size * rows, columns // self.fsdp).astype(F32)


def local(
    tokens,
    cont_lengths,
    w_query,
    w_key,
    w_value,
    w_output,
    query_gain,
    key_gain,
    attn_gain,
    w_gate,
    w_up,
    w_down,
    mlp_gain,
    cotangent,
):
    rows = tokens.shape[0]
    width = tokens.shape[1]
    fsdp = lax.axis_size("fsdp")
    tensor = lax.axis_size("tensor")
    local_heads = query_gain.shape[0]
    head_size = w_query.shape[1] // local_heads
    own_rows = rows // tensor
    team = Team(local_heads, own_rows, width)
    groups = team.size
    team_rows = groups * rows
    heads = local_heads // team.size
    later = lax.axis_index("context") == 1

    tokens_own = lax.dynamic_slice_in_dim(tokens, team.core * own_rows, own_rows, 0)
    grad_out = lax.dynamic_slice_in_dim(cotangent, team.core * own_rows, own_rows, 0)
    tokens_all = team.first(tokens_own)

    qkv_w = team.columns_in([w_query, w_key, w_value])
    output_w = team.rows_in(w_output)

    fsdp_gains = jnp.concatenate(
        [query_gain.reshape(-1), key_gain.reshape(-1), attn_gain, mlp_gain]
    )
    all_gains = lax.all_gather(fsdp_gains, "fsdp", axis=0, tiled=False).astype(F32)
    cut = query_gain.size
    query_gains = all_gains[:, :cut].reshape(fsdp, local_heads, -1)
    key_gains = all_gains[:, cut : 2 * cut].reshape(fsdp, local_heads, -1)
    query_gains = query_gains.transpose(1, 0, 2).reshape(local_heads, head_size)
    key_gains = key_gains.transpose(1, 0, 2).reshape(local_heads, head_size)
    flat_query = lax.dynamic_slice_in_dim(query_gains, team.member * heads, heads, 0).reshape(-1)
    flat_key = lax.dynamic_slice_in_dim(key_gains, team.member * heads, heads, 0).reshape(-1)
    gain_attn = all_gains[:, 2 * cut : 2 * cut + attn_gain.size].reshape(1, -1)
    gain_mlp = all_gains[:, 2 * cut + attn_gain.size :].reshape(1, -1)

    lengths = lax.all_gather(
        cont_lengths, "fsdp", axis=0, tiled=True, axis_index_groups=team.groups
    )
    segment, offset = jax.vmap(lambda one: layout(one, rows))(lengths)
    row_index = jnp.arange(rows, dtype=jnp.int32)
    positions = jnp.where(later, rows + offset, row_index[None, :])
    own_segment = jnp.where(later, segment, -1)
    cosine, sine = rotary_tables(positions, head_size)
    cosine = cosine[:, :, None, :]
    sine = sine[:, :, None, :]

    pair_w = team.columns_in([w_gate, w_up])
    down_w = team.rows_in(w_down)

    by_head = (groups, rows, heads, head_size)
    raw = product(tokens_all, qkv_w)
    query_raw, key_raw, value_raw = jnp.split(raw, 3, axis=1)
    sums = team.total(
        jnp.stack([jnp.sum(query_raw * query_raw, axis=1), jnp.sum(key_raw * key_raw, axis=1)])
    )
    scale_query = lax.rsqrt(sums[0] / width + EPS)[:, None]
    scale_key = lax.rsqrt(sums[1] / width + EPS)[:, None]
    query_norm = query_raw * scale_query * flat_query
    key_norm = key_raw * scale_key * flat_key
    query_low = rotate(query_norm.reshape(by_head), cosine, sine).astype(BF)
    key_low = rotate(key_norm.reshape(by_head), cosine, sine).astype(BF)
    value_low = value_raw.reshape(by_head).astype(BF)
    sent = lax.ppermute(jnp.stack([key_low, value_low]), "context", [(0, 1)])
    keys_all = jnp.concatenate([sent[0], key_low], axis=1)
    values_all = jnp.concatenate([sent[1], value_low], axis=1)
    key_index = jnp.arange(2 * rows, dtype=jnp.int32)
    key_segment = jnp.concatenate([jnp.full((groups, rows), -2, jnp.int32), own_segment], axis=1)
    remote = (key_index < rows)[None, None, :] & later
    own_keys = (
        (key_index >= rows)[None, None, :]
        & (key_index[None, None, :] - rows <= row_index[None, :, None])
        & (key_segment[:, None, :] == own_segment[:, :, None])
    )
    allowed = (remote | own_keys)[:, None]
    scale = 1.0 / math.sqrt(head_size)
    scores = (
        jnp.einsum("gqhd,gkhd->ghqk", query_low, keys_all, preferred_element_type=F32) * scale
    )
    scores = jnp.where(allowed, scores, -1e30)
    highest = jnp.max(scores, axis=-1, keepdims=True)
    weights = jnp.exp(scores - highest)
    probs = weights / jnp.sum(weights, axis=-1, keepdims=True)
    probs_low = probs.astype(BF)
    mixed = jnp.einsum("ghqk,gkhd->gqhd", probs_low, values_all, preferred_element_type=F32)
    attended_low = mixed.reshape(team_rows, heads * head_size).astype(BF)
    hidden_all, attn_sum, hidden = team.hidden(
        product(attended_low, output_w).astype(BF), tokens_own, gain_attn
    )

    gate, upward = jnp.split(product(hidden_all, pair_w), 2, axis=1)
    sigma = jax.nn.sigmoid(gate)
    inner_low = (gate * sigma * upward).astype(BF)
    grad_mlp_all, outputs, grad_mlp_gain = team.turn(
        product(inner_low, down_w).astype(BF), hidden, grad_out, gain_mlp
    )
    grad_w_down = team.rows_out(product_left(inner_low, grad_mlp_all))
    grad_inner = product_right(grad_mlp_all, down_w)
    grad_gate_low = (grad_inner * upward * sigma * (1.0 + gate * (1.0 - sigma))).astype(BF)
    grad_up_low = (grad_inner * gate * sigma).astype(BF)
    grad_pair = jnp.concatenate([grad_gate_low, grad_up_low], axis=1)
    grad_w_gate, grad_w_up = team.columns_out(product_left(hidden_all, grad_pair), 2)
    grad_branch_all, grad_hidden, grad_attn_gain = team.branch(
        product_right(grad_pair, pair_w).astype(BF), attn_sum, grad_out, gain_attn
    )
    grad_w_output = team.rows_out(product_left(attended_low, grad_branch_all))
    grad_attended = product_right(grad_branch_all, output_w).astype(BF).reshape(by_head)

    grad_probs = jnp.einsum("gqhd,gkhd->ghqk", grad_attended, values_all, preferred_element_type=F32)
    centre = jnp.sum(probs * grad_probs, axis=-1, keepdims=True)
    grad_scores = (probs * (grad_probs - centre)).astype(BF)
    grad_query_rot = (
        jnp.einsum("ghqk,gkhd->gqhd", grad_scores, keys_all, preferred_element_type=F32) * scale
    )
    grad_keys = (
        jnp.einsum("ghqk,gqhd->gkhd", grad_scores, query_low, preferred_element_type=F32) * scale
    )
    grad_values = jnp.einsum("ghqk,gqhd->gkhd", probs_low, grad_attended, preferred_element_type=F32)
    returned = lax.ppermute(
        jnp.stack([grad_keys[:, :rows], grad_values[:, :rows]]).astype(BF), "context", [(1, 0)]
    ).astype(F32)
    grad_key_rot = grad_keys[:, rows:] + returned[0]
    grad_value_low = (grad_values[:, rows:] + returned[1]).reshape(team_rows, -1).astype(BF)
    grad_query_norm = rotate_back(grad_query_rot, cosine, sine).reshape(team_rows, -1)
    grad_key_norm = rotate_back(grad_key_rot, cosine, sine).reshape(team_rows, -1)
    grad_query_gain = jnp.sum(grad_query_norm * query_raw * scale_query, axis=0)
    grad_key_gain = jnp.sum(grad_key_norm * key_raw * scale_key, axis=0)
    totals = team.total(
        jnp.stack(
            [
                jnp.sum(query_raw * flat_query * grad_query_norm, axis=1),
                jnp.sum(key_raw * flat_key * grad_key_norm, axis=1),
            ]
        )
    )
    grad_query_low = norm_back(
        query_raw, scale_query, flat_query, grad_query_norm, totals[0][:, None], width
    ).astype(BF)
    grad_key_low = norm_back(
        key_raw, scale_key, flat_key, grad_key_norm, totals[1][:, None], width
    ).astype(BF)
    grad_qkv = jnp.concatenate([grad_query_low, grad_key_low, grad_value_low], axis=1)
    grad_w_query, grad_w_key, grad_w_value = team.columns_out(product_left(tokens_all, grad_qkv), 3)
    input_grad = team.last(product_right(grad_qkv, qkv_w).astype(BF), grad_hidden)

    all_width = heads * head_size
    place = (team.core * team.size + team.member) * all_width
    spread = jnp.zeros((2, tensor * local_heads * head_size), F32)
    spread = lax.dynamic_update_slice(
        spread, jnp.stack([grad_query_gain, grad_key_gain]), (0, place)
    )
    gains = lax.psum(
        jnp.concatenate([spread.reshape(-1), grad_attn_gain.reshape(-1), grad_mlp_gain.reshape(-1)]),
        ("fsdp", "context", "tensor"),
    )
    device = lax.axis_index("fsdp")
    head_gains = gains[: 2 * tensor * local_heads * head_size].reshape(
        2, tensor, local_heads, fsdp, head_size // fsdp
    )
    head_gains = lax.dynamic_slice(
        head_gains,
        (0, team.core, 0, device, 0),
        (2, 1, local_heads, 1, head_size // fsdp),
    ).reshape(2, local_heads, head_size // fsdp)
    row_gains = gains[2 * tensor * local_heads * head_size :].reshape(2, fsdp, width // fsdp)
    row_gains = lax.dynamic_slice_in_dim(row_gains, device, 1, 1).reshape(2, width // fsdp)
    return (
        outputs,
        input_grad,
        grad_w_query,
        grad_w_key,
        grad_w_value,
        grad_w_output,
        head_gains[0],
        head_gains[1],
        row_gains[0],
        grad_w_gate,
        grad_w_up,
        grad_w_down,
        row_gains[1],
    )


def solution(mesh):
    return jax.shard_map(
        local,
        mesh=mesh,
        in_specs=(
            P(("fsdp", "context"), None),
            P("fsdp", None),
            P("fsdp", "tensor"),
            P("fsdp", "tensor"),
            P("fsdp", "tensor"),
            P("tensor", "fsdp"),
            P("tensor", "fsdp"),
            P("tensor", "fsdp"),
            P("fsdp"),
            P("fsdp", "tensor"),
            P("fsdp", "tensor"),
            P("tensor", "fsdp"),
            P("fsdp"),
            P(("fsdp", "context"), None),
        ),
        out_specs=(
            P(("fsdp", "context"), None),
            P(("fsdp", "context"), None),
            P("fsdp", "tensor"),
            P("fsdp", "tensor"),
            P("fsdp", "tensor"),
            P("tensor", "fsdp"),
            P("tensor", "fsdp"),
            P("tensor", "fsdp"),
            P("fsdp"),
            P("fsdp", "tensor"),
            P("fsdp", "tensor"),
            P("tensor", "fsdp"),
            P("fsdp"),
        ),
        check_vma=False,
    )
```

time: 3920 us -> 1100 us (0.28)
  waiting for transfers between devices: 3500 us -> 134 us
  Pallas kernels: 0 us -> 498 us
  starting transfers between devices: 10.6 us -> 59.8 us
  matrix products: 182 us -> 137 us
    reduce_scatter x7 -> x4, waiting for transfers between devices: 2090 us -> 58.8 us  [back(): lax.psum_scatter(pieces.astype(BF), 'context', scatter_dimension=1, tiled...]
    all_gather x7 -> x6, waiting for transfers between devices: 857 us -> 0.01 us  [the longest x3 0.01 us: back(): return lax.all_gather(came, 'context', axis=1, tiled=True)]
    pallas_call x0 -> x7, Pallas kernels: none -> 498 us  [call(): pl.pallas_call(kernel, out_shape=shapes, in_specs=specs[0], out_specs=spe...]
    psum x5 -> x0, waiting for transfers between devices: 425 us -> none  [the longest x1 379 us: local(): lax.psum((shards[0], shards[1], shards[2], shards[3], shards[4], shards[5...]
    unnamed x23 -> x10, waiting for transfers between devices: 102 us -> 1.58 us
    all_to_all x0 -> x8, starting transfers between devices: none -> 54.5 us  [the longest x4 29.1 us: swap(): lax.all_to_all(pieces, 'fsdp', split_axis=0, concat_axis=0, tiled=True)]
    all_to_all x0 -> x8, waiting for transfers between devices: none -> 52.2 us  [the longest x4 44.6 us: back(): lax.all_to_all(pieces, 'fsdp', split_axis=0, concat_axis=0, tiled=True)]
    dot_general x27 -> x17, matrix products: 182 us -> 131 us  [the longest x4 43.9 us: product_right(): return jnp.einsum('rf,df->rd', left, right, preferred_element_type=F32)]
  transfers between devices with their start and end apart: 25 -> 20, of which waited for: 24 -> 7; matrix products, arithmetic and copies ran while one was open for 4% -> 15% of each run, Pallas kernels for 0% -> 26%
where the time goes in v1:
time: 1100 us; the launch traced here: 1090 us
  Pallas kernels  498 us (45%)
  matrix products  137 us (12%)
  waiting for transfers between devices  134 us (12%)
  blocking collectives  123 us (11%)
  local copies, waits for them, and re-layouts  66.2 us (6%)
  starting transfers between devices  59.8 us (5%)
  other arithmetic  57.3 us (5%)
  between operations  15.3 us (1%)
    pallas_call x7, Pallas kernels, call(): pl.pallas_call(kernel, out_shape=shapes, in_specs=specs[0], out_specs=spe...  498 us
    reduce_scatter x4, waiting for transfers between devices, back(): lax.psum_scatter(pieces.astype(BF), 'context', scatter_dimension=1, tiled...  58.8 us
    all_to_all x4, waiting for transfers between devices, back(): lax.all_to_all(pieces, 'fsdp', split_axis=0, concat_axis=0, tiled=True)  44.6 us
    dot_general x4, matrix products, product_right(): return jnp.einsum('rf,df->rd', left, right, preferred_element_type=F32)  43.9 us
    psum x1, blocking collectives, local(): lax.psum(jnp.concatenate([spread.reshape(-1), grad_attn_gain.reshape(-1),...  40.1 us
    dot_general x4, matrix products, product_left(): return jnp.einsum('rd,rf->df', left, right, preferred_element_type=F32)  39.1 us
    dot_general x4, matrix products, product(): return jnp.dot(left, right, preferred_element_type=F32)  36.3 us
    all_gather x1, blocking collectives, local(): lax.all_gather(fsdp_gains, 'fsdp', axis=0, tiled=False).astype(F32)  29.3 us
  transfers between devices with their start and end apart: 20, of which 7 were waited for; matrix products, arithmetic and copies ran while one was open for 15% of the time, Pallas kernels for 26%

profile of v1, /device:TPU:16, one launch (start us, length us, event | category | flops | bytes accessed | tf_op | source)
XLA Modules:
  0.0 1090.2 jit_solution(13457970077645626667)
XLA Ops:
  10.9 6.2 all-to-all-start
  17.0 2.7 constant_dynamic-slice_fusion.5
  19.7 2.3 copy.205
  23.3 3.0 pad_maximum_fusion.3
  26.3 7.6 all-to-all-done
  33.9 7.6 all-to-all-start.2
  42.7 94.2 %first_kernel.1 = bf16[2048,2048]{1,0:T(8,128)(2,1)} custom-call(bf16[128,2048]{1,0:T(8,128)(2,1)S(1)} %constant_dynamic-slice_fusion.14.own_ref.tokens), custom_call_target="tpu_custom_call" | custom-call | bytes 150000000 | tf_op jit(solution)/shard_map/first_kernel/pallas_call | solution.py:561
  137.2 29.3 %all-gather.1 = bf16[8,1,768]{2,1,0:T(2,128)(2,1)S(1)} all-gather(bf16[1,1,768]{2,1,0:T(2,128)(2,1)S(1)} %reshape.689), channel_id=2, replica_groups=mesh['fsdp'=8,'context'=2,'tensor'=2] {'fsdp'}, dimensions={0}, use_global_device_ids=true | all-gather | bytes 13824 | tf_op jit(solution)/shard_map/all_gather | solution.py:750
  166.8 17.0 %all-gather.2 = s32[8,1,4]{2,1,0:T(1,128)S(1)} all-gather(s32[1,1,4]{2,1,0:T(1,128)S(1)} %bitcast.305), channel_id=1, replica_groups=mesh['fsdp'=8,'context'=2,'tensor'=2] {'fsdp'}, dimensions={0}, use_global_device_ids=true | all-gather | bytes 144 | tf_op jit(solution)/shard_map/all_gather | solution.py:761
  185.0 9.3 all-to-all-start.1
  199.4 2.6 copy.164
  202.0 7.5 fusion.63
  211.9 6.0 all-to-all-start.3
  218.0 21.8 %sum_kernel.2 = f32[32,128]{1,0:T(8,128)S(1)} custom-call(f32[32,128]{1,0:T(8,128)S(1)} %reshape.650.value), custom_call_target="tpu_custom_call" | custom-call | bytes 30000000 | tf_op jit(solution)/shard_map/sum_kernel/pallas_call | solution.py:561
  239.9 2.7 multiply_multiply_fusion
  244.3 4.7 fusion.16
  250.1 3.4 collective-permute-start
  253.5 27.4 %all_gather.37 = bf16[128,2048]{1,0:T(8,128)(2,1)} all-gather(bf16[64,2048]{1,0:T(8,128)(2,1)S(1)} %bitcast.277), channel_id=1, replica_groups=mesh['fsdp'=8,'context'=2,'tensor'=2] {'context'}, dimensions={0}, use_global_device_ids=true | all-gather | bytes 786432 | tf_op jit(solution)/shard_map/all_gather | solution.py:685
  280.9 2.2 copy.174
  283.5 5.8 fusion.20
  291.4 5.0 fusion.18
  296.5 2.1 slice_bitcast_fusion.3
  298.6 5.1 fusion.62
  303.7 4.1 fusion.10
  309.2 5.6 convolution_convert_fusion.3.partial
  314.9 107.5 %hidden_kernel.1 = (bf16[2048,2048]{1,0:T(8,128)(2,1)}, f32[128,2048]{1,0:T(8,128)S(1)}, f32[128,2048]{1,0:T(8,128)S(1)}) custom-call(bf16[2048,2048]{1,0:T(8,128)(2,1)} %convolution_convert_fusion.3.partial, bf16[128,2048]{1,0:T(8,128)(2,1)S(1)} %constant_dynamic-slice_fusion.14.own_ref.tokens, f32[1,2048]{1,0:T(1,128)S(1)} %bitcast.247), custom_call_target="tpu_custom_call" | custom-call | bytes 300000000 | tf_op jit(solution)/shard_map/hidden_kernel/pallas_call | solution.py:561
  423.4 6.4 copy.173
  429.8 13.1 %fusion.64 = f32[2048,1024]{0,1:T(8,128)S(1)} fusion(bf16[2048,2048]{1,0:T(8,128)(2,1)} %get-tuple-element.22, bf16[2048,1024]{1,0:T(8,128)(2,1)} %bitcast.265), kind=kOutput, calls=%fused_computation.177 | convolution fusion | flops 8589934592 | bytes 20971520 | tf_op jit(solution)/shard_map/dot_general | solution.py:18
  442.9 3.3 copy-done.12
  446.2 2.6 multiply_convert_fusion.3
  448.8 10.1 convolution_convert_fusion.2.partial
  458.9 103.9 %turn_kernel.1 = (bf16[2048,2048]{1,0:T(8,128)(2,1)}, bf16[256,2048]{1,0:T(8,128)(2,1)S(1)}, f32[1,2048]{1,0:T(1,128)S(1)}) custom-call(bf16[2048,2048]{1,0:T(8,128)(2,1)} %convolution_convert_fusion.2.partial, f32[128,2048]{1,0:T(8,128)S(1)} %get-tuple-element.23.hidden, bf16[128,2048]{1,0:T(8,128)(2,1)S(1)} %constant_dynamic-slice_fusion.3.cotangent, ...), custom_call_target="tpu_custom_call" | custom-call | bytes 300000000 | tf_op jit(solution)/shard_map/turn_kernel/pallas_call | solution.py:561
  562.8 14.6 %multiply_convert_fusion.2 = (bf16[2048,512]{0,1:T(8,128)(2,1)}, bf16[2048,512]{0,1:T(8,128)(2,1)}) fusion(f32[2048,1024]{0,1:T(8,128)} %copy-done.12, bf16[2048,2048]{1,0:T(8,128)(2,1)} %get-tuple-element.25, bf16[512,2048]{0,1:T(8,128)(2,1)} %all-gather.14.cloned.1.call-done), kind=kOutput, calls=%fused_computation.11 | convolution fusion | flops 4308598784 | bytes 23068672 | tf_op jit(solution)/shard_map/rf,df->rd/dot_general | solution.py:26
  577.4 13.6 %convolution_convert_fusion.1.partial = bf16[2048,2048]{1,0:T(8,128)(2,1)} fusion(bf16[2048,1024]{1,0:T(8,128)(2,1)S(1)} %bitcast.266, bf16[2048,512]{0,1:T(8,128)(2,1)} %get-tuple-element.40, bf16[2048,512]{0,1:T(8,128)(2,1)} %get-tuple-element.39), kind=kOutput, calls=%fused_computation.2 | convolution fusion | flops 8602517504 | bytes 16777216 | tf_op jit(solution)/shard_map/rf,df->rd/dot_general | solution.py:26
  591.1 103.2 %branch_kernel.1 = (bf16[2048,2048]{1,0:T(8,128)(2,1)}, f32[128,2048]{1,0:T(8,128)S(1)}, f32[1,2048]{1,0:T(1,128)S(1)}) custom-call(bf16[2048,2048]{1,0:T(8,128)(2,1)} %convolution_convert_fusion.1.partial, f32[128,2048]{1,0:T(8,128)S(1)} %copy-done.5, bf16[128,2048]{1,0:T(8,128)(2,1)S(1)} %constant_dynamic-slice_fusion.3.cotangent, f32[1,2048]{1,0:T(1,128)S(1)} %bitcast.248), custom_call_target="tpu_custom_call" | custom-call | bytes 300000000 | tf_op jit(solution)/shard_map/branch_kernel/pallas_call | solution.py:561
  694.3 5.9 convolution_convert_fusion.7
  706.4 4.6 fusion.38
  711.4 21.4 %collective-permute-done.1 = bf16[2,8,256,1,128]{4,2,1,3,0:T(8,128)(2,1)S(1)} collective-permute-done((bf16[2,8,256,1,128]{4,2,1,3,0:T(8,128)(2,1)S(1)}, bf16[2,8,256,1,128]{4,2,1,3,0:T(8,128)(2,1)S(1)}, u32[]{:S(2)}, u32[]{:S(2)}) %collective-permute-start.1) | collective-permute-done | bytes 1048608 | tf_op jit(solution)/shard_map/ppermute | solution.py:843
  733.0 4.8 maximum_add_fusion
  738.2 4.2 maximum_add_fusion.1
  744.0 8.5 sum_kernel.3
  752.6 3.7 fusion.27
  756.3 9.5 convolution_convert_fusion.6
  766.0 8.5 convolution_convert_fusion.5
  776.1 13.9 %convolution_convert_fusion.4 = bf16[2048,1024]{1,0:T(8,128)(2,1)} fusion(bf16[2048,2048]{1,0:T(8,128)(2,1)} %get-tuple-element.22, bf16[2048,512]{0,1:T(8,128)(2,1)} %get-tuple-element.40, bf16[2048,512]{0,1:T(8,128)(2,1)} %get-tuple-element.39), kind=kOutput, calls=%fused_computation.16 | convolution fusion | flops 8600420352 | bytes 16777216 | tf_op jit(solution)/shard_map/rd,rf->df/dot_general | solution.py:22
  791.5 6.0 all-to-all-start.4
  797.6 28.6 %reduce-scatter.11.cloned.1.call-done = bf16[8,256,256]{2,1,0:T(8,128)(2,1)} async-done(((bf16[8,512,256]{2,1,0:T(8,128)(2,1)}), bf16[8,256,256]{2,1,0:T(8,128)(2,1)}) %reduce-scatter.11.cloned.1.call-update) | async-done | bytes 1048592 | tf_op jit(solution)/shard_map/reduce_scatter | solution.py:688
  826.1 6.0 all-to-all-start.7
  832.2 11.7 %copy.200 = bf16[2048,2048]{1,0:T(8,128)(2,1)} copy(bf16[2048,2048]{0,1:T(8,128)(2,1)} %bitcast.258) | data formatting | bytes 16777216 | tf_op jit(solution)/shard_map/rd,rf->df/dot_general | solution.py:22
  843.9 7.2 fusion.9
  851.2 3.4 all-to-all-done.7
  854.6 28.7 %reduce-scatter.9.cloned.1.call-done = bf16[8,128,1024]{2,1,0:T(8,128)(2,1)} async-done(((bf16[8,256,1024]{2,1,0:T(8,128)(2,1)}), bf16[8,128,1024]{2,1,0:T(8,128)(2,1)}) %reduce-scatter.9.cloned.1.call-update) | async-done | bytes 2097168 | tf_op jit(solution)/shard_map/reduce_scatter | solution.py:688
  883.3 6.0 all-to-all-start.6
  890.1 2.8 copy.189
  892.9 41.2 %all-to-all-done.6 = bf16[8,128,1024]{2,1,0:T(8,128)(2,1)} async-done(((bf16[8,128,1024]{2,1,0:T(8,128)(2,1)}), bf16[8,128,1024]{2,1,0:T(8,128)(2,1)}, u32[]{:S(2)}, u32[]{:S(2)}) %all-to-all-start.6) | async-done | bytes 2097184 | tf_op jit(solution)/shard_map/all_to_all | solution.py:691
  934.2 7.3 all-to-all-start.5
  941.5 9.7 convolution_convert_fusion.partial
  951.3 40.1 %psum.7 = f32[8192]{0:T(1024)S(1)} all-reduce(f32[8192]{0:T(1024)S(1)} %pad_maximum_fusion.13), channel_id=1, replica_groups=mesh['fsdp'=8,'context'=2,'tensor'=2] {'fsdp','context','tensor'}, use_global_device_ids=true, to_apply=%region_14.15 | all-reduce | flops 8192 | bytes 65536 | tf_op jit(solution)/shard_map/psum | solution.py:876
  991.5 58.7 %last_kernel.1 = f32[256,2048]{1,0:T(8,128)S(1)} custom-call(bf16[2048,2048]{1,0:T(8,128)(2,1)} %convolution_convert_fusion.partial, f32[128,2048]{1,0:T(8,128)S(1)} %get-tuple-element.28.grad_hidden), custom_call_target="tpu_custom_call" | custom-call | bytes 150000000 | tf_op jit(solution)/shard_map/last_kernel/pallas_call | solution.py:561
  1052.7 9.3 all_gather.41
  1070.0 2.5 bitcast_convert_fusion
  1072.5 3.4 convert_bitcast_fusion
  1075.8 2.5 copy.212
  1078.3 2.6 copy.213
  (199 shorter events, 48.3 us)
Async XLA Ops:
  7.2 187.8 %copy-start = (bf16[4096,256]{1,0:T(8,128)(2,1)S(1)}, bf16[4096,256]{1,0:T(8,128)(2,1)}, u32[]{:S(2)}) copy-start(bf16[4096,256]{1,0:T(8,128)(2,1)} %param.25) | copy-start | bytes 6291460
  10.9 23.1 %all-to-all-start = ((bf16[8,128,384]{1,2,0:T(8,128)(2,1)}), bf16[8,128,384]{1,2,0:T(8,128)(2,1)}, u32[]{:S(2)}, u32[]{:S(2)}) async-start(bf16[8,128,384]{1,2,0:T(8,128)(2,1)} %pad_maximum_fusion.10), calls=%async_computation | async-start | bytes 1572864 | tf_op jit(solution)/shard_map/all_to_all | solution.py:668
  33.9 151.0 %all-to-all-start.2 = ((bf16[8,128,1024]{1,2,0:T(8,128)(2,1)}), bf16[8,128,1024]{1,2,0:T(8,128)(2,1)}, u32[]{:S(2)}, u32[]{:S(2)}) async-start(bf16[8,128,1024]{1,2,0:T(8,128)(2,1)} %pad_maximum_fusion.3), calls=%async_computation.2 | async-start | bytes 4194304 | tf_op jit(solution)/shard_map/all_to_all | solution.py:668
  41.6 157.8 %all-gather.10.cloned.1.call-start = ((), (), s32[]{:S(2)}) async-start(), calls=%async_computation.12 | async-start | bytes 2359296 | tf_op jit(solution)/shard_map/all_gather | solution.py:677
  42.6 94.3 %copy-start.36 = (bf16[8,16]{1,0:T(8,128)(2,1)S(1)}, bf16[8,16]{1,0:T(8,128)(2,1)}, u32[]{:S(2)}) copy-start(bf16[8,16]{1,0:T(8,128)(2,1)} %param.20) | copy-start | bytes 772
  42.7 94.4 %copy-start.37 = (bf16[8,16]{1,0:T(8,128)(2,1)S(1)}, bf16[8,16]{1,0:T(8,128)(2,1)}, u32[]{:S(2)}) copy-start(bf16[8,16]{1,0:T(8,128)(2,1)} %param.21) | copy-start | bytes 772
  42.7 94.5 %copy-start.39 = (bf16[256]{0:T(256)(128)(2,1)S(1)}, bf16[256]{0:T(256)(128)(2,1)}, u32[]{:S(2)}) copy-start(bf16[256]{0:T(256)(128)(2,1)} %param.26) | copy-start | bytes 1540
  42.7 94.5 %copy-start.40 = (bf16[256]{0:T(256)(128)(2,1)S(1)}, bf16[256]{0:T(256)(128)(2,1)}, u32[]{:S(2)}) copy-start(bf16[256]{0:T(256)(128)(2,1)} %param.22) | copy-start | bytes 1540
  42.7 124.1 %copy-start.38 = (s32[1,4]{1,0:T(1,128)S(1)}, s32[1,4]{1,0:T(1,128)}, u32[]{:S(2)}) copy-start(s32[1,4]{1,0:T(1,128)} %param.15) | copy-start | bytes 52
  42.7 141.5 %copy-start.35 = (bf16[1024,256]{1,0:T(8,128)(2,1)S(1)}, bf16[1024,256]{1,0:T(8,128)(2,1)}, u32[]{:S(2)}) copy-start(bf16[1024,256]{1,0:T(8,128)(2,1)} %param.19) | copy-start | bytes 1572868
  185.0 26.9 %all-to-all-start.1 = ((bf16[8,64,256]{2,1,0:T(8,128)(2,1)}), bf16[8,64,256]{2,1,0:T(8,128)(2,1)S(1)}, u32[]{:S(2)}, u32[]{:S(2)}) async-start(bf16[8,64,256]{2,1,0:T(8,128)(2,1)} %constant_dynamic-slice_fusion.7), calls=%async_computation.1 | async-start | bytes 524288 | tf_op jit(solution)/shard_map/all_to_all | solution.py:668
  194.3 229.1 %all-gather.12.cloned.1.call-start = ((), (), s32[]{:S(2)}) async-start(), calls=%async_computation.13 | async-start | bytes 6291456 | tf_op jit(solution)/shard_map/all_gather | solution.py:677
  209.4 1.8 copy-start.7
  211.9 69.0 %all-to-all-start.3 = ((bf16[8,256,256]{2,1,0:T(8,128)(2,1)}), bf16[8,256,256]{2,1,0:T(8,128)(2,1)}, u32[]{:S(2)}, u32[]{:S(2)}) async-start(bf16[8,256,256]{2,1,0:T(8,128)(2,1)} %constant_dynamic-slice_fusion.4), calls=%async_computation.3 | async-start | bytes 2097152 | tf_op jit(solution)/shard_map/all_to_all | solution.py:668
  217.9 230.9 %all-gather.14.cloned.1.call-start = ((), (), s32[]{:S(2)}) async-start(), calls=%async_computation.14 | async-start | bytes 3145728 | tf_op jit(solution)/shard_map/all_gather | solution.py:685
  242.5 1.7 copy-start.18
  242.5 6.4 copy-start.25
  250.1 46.4 %collective-permute-start = (bf16[2,8,256,1,128]{4,2,1,3,0:T(8,128)(2,1)}, bf16[2,8,256,1,128]{4,2,1,3,0:T(8,128)(2,1)}, u32[]{:S(2)}, u32[]{:S(2)}) collective-permute-start(bf16[2,8,256,1,128]{4,2,1,3,0:T(8,128)(2,1)} %pad_maximum_fusion.6), channel_id=1, source_target_pairs={{0,2},{1,3},{4,6},{5,7},{8,10},{9,11},{12,14},{13,15},{16,18},{17,... | collective-permute-start | bytes 3145736 | tf_op jit(solution)/shard_map/ppermute | solution.py:788
  283.2 508.3 %reduce-scatter.5.cloned.1.call-start = ((), (), s32[]{:S(2)}) async-start(), calls=%async_computation.15 | async-start | bytes 2359296 | tf_op jit(solution)/shard_map/reduce_scatter | solution.py:688
  283.4 8.0 copy-start.9
  283.5 8.0 copy-start.17
  289.3 9.3 copy-start.20
  298.6 5.2 copy-start.23
  298.6 5.2 copy-start.26
  303.7 5.5 copy-start.28
  309.2 5.7 copy-start.13
  422.4 1.0 copy-start.4
  442.9 3.3 copy-start.12
  562.8 14.6 %copy-start.16 = (bf16[8,256,1024]{2,1,0:T(8,128)(2,1)S(1)}, bf16[8,256,1024]{2,1,0:T(8,128)(2,1)}, u32[]{:S(2)}) copy-start(bf16[8,256,1024]{2,1,0:T(8,128)(2,1)} %copy.173) | copy-start | bytes 12582916
  577.4 13.6 %copy-start.5 = (f32[128,2048]{1,0:T(8,128)S(1)}, f32[128,2048]{1,0:T(8,128)}, u32[]{:S(2)}) copy-start(f32[128,2048]{1,0:T(8,128)} %copy-done.4) | copy-start | bytes 3145732
  591.1 103.2 %copy-start.29 = (bf16[128,2048]{1,0:T(8,128)(2,1)S(1)}, bf16[128,2048]{1,0:T(8,128)(2,1)}, u32[]{:S(2)}) copy-start(bf16[128,2048]{1,0:T(8,128)(2,1)} %all_gather.37) | copy-start | bytes 1572868
  694.3 5.9 copy-start.15
  694.3 5.9 copy-start.27
  694.3 5.9 copy-start.34
  702.9 1.0 copy-start.22
  703.9 2.4 copy-start.6
  703.9 2.4 copy-start.21
  703.9 2.5 copy-start.24
  705.0 27.8 %collective-permute-start.1 = (bf16[2,8,256,1,128]{4,2,1,3,0:T(8,128)(2,1)S(1)}, bf16[2,8,256,1,128]{4,2,1,3,0:T(8,128)(2,1)S(1)}, u32[]{:S(2)}, u32[]{:S(2)}) collective-permute-start(bf16[2,8,256,1,128]{4,2,1,3,0:T(8,128)(2,1)S(1)} %pad_maximum_fusion.9), channel_id=1, source_target_pairs={{2,0},{3,1},{6,4},{7,5},{10,8},{11,9},{14,12},{15,13},{18,16},{19,... | collective-permute-start | bytes 3145736 | tf_op jit(solution)/shard_map/ppermute | solution.py:843
  737.8 4.6 copy-start.11
  738.2 4.3 copy-start.8
  742.4 1.5 copy-start.10
  742.4 13.9 %copy-start.30 = (bf16[8,256,1,128]{3,1,0,2:T(8,128)(2,1)}, bf16[8,256,1,128]{3,1,0,2:T(8,128)(2,1)S(1)}, u32[]{:S(2)}) copy-start(bf16[8,256,1,128]{3,1,0,2:T(8,128)(2,1)S(1)} %get-tuple-element.48) | copy-start | bytes 1572868
  756.3 9.5 copy-start.32
  756.3 9.5 copy-start.33
  765.8 60.3 %reduce-scatter.11.cloned.1.call-start = ((), (), s32[]{:S(2)}) async-start(), calls=%async_computation.20 | async-start | bytes 3145728 | tf_op jit(solution)/shard_map/reduce_scatter | solution.py:688
  776.0 107.3 %reduce-scatter.9.cloned.1.call-start = ((), (), s32[]{:S(2)}) async-start(), calls=%async_computation.18 | async-start | bytes 6291456 | tf_op jit(solution)/shard_map/reduce_scatter | solution.py:688
  791.5 34.6 %all-to-all-start.4 = ((bf16[8,128,384]{2,1,0:T(8,128)(2,1)}), bf16[8,128,384]{2,1,0:T(8,128)(2,1)S(1)}, u32[]{:S(2)}, u32[]{:S(2)}) async-start(bf16[8,128,384]{2,1,0:T(8,128)(2,1)} %reduce-scatter.5.cloned.1.call-done), calls=%async_computation.5 | async-start | bytes 1572864 | tf_op jit(solution)/shard_map/all_to_all | solution.py:691
  826.1 6.0 copy-start.19
  826.1 28.4 %all-to-all-start.7 = ((bf16[8,256,256]{2,1,0:T(8,128)(2,1)}), bf16[8,256,256]{2,1,0:T(8,128)(2,1)}, u32[]{:S(2)}, u32[]{:S(2)}) async-start(bf16[8,256,256]{2,1,0:T(8,128)(2,1)} %reduce-scatter.11.cloned.1.call-done), calls=%async_computation.11 | async-start | bytes 2097152 | tf_op jit(solution)/shard_map/all_to_all | solution.py:691
  832.2 102.0 %reduce-scatter.7.cloned.1.call-start = ((), (), s32[]{:S(2)}) async-start(), calls=%async_computation.17 | async-start | bytes 786432 | tf_op jit(solution)/shard_map/reduce_scatter | solution.py:688
  832.2 11.7 %copy-start.14 = (bf16[8,256,1,128]{3,1,0,2:T(8,128)(2,1)S(1)}, bf16[8,256,1,128]{3,1,0,2:T(8,128)(2,1)}, u32[]{:S(2)}) copy-start(bf16[8,256,1,128]{3,1,0,2:T(8,128)(2,1)} %copy-done.13) | copy-start | bytes 1572868
  883.3 50.8 %all-to-all-start.6 = ((bf16[8,128,1024]{2,1,0:T(8,128)(2,1)}), bf16[8,128,1024]{2,1,0:T(8,128)(2,1)}, u32[]{:S(2)}, u32[]{:S(2)}) async-start(bf16[8,128,1024]{2,1,0:T(8,128)(2,1)} %reduce-scatter.9.cloned.1.call-done), calls=%async_computation.9 | async-start | bytes 4194304 | tf_op jit(solution)/shard_map/all_to_all | solution.py:691
  889.3 52.2 %copy-start.31 = (bf16[8,256,1,128]{3,1,0,2:T(8,128)(2,1)S(1)}, bf16[8,256,1,128]{3,1,0,2:T(8,128)(2,1)}, u32[]{:S(2)}) copy-start(bf16[8,256,1,128]{3,1,0,2:T(8,128)(2,1)} %copy-done.30) | copy-start | bytes 1572868
  889.3 173.7 %all-gather.16.cloned.1.call-start = ((), (), s32[]{:S(2)}) async-start(), calls=%async_computation.16 | async-start | bytes 2359296 | tf_op jit(solution)/shard_map/all_gather | solution.py:695
  890.0 177.9 %all-gather.20.cloned.1.call-start = ((), (), s32[]{:S(2)}) async-start(), calls=%async_computation.21 | async-start | bytes 3145728 | tf_op jit(solution)/shard_map/all_gather | solution.py:695
  892.9 179.6 %all-gather.18.cloned.1.call-start = ((), (), s32[]{:S(2)}) async-start(), calls=%async_computation.19 | async-start | bytes 6291456 | tf_op jit(solution)/shard_map/all_gather | solution.py:695
  934.2 118.5 %all-to-all-start.5 = ((bf16[8,64,256]{2,1,0:T(8,128)(2,1)}), bf16[8,64,256]{2,1,0:T(8,128)(2,1)S(1)}, u32[]{:S(2)}, u32[]{:S(2)}) async-start(bf16[8,64,256]{2,1,0:T(8,128)(2,1)} %reduce-scatter.7.cloned.1.call-done), calls=%async_computation.7 | async-start | bytes 524288 | tf_op jit(solution)/shard_map/all_to_all | solution.py:691
  1050.2 1.3 copy-start.2
  1078.3 3.6 copy-start.3
  1078.3 4.9 copy-start.1
Sparse Core Ops, SparseCore 0:
  166.6 30.0 all-gather.9
  198.2 56.8 all-gather.11
  283.3 35.0 all-gather.13
  765.9 25.5 reduce-scatter.4
  794.2 31.8 reduce-scatter.10
  828.8 54.3 reduce-scatter.8
  886.1 14.6 reduce-scatter.6
  902.9 27.1 all-gather.15
  932.2 33.6 all-gather.19
  967.3 57.5 all-gather.17

commit v2 on v1

--- a/solution.py
+++ b/solution.py
@@ -77,6 +77,12 @@
         self.z = member // 2
         self.y = lax.rem(member, 2)
         self.core = lax.axis_index("tensor")
+        self.side = lax.axis_index("context")
+        self.device = device
+        self.count = lax.axis_size("fsdp")
+
+    def across(self):
+        return {"context": 1 - self.side}
 
     def at(self, z, y, core):
         return {"fsdp": self.base + 2 * z + y, "tensor": core}
@@ -99,16 +105,31 @@
         pl.when(condition)(action)
 
 
-def greet(place):
+def signal(barrier, device):
+    pl.semaphore_signal(barrier, inc=1, device_id=device, device_id_type=MESH_ID)
+
+
+def greet(place, across=False):
     barrier = pltpu.get_barrier_semaphore()
     for condition, device in place.near():
-
-        def signal(device=device):
-            pl.semaphore_signal(barrier, inc=1, device_id=device, device_id_type=MESH_ID)
-
-        guarded(condition, signal)
+        guarded(condition, functools.partial(signal, barrier, device))
+    if across:
+        signal(barrier, place.across())
     inside = (place.z > 0) & (place.z < LINE - 1)
-    pl.semaphore_wait(barrier, jnp.where(inside, 4, 3))
+    pl.semaphore_wait(barrier, jnp.where(inside, 4, 3) + int(across))
+
+
+def greet_all(place):
+    barrier = pltpu.get_barrier_semaphore()
+
+    def one(step, carry):
+        signal(barrier, {"fsdp": lax.rem(place.device + step, place.count)})
+        return carry
+
+    lax.fori_loop(1, place.count, one, 0)
+    signal(barrier, place.across())
+    signal(barrier, place.at(place.z, place.y, 1 - place.core))
+    pl.semaphore_wait(barrier, place.count + 1)
 
 
 class Sender:
@@ -164,7 +185,7 @@
     ]
 
 
-def reduce_phase(place, sender, partial, scratch):
+def reduce_phase(place, sender, partial, scratch, between=None):
     mine, core_in, y_in, line_in, total, local_sem, core_sem, y_sem, line_sem = scratch
     rows = total.shape[0]
     z, y, core = place.z, place.y, place.core
@@ -238,6 +259,8 @@
 
         by_rows(rows, add)
         sender(None, functools.partial(to_y, block))
+    if between is not None:
+        between()
 
     for block in order[:-1]:
         slot = 2 * block + y
@@ -299,7 +322,7 @@
     ]
 
 
-def gather_phase(place, sender, gathered, scratch):
+def gather_phase(place, sender, gathered, scratch, between=None):
     own, local_sem, core_sem, y_sem, line_sem = scratch
     rows = own.shape[0]
     z, y, core = place.z, place.y, place.core
@@ -340,6 +363,8 @@
     sender(z > 0, functools.partial(to_line, own, z, -1, LINE + 1))
     sender(None, functools.partial(to_y, own, z))
     sender(None, functools.partial(to_core, own, z, y))
+    if between is not None:
+        between()
 
     def took_y(block):
         remote(
@@ -414,24 +439,159 @@
     return finish
 
 
+def swap_scratch(count, arrays):
+    return [DMA((arrays,)), DMA((2, arrays, count)), DMA((2, arrays, count))]
+
+
+class Swap:
+    def __init__(self, place, pieces, wholes, scratch):
+        self.place = place
+        self.pairs = list(zip(pieces, wholes))
+        self.local_sem, self.out_sem, self.side_sem = scratch
+
+    def send(self, index, step):
+        place = self.place
+        pieces, whole = self.pairs[index]
+        target = lax.rem(place.device + step, place.count)
+        return remote(
+            pieces.at[target],
+            whole.at[place.device, place.side],
+            self.out_sem.at[0, index, step],
+            self.out_sem.at[1, index, step],
+            {"fsdp": target},
+        )
+
+    def taken(self, index, step, side):
+        source = lax.rem(self.place.device + self.place.count - step, self.place.count)
+        return self.pairs[index][1].at[source, side]
+
+    def come(self, index, step):
+        place = self.place
+        return remote(
+            self.pairs[index][0].at[0],
+            self.taken(index, step, place.side),
+            self.out_sem.at[0, index, step],
+            self.out_sem.at[1, index, step],
+            place.across(),
+        )
+
+    def share(self, index, step, source=None):
+        spot = self.taken(index, step, self.place.side)
+        return remote(
+            spot if source is None else source,
+            spot,
+            self.side_sem.at[0, index, step],
+            self.side_sem.at[1, index, step],
+            self.place.across(),
+        )
+
+    def shared(self, index, step):
+        spot = self.taken(index, step, 1 - self.place.side)
+        return remote(
+            spot,
+            spot,
+            self.side_sem.at[0, index, step],
+            self.side_sem.at[1, index, step],
+            self.place.across(),
+        )
+
+    def keep(self, index):
+        place = self.place
+        pieces, whole = self.pairs[index]
+        return pltpu.make_async_copy(
+            pieces.at[place.device], whole.at[place.device, place.side], self.local_sem.at[index]
+        )
+
+    def each(self, first, body):
+        def step(number, carry):
+            for index in range(len(self.pairs)):
+                body(index, number)
+            return carry
+
+        lax.fori_loop(first, self.place.count, step, 0)
+
+    def start(self):
+        self.each(1, lambda index, step: self.send(index, step).start())
+        for index, (pieces, whole) in enumerate(self.pairs):
+            self.keep(index).start()
+            self.share(index, 0, pieces.at[self.place.device]).start()
+
+    def pass_on(self):
+        def one(index, step):
+            self.come(index, step).wait_recv()
+            self.share(index, step).start()
+
+        self.each(1, one)
+
+    def finish(self):
+        for index in range(len(self.pairs)):
+            self.keep(index).wait()
+        self.each(0, lambda index, step: self.shared(index, step).wait_recv())
+        self.each(1, lambda index, step: self.send(index, step).wait_send())
+        self.each(0, lambda index, step: self.share(index, step).wait_send())
+
+
+def halves_scratch(arrays):
+    return [DMA((3, arrays))]
+
+
+class Halves:
+    def __init__(self, place, halves, wholes, scratch):
+        self.place = place
+        self.pairs = list(zip(halves, wholes))
+        (self.sem,) = scratch
+
+    def keep(self, index):
+        half, whole = self.pairs[index]
+        return pltpu.make_async_copy(half, whole.at[:, self.place.side], self.sem.at[0, index])
+
+    def copy(self, index, side):
+        half, whole = self.pairs[index]
+        return remote(
+            half,
+            whole.at[:, side],
+            self.sem.at[1, index],
+            self.sem.at[2, index],
+            self.place.across(),
+        )
+
+    def start(self):
+        for index in range(len(self.pairs)):
+            self.copy(index, self.place.side).start()
+            self.keep(index).start()
+
+    def finish(self):
+        for index in range(len(self.pairs)):
+            self.keep(index).wait()
+            self.copy(index, 1 - self.place.side).wait_recv()
+            self.copy(index, self.place.side).wait_send()
+
+
 REDUCE = 9
 GATHER = 5
 
 
-def first_kernel(own_ref, gathered, *scratch):
+def first_kernel(own_ref, qkv, out, small, gathered, qkv_all, out_all, small_all, *scratch):
     place = Place()
     sender = Sender()
     own = scratch[0]
     own[...] = own_ref[...]
-    greet(place)
-    gather_phase(place, sender, gathered, scratch)
+    greet_all(place)
+    swap = Swap(place, (small, qkv, out), (small_all, qkv_all, out_all), scratch[GATHER:])
+    gather_phase(place, sender, gathered, scratch[:GATHER], swap.start)
+    swap.pass_on()
+    swap.finish()
     sender.drain()
 
 
-def hidden_kernel(partial, tokens, gain, gathered, branch, hidden, *scratch):
+def hidden_kernel(
+    partial, tokens, gain, pair, down, gathered, branch, hidden, pair_all, down_all, *scratch
+):
     place = Place()
     sender = Sender()
-    greet(place)
+    greet(place, True)
+    halves = Halves(place, (pair, down), (pair_all, down_all), scratch[REDUCE + GATHER :])
+    halves.start()
     reduce_phase(place, sender, partial, scratch[:REDUCE])
     total, own = scratch[4], scratch[REDUCE]
     rows, width = total.shape
@@ -445,7 +605,8 @@
         own[at] = result.astype(BF)
 
     by_rows(rows, body)
-    gather_phase(place, sender, gathered, scratch[REDUCE:])
+    gather_phase(place, sender, gathered, scratch[REDUCE : REDUCE + GATHER])
+    halves.finish()
     sender.drain()
 
 
@@ -477,10 +638,33 @@
     sender.drain()
 
 
-def branch_kernel(partial, branch, cotangent, gain, gathered, grad_hidden, gain_grad, *scratch):
+def branch_kernel(
+    partial,
+    branch,
+    cotangent,
+    gain,
+    pair_grad,
+    down_grad,
+    gathered,
+    grad_hidden,
+    gain_grad,
+    pair_other,
+    down_other,
+    *scratch,
+):
     place = Place()
     sender = Sender()
-    greet(place)
+    greet(place, True)
+    (side_sem,) = scratch[REDUCE + GATHER :]
+    count = down_other.shape[0]
+    rows_out = pl.ds(pl.multiple_of((1 - place.side) * count, count), count)
+    sources = (pair_grad.at[:, 1 - place.side], down_grad.at[rows_out])
+    crossings = [
+        remote(source, target, side_sem.at[0, index], side_sem.at[1, index], place.across())
+        for index, (source, target) in enumerate(zip(sources, (pair_other, down_other)))
+    ]
+    for crossing in crossings:
+        crossing.start()
     reduce_phase(place, sender, partial, scratch[:REDUCE])
     total, own = scratch[4], scratch[REDUCE]
     rows, width = total.shape
@@ -498,23 +682,100 @@
         own[at] = (scale * (gained - normed * (inner / width))).astype(BF)
 
     by_rows(rows, body)
-    gather_phase(place, sender, gathered, scratch[REDUCE:])
+    gather_phase(place, sender, gathered, scratch[REDUCE : REDUCE + GATHER])
+    for crossing in crossings:
+        crossing.wait()
     sender.drain()
 
 
-def last_kernel(partial, grad_hidden, result, *scratch):
+def last_kernel(
+    partial,
+    grad_hidden,
+    qkv,
+    out,
+    small,
+    pair,
+    down,
+    result,
+    qkv_all,
+    out_all,
+    small_all,
+    pair_all,
+    down_all,
+    *scratch,
+):
     place = Place()
     sender = Sender()
-    greet(place)
-    reduce_phase(place, sender, partial, scratch[:REDUCE])
+    parts = scratch[REDUCE + 1 :]
+    swap_sems, halves_sems, parts = parts[:3], parts[3:4], parts[4:]
+    qkv_own, qkv_other, out_own, out_other, small_own, small_other, fetch_sem, side_sem = parts
+    greet_all(place)
+    fetches, crossings = [], []
+    for index, (grad, own, other) in enumerate(
+        ((qkv, qkv_own, qkv_other), (out, out_own, out_other))
+    ):
+        fetches.append(
+            pltpu.make_async_copy(grad.at[:, place.side], own, fetch_sem.at[index])
+        )
+        crossings.append(
+            remote(
+                grad.at[:, 1 - place.side],
+                other,
+                side_sem.at[0, index],
+                side_sem.at[1, index],
+                place.across(),
+            )
+        )
+    crossings.append(
+        remote(
+            small,
+            small_other,
+            side_sem.at[0, 2],
+            side_sem.at[1, 2],
+            place.at(place.z, place.y, 1 - place.core),
+        )
+    )
+    for copy in fetches + crossings:
+        copy.start()
+    swap = Swap(
+        place, (small_own, qkv_own, out_own), (small_all, qkv_all, out_all), swap_sems
+    )
+    halves = Halves(place, (pair, down), (pair_all, down_all), halves_sems)
+    shared_rows = 2 * partial.shape[1] // place.count // 128
+
+    def between():
+        for fetch in fetches:
+            fetch.wait()
+        for crossing in crossings:
+            crossing.wait()
+        halves.start()
+        small_own[...] = small[...]
+        small_own[:, :shared_rows] += small_other[:, :shared_rows]
+
+        def one(index, carry):
+            qkv_own[index] = (
+                qkv_own[index].astype(F32) + qkv_other[index].astype(F32)
+            ).astype(BF)
+            out_own[index] = (
+                out_own[index].astype(F32) + out_other[index].astype(F32)
+            ).astype(BF)
+            return carry
+
+        lax.fori_loop(0, place.count, one, 0)
+        swap.start()
+
+    reduce_phase(place, sender, partial, scratch[:REDUCE], between)
     total = scratch[4]
 
     def body(at):
         total[at] += grad_hidden[at]
 
     by_rows(total.shape[0], body)
-    finish = pair_phase(place, sender, total, result, scratch[REDUCE:])
+    finish = pair_phase(place, sender, total, result, scratch[REDUCE : REDUCE + 1])
+    swap.pass_on()
     finish()
+    halves.finish()
+    swap.finish()
     sender.drain()
 
 
@@ -599,18 +860,29 @@
         self.reduces = reduce_scratch(rows, width)
         self.gathers = gather_scratch(rows, width)
 
-    def first(self, own):
-        return talk(first_kernel, 0, self.all_low, ([VMEM], HBM), self.gathers, 50)(own)
-
-    def hidden(self, partial, tokens, gain):
+    def whole(self, pieces):
+        shape = (pieces.shape[0], 2) + pieces.shape[1:]
+        return jax.ShapeDtypeStruct(shape, pieces.dtype)
+
+    def first(self, own, qkv, out, small):
+        return talk(
+            first_kernel,
+            0,
+            (self.all_low, self.whole(qkv), self.whole(out), self.whole(small)),
+            ([VMEM] * 4, (HBM,) * 4),
+            self.gathers + swap_scratch(self.fsdp, 3),
+            80,
+        )(own, qkv, out, small)
+
+    def hidden(self, partial, tokens, gain, pair, down):
         return talk(
             hidden_kernel,
             1,
-            (self.all_low, self.own_wide, self.own_wide),
-            ([HBM, VMEM, VMEM], (HBM, VMEM, VMEM)),
-            self.reduces + self.gathers,
+            (self.all_low, self.own_wide, self.own_wide, self.whole(pair), self.whole(down)),
+            ([HBM, VMEM, VMEM, VMEM, VMEM], (HBM, VMEM, VMEM, HBM, HBM)),
+            self.reduces + self.gathers + halves_scratch(2),
             100,
-        )(partial, tokens, gain)
+        )(partial, tokens, gain, pair, down)
 
     def turn(self, partial, hidden, cotangent, gain):
         pair = jax.ShapeDtypeStruct((2 * self.rows, self.width), BF)
@@ -623,26 +895,41 @@
             100,
         )(partial, hidden, cotangent, gain)
 
-    def branch(self, partial, branch, cotangent, gain):
+    def branch(self, partial, branch, cotangent, gain, pair_grad, down_grad):
+        shape = pair_grad.shape
+        pair_other = jax.ShapeDtypeStruct((shape[0],) + shape[2:], BF)
+        down_other = jax.ShapeDtypeStruct((down_grad.shape[0] // 2, down_grad.shape[1]), BF)
         return talk(
             branch_kernel,
             3,
-            (self.all_low, self.own_wide, self.line_wide),
-            ([HBM, VMEM, VMEM, VMEM], (HBM, VMEM, VMEM)),
-            self.reduces + self.gathers,
+            (self.all_low, self.own_wide, self.line_wide, pair_other, down_other),
+            ([HBM, VMEM, VMEM, VMEM, HBM, HBM], (HBM, VMEM, VMEM, HBM, HBM)),
+            self.reduces + self.gathers + [DMA((2, 2))],
             100,
-        )(partial, branch, cotangent, gain)
-
-    def last(self, partial, grad_hidden):
-        pair = jax.ShapeDtypeStruct((2 * self.rows, self.width), F32)
+        )(partial, branch, cotangent, gain, pair_grad, down_grad)
+
+    def last(self, partial, grad_hidden, qkv, out, small, pair, down):
+        both = jax.ShapeDtypeStruct((2 * self.rows, self.width), F32)
+
+        def same(array):
+            return jax.ShapeDtypeStruct(array.shape, array.dtype)
+
+        def half(array):
+            return pltpu.VMEM((array.shape[0],) + array.shape[2:], array.dtype)
+
+        held = pltpu.VMEM(small.shape, small.dtype)
         return talk(
             last_kernel,
             4,
-            pair,
-            ([HBM, VMEM], HBM),
-            self.reduces + pair_scratch(),
-            50,
-        )(partial, grad_hidden)
+            (both, same(qkv), same(out), self.whole(small), self.whole(pair), self.whole(down)),
+            ([HBM, VMEM, HBM, HBM, VMEM, VMEM, VMEM], (HBM,) * 6),
+            self.reduces
+            + pair_scratch()
+            + swap_scratch(self.fsdp, 3)
+            + halves_scratch(2)
+            + [half(qkv), half(qkv), half(out), half(out), held, held, DMA((2,)), DMA((2, 3))],
+            80,
+        )(partial, grad_hidden, qkv, out, small, pair, down)
 
     def total(self, values):
         flat = values.reshape(-1, 128)
@@ -663,49 +950,56 @@
         return lax.dynamic_slice_in_dim(array, self.context * count, count, axis)
 
     def swap(self, pieces):
-        if self.teams > 1:
-            pieces = jnp.concatenate([pieces] * self.teams, axis=0)
         return lax.all_to_all(pieces, "fsdp", split_axis=0, concat_axis=0, tiled=True)
 
-    def columns_in(self, weights):
+    def repeat(self, pieces):
+        return jnp.concatenate([pieces] * self.teams, axis=0) if self.teams > 1 else pieces
+
+    def column_pieces(self, weights):
         pieces = []
         for weight in weights:
             rows, columns = weight.shape
             part = self.half(weight, 0).reshape(rows // 2, self.size, columns // self.size)
             pieces.append(part.transpose(1, 0, 2))
-        came = self.swap(jnp.concatenate(pieces, axis=2))
-        whole = lax.all_gather(came, "context", axis=1, tiled=True)
-        return whole.reshape(self.fsdp * rows, whole.shape[2])
-
-    def rows_in(self, weight):
+        return self.repeat(jnp.concatenate(pieces, axis=2))
+
+    def row_pieces(self, weight):
         rows, columns = weight.shape
-        pieces = self.half(weight.reshape(self.size, rows // self.size, columns), 1)
-        came = self.swap(pieces).transpose(1, 0, 2)
-        came = came.reshape(came.shape[0], self.fsdp * columns)
-        return lax.all_gather(came, "context", axis=0, tiled=True)
-
-    def back(self, pieces):
-        pieces = lax.psum_scatter(
-            pieces.astype(BF), "context", scatter_dimension=1, tiled=True
-        )
-        came = lax.all_to_all(pieces, "fsdp", split_axis=0, concat_axis=0, tiled=True)
-        if self.teams > 1:
-            came = came.reshape((self.teams, self.size) + came.shape[1:]).astype(F32)
-            came = jnp.sum(came, axis=0).astype(BF)
-        return lax.all_gather(came, "context", axis=1, tiled=True)
-
-    def columns_out(self, grad, count):
+        return self.repeat(self.half(weight.reshape(self.size, rows // self.size, columns), 1))
+
+    def columns_whole(self, came):
+        return came.reshape(-1, came.shape[-1])
+
+    def rows_whole(self, came):
+        fsdp, two, rows, columns = came.shape
+        return came.transpose(1, 2, 0, 3).reshape(two * rows, fsdp * columns)
+
+    def of_columns(self, grad):
         rows, columns = grad.shape
-        came = self.back(grad.reshape(self.fsdp, rows // self.fsdp, columns))
+        return grad.astype(BF).reshape(self.fsdp, 2, rows // self.fsdp // 2, columns)
+
+    def of_rows(self, grad):
+        rows, columns = grad.shape
+        cut = grad.astype(BF).reshape(2, rows // 2, self.fsdp, columns // self.fsdp)
+        return cut.transpose(2, 0, 1, 3)
+
+    def added(self, came):
+        if self.teams == 1:
+            return came.astype(F32)
+        came = came.reshape((self.teams, self.size) + came.shape[1:])
+        return jnp.sum(came.astype(F32), axis=0)
+
+    def columns_out(self, came, count):
+        size, two, rows, columns = came.shape
         return [
-            part.transpose(1, 0, 2).reshape(rows // self.fsdp, -1).astype(F32)
-            for part in jnp.split(came, count, axis=2)
+            self.added(part.reshape(size, two * rows, -1))
+            .transpose(1, 0, 2)
+            .reshape(two * rows, -1)
+            for part in jnp.split(came, count, axis=3)
         ]
 
-    def rows_out(self, grad):
-        rows, columns = grad.shape
-        came = self.back(grad.reshape(rows, self.fsdp, columns // self.fsdp).transpose(1, 0, 2))
-        return came.reshape(self.size * rows, columns // self.fsdp).astype(F32)
+    def rows_out(self, came):
+        return self.added(came).reshape(-1, came.shape[-1])
 
 
 def local(
@@ -739,28 +1033,33 @@
 
     tokens_own = lax.dynamic_slice_in_dim(tokens, team.core * own_rows, own_rows, 0)
     grad_out = lax.dynamic_slice_in_dim(cotangent, team.core * own_rows, own_rows, 0)
-    tokens_all = team.first(tokens_own)
-
-    qkv_w = team.columns_in([w_query, w_key, w_value])
-    output_w = team.rows_in(w_output)
-
-    fsdp_gains = jnp.concatenate(
-        [query_gain.reshape(-1), key_gain.reshape(-1), attn_gain, mlp_gain]
-    )
-    all_gains = lax.all_gather(fsdp_gains, "fsdp", axis=0, tiled=False).astype(F32)
     cut = query_gain.size
-    query_gains = all_gains[:, :cut].reshape(fsdp, local_heads, -1)
-    key_gains = all_gains[:, cut : 2 * cut].reshape(fsdp, local_heads, -1)
+    share = attn_gain.size
+    small = [query_gain.reshape(-1), key_gain.reshape(-1), attn_gain, mlp_gain]
+    small = jnp.concatenate([one.astype(F32) for one in small + [cont_lengths.reshape(-1)]])
+    small = jnp.pad(small, (0, 8 * 128 - small.size)).reshape(1, 8, 128)
+    tokens_all, qkv_came, output_came, small_came = team.first(
+        tokens_own,
+        team.column_pieces([w_query, w_key, w_value]),
+        team.row_pieces(w_output),
+        jnp.broadcast_to(small, (fsdp, 8, 128)),
+    )
+    qkv_w = team.columns_whole(qkv_came)
+    output_w = team.rows_whole(output_came)
+    all_small = small_came[:, 0].reshape(fsdp, -1)
+    query_gains = all_small[:, :cut].reshape(fsdp, local_heads, -1)
+    key_gains = all_small[:, cut : 2 * cut].reshape(fsdp, local_heads, -1)
     query_gains = query_gains.transpose(1, 0, 2).reshape(local_heads, head_size)
     key_gains = key_gains.transpose(1, 0, 2).reshape(local_heads, head_size)
     flat_query = lax.dynamic_slice_in_dim(query_gains, team.member * heads, heads, 0).reshape(-1)
     flat_key = lax.dynamic_slice_in_dim(key_gains, team.member * heads, heads, 0).reshape(-1)
-    gain_attn = all_gains[:, 2 * cut : 2 * cut + attn_gain.size].reshape(1, -1)
-    gain_mlp = all_gains[:, 2 * cut + attn_gain.size :].reshape(1, -1)
-
-    lengths = lax.all_gather(
-        cont_lengths, "fsdp", axis=0, tiled=True, axis_index_groups=team.groups
-    )
+    gain_attn = all_small[:, 2 * cut : 2 * cut + share].reshape(1, -1)
+    gain_mlp = all_small[:, 2 * cut + share : 2 * cut + 2 * share].reshape(1, -1)
+
+    conts = cont_lengths.shape[1]
+    lengths = all_small[:, 2 * cut + 2 * share : 2 * cut + 2 * share + conts].astype(jnp.int32)
+    first_group = lax.axis_index("fsdp") - team.member
+    lengths = lax.dynamic_slice_in_dim(lengths, first_group, groups, 0)
     segment, offset = jax.vmap(lambda one: layout(one, rows))(lengths)
     row_index = jnp.arange(rows, dtype=jnp.int32)
     positions = jnp.where(later, rows + offset, row_index[None, :])
@@ -769,8 +1068,11 @@
     cosine = cosine[:, :, None, :]
     sine = sine[:, :, None, :]
 
-    pair_w = team.columns_in([w_gate, w_up])
-    down_w = team.rows_in(w_down)
+    pair_mine, down_mine, tokens_all = lax.optimization_barrier(
+        (team.column_pieces([w_gate, w_up]), team.row_pieces(w_down), tokens_all)
+    )
+    pair_came = team.swap(pair_mine)
+    down_came = team.swap(down_mine)
 
     by_head = (groups, rows, heads, head_size)
     raw = product(tokens_all, qkv_w)
@@ -785,9 +1087,10 @@
     query_low = rotate(query_norm.reshape(by_head), cosine, sine).astype(BF)
     key_low = rotate(key_norm.reshape(by_head), cosine, sine).astype(BF)
     value_low = value_raw.reshape(by_head).astype(BF)
-    sent = lax.ppermute(jnp.stack([key_low, value_low]), "context", [(0, 1)])
-    keys_all = jnp.concatenate([sent[0], key_low], axis=1)
-    values_all = jnp.concatenate([sent[1], value_low], axis=1)
+    sent_value = lax.ppermute(value_low, "context", [(0, 1)])
+    sent_key = lax.ppermute(key_low, "context", [(0, 1)])
+    keys_all = jnp.concatenate([sent_key, key_low], axis=1)
+    values_all = jnp.concatenate([sent_value, value_low], axis=1)
     key_index = jnp.arange(2 * rows, dtype=jnp.int32)
     key_segment = jnp.concatenate([jnp.full((groups, rows), -2, jnp.int32), own_segment], axis=1)
     remote = (key_index < rows)[None, None, :] & later
@@ -808,9 +1111,11 @@
     probs_low = probs.astype(BF)
     mixed = jnp.einsum("ghqk,gkhd->gqhd", probs_low, values_all, preferred_element_type=F32)
     attended_low = mixed.reshape(team_rows, heads * head_size).astype(BF)
-    hidden_all, attn_sum, hidden = team.hidden(
-        product(attended_low, output_w).astype(BF), tokens_own, gain_attn
-    )
+    hidden_all, attn_sum, hidden, pair_came, down_came = team.hidden(
+        product(attended_low, output_w).astype(BF), tokens_own, gain_attn, pair_came, down_came
+    )
+    pair_w = team.columns_whole(pair_came)
+    down_w = team.rows_whole(down_came)
 
     gate, upward = jnp.split(product(hidden_all, pair_w), 2, axis=1)
     sigma = jax.nn.sigmoid(gate)
@@ -818,16 +1123,27 @@
     grad_mlp_all, outputs, grad_mlp_gain = team.turn(
         product(inner_low, down_w).astype(BF), hidden, grad_out, gain_mlp
     )
-    grad_w_down = team.rows_out(product_left(inner_low, grad_mlp_all))
+    down_grad = product_left(inner_low, grad_mlp_all).astype(BF)
     grad_inner = product_right(grad_mlp_all, down_w)
     grad_gate_low = (grad_inner * upward * sigma * (1.0 + gate * (1.0 - sigma))).astype(BF)
     grad_up_low = (grad_inner * gate * sigma).astype(BF)
     grad_pair = jnp.concatenate([grad_gate_low, grad_up_low], axis=1)
-    grad_w_gate, grad_w_up = team.columns_out(product_left(hidden_all, grad_pair), 2)
-    grad_branch_all, grad_hidden, grad_attn_gain = team.branch(
-        product_right(grad_pair, pair_w).astype(BF), attn_sum, grad_out, gain_attn
-    )
-    grad_w_output = team.rows_out(product_left(attended_low, grad_branch_all))
+    pair_grad = team.of_columns(product_left(hidden_all, grad_pair))
+    grad_branch_all, grad_hidden, grad_attn_gain, pair_other, down_other = team.branch(
+        product_right(grad_pair, pair_w).astype(BF),
+        attn_sum,
+        grad_out,
+        gain_attn,
+        pair_grad,
+        down_grad,
+    )
+    pair_mine = lax.dynamic_index_in_dim(pair_grad, team.context, 1, keepdims=False)
+    pair_mine = (pair_mine.astype(F32) + pair_other.astype(F32)).astype(BF)
+    down_mine = (team.half(down_grad, 0).astype(F32) + down_other.astype(F32)).astype(BF)
+    down_mine = down_mine.reshape(down_mine.shape[0], fsdp, -1).transpose(1, 0, 2)
+    pair_came = team.swap(pair_mine)
+    down_came = team.swap(down_mine)
+    output_grad = team.of_rows(product_left(attended_low, grad_branch_all))
     grad_attended = product_right(grad_branch_all, output_w).astype(BF).reshape(by_head)
 
     grad_probs = jnp.einsum("gqhd,gkhd->ghqk", grad_attended, values_all, preferred_element_type=F32)
@@ -840,11 +1156,12 @@
         jnp.einsum("ghqk,gqhd->gkhd", grad_scores, query_low, preferred_element_type=F32) * scale
     )
     grad_values = jnp.einsum("ghqk,gqhd->gkhd", probs_low, grad_attended, preferred_element_type=F32)
-    returned = lax.ppermute(
-        jnp.stack([grad_keys[:, :rows], grad_values[:, :rows]]).astype(BF), "context", [(1, 0)]
-    ).astype(F32)
-    grad_key_rot = grad_keys[:, rows:] + returned[0]
-    grad_value_low = (grad_values[:, rows:] + returned[1]).reshape(team_rows, -1).astype(BF)
+    back_value = lax.ppermute(grad_values[:, :rows].astype(BF), "context", [(1, 0)])
+    back_key = lax.ppermute(grad_keys[:, :rows].astype(BF), "context", [(1, 0)])
+    grad_key_rot = grad_keys[:, rows:] + back_key.astype(F32)
+    grad_value_low = (
+        (grad_values[:, rows:] + back_value.astype(F32)).reshape(team_rows, -1).astype(BF)
+    )
     grad_query_norm = rotate_back(grad_query_rot, cosine, sine).reshape(team_rows, -1)
     grad_key_norm = rotate_back(grad_key_rot, cosine, sine).reshape(team_rows, -1)
     grad_query_gain = jnp.sum(grad_query_norm * query_raw * scale_query, axis=0)
@@ -864,30 +1181,33 @@
         key_raw, scale_key, flat_key, grad_key_norm, totals[1][:, None], width
     ).astype(BF)
     grad_qkv = jnp.concatenate([grad_query_low, grad_key_low, grad_value_low], axis=1)
-    grad_w_query, grad_w_key, grad_w_value = team.columns_out(product_left(tokens_all, grad_qkv), 3)
-    input_grad = team.last(product_right(grad_qkv, qkv_w).astype(BF), grad_hidden)
-
-    all_width = heads * head_size
-    place = (team.core * team.size + team.member) * all_width
-    spread = jnp.zeros((2, tensor * local_heads * head_size), F32)
-    spread = lax.dynamic_update_slice(
-        spread, jnp.stack([grad_query_gain, grad_key_gain]), (0, place)
-    )
-    gains = lax.psum(
-        jnp.concatenate([spread.reshape(-1), grad_attn_gain.reshape(-1), grad_mlp_gain.reshape(-1)]),
-        ("fsdp", "context", "tensor"),
-    )
-    device = lax.axis_index("fsdp")
-    head_gains = gains[: 2 * tensor * local_heads * head_size].reshape(
-        2, tensor, local_heads, fsdp, head_size // fsdp
-    )
-    head_gains = lax.dynamic_slice(
-        head_gains,
-        (0, team.core, 0, device, 0),
-        (2, 1, local_heads, 1, head_size // fsdp),
-    ).reshape(2, local_heads, head_size // fsdp)
-    row_gains = gains[2 * tensor * local_heads * head_size :].reshape(2, fsdp, width // fsdp)
-    row_gains = lax.dynamic_slice_in_dim(row_gains, device, 1, 1).reshape(2, width // fsdp)
+    qkv_grad = team.of_columns(product_left(tokens_all, grad_qkv))
+    head_share = head_size // fsdp
+    small = [
+        grad_attn_gain.reshape(fsdp, share),
+        grad_mlp_gain.reshape(fsdp, share),
+        grad_query_gain.reshape(heads, fsdp, head_share).transpose(1, 0, 2).reshape(fsdp, -1),
+        grad_key_gain.reshape(heads, fsdp, head_share).transpose(1, 0, 2).reshape(fsdp, -1),
+    ]
+    used = 2 * share + 2 * heads * head_share
+    small = jnp.concatenate(small + [jnp.zeros((fsdp, 8 * 128 - used), F32)], axis=1)
+    input_grad, qkv_came, output_came, small_came, pair_came, down_came = team.last(
+        product_right(grad_qkv, qkv_w).astype(BF),
+        grad_hidden,
+        qkv_grad,
+        output_grad,
+        small.reshape(fsdp, 8, 128),
+        pair_came,
+        down_came,
+    )
+    grad_w_query, grad_w_key, grad_w_value = team.columns_out(qkv_came, 3)
+    grad_w_gate, grad_w_up = team.columns_out(pair_came, 2)
+    grad_w_output = team.rows_out(output_came)
+    grad_w_down = team.rows_out(down_came)
+    came = jnp.sum(small_came, axis=1).reshape(fsdp, -1)
+    row_gains = jnp.sum(came[:, : 2 * share], axis=0).reshape(2, share)
+    head_gains = team.added(came[:, 2 * share : used]).reshape(team.size, 2, heads, head_share)
+    head_gains = head_gains.transpose(1, 0, 2, 3).reshape(2, local_heads, head_share)
     return (
         outputs,
         input_grad,

time: 1100 us -> 894 us (0.81)
  waiting for transfers between devices: 134 us -> 1.4 us
  blocking collectives: 123 us -> 0 us
  Pallas kernels: 498 us -> 578 us
  starting transfers between devices: 59.8 us -> 42.9 us
  between operations: 15.3 us -> 2.2 us
    all_gather x4 -> x0, blocking collectives: 83 us -> none  [the longest x1 29.3 us: local(): lax.all_gather(fsdp_gains, 'fsdp', axis=0, tiled=False).astype(F32)]
    pallas_call x7, Pallas kernels: 498 us -> 578 us  [call(): pl.pallas_call(kernel, out_shape=shapes, in_specs=specs[0], out_specs=spe...]
    reduce_scatter x4 -> x0, waiting for transfers between devices: 58.8 us -> none  [back(): lax.psum_scatter(pieces.astype(BF), 'context', scatter_dimension=1, tiled...]
    all_to_all x4 -> x0, waiting for transfers between devices: 44.6 us -> none  [back(): lax.all_to_all(pieces, 'fsdp', split_axis=0, concat_axis=0, tiled=True)]
    psum x1 -> x0, blocking collectives: 40.1 us -> none  [local(): lax.psum(jnp.concatenate([spread.reshape(-1), grad_attn_gain.reshape(-1),...]
    all_to_all x4 -> x0, starting transfers between devices: 25.4 us -> none  [back(): lax.all_to_all(pieces, 'fsdp', split_axis=0, concat_axis=0, tiled=True)]
    ppermute x2 -> x4, waiting for transfers between devices: 21.4 us -> 1.34 us  [the longest x1 1.33 us: local(): sent_value = lax.ppermute(value_low, 'context', [(0, 1)])]
    reshape x6 -> x16, local copies, waits for them, and re-layouts: 0.43 us -> 15.2 us  [the longest x5 6.42 us: column_pieces(): self.half(weight, 0).reshape(rows // 2, self.size, columns // self.size)]
  transfers between devices with their start and end apart: 20 -> 8, of which waited for: 7 -> 2; matrix products, arithmetic and copies ran while one was open for 15% -> 14% of each run, Pallas kernels for 26% -> 6%
where the time goes in v2:
time: 894 us; the launch traced here: 881 us
  Pallas kernels  578 us (65%)
  matrix products  130 us (15%)
  other arithmetic  68.2 us (8%)
  local copies, waits for them, and re-layouts  59.1 us (7%)
  starting transfers between devices  42.9 us (5%)
    pallas_call x7, Pallas kernels, call(): pl.pallas_call(kernel, out_shape=shapes, in_specs=specs[0], out_specs=spe...  578 us
    dot_general x4, matrix products, product(): return jnp.dot(left, right, preferred_element_type=F32)  38.3 us
    dot_general x4, matrix products, product_right(): return jnp.einsum('rf,df->rd', left, right, preferred_element_type=F32)  36.1 us
    all_to_all x4, starting transfers between devices, swap(): lax.all_to_all(pieces, 'fsdp', split_axis=0, concat_axis=0, tiled=True)  34.8 us
    dot_general x4, matrix products, product_left(): return jnp.einsum('rd,rf->df', left, right, preferred_element_type=F32)  32.7 us
    unnamed x115, local copies, waits for them, and re-layouts  18 us
  transfers between devices with their start and end apart: 8, of which 2 were waited for; matrix products, arithmetic and copies ran while one was open for 14% of the time, Pallas kernels for 6%

profile of v2, /device:TPU:16, one launch (start us, length us, event | category | flops | bytes accessed | tf_op | source)
XLA Modules:
  0.0 881.3 jit_solution(14814033539530905688)
XLA Ops:
  5.6 2.7 constant_dynamic-slice_fusion.9
  8.3 2.3 copy.151
  10.6 2.3 copy.111
  12.8 1.3 copy.152
  14.1 2.3 copy.113
  18.5 3.1 pad_maximum_fusion.3
  23.7 85.6 %first_kernel.1 = (bf16[2048,2048]{1,0:T(8,128)(2,1)}, bf16[8,2,128,384]{3,2,1,0:T(8,128)(2,1)S(1)}, bf16[8,2,64,256]{3,2,1,0:T(8,128)(2,1)S(1)}, f32[8,2,8,128]{3,2,1,0:T(8,128)S(1)}) custom-call(bf16[128,2048]{1,0:T(8,128)(2,1)S(1)} %constant_dynamic-slice_fusion.7.own_ref.tokens, bf16[8,128,384]{2,1,0:T(8,128)(2,1)S(1)} %pad_maximum_fusion.7.qkv, ...), custom_call_target="tpu_custom_call" | custom-call | bytes 240000000 | tf_op jit(solution)/shard_map/first_kernel/pallas_call | solution.py:822
  110.6 17.0 %all-to-all-start.1 = ((bf16[8,256,256]{2,1,0:T(8,128)(2,1)}), bf16[8,256,256]{2,1,0:T(8,128)(2,1)S(1)}, u32[]{:S(2)}, u32[]{:S(2)}) async-start(bf16[8,256,256]{2,1,0:T(8,128)(2,1)} %constant_dynamic-slice_fusion.8), calls=%async_computation.1 | async-start | bytes 2097152 | tf_op jit(solution)/shard_map/all_to_all | solution.py:953
  128.0 10.0 %fusion.61 = f32[2048,384]{1,0:T(8,128)} fusion(bf16[2048,2048]{1,0:T(8,128)(2,1)} %get-tuple-element.40, bf16[2048,384]{1,0:T(8,128)(2,1)} %bitcast.249), kind=kOutput, calls=%fused_computation.172 | convolution fusion | flops 3221225472 | bytes 13107200 | tf_op jit(solution)/shard_map/dot_general | solution.py:18
  137.9 2.2 multiply_reduce_fusion.2
  140.2 14.2 %sum_kernel.2 = f32[32,128]{1,0:T(8,128)S(1)} custom-call(f32[32,128]{1,0:T(8,128)S(1)} %reshape.558.value), custom_call_target="tpu_custom_call" | custom-call | bytes 30000000 | tf_op jit(solution)/shard_map/sum_kernel/pallas_call | solution.py:822
  155.0 2.7 multiply_multiply_fusion
  158.7 1.7 slice_negate_fusion.2
  160.3 6.1 all-to-all-start
  166.4 1.7 fusion.36
  168.1 6.4 fusion.16
  174.6 3.2 collective-permute-start.1
  180.1 2.3 collective-permute-start
  184.8 1.9 fusion.12
  186.8 6.3 fusion.14
  193.1 5.1 fusion.60
  198.2 1.3 collective-permute-done
  199.5 4.2 fusion.10
  203.7 1.3 copy.126
  205.1 6.8 convolution_convert_fusion.3.partial
  212.0 108.6 %hidden_kernel.1 = (bf16[2048,2048]{1,0:T(8,128)(2,1)}, f32[128,2048]{1,0:T(8,128)S(1)}, f32[128,2048]{1,0:T(8,128)S(1)}, bf16[8,2,128,1024]{3,2,1,0:T(8,128)(2,1)}, bf16[8,2,256,256]{3,2,1,0:T(8,128)(2,1)S(1)}) custom-call(bf16[2048,2048]{1,0:T(8,128)(2,1)} %convolution_convert_fusion.3.partial, ...), custom_call_target="tpu_custom_call" | custom-call | bytes 300000000 | tf_op jit(solution)/shard_map/hidden_kernel/pallas_call | solution.py:822
  320.6 14.6 %fusion.62 = f32[2048,1024]{0,1:T(8,128)} fusion(bf16[2048,2048]{1,0:T(8,128)(2,1)} %get-tuple-element.46, bf16[2048,1024]{1,0:T(8,128)(2,1)} %bitcast.305), kind=kOutput, calls=%fused_computation.173 | convolution fusion | flops 8589934592 | bytes 20971520 | tf_op jit(solution)/shard_map/dot_general | solution.py:18
  335.2 4.7 multiply_convert_fusion.3
  341.8 6.8 convolution_convert_fusion.2.partial
  348.6 104.4 %turn_kernel.1 = (bf16[2048,2048]{1,0:T(8,128)(2,1)}, bf16[256,2048]{1,0:T(8,128)(2,1)S(1)}, f32[1,2048]{1,0:T(1,128)S(1)}) custom-call(bf16[2048,2048]{1,0:T(8,128)(2,1)} %convolution_convert_fusion.2.partial, f32[128,2048]{1,0:T(8,128)S(1)} %get-tuple-element.49.hidden, bf16[128,2048]{1,0:T(8,128)(2,1)S(1)} %constant_dynamic-slice_fusion.cotangent, ...), custom_call_target="tpu_custom_call" | custom-call | bytes 300000000 | tf_op jit(solution)/shard_map/turn_kernel/pallas_call | solution.py:822
  453.1 9.4 %convolution_convert_fusion.5.down_grad = bf16[512,2048]{1,0:T(8,128)(2,1)} fusion(bf16[2048,512]{0,1:T(8,128)(2,1)S(1)} %multiply_convert_fusion.3, bf16[2048,2048]{1,0:T(8,128)(2,1)} %get-tuple-element.51), kind=kOutput, calls=%fused_computation.19 | convolution fusion | flops 4296015872 | bytes 12582912 | tf_op jit(solution)/shard_map/rd,rf->df/dot_general | solution.py:22
  462.5 10.8 %multiply_convert_fusion.2 = (bf16[2048,512]{0,1:T(8,128)(2,1)S(1)}, bf16[2048,512]{0,1:T(8,128)(2,1)S(1)}) fusion(f32[2048,1024]{0,1:T(8,128)} %fusion.62, bf16[2048,2048]{1,0:T(8,128)(2,1)} %get-tuple-element.51, bf16[512,2048]{1,0:T(8,128)(2,1)S(1)} %bitcast.270), kind=kOutput, calls=%fused_computation.13 | convolution fusion | flops 4308598784 | bytes 23068672 | tf_op jit(solution)/shard_map/rf,df->rd/dot_general | solution.py:26
  473.3 12.0 %convolution_convert_fusion.4 = bf16[2048,1024]{1,0:T(8,128)(2,1)} fusion(bf16[2048,2048]{1,0:T(8,128)(2,1)S(1)} %bitcast.304, bf16[2048,512]{0,1:T(8,128)(2,1)S(1)} %get-tuple-element.74, bf16[2048,512]{0,1:T(8,128)(2,1)S(1)} %get-tuple-element.73), kind=kOutput, calls=%fused_computation.18 | convolution fusion | flops 8600420352 | bytes 16777216 | tf_op jit(solution)/shard_map/rd,rf->df/dot_general | solution.py:22
  485.4 11.5 %convolution_convert_fusion.1.partial = bf16[2048,2048]{1,0:T(8,128)(2,1)} fusion(bf16[2048,1024]{1,0:T(8,128)(2,1)S(1)} %bitcast.306, bf16[2048,512]{0,1:T(8,128)(2,1)S(1)} %get-tuple-element.74, bf16[2048,512]{0,1:T(8,128)(2,1)S(1)} %get-tuple-element.73), kind=kOutput, calls=%fused_computation.2 | convolution fusion | flops 8602517504 | bytes 16777216 | tf_op jit(solution)/shard_map/rf,df->rd/dot_general | solution.py:26
  496.9 102.8 %branch_kernel.1 = (bf16[2048,2048]{1,0:T(8,128)(2,1)}, f32[128,2048]{1,0:T(8,128)S(1)}, f32[1,2048]{1,0:T(1,128)S(1)}, bf16[8,128,1024]{2,1,0:T(8,128)(2,1)S(1)}, bf16[256,2048]{1,0:T(8,128)(2,1)S(1)}) custom-call(bf16[2048,2048]{1,0:T(8,128)(2,1)} %convolution_convert_fusion.1.partial, f32[128,2048]{1,0:T(8,128)S(1)} %get-tuple-element.52.branch, ...), custom_call_target="tpu_custom_call" | custom-call | bytes 300000000 | tf_op jit(solution)/shard_map/branch_kernel/pallas_call | solution.py:822
  599.8 6.9 convolution_convert_fusion.8
  606.7 2.1 convolution_convert_fusion.7
  609.2 1.3 copy.138
  610.5 2.3 copy.139
  612.8 5.2 all-to-all-start.3
  618.1 4.6 convolution_bitcast_fusion
  622.7 2.0 multiply_reduce_fusion
  625.5 1.3 copy-done.12
  627.7 1.3 copy-done.14
  635.1 2.1 slice.171
  638.5 6.1 fusion.34
  645.0 2.3 fusion.1
  647.3 6.2 maximum_add_fusion
  653.5 1.7 fusion.56
  655.2 6.4 all-to-all-start.2
  661.7 5.6 maximum_add_fusion.1
  667.4 2.8 fusion.21
  670.5 39.1 %sum_kernel.3 = f32[32,128]{1,0:T(8,128)S(1)} custom-call(f32[32,128]{1,0:T(8,128)S(1)} %reshape.576.value), custom_call_target="tpu_custom_call" | custom-call | bytes 30000000 | tf_op jit(solution)/shard_map/sum_kernel/pallas_call | solution.py:822
  709.6 2.4 fusion.11
  712.0 2.0 copy.135
  714.1 3.7 fusion.23
  717.8 6.8 convolution_convert_fusion.partial
  724.7 9.2 %convolution_convert_fusion.6 = bf16[2048,384]{1,0:T(8,128)(2,1)} fusion(bf16[2048,2048]{1,0:T(8,128)(2,1)} %get-tuple-element.40, bf16[2048,128]{1,0:T(8,128)(2,1)S(1)} %bitcast.284, bf16[2048,128]{1,0:T(8,128)(2,1)S(1)} %get-tuple-element.78, bf16[2048,128]{1,0:T(8,128)(2,1)S(1)} %get-tuple-element.77), kind=kOutput, calls=%fused_computation.20 | convolution fusion | flops 3226730496 | bytes 11534336 | tf_op jit(solution)/shard_map/rd,rf->df/dot_general | solution.py:22
  735.1 122.8 %last_kernel.1 = (f32[256,2048]{1,0:T(8,128)}, bf16[8,2,128,384]{3,2,1,0:T(8,128)(2,1)S(1)}, bf16[8,2,64,256]{3,2,1,0:T(8,128)(2,1)S(1)}, f32[8,2,8,128]{3,2,1,0...) custom-call(bf16[2048,2048]{1,0:T(8,128)(2,1)} %convolution_convert_fusion.partial, ...), custom_call_target="tpu_custom_call" | custom-call | bytes 240000000 | tf_op jit(solution)/shard_map/last_kernel/pallas_call | solution.py:822
  858.7 2.5 fusion.53
  862.0 2.7 copy.160
  865.3 2.7 copy.161
  868.0 2.5 bitcast_convert_fusion
  877.6 3.1 copy.193
  (200 shorter events, 39.5 us)
Async XLA Ops:
  0.6 21.0 %copy-start = (bf16[4096,256]{1,0:T(8,128)(2,1)S(1)}, bf16[4096,256]{1,0:T(8,128)(2,1)}, u32[]{:S(2)}) copy-start(bf16[4096,256]{1,0:T(8,128)(2,1)} %param.25) | copy-start | bytes 6291460
  0.7 4.7 copy-start.39
  0.7 4.8 copy-start.40
  0.7 4.9 copy-start.42
  0.7 4.9 copy-start.43
  0.7 4.9 copy-start.44
  16.4 6.3 copy-start.28
  109.4 1.2 copy-start.9
  110.6 49.8 %all-to-all-start.1 = ((bf16[8,256,256]{2,1,0:T(8,128)(2,1)}), bf16[8,256,256]{2,1,0:T(8,128)(2,1)S(1)}, u32[]{:S(2)}, u32[]{:S(2)}) async-start(bf16[8,256,256]{2,1,0:T(8,128)(2,1)} %constant_dynamic-slice_fusion.8), calls=%async_computation.1 | async-start | bytes 2097152 | tf_op jit(solution)/shard_map/all_to_all | solution.py:953
  154.8 5.6 copy-start.35
  154.8 5.5 copy-start.37
  155.0 5.3 copy-start.31
  155.0 5.3 copy-start.33
  157.7 1.0 copy-start.13
  160.3 51.6 %all-to-all-start = ((bf16[8,128,1024]{2,1,0:T(8,128)(2,1)}), bf16[8,128,1024]{2,1,0:T(8,128)(2,1)}, u32[]{:S(2)}, u32[]{:S(2)}) async-start(bf16[8,128,1024]{2,1,0:T(8,128)(2,1)} %pad_maximum_fusion.3), calls=%async_computation | async-start | bytes 4194304 | tf_op jit(solution)/shard_map/all_to_all | solution.py:953
  174.6 18.5 %copy-start.25 = (bf16[8,256,1,128]{3,1,0,2:T(8,128)(2,1)}, bf16[8,256,1,128]{3,1,0,2:T(8,128)(2,1)S(1)}, u32[]{:S(2)}) copy-start(bf16[8,256,1,128]{3,1,0,2:T(8,128)(2,1)S(1)} %fusion.16) | copy-start | bytes 1572868
  174.6 18.5 %collective-permute-start.1 = (bf16[8,256,1,128]{3,1,0,2:T(8,128)(2,1)S(1)}, bf16[8,256,1,128]{3,1,0,2:T(8,128)(2,1)}, u32[]{:S(2)}, u32[]{:S(2)}) collective-permute-start(bf16[8,256,1,128]{3,1,0,2:T(8,128)(2,1)S(1)} %fusion.16), channel_id=1, source_target_pairs={{0,2},{1,3},{4,6},{5,7},{8,10},{9,11},{12,14},{13,15},{16,18},{17,... | collective-permute-start | bytes 1572872 | tf_op jit(solution)/shard_map/ppermute | solution.py:1091
  180.1 19.4 %collective-permute-start = (bf16[8,256,1,128]{1,3,0,2:T(8,128)(2,1)}, bf16[8,256,1,128]{1,3,0,2:T(8,128)(2,1)}, u32[]{:S(2)}, u32[]{:S(2)}) collective-permute-start(bf16[8,256,1,128]{1,3,0,2:T(8,128)(2,1)} %copy.120), channel_id=1, source_target_pairs={{0,2},{1,3},{4,6},{5,7},{8,10},{9,11},{12,14},{13,15},{16,18},{17,... | collective-permute-start | bytes 1572872 | tf_op jit(solution)/shard_map/ppermute | solution.py:1090
  205.1 6.9 copy-start.17
  453.0 9.5 %copy-start.5 = (bf16[256,2048]{1,0:T(8,128)(2,1)}, bf16[256,2048]{1,0:T(8,128)(2,1)S(1)}, u32[]{:S(2)}) copy-start(bf16[256,2048]{1,0:T(8,128)(2,1)S(1)} %get-tuple-element.131) | copy-start | bytes 3145732
  453.1 20.2 %slice-start = ((s8[8388608]{0:T(1024)(128)(4,1)}), s8[4194304]{0:T(1024)(128)(4,1)S(1)}, s32[]{:S(2)}) async-start(s8[8388608]{0:T(1024)(128)(4,1)} %bitcast.303), calls=%async_computation.4 | async-start | bytes 8388608
  462.5 10.8 %slice-start.1 = ((s8[8388608]{0:T(1024)(128)(4,1)}), s8[4194304]{0:T(1024)(128)(4,1)S(1)}, s32[]{:S(2)}) async-start(s8[8388608]{0:T(1024)(128)(4,1)} %bitcast.303), calls=%async_computation.5 | async-start | bytes 8388608
  473.3 12.1 %copy-start.41 = (bf16[8,2,128,1024]{3,2,1,0:T(8,128)(2,1)S(1)}, bf16[8,2,128,1024]{3,2,1,0:T(8,128)(2,1)}, u32[]{:S(2)}) copy-start(bf16[8,2,128,1024]{3,2,1,0:T(8,128)(2,1)} %get-tuple-element.47) | copy-start | bytes 12582916
  496.9 102.8 %copy-start.27 = (bf16[16,8,8,256]{3,1,2,0:T(8,128)(2,1)S(1)}, bf16[16,8,8,256]{3,1,2,0:T(8,128)(2,1)}, u32[]{:S(2)}) copy-start(bf16[16,8,8,256]{3,1,2,0:T(8,128)(2,1)} %copy.163) | copy-start | bytes 1572868
  599.7 7.0 copy-start.3
  599.8 7.0 copy-start.11
  599.8 7.0 copy-start.18
  606.7 2.1 copy-start.22
  612.8 42.4 %all-to-all-start.3 = ((bf16[8,256,256]{2,1,0:T(8,128)(2,1)}), bf16[8,256,256]{2,1,0:T(8,128)(2,1)S(1)}, u32[]{:S(2)}, u32[]{:S(2)}) async-start(bf16[8,256,256]{2,1,0:T(8,128)(2,1)} %bitcast.262), calls=%async_computation.3 | async-start | bytes 2097152 | tf_op jit(solution)/shard_map/all_to_all | solution.py:953
  618.0 4.6 copy-start.23
  618.0 4.6 copy-start.29
  618.1 4.6 copy-start.45
  624.7 2.1 copy-start.26
  625.5 1.3 copy-start.12
  627.7 1.4 copy-start.14
  629.9 17.4 %collective-permute-start.2 = (bf16[8,256,1,128]{3,1,0,2:T(8,128)(2,1)}, bf16[8,256,1,128]{3,1,0,2:T(8,128)(2,1)}, u32[]{:S(2)}, u32[]{:S(2)}) collective-permute-start(bf16[8,256,1,128]{3,1,0,2:T(8,128)(2,1)} %slice.172), channel_id=1, source_target_pairs={{2,0},{3,1},{6,4},{7,5},{10,8},{11,9},{14,12},{15,13},{18,16},{19,... | collective-permute-start | bytes 1572872 | tf_op jit(solution)/shard_map/ppermute | solution.py:1160
  637.2 72.4 %collective-permute-start.3 = (bf16[8,256,1,128]{1,3,0,2:T(8,128)(2,1)}, bf16[8,256,1,128]{1,3,0,2:T(8,128)(2,1)}, u32[]{:S(2)}, u32[]{:S(2)}) collective-permute-start(bf16[8,256,1,128]{1,3,0,2:T(8,128)(2,1)} %slice.171), channel_id=1, source_target_pairs={{2,0},{3,1},{6,4},{7,5},{10,8},{11,9},{14,12},{15,13},{18,16},{19,... | collective-permute-start | bytes 1572872 | tf_op jit(solution)/shard_map/ppermute | solution.py:1159
  638.5 6.5 copy-start.19
  644.9 2.4 copy-start.15
  653.5 8.2 copy-start.16
  655.2 12.1 %copy-start.32 = (f32[2048]{0:T(1024)S(1)}, f32[2048]{0:T(1024)}, u32[]{:S(2)}) copy-start(f32[2048]{0:T(1024)} %copy-done.31) | copy-start | bytes 24580
  655.2 12.1 %copy-start.34 = (f32[2048]{0:T(1024)S(1)}, f32[2048]{0:T(1024)}, u32[]{:S(2)}) copy-start(f32[2048]{0:T(1024)} %copy-done.33) | copy-start | bytes 24580
  655.2 12.2 %copy-start.36 = (f32[128]{0:T(128)S(1)}, f32[128]{0:T(128)}, u32[]{:S(2)}) copy-start(f32[128]{0:T(128)} %copy-done.35) | copy-start | bytes 1540
  655.2 12.2 %copy-start.38 = (f32[128]{0:T(128)S(1)}, f32[128]{0:T(128)}, u32[]{:S(2)}) copy-start(f32[128]{0:T(128)} %copy-done.37) | copy-start | bytes 1540
  655.2 78.6 %all-to-all-start.2 = ((bf16[8,128,1024]{2,1,0:T(8,128)(2,1)}), bf16[8,128,1024]{2,1,0:T(8,128)(2,1)}, u32[]{:S(2)}, u32[]{:S(2)}) async-start(bf16[8,128,1024]{2,1,0:T(8,128)(2,1)} %fusion.1), calls=%async_computation.2 | async-start | bytes 4194304 | tf_op jit(solution)/shard_map/all_to_all | solution.py:953
  661.7 5.7 copy-start.20
  667.3 2.9 copy-start.21
  709.6 8.2 copy-start.10
  714.1 3.8 copy-start.30
  724.7 9.2 %copy-start.2 = (bf16[2,64,8,256]{3,1,0,2:T(8,128)(2,1)S(1)}, bf16[2,64,8,256]{3,1,0,2:T(8,128)(2,1)}, u32[]{:S(2)}) copy-start(bf16[2,64,8,256]{3,1,0,2:T(8,128)(2,1)} %copy.179) | copy-start | bytes 1572868
  733.9 1.2 copy-start.4
  857.9 0.8 copy-start.7
  865.3 2.7 copy-start.24
  870.5 3.8 copy-start.8
  870.9 5.7 copy-start.6
  873.2 7.6 copy-start.1

commit v3 on v2

--- a/solution.py
+++ b/solution.py
@@ -322,7 +322,7 @@
     ]
 
 
-def gather_phase(place, sender, gathered, scratch, between=None):
+def gather_phase(place, sender, gathered, scratch, between=None, later=None):
     own, local_sem, core_sem, y_sem, line_sem = scratch
     rows = own.shape[0]
     z, y, core = place.z, place.y, place.core
@@ -398,6 +398,8 @@
         else:
             across(z >= distance - 1, z - distance + 1)
             across(z + distance - 1 < LINE, z + distance - 1)
+        if distance == 1 and later is not None:
+            later()
 
     keep.wait()
     for block in range(LINE):
@@ -444,31 +446,31 @@
 
 
 class Swap:
-    def __init__(self, place, pieces, wholes, scratch):
+    def __init__(self, place, pairs, scratch):
         self.place = place
-        self.pairs = list(zip(pieces, wholes))
+        self.pairs = pairs
         self.local_sem, self.out_sem, self.side_sem = scratch
 
     def send(self, index, step):
         place = self.place
-        pieces, whole = self.pairs[index]
+        source, spot = self.pairs[index]
         target = lax.rem(place.device + step, place.count)
         return remote(
-            pieces.at[target],
-            whole.at[place.device, place.side],
+            source(target),
+            spot(place.device, place.side),
             self.out_sem.at[0, index, step],
             self.out_sem.at[1, index, step],
             {"fsdp": target},
         )
 
     def taken(self, index, step, side):
-        source = lax.rem(self.place.device + self.place.count - step, self.place.count)
-        return self.pairs[index][1].at[source, side]
+        device = lax.rem(self.place.device + self.place.count - step, self.place.count)
+        return self.pairs[index][1](device, side)
 
     def come(self, index, step):
         place = self.place
         return remote(
-            self.pairs[index][0].at[0],
+            self.pairs[index][0](place.device),
             self.taken(index, step, place.side),
             self.out_sem.at[0, index, step],
             self.out_sem.at[1, index, step],
@@ -497,9 +499,9 @@
 
     def keep(self, index):
         place = self.place
-        pieces, whole = self.pairs[index]
+        source, spot = self.pairs[index]
         return pltpu.make_async_copy(
-            pieces.at[place.device], whole.at[place.device, place.side], self.local_sem.at[index]
+            source(place.device), spot(place.device, place.side), self.local_sem.at[index]
         )
 
     def each(self, first, body):
@@ -512,9 +514,9 @@
 
     def start(self):
         self.each(1, lambda index, step: self.send(index, step).start())
-        for index, (pieces, whole) in enumerate(self.pairs):
+        for index, (source, _) in enumerate(self.pairs):
             self.keep(index).start()
-            self.share(index, 0, pieces.at[self.place.device]).start()
+            self.share(index, 0, source(self.place.device)).start()
 
     def pass_on(self):
         def one(index, step):
@@ -529,6 +531,10 @@
         self.each(0, lambda index, step: self.shared(index, step).wait_recv())
         self.each(1, lambda index, step: self.send(index, step).wait_send())
         self.each(0, lambda index, step: self.share(index, step).wait_send())
+
+
+def whole_pair(pieces, whole):
+    return (lambda target: pieces.at[target], lambda device, side: whole.at[device, side])
 
 
 def halves_scratch(arrays):
@@ -571,15 +577,44 @@
 GATHER = 5
 
 
-def first_kernel(own_ref, qkv, out, small, gathered, qkv_all, out_all, small_all, *scratch):
+def first_kernel(
+    own_ref, query, key, value, out, small, gathered, qkv_all, out_all, small_all, *scratch
+):
     place = Place()
     sender = Sender()
     own = scratch[0]
     own[...] = own_ref[...]
     greet_all(place)
-    swap = Swap(place, (small, qkv, out), (small_all, qkv_all, out_all), scratch[GATHER:])
-    gather_phase(place, sender, gathered, scratch[:GATHER], swap.start)
-    swap.pass_on()
+    half, columns = qkv_all.shape[2], qkv_all.shape[3] // 3
+    out_half = out_all.shape[2]
+    rows = pl.ds(pl.multiple_of(place.side * half, half), half)
+
+    def member(target):
+        return lax.rem(target, 2 * LINE)
+
+    def column_pair(weight, index):
+        def source(target):
+            start = pl.multiple_of(member(target) * columns, columns)
+            return weight.at[rows, pl.ds(start, columns)]
+
+        def spot(device, side):
+            return qkv_all.at[device, side, :, pl.ds(index * columns, columns)]
+
+        return (source, spot)
+
+    def out_source(target):
+        start = (2 * member(target) + place.side) * out_half
+        return out.at[pl.ds(pl.multiple_of(start, out_half), out_half)]
+
+    pairs = [
+        (lambda target: small, lambda device, side: small_all.at[device, side]),
+        column_pair(query, 0),
+        column_pair(key, 1),
+        column_pair(value, 2),
+        (out_source, lambda device, side: out_all.at[device, side]),
+    ]
+    swap = Swap(place, pairs, scratch[GATHER:])
+    gather_phase(place, sender, gathered, scratch[:GATHER], swap.start, swap.pass_on)
     swap.finish()
     sender.drain()
 
@@ -694,20 +729,16 @@
     qkv,
     out,
     small,
-    pair,
-    down,
     result,
     qkv_all,
     out_all,
     small_all,
-    pair_all,
-    down_all,
     *scratch,
 ):
     place = Place()
     sender = Sender()
     parts = scratch[REDUCE + 1 :]
-    swap_sems, halves_sems, parts = parts[:3], parts[3:4], parts[4:]
+    swap_sems, parts = parts[:3], parts[3:]
     qkv_own, qkv_other, out_own, out_other, small_own, small_other, fetch_sem, side_sem = parts
     greet_all(place)
     fetches, crossings = [], []
@@ -737,10 +768,8 @@
     )
     for copy in fetches + crossings:
         copy.start()
-    swap = Swap(
-        place, (small_own, qkv_own, out_own), (small_all, qkv_all, out_all), swap_sems
-    )
-    halves = Halves(place, (pair, down), (pair_all, down_all), halves_sems)
+    pairs = ((small_own, small_all), (qkv_own, qkv_all), (out_own, out_all))
+    swap = Swap(place, [whole_pair(*pair) for pair in pairs], swap_sems)
     shared_rows = 2 * partial.shape[1] // place.count // 128
 
     def between():
@@ -748,7 +777,6 @@
             fetch.wait()
         for crossing in crossings:
             crossing.wait()
-        halves.start()
         small_own[...] = small[...]
         small_own[:, :shared_rows] += small_other[:, :shared_rows]
 
@@ -774,21 +802,26 @@
     finish = pair_phase(place, sender, total, result, scratch[REDUCE : REDUCE + 1])
     swap.pass_on()
     finish()
-    halves.finish()
     swap.finish()
     sender.drain()
 
 
-def sum_kernel(value, result, core_in, y_in, held, line_in, sem):
+def sum_kernel(carried, value, *rest):
+    if carried:
+        moved, result, arrived, core_in, y_in, held, line_in, sem, side_sem = rest
+    else:
+        result, core_in, y_in, held, line_in, sem = rest
     place = Place()
-    sender = Sender()
     z, y, core = place.z, place.y, place.core
     barrier = pltpu.get_barrier_semaphore()
     others = [place.at(z, y, 1 - core), place.at(z, 1 - y, core)]
     others += [place.at(lax.rem(z + k, LINE), y, core) for k in range(1, LINE)]
-    for device in others:
-        pl.semaphore_signal(barrier, inc=1, device_id=device, device_id_type=MESH_ID)
-    pl.semaphore_wait(barrier, len(others))
+    for device in others + [place.across()] * carried:
+        signal(barrier, device)
+    pl.semaphore_wait(barrier, len(others) + carried)
+    if carried:
+        side = remote(moved, arrived, side_sem.at[0], side_sem.at[1], place.across())
+        side.start()
     first = remote(value, core_in, sem.at[0, 0], sem.at[1, 0], others[0])
     first.start()
     first.wait_recv()
@@ -815,9 +848,18 @@
     second.wait_send()
     for send in sends:
         send.wait_send()
-
-
-def talk(kernel, which, shapes, specs, scratch, microseconds):
+    if carried:
+        side.wait()
+
+
+def pack_kernel(side, gate, up, down, pair_out, down_out):
+    columns = gate.shape[1]
+    pair_out[0, :, :columns] = gate[...]
+    pair_out[0, :, columns:] = up[...]
+    down_out[0] = down[...]
+
+
+def talk(kernel, which, shapes, specs, scratch, microseconds, name=None):
     def call(*operands):
         return pl.pallas_call(
             kernel,
@@ -831,7 +873,7 @@
             cost_estimate=pl.CostEstimate(
                 flops=0, bytes_accessed=int(microseconds * 3.0e6), transcendentals=0
             ),
-            name=kernel.__name__,
+            name=name or kernel.__name__,
         )(*operands)
 
     return call
@@ -864,15 +906,55 @@
         shape = (pieces.shape[0], 2) + pieces.shape[1:]
         return jax.ShapeDtypeStruct(shape, pieces.dtype)
 
-    def first(self, own, qkv, out, small):
+    def first(self, own, weights, out, small):
+        rows, columns = weights[0].shape
+        rows, columns = rows // 2, columns // self.size
+        out_rows = out.shape[0] // self.size // 2
         return talk(
             first_kernel,
             0,
-            (self.all_low, self.whole(qkv), self.whole(out), self.whole(small)),
-            ([VMEM] * 4, (HBM,) * 4),
-            self.gathers + swap_scratch(self.fsdp, 3),
+            (
+                self.all_low,
+                jax.ShapeDtypeStruct((self.fsdp, 2, rows, 3 * columns), BF),
+                jax.ShapeDtypeStruct((self.fsdp, 2, out_rows, out.shape[1]), BF),
+                jax.ShapeDtypeStruct((self.fsdp, 2) + small.shape, F32),
+            ),
+            ([VMEM] * 6, (HBM,) * 4),
+            self.gathers + swap_scratch(self.fsdp, 5),
             80,
-        )(own, qkv, out, small)
+        )(own, *weights, out, small)
+
+    def pack(self, gate, up, down):
+        rows, columns = gate.shape
+        rows, columns = rows // 2, columns // self.size
+        down_rows, down_columns = down.shape
+        down_rows = down_rows // self.size // 2
+
+        def column_spec():
+            return pl.BlockSpec((rows, columns), lambda d, side: (side[0], d))
+
+        def piece_spec(*shape):
+            return pl.BlockSpec((1,) + shape, lambda d, side: (d, 0, 0))
+
+        pair, low = pl.pallas_call(
+            pack_kernel,
+            grid_spec=pltpu.PrefetchScalarGridSpec(
+                num_scalar_prefetch=1,
+                grid=(self.size,),
+                in_specs=[
+                    column_spec(),
+                    column_spec(),
+                    pl.BlockSpec((down_rows, down_columns), lambda d, side: (2 * d + side[0], 0)),
+                ],
+                out_specs=[piece_spec(rows, 2 * columns), piece_spec(down_rows, down_columns)],
+            ),
+            out_shape=[
+                jax.ShapeDtypeStruct((self.size, rows, 2 * columns), BF),
+                jax.ShapeDtypeStruct((self.size, down_rows, down_columns), BF),
+            ],
+            name="pack_kernel",
+        )(self.context.reshape(1).astype(jnp.int32), gate, up, down)
+        return self.repeat(pair), self.repeat(low)
 
     def hidden(self, partial, tokens, gain, pair, down):
         return talk(
@@ -908,7 +990,7 @@
             100,
         )(partial, branch, cotangent, gain, pair_grad, down_grad)
 
-    def last(self, partial, grad_hidden, qkv, out, small, pair, down):
+    def last(self, partial, grad_hidden, qkv, out, small):
         both = jax.ShapeDtypeStruct((2 * self.rows, self.width), F32)
 
         def same(array):
@@ -921,27 +1003,32 @@
         return talk(
             last_kernel,
             4,
-            (both, same(qkv), same(out), self.whole(small), self.whole(pair), self.whole(down)),
-            ([HBM, VMEM, HBM, HBM, VMEM, VMEM, VMEM], (HBM,) * 6),
+            (both, same(qkv), same(out), self.whole(small)),
+            ([HBM, VMEM, HBM, HBM, VMEM], (HBM,) * 4),
             self.reduces
             + pair_scratch()
             + swap_scratch(self.fsdp, 3)
-            + halves_scratch(2)
             + [half(qkv), half(qkv), half(out), half(out), held, held, DMA((2,)), DMA((2, 3))],
             80,
-        )(partial, grad_hidden, qkv, out, small, pair, down)
-
-    def total(self, values):
+        )(partial, grad_hidden, qkv, out, small)
+
+    def total(self, values, moved=None):
         flat = values.reshape(-1, 128)
+        carried = int(moved is not None)
         shape = jax.ShapeDtypeStruct(flat.shape, F32)
         scratch = [pltpu.VMEM(flat.shape, F32)] * 2
         scratch += [pltpu.VMEM((2,) + flat.shape, F32), pltpu.VMEM((LINE,) + flat.shape, F32)]
-        scratch += [DMA((2, LINE + 1))]
+        scratch += [DMA((2, LINE + 1))] + [DMA((2,))] * carried
         which = 5 + self.sums
         self.sums += 1
-        return talk(sum_kernel, which, shape, ([VMEM], VMEM), scratch, 10)(flat).reshape(
-            values.shape
-        )
+        kernel = functools.partial(sum_kernel, carried)
+        if not carried:
+            call = talk(kernel, which, shape, ([VMEM], VMEM), scratch, 10, "sum_kernel")
+            return call(flat).reshape(values.shape)
+        shapes = (shape, jax.ShapeDtypeStruct(moved.shape, moved.dtype))
+        call = talk(kernel, which, shapes, ([VMEM] * 2, (VMEM,) * 2), scratch, 10, "sum_kernel")
+        total, came = call(flat, moved)
+        return total.reshape(values.shape), came
 
     sums = 0
 
@@ -955,17 +1042,11 @@
     def repeat(self, pieces):
         return jnp.concatenate([pieces] * self.teams, axis=0) if self.teams > 1 else pieces
 
-    def column_pieces(self, weights):
-        pieces = []
-        for weight in weights:
-            rows, columns = weight.shape
-            part = self.half(weight, 0).reshape(rows // 2, self.size, columns // self.size)
-            pieces.append(part.transpose(1, 0, 2))
-        return self.repeat(jnp.concatenate(pieces, axis=2))
-
-    def row_pieces(self, weight):
-        rows, columns = weight.shape
-        return self.repeat(self.half(weight.reshape(self.size, rows // self.size, columns), 1))
+    def both_sides(self, half):
+        other = lax.ppermute(half, "context", [(0, 1), (1, 0)])
+        low = jnp.where(self.context == 0, half, other)
+        high = jnp.where(self.context == 0, other, half)
+        return jnp.stack([low, high], axis=1)
 
     def columns_whole(self, came):
         return came.reshape(-1, came.shape[-1])
@@ -1037,12 +1118,9 @@
     share = attn_gain.size
     small = [query_gain.reshape(-1), key_gain.reshape(-1), attn_gain, mlp_gain]
     small = jnp.concatenate([one.astype(F32) for one in small + [cont_lengths.reshape(-1)]])
-    small = jnp.pad(small, (0, 8 * 128 - small.size)).reshape(1, 8, 128)
+    small = jnp.pad(small, (0, 8 * 128 - small.size)).reshape(8, 128)
     tokens_all, qkv_came, output_came, small_came = team.first(
-        tokens_own,
-        team.column_pieces([w_query, w_key, w_value]),
-        team.row_pieces(w_output),
-        jnp.broadcast_to(small, (fsdp, 8, 128)),
+        tokens_own, [w_query, w_key, w_value], w_output, small
     )
     qkv_w = team.columns_whole(qkv_came)
     output_w = team.rows_whole(output_came)
@@ -1069,7 +1147,7 @@
     sine = sine[:, :, None, :]
 
     pair_mine, down_mine, tokens_all = lax.optimization_barrier(
-        (team.column_pieces([w_gate, w_up]), team.row_pieces(w_down), tokens_all)
+        team.pack(w_gate, w_up, w_down) + (tokens_all,)
     )
     pair_came = team.swap(pair_mine)
     down_came = team.swap(down_mine)
@@ -1077,17 +1155,18 @@
     by_head = (groups, rows, heads, head_size)
     raw = product(tokens_all, qkv_w)
     query_raw, key_raw, value_raw = jnp.split(raw, 3, axis=1)
-    sums = team.total(
-        jnp.stack([jnp.sum(query_raw * query_raw, axis=1), jnp.sum(key_raw * key_raw, axis=1)])
-    )
+    value_low = value_raw.astype(BF)
+    sums, sent_value = team.total(
+        jnp.stack([jnp.sum(query_raw * query_raw, axis=1), jnp.sum(key_raw * key_raw, axis=1)]),
+        value_low,
+    )
+    value_low, sent_value = value_low.reshape(by_head), sent_value.reshape(by_head)
     scale_query = lax.rsqrt(sums[0] / width + EPS)[:, None]
     scale_key = lax.rsqrt(sums[1] / width + EPS)[:, None]
     query_norm = query_raw * scale_query * flat_query
     key_norm = key_raw * scale_key * flat_key
     query_low = rotate(query_norm.reshape(by_head), cosine, sine).astype(BF)
     key_low = rotate(key_norm.reshape(by_head), cosine, sine).astype(BF)
-    value_low = value_raw.reshape(by_head).astype(BF)
-    sent_value = lax.ppermute(value_low, "context", [(0, 1)])
     sent_key = lax.ppermute(key_low, "context", [(0, 1)])
     keys_all = jnp.concatenate([sent_key, key_low], axis=1)
     values_all = jnp.concatenate([sent_value, value_low], axis=1)
@@ -1191,14 +1270,14 @@
     ]
     used = 2 * share + 2 * heads * head_share
     small = jnp.concatenate(small + [jnp.zeros((fsdp, 8 * 128 - used), F32)], axis=1)
-    input_grad, qkv_came, output_came, small_came, pair_came, down_came = team.last(
+    pair_came = team.both_sides(pair_came)
+    down_came = team.both_sides(down_came)
+    input_grad, qkv_came, output_came, small_came = team.last(
         product_right(grad_qkv, qkv_w).astype(BF),
         grad_hidden,
         qkv_grad,
         output_grad,
         small.reshape(fsdp, 8, 128),
-        pair_came,
-        down_came,
     )
     grad_w_query, grad_w_key, grad_w_value = team.columns_out(qkv_came, 3)
     grad_w_gate, grad_w_up = team.columns_out(pair_came, 2)

time: 894 us -> 883 us (0.988)
  Pallas kernels: 578 us -> 512 us
  waiting for transfers between devices: 1.4 us -> 59.4 us
    pallas_call x7, Pallas kernels: 578 us -> 506 us  [call(): pl.pallas_call(kernel, out_shape=shapes, in_specs=specs[0], out_specs=spe...]
    ppermute x1 -> x2, waiting for transfers between devices: 1.33 us -> 56.3 us  [both_sides(): other = lax.ppermute(half, 'context', [(0, 1), (1, 0)])]
    reshape x2 -> x4, local copies, waits for them, and re-layouts: 5.32 us -> 18.3 us  [columns_out(): return [self.added(part.reshape(size, two * rows, -1)).transpose(1, 0, 2)...]
    unnamed x115 -> x102, local copies, waits for them, and re-layouts: 18 us -> 23.3 us
  transfers between devices with their start and end apart: 8 -> 9, of which waited for: 2 -> 4; matrix products, arithmetic and copies ran while one was open for 14% -> 14% of each run, Pallas kernels for 6% -> 14%
where the time goes in v3:
time: 883 us; the launch traced here: 871 us
  Pallas kernels  512 us (58%)
  matrix products  125 us (14%)
  other arithmetic  70.2 us (8%)
  waiting for transfers between devices  59.4 us (7%)
  local copies, waits for them, and re-layouts  58.5 us (7%)
  starting transfers between devices  43.5 us (5%)
    pallas_call x7, Pallas kernels, call(): pl.pallas_call(kernel, out_shape=shapes, in_specs=specs[0], out_specs=spe...  506 us
    ppermute x2, waiting for transfers between devices, both_sides(): other = lax.ppermute(half, 'context', [(0, 1), (1, 0)])  56.3 us
    dot_general x4, matrix products, product(): return jnp.dot(left, right, preferred_element_type=F32)  38.2 us
    dot_general x4, matrix products, product_right(): return jnp.einsum('rf,df->rd', left, right, preferred_element_type=F32)  35.2 us
    all_to_all x4, starting transfers between devices, swap(): lax.all_to_all(pieces, 'fsdp', split_axis=0, concat_axis=0, tiled=True)  35.2 us
    dot_general x4, matrix products, product_left(): return jnp.einsum('rd,rf->df', left, right, preferred_element_type=F32)  30.8 us
    unnamed x102, local copies, waits for them, and re-layouts  23.3 us
    reshape x4, local copies, waits for them, and re-layouts, columns_out(): return [self.added(part.reshape(size, two * rows, -1)).transpose(1, 0, 2)...  18.3 us
  transfers between devices with their start and end apart: 9, of which 4 were waited for; matrix products, arithmetic and copies ran while one was open for 14% of the time, Pallas kernels for 14%

profile of v3, /device:TPU:16, one launch (start us, length us, event | category | flops | bytes accessed | tf_op | source)
XLA Modules:
  0.0 871.0 jit_solution(12540183013558981634)
XLA Ops:
  4.5 6.3 pack_kernel.1
  10.8 65.9 %first_kernel.1 = (bf16[2048,2048]{1,0:T(8,128)(2,1)}, bf16[8,2,128,384]{3,2,1,0:T(8,128)(2,1)S(1)}, bf16[8,2,64,256]{3,2,1,0:T(8,128)(2,1)S(1)}, f32[8,2,8,128]{3,2,1,0:T(8,128)S(1)}) custom-call(bf16[128,2048]{1,0:T(8,128)(2,1)S(1)} %constant_dynamic-slice_fusion.3.own_ref.tokens, bf16[256,1024]{1,0:T(8,128)(2,1)S(1)} %copy-done.6, ...), custom_call_target="tpu_custom_call" | custom-call | bytes 240000000 | tf_op jit(solution)/shard_map/first_kernel/pallas_call | solution.py:864
  77.9 17.3 %all-to-all-start.1 = ((bf16[8,256,256]{2,1,0:T(8,128)(2,1)}), bf16[8,256,256]{2,1,0:T(8,128)(2,1)S(1)}, u32[]{:S(2)}, u32[]{:S(2)}) async-start(bf16[8,256,256]{2,1,0:T(8,128)(2,1)} %get-tuple-element.51), calls=%async_computation.1 | async-start | bytes 2097152 | tf_op jit(solution)/shard_map/all_to_all | solution.py:1040
  95.2 9.9 %fusion.63 = f32[2048,384]{1,0:T(8,128)} fusion(bf16[2048,2048]{1,0:T(8,128)(2,1)} %get-tuple-element.44, bf16[2048,384]{1,0:T(8,128)(2,1)} %bitcast.248), kind=kOutput, calls=%fused_computation.172 | convolution fusion | flops 3221225472 | bytes 13107200 | tf_op jit(solution)/shard_map/dot_general | solution.py:18
  105.2 2.2 multiply_reduce_fusion.2
  109.3 15.0 %sum_kernel.2 = (f32[32,128]{1,0:T(8,128)S(1)}, bf16[2048,128]{1,0:T(8,128)(2,1)S(1)}) custom-call(f32[32,128]{1,0:T(8,128)S(1)} %reshape.525.value, bf16[2048,128]{1,0:T(8,128)(2,1)S(1)} %split.72.rest_0_), custom_call_target="tpu_custom_call" | custom-call | bytes 30000000 | tf_op jit(solution)/shard_map/sum_kernel/pallas_call | solution.py:864
  124.9 2.7 multiply_multiply_fusion
  128.5 1.7 slice_negate_fusion.2
  130.2 6.6 all-to-all-start
  136.8 1.3 fusion.39
  139.2 6.2 fusion.19
  145.4 3.4 collective-permute-start
  148.9 1.7 fusion.15
  155.0 6.1 fusion.17
  161.1 5.3 fusion.62
  166.5 4.2 fusion.13
  170.7 1.3 copy.145
  172.0 6.7 convolution_convert_fusion.3.partial
  178.7 2.8 all-to-all-done.pair
  181.5 108.6 %hidden_kernel.1 = (bf16[2048,2048]{1,0:T(8,128)(2,1)}, f32[128,2048]{1,0:T(8,128)S(1)}, f32[128,2048]{1,0:T(8,128)S(1)}, bf16[8,2,128,1024]{3,2,1,0:T(8,128)(2,1)}, bf16[8,2,256,256]{3,2,1,0:T(8,128)(2,1)S(1)}) custom-call(bf16[2048,2048]{1,0:T(8,128)(2,1)} %convolution_convert_fusion.3.partial, ...), custom_call_target="tpu_custom_call" | custom-call | bytes 300000000 | tf_op jit(solution)/shard_map/hidden_kernel/pallas_call | solution.py:864
  290.1 14.7 %fusion.64 = f32[2048,1024]{0,1:T(8,128)} fusion(bf16[2048,2048]{1,0:T(8,128)(2,1)} %get-tuple-element.52, bf16[2048,1024]{1,0:T(8,128)(2,1)} %bitcast.293), kind=kOutput, calls=%fused_computation.173 | convolution fusion | flops 8589934592 | bytes 20971520 | tf_op jit(solution)/shard_map/dot_general | solution.py:18
  304.8 4.7 multiply_convert_fusion.3
  311.4 6.9 convolution_convert_fusion.2.partial
  318.3 104.4 %turn_kernel.1 = (bf16[2048,2048]{1,0:T(8,128)(2,1)}, bf16[256,2048]{1,0:T(8,128)(2,1)S(1)}, f32[1,2048]{1,0:T(1,128)S(1)}) custom-call(bf16[2048,2048]{1,0:T(8,128)(2,1)} %convolution_convert_fusion.2.partial, f32[128,2048]{1,0:T(8,128)S(1)} %get-tuple-element.55.hidden, bf16[128,2048]{1,0:T(8,128)(2,1)S(1)} %constant_dynamic-slice_fusion.cotangent, ...), custom_call_target="tpu_custom_call" | custom-call | bytes 300000000 | tf_op jit(solution)/shard_map/turn_kernel/pallas_call | solution.py:864
  422.7 9.5 %convolution_convert_fusion.5.down_grad = bf16[512,2048]{1,0:T(8,128)(2,1)} fusion(bf16[2048,512]{0,1:T(8,128)(2,1)S(1)} %multiply_convert_fusion.3, bf16[2048,2048]{1,0:T(8,128)(2,1)} %get-tuple-element.57), kind=kOutput, calls=%fused_computation.19 | convolution fusion | flops 4296015872 | bytes 12582912 | tf_op jit(solution)/shard_map/rd,rf->df/dot_general | solution.py:22
  432.1 10.8 %multiply_convert_fusion.2 = (bf16[2048,512]{0,1:T(8,128)(2,1)S(1)}, bf16[2048,512]{0,1:T(8,128)(2,1)S(1)}) fusion(f32[2048,1024]{0,1:T(8,128)} %fusion.64, bf16[2048,2048]{1,0:T(8,128)(2,1)} %get-tuple-element.57, bf16[512,2048]{1,0:T(8,128)(2,1)S(1)} %bitcast.267), kind=kOutput, calls=%fused_computation.13 | convolution fusion | flops 4308598784 | bytes 23068672 | tf_op jit(solution)/shard_map/rf,df->rd/dot_general | solution.py:26
  442.9 12.0 %convolution_convert_fusion.4 = bf16[2048,1024]{1,0:T(8,128)(2,1)} fusion(bf16[2048,2048]{1,0:T(8,128)(2,1)S(1)} %bitcast.292, bf16[2048,512]{0,1:T(8,128)(2,1)S(1)} %get-tuple-element.130, bf16[2048,512]{0,1:T(8,128)(2,1)S(1)} %get-tuple-element.129), kind=kOutput, calls=%fused_computation.18 | convolution fusion | flops 8600420352 | bytes 16777216 | tf_op jit(solution)/shard_map/rd,rf->df/dot_general | solution.py:22
  455.0 11.5 %convolution_convert_fusion.1.partial = bf16[2048,2048]{1,0:T(8,128)(2,1)} fusion(bf16[2048,1024]{1,0:T(8,128)(2,1)S(1)} %bitcast.294, bf16[2048,512]{0,1:T(8,128)(2,1)S(1)} %get-tuple-element.130, bf16[2048,512]{0,1:T(8,128)(2,1)S(1)} %get-tuple-element.129), kind=kOutput, calls=%fused_computation.2 | convolution fusion | flops 8602517504 | bytes 16777216 | tf_op jit(solution)/shard_map/rf,df->rd/dot_general | solution.py:26
  466.5 102.8 %branch_kernel.1 = (bf16[2048,2048]{1,0:T(8,128)(2,1)}, f32[128,2048]{1,0:T(8,128)S(1)}, f32[1,2048]{1,0:T(1,128)S(1)}, bf16[8,128,1024]{2,1,0:T(8,128)(2,1)S(1)}, bf16[256,2048]{1,0:T(8,128)(2,1)S(1)}) custom-call(bf16[2048,2048]{1,0:T(8,128)(2,1)} %convolution_convert_fusion.1.partial, f32[128,2048]{1,0:T(8,128)S(1)} %get-tuple-element.58.branch, ...), custom_call_target="tpu_custom_call" | custom-call | bytes 300000000 | tf_op jit(solution)/shard_map/branch_kernel/pallas_call | solution.py:864
  569.3 6.1 convolution_convert_fusion.8
  577.9 2.4 multiply_reduce_fusion
  580.4 2.1 convolution_bitcast_fusion
  584.0 5.7 all-to-all-start.3
  589.6 3.9 multiply_convert_fusion
  594.4 1.3 copy-done.18
  596.7 1.3 collective-permute-start.1
  597.9 2.1 slice.171
  600.0 1.3 collective-permute-start.2
  601.3 2.3 fusion.1
  603.6 5.8 fusion.37
  609.5 1.7 fusion.57
  613.5 5.9 maximum_add_fusion
  619.9 4.1 maximum_add_fusion.1
  624.1 3.0 fusion.24
  627.1 9.4 %sum_kernel.3 = f32[32,128]{1,0:T(8,128)S(1)} custom-call(f32[32,128]{1,0:T(8,128)S(1)} %reshape.546.value), custom_call_target="tpu_custom_call" | custom-call | bytes 30000000 | tf_op jit(solution)/shard_map/sum_kernel/pallas_call | solution.py:864
  637.7 5.6 all-to-all-start.2
  644.6 3.7 fusion.26
  648.4 6.8 convolution_convert_fusion.partial
  655.2 8.0 convolution_convert_fusion.6
  663.2 100.0 %last_kernel.1 = (f32[256,2048]{1,0:T(8,128)}, bf16[8,2,128,384]{3,2,1,0:T(8,128)(2,1)S(1)}, bf16[8,2,64,256]{3,2,1,0:T(8,128)(2,1)S(1)}, f32[8,2,8,128]{3,2,1,0:T(8,128)S(1)}) custom-call(bf16[2048,2048]{1,0:T(8,128)(2,1)} %convolution_convert_fusion.partial, f32[128,2048]{1,0:T(8,128)S(1)} %copy-done.5, bf16[8,2,128,384]{3,2,1,0:T(8,128)(2,1)S(1)} %bitcast.241, ...), custom_call_target="tpu_custom_call" | custom-call | bytes 240000000 | tf_op jit(solution)/shard_map/last_kernel/pallas_call | solution.py:864
  765.4 2.4 collective-permute-start.4
  771.8 20.3 %collective-permute-done.4 = bf16[8,256,256]{2,1,0:T(8,128)(2,1)S(1)} collective-permute-done((bf16[8,256,256]{2,1,0:T(8,128)(2,1)}, bf16[8,256,256]{2,1,0:T(8,128)(2,1)S(1)}, u32[]{:S(2)}, u32[]{:S(2)}) %collective-permute-start.4) | collective-permute-done | bytes 1048608 | tf_op jit(solution)/shard_map/ppermute | solution.py:1046
  792.1 1.4 select_bitcast_fusion.3
  793.6 2.5 bitcast_convert_fusion
  796.1 36.0 %collective-permute-done.3 = bf16[8,128,1024]{2,1,0:T(8,128)(2,1)S(1)} collective-permute-done((bf16[8,128,1024]{2,1,0:T(8,128)(2,1)}, bf16[8,128,1024]{2,1,0:T(8,128)(2,1)S(1)}, u32[]{:S(2)}, u32[]{:S(2)}) %collective-permute-start.3) | collective-permute-done | bytes 2097184 | tf_op jit(solution)/shard_map/ppermute | solution.py:1046
  832.1 2.1 select_bitcast_fusion
  834.2 2.5 fusion.5
  836.8 2.7 copy.159
  839.5 5.4 copy.160
  844.8 5.6 copy.165
  850.4 4.8 copy.161
  855.2 5.5 copy.162
  860.7 5.7 copy.166
  867.4 3.1 copy.210
  (179 shorter events, 33.9 us)
Async XLA Ops:
  0.6 3.8 copy-start
  0.7 10.1 %copy-start.6 = (bf16[256,1024]{1,0:T(8,128)(2,1)S(1)}, bf16[256,1024]{1,0:T(8,128)(2,1)}, u32[]{:S(2)}) copy-start(bf16[256,1024]{1,0:T(8,128)(2,1)} %query.1) | copy-start | bytes 1572868
  0.7 10.1 %copy-start.7 = (bf16[256,1024]{1,0:T(8,128)(2,1)S(1)}, bf16[256,1024]{1,0:T(8,128)(2,1)}, u32[]{:S(2)}) copy-start(bf16[256,1024]{1,0:T(8,128)(2,1)} %key.1) | copy-start | bytes 1572868
  0.7 10.1 %copy-start.8 = (bf16[256,1024]{1,0:T(8,128)(2,1)S(1)}, bf16[256,1024]{1,0:T(8,128)(2,1)}, u32[]{:S(2)}) copy-start(bf16[256,1024]{1,0:T(8,128)(2,1)} %value.1) | copy-start | bytes 1572868
  4.5 6.3 copy-start.9
  76.7 1.1 copy-start.10
  77.9 52.3 %all-to-all-start.1 = ((bf16[8,256,256]{2,1,0:T(8,128)(2,1)}), bf16[8,256,256]{2,1,0:T(8,128)(2,1)S(1)}, u32[]{:S(2)}, u32[]{:S(2)}) async-start(bf16[8,256,256]{2,1,0:T(8,128)(2,1)} %get-tuple-element.51), calls=%async_computation.1 | async-start | bytes 2097152 | tf_op jit(solution)/shard_map/all_to_all | solution.py:1040
  124.3 0.5 copy-start.36
  124.4 3.2 copy-start.38
  124.5 5.6 copy-start.32
  124.6 5.6 copy-start.34
  127.5 1.0 copy-start.17
  130.2 51.3 %all-to-all-start = ((bf16[8,128,1024]{2,1,0:T(8,128)(2,1)}), bf16[8,128,1024]{2,1,0:T(8,128)(2,1)}, u32[]{:S(2)}, u32[]{:S(2)}) async-start(bf16[8,128,1024]{2,1,0:T(8,128)(2,1)} %get-tuple-element.50), calls=%async_computation | async-start | bytes 4194304 | tf_op jit(solution)/shard_map/all_to_all | solution.py:1040
  136.8 12.1 %copy-start.16 = (f32[2048,128]{1,0:T(8,128)S(1)}, f32[2048,128]{1,0:T(8,128)}, u32[]{:S(2)}) copy-start(f32[2048,128]{1,0:T(8,128)} %get-tuple-element.138) | copy-start | bytes 3145732
  138.2 1.0 copy-start.13
  145.4 15.7 %collective-permute-start = (bf16[8,256,1,128]{3,1,0,2:T(8,128)(2,1)}, bf16[8,256,1,128]{3,1,0,2:T(8,128)(2,1)}, u32[]{:S(2)}, u32[]{:S(2)}) collective-permute-start(bf16[8,256,1,128]{3,1,0,2:T(8,128)(2,1)} %fusion.19), channel_id=1, source_target_pairs={{0,2},{1,3},{4,6},{5,7},{8,10},{9,11},{12,14},{13,15},{16,18},{17,... | collective-permute-start | bytes 1572872 | tf_op jit(solution)/shard_map/ppermute | solution.py:1170
  161.1 5.4 copy-start.25
  422.7 9.5 %copy-start.2 = (bf16[256,2048]{1,0:T(8,128)(2,1)}, bf16[256,2048]{1,0:T(8,128)(2,1)S(1)}, u32[]{:S(2)}) copy-start(bf16[256,2048]{1,0:T(8,128)(2,1)S(1)} %get-tuple-element.189) | copy-start | bytes 3145732
  422.7 20.2 %slice-start = ((s8[8388608]{0:T(1024)(128)(4,1)}), s8[4194304]{0:T(1024)(128)(4,1)S(1)}, s32[]{:S(2)}) async-start(s8[8388608]{0:T(1024)(128)(4,1)} %bitcast.291), calls=%async_computation.4 | async-start | bytes 8388608
  432.1 10.8 %slice-start.1 = ((s8[8388608]{0:T(1024)(128)(4,1)}), s8[4194304]{0:T(1024)(128)(4,1)S(1)}, s32[]{:S(2)}) async-start(s8[8388608]{0:T(1024)(128)(4,1)} %bitcast.291), calls=%async_computation.5 | async-start | bytes 8388608
  442.9 12.1 %copy-start.40 = (bf16[8,2,128,1024]{3,2,1,0:T(8,128)(2,1)S(1)}, bf16[8,2,128,1024]{3,2,1,0:T(8,128)(2,1)}, u32[]{:S(2)}) copy-start(bf16[8,2,128,1024]{3,2,1,0:T(8,128)(2,1)} %get-tuple-element.53) | copy-start | bytes 12582916
  466.5 102.8 %copy-start.27 = (bf16[16,8,8,256]{3,1,2,0:T(8,128)(2,1)S(1)}, bf16[16,8,8,256]{3,1,2,0:T(8,128)(2,1)}, u32[]{:S(2)}) copy-start(bf16[16,8,8,256]{3,1,2,0:T(8,128)(2,1)} %copy.178) | copy-start | bytes 1572868
  569.3 6.2 copy-start.4
  569.3 6.2 copy-start.12
  575.5 2.2 copy-start.24
  575.5 2.3 copy-start.29
  575.5 2.4 copy-start.30
  580.4 2.1 copy-start.23
  584.0 53.8 %all-to-all-start.3 = ((bf16[8,256,256]{2,1,0:T(8,128)(2,1)}), bf16[8,256,256]{2,1,0:T(8,128)(2,1)}, u32[]{:S(2)}, u32[]{:S(2)}) async-start(bf16[8,256,256]{2,1,0:T(8,128)(2,1)} %bitcast.263), calls=%async_computation.3 | async-start | bytes 2097152 | tf_op jit(solution)/shard_map/all_to_all | solution.py:1040
  589.6 3.9 copy-start.26
  593.6 7.7 copy-start.20
  594.4 1.3 copy-start.18
  595.8 7.9 copy-start.14
  596.7 16.9 %collective-permute-start.1 = (bf16[8,256,1,128]{3,1,0,2:T(8,128)(2,1)}, bf16[8,256,1,128]{3,1,0,2:T(8,128)(2,1)S(1)}, u32[]{:S(2)}, u32[]{:S(2)}) collective-permute-start(bf16[8,256,1,128]{3,1,0,2:T(8,128)(2,1)} %slice.172), channel_id=1, source_target_pairs={{2,0},{3,1},{6,4},{7,5},{10,8},{11,9},{14,12},{15,13},{18,16},{19,... | collective-permute-start | bytes 1572872 | tf_op jit(solution)/shard_map/ppermute | solution.py:1239
  600.0 36.5 %collective-permute-start.2 = (bf16[8,256,1,128]{1,3,0,2:T(8,128)(2,1)}, bf16[8,256,1,128]{1,3,0,2:T(8,128)(2,1)}, u32[]{:S(2)}, u32[]{:S(2)}) collective-permute-start(bf16[8,256,1,128]{1,3,0,2:T(8,128)(2,1)} %slice.171), channel_id=1, source_target_pairs={{2,0},{3,1},{6,4},{7,5},{10,8},{11,9},{14,12},{15,13},{18,16},{19,... | collective-permute-start | bytes 1572872 | tf_op jit(solution)/shard_map/ppermute | solution.py:1238
  609.5 4.1 copy-start.15
  613.5 6.3 copy-start.19
  619.4 4.6 copy-start.21
  619.4 4.6 copy-start.33
  619.5 4.6 copy-start.35
  619.5 4.6 copy-start.37
  619.5 4.6 copy-start.39
  624.0 3.1 copy-start.22
  624.0 12.5 %copy-start.28 = (f32[8,512,1,128]{1,3,0,2:T(8,128)S(1)}, f32[8,512,1,128]{1,3,0,2:T(8,128)}, u32[]{:S(2)}) copy-start(f32[8,512,1,128]{1,3,0,2:T(8,128)} %convolution_bitcast_fusion) | copy-start | bytes 6291460
  637.7 131.3 %all-to-all-start.2 = ((bf16[8,128,1024]{2,1,0:T(8,128)(2,1)}), bf16[8,128,1024]{2,1,0:T(8,128)(2,1)}, u32[]{:S(2)}, u32[]{:S(2)}) async-start(bf16[8,128,1024]{2,1,0:T(8,128)(2,1)} %fusion.1), calls=%async_computation.2 | async-start | bytes 4194304 | tf_op jit(solution)/shard_map/all_to_all | solution.py:1040
  643.3 5.0 copy-start.11
  644.6 3.7 copy-start.31
  655.2 8.0 copy-start.5
  765.4 26.6 %collective-permute-start.4 = (bf16[8,256,256]{2,1,0:T(8,128)(2,1)}, bf16[8,256,256]{2,1,0:T(8,128)(2,1)S(1)}, u32[]{:S(2)}, u32[]{:S(2)}) collective-permute-start(bf16[8,256,256]{2,1,0:T(8,128)(2,1)} %all-to-all-done.3), channel_id=1, source_target_pairs={{0,2},{2,0},{1,3},{3,1},{4,6},{6,4},{5,7},{7,5},{8,10},{10,8},{9,1... | collective-permute-start | bytes 3145736 | tf_op jit(solution)/shard_map/ppermute | solution.py:1046
  769.0 63.1 %collective-permute-start.3 = (bf16[8,128,1024]{2,1,0:T(8,128)(2,1)}, bf16[8,128,1024]{2,1,0:T(8,128)(2,1)S(1)}, u32[]{:S(2)}, u32[]{:S(2)}) collective-permute-start(bf16[8,128,1024]{2,1,0:T(8,128)(2,1)} %all-to-all-done.2), channel_id=1, source_target_pairs={{0,2},{2,0},{1,3},{3,1},{4,6},{6,4},{5,7},{7,5},{8,10},{10,8},{9,1... | collective-permute-start | bytes 6291464 | tf_op jit(solution)/shard_map/ppermute | solution.py:1046
  860.7 5.8 copy-start.3
  860.7 9.9 %copy-start.1 = (bf16[256,2048]{1,0:T(8,128)(2,1)S(1)}, bf16[256,2048]{1,0:T(8,128)(2,1)}, u32[]{:S(2)}) copy-start(bf16[256,2048]{1,0:T(8,128)(2,1)} %param.14) | copy-start | bytes 3145732

commit v4 on v3

--- a/solution.py
+++ b/solution.py
@@ -259,10 +259,10 @@
 
         by_rows(rows, add)
         sender(None, functools.partial(to_y, block))
-    if between is not None:
-        between()
-
-    for block in order[:-1]:
+
+    for number, block in enumerate(order[:-1]):
+        if number == LINE - 2 and between is not None:
+            between()
         slot = 2 * block + y
         fetch(slot).wait()
         to_core(slot).wait_recv()
@@ -729,16 +729,18 @@
     qkv,
     out,
     small,
+    down,
     result,
     qkv_all,
     out_all,
     small_all,
+    down_all,
     *scratch,
 ):
     place = Place()
     sender = Sender()
     parts = scratch[REDUCE + 1 :]
-    swap_sems, parts = parts[:3], parts[3:]
+    swap_sems, halves_sems, parts = parts[:3], parts[3:4], parts[4:]
     qkv_own, qkv_other, out_own, out_other, small_own, small_other, fetch_sem, side_sem = parts
     greet_all(place)
     fetches, crossings = [], []
@@ -770,6 +772,7 @@
         copy.start()
     pairs = ((small_own, small_all), (qkv_own, qkv_all), (out_own, out_all))
     swap = Swap(place, [whole_pair(*pair) for pair in pairs], swap_sems)
+    halves = Halves(place, (down,), (down_all,), halves_sems)
     shared_rows = 2 * partial.shape[1] // place.count // 128
 
     def between():
@@ -791,6 +794,7 @@
 
         lax.fori_loop(0, place.count, one, 0)
         swap.start()
+        halves.start()
 
     reduce_phase(place, sender, partial, scratch[:REDUCE], between)
     total = scratch[4]
@@ -802,6 +806,7 @@
     finish = pair_phase(place, sender, total, result, scratch[REDUCE : REDUCE + 1])
     swap.pass_on()
     finish()
+    halves.finish()
     swap.finish()
     sender.drain()
 
@@ -859,6 +864,16 @@
     down_out[0] = down[...]
 
 
+def unpack_kernel(side, own, other, down, gate_out, up_out, down_out):
+    half, columns = own.shape[2], gate_out.shape[1]
+    for part, start in ((own, side[0]), (other, 1 - side[0])):
+        value = jnp.sum(part[:, 0].astype(F32), axis=0)
+        rows = pl.ds(pl.multiple_of(start * half, half), half)
+        gate_out[rows] = value[:, :columns]
+        up_out[rows] = value[:, columns:]
+    down_out[...] = jnp.sum(down[:, 0].astype(F32), axis=0)
+
+
 def talk(kernel, which, shapes, specs, scratch, microseconds, name=None):
     def call(*operands):
         return pl.pallas_call(
@@ -990,7 +1005,7 @@
             100,
         )(partial, branch, cotangent, gain, pair_grad, down_grad)
 
-    def last(self, partial, grad_hidden, qkv, out, small):
+    def last(self, partial, grad_hidden, qkv, out, small, down):
         both = jax.ShapeDtypeStruct((2 * self.rows, self.width), F32)
 
         def same(array):
@@ -1003,14 +1018,15 @@
         return talk(
             last_kernel,
             4,
-            (both, same(qkv), same(out), self.whole(small)),
-            ([HBM, VMEM, HBM, HBM, VMEM], (HBM,) * 4),
+            (both, same(qkv), same(out), self.whole(small), self.whole(down)),
+            ([HBM, VMEM, HBM, HBM, VMEM, VMEM], (HBM,) * 5),
             self.reduces
             + pair_scratch()
             + swap_scratch(self.fsdp, 3)
+            + halves_scratch(1)
             + [half(qkv), half(qkv), half(out), half(out), held, held, DMA((2,)), DMA((2, 3))],
             80,
-        )(partial, grad_hidden, qkv, out, small)
+        )(partial, grad_hidden, qkv, out, small, down)
 
     def total(self, values, moved=None):
         flat = values.reshape(-1, 128)
@@ -1042,11 +1058,39 @@
     def repeat(self, pieces):
         return jnp.concatenate([pieces] * self.teams, axis=0) if self.teams > 1 else pieces
 
-    def both_sides(self, half):
-        other = lax.ppermute(half, "context", [(0, 1), (1, 0)])
-        low = jnp.where(self.context == 0, half, other)
-        high = jnp.where(self.context == 0, other, half)
-        return jnp.stack([low, high], axis=1)
+    def unpack(self, own, down):
+        other = lax.ppermute(own, "context", [(0, 1), (1, 0)])
+        half, columns = own.shape[1], own.shape[2] // 2
+        rows, down_columns = 2 * down.shape[2], down.shape[3]
+
+        def cut(array, *shape):
+            return array.reshape((self.teams, self.size) + shape)
+
+        def piece_spec(*shape):
+            return pl.BlockSpec((self.teams, 1) + shape, lambda d, side: (0, d, 0, 0))
+
+        wide = pl.BlockSpec((2 * half, columns), lambda d, side: (0, d))
+        wide_shape = jax.ShapeDtypeStruct((2 * half, self.size * columns), F32)
+        return pl.pallas_call(
+            unpack_kernel,
+            grid_spec=pltpu.PrefetchScalarGridSpec(
+                num_scalar_prefetch=1,
+                grid=(self.size,),
+                in_specs=[piece_spec(half, 2 * columns)] * 2 + [piece_spec(rows, down_columns)],
+                out_specs=[wide, wide, pl.BlockSpec((rows, down_columns), lambda d, side: (d, 0))],
+            ),
+            out_shape=[
+                wide_shape,
+                wide_shape,
+                jax.ShapeDtypeStruct((self.size * rows, down_columns), F32),
+            ],
+            name="unpack_kernel",
+        )(
+            self.context.reshape(1).astype(jnp.int32),
+            cut(own, half, 2 * columns),
+            cut(other, half, 2 * columns),
+            cut(down, rows, down_columns),
+        )
 
     def columns_whole(self, came):
         return came.reshape(-1, came.shape[-1])
@@ -1221,7 +1265,6 @@
     down_mine = (team.half(down_grad, 0).astype(F32) + down_other.astype(F32)).astype(BF)
     down_mine = down_mine.reshape(down_mine.shape[0], fsdp, -1).transpose(1, 0, 2)
     pair_came = team.swap(pair_mine)
-    down_came = team.swap(down_mine)
     output_grad = team.of_rows(product_left(attended_low, grad_branch_all))
     grad_attended = product_right(grad_branch_all, output_w).astype(BF).reshape(by_head)
 
@@ -1253,6 +1296,8 @@
             ]
         )
     )
+    down_mine, totals = lax.optimization_barrier((down_mine, totals))
+    down_came = team.swap(down_mine)
     grad_query_low = norm_back(
         query_raw, scale_query, flat_query, grad_query_norm, totals[0][:, None], width
     ).astype(BF)
@@ -1270,19 +1315,20 @@
     ]
     used = 2 * share + 2 * heads * head_share
     small = jnp.concatenate(small + [jnp.zeros((fsdp, 8 * 128 - used), F32)], axis=1)
-    pair_came = team.both_sides(pair_came)
-    down_came = team.both_sides(down_came)
-    input_grad, qkv_came, output_came, small_came = team.last(
-        product_right(grad_qkv, qkv_w).astype(BF),
+    partial, pair_came = lax.optimization_barrier(
+        (product_right(grad_qkv, qkv_w).astype(BF), pair_came)
+    )
+    input_grad, qkv_came, output_came, small_came, down_came = team.last(
+        partial,
         grad_hidden,
         qkv_grad,
         output_grad,
         small.reshape(fsdp, 8, 128),
+        down_came,
     )
     grad_w_query, grad_w_key, grad_w_value = team.columns_out(qkv_came, 3)
-    grad_w_gate, grad_w_up = team.columns_out(pair_came, 2)
+    grad_w_gate, grad_w_up, grad_w_down = team.unpack(pair_came, down_came)
     grad_w_output = team.rows_out(output_came)
-    grad_w_down = team.rows_out(down_came)
     came = jnp.sum(small_came, axis=1).reshape(fsdp, -1)
     row_gains = jnp.sum(came[:, : 2 * share], axis=0).reshape(2, share)
     head_gains = team.added(came[:, 2 * share : used]).reshape(team.size, 2, heads, head_share)

time: 883 us -> 831 us (0.941)
  waiting for transfers between devices: 59.4 us -> 3.99 us
  Pallas kernels: 512 us -> 545 us
  local copies, waits for them, and re-layouts: 58.5 us -> 34.7 us
  other arithmetic: 70.2 us -> 61.1 us
    ppermute x2 -> x1, waiting for transfers between devices: 56.3 us -> 0.01 us  [unpack(): other = lax.ppermute(own, 'context', [(0, 1), (1, 0)])]
    pallas_call x7, Pallas kernels: 506 us -> 530 us  [call(): pl.pallas_call(kernel, out_shape=shapes, in_specs=specs[0], out_specs=spe...]
    reshape x4 -> x1, local copies, waits for them, and re-layouts: 18.3 us -> 0.01 us  [total(): return call(flat).reshape(values.shape)]
    unnamed x102 -> x104, local copies, waits for them, and re-layouts: 23.3 us -> 14.2 us
  transfers between devices with their start and end apart: 9 -> 8, of which waited for: 4 -> 2; matrix products, arithmetic and copies ran while one was open for 14% -> 15% of each run, Pallas kernels for 14% -> 18%
where the time goes in v4:
time: 831 us; the launch traced here: 821 us
  Pallas kernels  545 us (66%)
  matrix products  130 us (16%)
  other arithmetic  61.1 us (7%)
  starting transfers between devices  44.8 us (5%)
  local copies, waits for them, and re-layouts  34.7 us (4%)
    pallas_call x7, Pallas kernels, call(): pl.pallas_call(kernel, out_shape=shapes, in_specs=specs[0], out_specs=spe...  530 us
    dot_general x4, matrix products, product(): return jnp.dot(left, right, preferred_element_type=F32)  38.1 us
    dot_general x4, matrix products, product_right(): return jnp.einsum('rf,df->rd', left, right, preferred_element_type=F32)  37.3 us
    dot_general x4, matrix products, product_left(): return jnp.einsum('rd,rf->df', left, right, preferred_element_type=F32)  35.4 us
    all_to_all x4, starting transfers between devices, swap(): lax.all_to_all(pieces, 'fsdp', split_axis=0, concat_axis=0, tiled=True)  35.2 us
  transfers between devices with their start and end apart: 8, of which 2 were waited for; matrix products, arithmetic and copies ran while one was open for 15% of the time, Pallas kernels for 18%

profile of v4, /device:TPU:16, one launch (start us, length us, event | category | flops | bytes accessed | tf_op | source)
XLA Modules:
  0.0 821.4 jit_solution(1642377282090254582)
XLA Ops:
  4.5 6.3 pack_kernel.1
  10.8 65.9 %first_kernel.1 = (bf16[2048,2048]{1,0:T(8,128)(2,1)}, bf16[8,2,128,384]{3,2,1,0:T(8,128)(2,1)S(1)}, bf16[8,2,64,256]{3,2,1,0:T(8,128)(2,1)S(1)}, f32[8,2,8,128]{3,2,1,0:T(8,128)S(1)}) custom-call(bf16[128,2048]{1,0:T(8,128)(2,1)S(1)} %constant_dynamic-slice_fusion.3.own_ref.tokens, bf16[256,1024]{1,0:T(8,128)(2,1)S(1)} %copy-done.7, ...), custom_call_target="tpu_custom_call" | custom-call | bytes 240000000 | tf_op jit(solution)/shard_map/first_kernel/pallas_call | solution.py:879
  76.7 1.2 copy-done.13
  77.9 17.3 %all-to-all-start.1 = ((bf16[8,256,256]{2,1,0:T(8,128)(2,1)}), bf16[8,256,256]{2,1,0:T(8,128)(2,1)S(1)}, u32[]{:S(2)}, u32[]{:S(2)}) async-start(bf16[8,256,256]{2,1,0:T(8,128)(2,1)} %get-tuple-element.59), calls=%async_computation.1 | async-start | bytes 2097152 | tf_op jit(solution)/shard_map/all_to_all | solution.py:1056
  95.3 10.0 %fusion.60 = f32[2048,384]{1,0:T(8,128)} fusion(bf16[2048,2048]{1,0:T(8,128)(2,1)} %get-tuple-element.52, bf16[2048,384]{1,0:T(8,128)(2,1)} %bitcast.224), kind=kOutput, calls=%fused_computation.159 | convolution fusion | flops 3221225472 | bytes 13107200 | tf_op jit(solution)/shard_map/dot_general | solution.py:18
  105.3 2.2 multiply_reduce_fusion.2
  107.6 1.3 split.54.rest_0_
  109.4 15.0 %sum_kernel.2 = (f32[32,128]{1,0:T(8,128)S(1)}, bf16[2048,128]{1,0:T(8,128)(2,1)S(1)}) custom-call(f32[32,128]{1,0:T(8,128)S(1)} %reshape.511.value, bf16[2048,128]{1,0:T(8,128)(2,1)S(1)} %split.54.rest_0_), custom_call_target="tpu_custom_call" | custom-call | bytes 30000000 | tf_op jit(solution)/shard_map/sum_kernel/pallas_call | solution.py:879
  125.0 2.7 multiply_multiply_fusion
  128.6 1.7 slice_negate_fusion.2
  130.3 6.6 all-to-all-start
  136.9 1.3 fusion.36
  139.3 6.2 fusion.16
  145.5 3.7 collective-permute-start
  149.4 1.7 fusion.12
  155.4 6.4 fusion.14
  161.9 5.3 fusion.59
  167.2 4.2 fusion.10
  171.4 1.3 copy.90
  172.8 6.7 convolution_convert_fusion.3.partial
  179.4 2.2 all-to-all-done.pair
  181.6 108.6 %hidden_kernel.1 = (bf16[2048,2048]{1,0:T(8,128)(2,1)}, f32[128,2048]{1,0:T(8,128)S(1)}, f32[128,2048]{1,0:T(8,128)S(1)}, bf16[8,2,128,1024]{3,2,1,0:T(8,128)(2,1)}, bf16[8,2,256,256]{3,2,1,0:T(8,128)(2,1)S(1)}) custom-call(bf16[2048,2048]{1,0:T(8,128)(2,1)} %convolution_convert_fusion.3.partial, ...), custom_call_target="tpu_custom_call" | custom-call | bytes 300000000 | tf_op jit(solution)/shard_map/hidden_kernel/pallas_call | solution.py:879
  290.2 14.6 %fusion.61 = f32[2048,1024]{0,1:T(8,128)} fusion(bf16[2048,2048]{1,0:T(8,128)(2,1)} %get-tuple-element.60, bf16[2048,1024]{1,0:T(8,128)(2,1)} %bitcast.269), kind=kOutput, calls=%fused_computation.160 | convolution fusion | flops 8589934592 | bytes 20971520 | tf_op jit(solution)/shard_map/dot_general | solution.py:18
  304.8 4.7 multiply_convert_fusion.3
  309.5 1.2 copy.92
  311.3 6.8 convolution_convert_fusion.2.partial
  318.2 104.2 %turn_kernel.1 = (bf16[2048,2048]{1,0:T(8,128)(2,1)}, bf16[256,2048]{1,0:T(8,128)(2,1)S(1)}, f32[1,2048]{1,0:T(1,128)S(1)}) custom-call(bf16[2048,2048]{1,0:T(8,128)(2,1)} %convolution_convert_fusion.2.partial, f32[128,2048]{1,0:T(8,128)S(1)} %get-tuple-element.63.hidden, bf16[128,2048]{1,0:T(8,128)(2,1)S(1)} %constant_dynamic-slice_fusion.cotangent, ...), custom_call_target="tpu_custom_call" | custom-call | bytes 300000000 | tf_op jit(solution)/shard_map/turn_kernel/pallas_call | solution.py:879
  422.4 9.5 %convolution_convert_fusion.5.down_grad = bf16[512,2048]{1,0:T(8,128)(2,1)} fusion(bf16[2048,512]{0,1:T(8,128)(2,1)S(1)} %multiply_convert_fusion.3, bf16[2048,2048]{1,0:T(8,128)(2,1)} %get-tuple-element.65), kind=kOutput, calls=%fused_computation.17 | convolution fusion | flops 4296015872 | bytes 12582912 | tf_op jit(solution)/shard_map/rd,rf->df/dot_general | solution.py:22
  431.8 10.8 %multiply_convert_fusion.2 = (bf16[2048,512]{0,1:T(8,128)(2,1)S(1)}, bf16[2048,512]{0,1:T(8,128)(2,1)S(1)}) fusion(f32[2048,1024]{0,1:T(8,128)} %fusion.61, bf16[2048,2048]{1,0:T(8,128)(2,1)} %get-tuple-element.65, bf16[512,2048]{1,0:T(8,128)(2,1)S(1)} %bitcast.240), kind=kOutput, calls=%fused_computation.11 | convolution fusion | flops 4308598784 | bytes 23068672 | tf_op jit(solution)/shard_map/rf,df->rd/dot_general | solution.py:26
  442.6 12.0 %convolution_convert_fusion.4 = bf16[2048,1024]{1,0:T(8,128)(2,1)} fusion(bf16[2048,2048]{1,0:T(8,128)(2,1)S(1)} %bitcast.268, bf16[2048,512]{0,1:T(8,128)(2,1)S(1)} %get-tuple-element.94, bf16[2048,512]{0,1:T(8,128)(2,1)S(1)} %get-tuple-element.93), kind=kOutput, calls=%fused_computation.16 | convolution fusion | flops 8600420352 | bytes 16777216 | tf_op jit(solution)/shard_map/rd,rf->df/dot_general | solution.py:22
  454.7 11.8 %convolution_convert_fusion.1.partial = bf16[2048,2048]{1,0:T(8,128)(2,1)} fusion(bf16[2048,1024]{1,0:T(8,128)(2,1)S(1)} %bitcast.270, bf16[2048,512]{0,1:T(8,128)(2,1)S(1)} %get-tuple-element.94, bf16[2048,512]{0,1:T(8,128)(2,1)S(1)} %get-tuple-element.93), kind=kOutput, calls=%fused_computation.2 | convolution fusion | flops 8602517504 | bytes 16777216 | tf_op jit(solution)/shard_map/rf,df->rd/dot_general | solution.py:26
  466.4 102.7 %branch_kernel.1 = (bf16[2048,2048]{1,0:T(8,128)(2,1)}, f32[128,2048]{1,0:T(8,128)S(1)}, f32[1,2048]{1,0:T(1,128)S(1)}, bf16[8,128,1024]{2,1,0:T(8,128)(2,1)S(1)}, bf16[256,2048]{1,0:T(8,128)(2,1)S(1)}) custom-call(bf16[2048,2048]{1,0:T(8,128)(2,1)} %convolution_convert_fusion.1.partial, f32[128,2048]{1,0:T(8,128)S(1)} %get-tuple-element.66.branch, ...), custom_call_target="tpu_custom_call" | custom-call | bytes 300000000 | tf_op jit(solution)/shard_map/branch_kernel/pallas_call | solution.py:879
  569.3 6.5 convolution_convert_fusion.8
  576.9 2.1 convolution_bitcast_fusion
  579.7 1.4 copy-done.17
  582.0 1.3 copy-done.21
  584.2 1.3 collective-permute-start.1
  587.4 2.9 add_convert_fusion
  590.3 2.3 copy.96
  592.6 2.3 copy.97
  594.8 2.1 slice.169
  596.9 1.5 collective-permute-start.2
  598.4 3.9 fusion.1
  602.3 5.6 all-to-all-start.2
  607.9 4.8 convolution_convert_fusion.7
  613.0 5.4 fusion.34
  618.8 4.8 maximum_add_fusion
  624.0 4.1 maximum_add_fusion.1
  628.2 2.8 fusion.21
  631.0 25.6 %sum_kernel.3 = f32[32,128]{1,0:T(8,128)S(1)} custom-call(f32[32,128]{1,0:T(8,128)S(1)} %reshape.533.value), custom_call_target="tpu_custom_call" | custom-call | bytes 30000000 | tf_op jit(solution)/shard_map/sum_kernel/pallas_call | solution.py:879
  656.7 1.5 fusion.11
  659.2 4.5 fusion.23
  663.7 5.7 all-to-all-start.3
  669.4 8.3 %convolution_convert_fusion.partial = bf16[2048,2048]{1,0:T(8,128)(2,1)} fusion(bf16[2048,384]{1,0:T(8,128)(2,1)S(1)} %bitcast.225, bf16[2048,128]{1,0:T(8,128)(2,1)} %bitcast.246, bf16[2048,128]{1,0:T(8,128)(2,1)} %get-tuple-element.96, bf16[2048,128]{1,0:T(8,128)(2,1)} %get-tuple-element.95), kind=kOutput, calls=%fused_computation.1 | convolution fusion | flops 3230138368 | bytes 11534336 | tf_op jit(solution)/shard_map/rf,df->rd/dot_general | solution.py:26
  677.7 3.2 collective-permute-start.3
  680.9 9.1 %convolution_convert_fusion.6 = bf16[2048,384]{1,0:T(8,128)(2,1)} fusion(bf16[2048,2048]{1,0:T(8,128)(2,1)} %get-tuple-element.52, bf16[2048,128]{1,0:T(8,128)(2,1)S(1)} %bitcast.247, bf16[2048,128]{1,0:T(8,128)(2,1)S(1)} %copy-done.30, bf16[2048,128]{1,0:T(8,128)(2,1)S(1)} %copy-done.29), kind=kOutput, calls=%fused_computation.18 | convolution fusion | flops 3226730496 | bytes 11534336 | tf_op jit(solution)/shard_map/rd,rf->df/dot_general | solution.py:22
  690.3 1.8 all-to-all-done.3.down
  692.1 1.2 copy-done.3
  693.3 108.2 %last_kernel.1 = (f32[256,2048]{1,0:T(8,128)}, bf16[8,2,128,384]{3,2,1,0:T(8,128)(2,1)S(1)}, bf16[8,2,64,256]{3,2,1,0:T(8,128)(2,1)S(1)}, f32[8,2,8,128]{3,2,1,0:T(8,128)S(1)}, bf16[8,2,256,256]{3,2,1,0:T(8,128)(2,1)}) custom-call(bf16[2048,2048]{1,0:T(8,128)(2,1)} %convolution_convert_fusion.partial, f32[128,2048]{1,0:T(8,128)S(1)} %copy-done.3, ...), custom_call_target="tpu_custom_call" | custom-call | bytes 240000000 | tf_op jit(solution)/shard_map/last_kernel/pallas_call | solution.py:879
  803.9 1.1 copy_bitcast_fusion
  805.0 1.1 copy_bitcast_fusion.1
  806.1 1.1 copy_bitcast_fusion.2
  808.4 8.6 %unpack_kernel.1 = (f32[256,4096]{1,0:T(8,128)}, f32[256,4096]{1,0:T(8,128)}, f32[4096,256]{1,0:T(8,128)}) custom-call(s32[1]{0:T(128)} %bitcast.side, bf16[1,8,128,1024]{3,2,1,0:T(8,128)(2,1)} %bitcast.61.own, bf16[1,8,128,1024]{3,2,1,0:T(8,128)(2,1)} %bitcast.62.other, bf16[1,8,512,256]{3,2,1,0:T(8,128)(2,1)} %bitcast.237), custom_call_target="tpu_custom_call" | custom-call | tf_op jit(solution)/shard_map/unpack_kernel/pallas_call | solution.py:1074
  818.0 3.1 copy.148
  (173 shorter events, 24.4 us)
Async XLA Ops:
  0.6 3.8 copy-start
  0.7 10.1 %copy-start.7 = (bf16[256,1024]{1,0:T(8,128)(2,1)S(1)}, bf16[256,1024]{1,0:T(8,128)(2,1)}, u32[]{:S(2)}) copy-start(bf16[256,1024]{1,0:T(8,128)(2,1)} %query.1) | copy-start | bytes 1572868
  0.7 10.1 %copy-start.8 = (bf16[256,1024]{1,0:T(8,128)(2,1)S(1)}, bf16[256,1024]{1,0:T(8,128)(2,1)}, u32[]{:S(2)}) copy-start(bf16[256,1024]{1,0:T(8,128)(2,1)} %key.1) | copy-start | bytes 1572868
  0.7 10.1 %copy-start.9 = (bf16[256,1024]{1,0:T(8,128)(2,1)S(1)}, bf16[256,1024]{1,0:T(8,128)(2,1)}, u32[]{:S(2)}) copy-start(bf16[256,1024]{1,0:T(8,128)(2,1)} %value.1) | copy-start | bytes 1572868
  4.5 6.3 copy-start.10
  76.7 1.2 copy-start.13
  77.9 52.4 %all-to-all-start.1 = ((bf16[8,256,256]{2,1,0:T(8,128)(2,1)}), bf16[8,256,256]{2,1,0:T(8,128)(2,1)S(1)}, u32[]{:S(2)}, u32[]{:S(2)}) async-start(bf16[8,256,256]{2,1,0:T(8,128)(2,1)} %get-tuple-element.59), calls=%async_computation.1 | async-start | bytes 2097152 | tf_op jit(solution)/shard_map/all_to_all | solution.py:1056
  124.4 0.5 copy-start.38
  124.5 3.2 copy-start.40
  124.6 5.6 copy-start.34
  124.7 5.6 copy-start.36
  127.6 1.0 copy-start.20
  130.3 51.3 %all-to-all-start = ((bf16[8,128,1024]{2,1,0:T(8,128)(2,1)}), bf16[8,128,1024]{2,1,0:T(8,128)(2,1)}, u32[]{:S(2)}, u32[]{:S(2)}) async-start(bf16[8,128,1024]{2,1,0:T(8,128)(2,1)} %get-tuple-element.58), calls=%async_computation | async-start | bytes 4194304 | tf_op jit(solution)/shard_map/all_to_all | solution.py:1056
  136.9 12.4 %copy-start.19 = (f32[2048,128]{1,0:T(8,128)S(1)}, f32[2048,128]{1,0:T(8,128)}, u32[]{:S(2)}) copy-start(f32[2048,128]{1,0:T(8,128)} %get-tuple-element.98) | copy-start | bytes 3145732
  138.3 1.0 copy-start.15
  145.5 16.4 %collective-permute-start = (bf16[8,256,1,128]{3,1,0,2:T(8,128)(2,1)}, bf16[8,256,1,128]{3,1,0,2:T(8,128)(2,1)}, u32[]{:S(2)}, u32[]{:S(2)}) collective-permute-start(bf16[8,256,1,128]{3,1,0,2:T(8,128)(2,1)} %fusion.16), channel_id=1, source_target_pairs={{0,2},{1,3},{4,6},{5,7},{8,10},{9,11},{12,14},{13,15},{16,18},{17,... | collective-permute-start | bytes 1572872 | tf_op jit(solution)/shard_map/ppermute | solution.py:1214
  161.9 5.4 copy-start.26
  422.3 9.5 %copy-start.4 = (bf16[256,2048]{1,0:T(8,128)(2,1)}, bf16[256,2048]{1,0:T(8,128)(2,1)S(1)}, u32[]{:S(2)}) copy-start(bf16[256,2048]{1,0:T(8,128)(2,1)S(1)} %get-tuple-element.147) | copy-start | bytes 3145732
  422.3 20.2 %slice-start = ((s8[8388608]{0:T(1024)(128)(4,1)}), s8[4194304]{0:T(1024)(128)(4,1)S(1)}, s32[]{:S(2)}) async-start(s8[8388608]{0:T(1024)(128)(4,1)} %bitcast.267), calls=%async_computation.4 | async-start | bytes 8388608
  431.8 10.8 %slice-start.1 = ((s8[8388608]{0:T(1024)(128)(4,1)}), s8[4194304]{0:T(1024)(128)(4,1)S(1)}, s32[]{:S(2)}) async-start(s8[8388608]{0:T(1024)(128)(4,1)} %bitcast.267), calls=%async_computation.5 | async-start | bytes 8388608
  442.6 12.1 %copy-start.42 = (bf16[8,2,128,1024]{3,2,1,0:T(8,128)(2,1)S(1)}, bf16[8,2,128,1024]{3,2,1,0:T(8,128)(2,1)}, u32[]{:S(2)}) copy-start(bf16[8,2,128,1024]{3,2,1,0:T(8,128)(2,1)} %get-tuple-element.61) | copy-start | bytes 12582916
  466.4 102.8 %copy-start.28 = (bf16[16,8,8,256]{3,1,2,0:T(8,128)(2,1)S(1)}, bf16[16,8,8,256]{3,1,2,0:T(8,128)(2,1)}, u32[]{:S(2)}) copy-start(bf16[16,8,8,256]{3,1,2,0:T(8,128)(2,1)} %copy.118) | copy-start | bytes 1572868
  569.2 6.6 copy-start.2
  569.2 7.7 copy-start.6
  569.2 6.5 copy-start.25
  569.2 6.5 copy-start.31
  569.2 6.5 copy-start.32
  579.0 2.1 copy-start.27
  579.7 1.4 copy-start.17
  582.0 1.3 copy-start.21
  584.2 34.5 %collective-permute-start.1 = (bf16[8,256,1,128]{3,1,0,2:T(8,128)(2,1)}, bf16[8,256,1,128]{3,1,0,2:T(8,128)(2,1)S(1)}, u32[]{:S(2)}, u32[]{:S(2)}) collective-permute-start(bf16[8,256,1,128]{3,1,0,2:T(8,128)(2,1)} %slice.170), channel_id=1, source_target_pairs={{2,0},{3,1},{6,4},{7,5},{10,8},{11,9},{14,12},{15,13},{18,16},{19,... | collective-permute-start | bytes 1572872 | tf_op jit(solution)/shard_map/ppermute | solution.py:1282
  596.9 59.7 %collective-permute-start.2 = (bf16[8,256,1,128]{1,3,0,2:T(8,128)(2,1)}, bf16[8,256,1,128]{1,3,0,2:T(8,128)(2,1)}, u32[]{:S(2)}, u32[]{:S(2)}) collective-permute-start(bf16[8,256,1,128]{1,3,0,2:T(8,128)(2,1)} %slice.169), channel_id=1, source_target_pairs={{2,0},{3,1},{6,4},{7,5},{10,8},{11,9},{14,12},{15,13},{18,16},{19,... | collective-permute-start | bytes 1572872 | tf_op jit(solution)/shard_map/ppermute | solution.py:1281
  602.3 61.4 %all-to-all-start.2 = ((bf16[8,128,1024]{2,1,0:T(8,128)(2,1)}), bf16[8,128,1024]{2,1,0:T(8,128)(2,1)}, u32[]{:S(2)}, u32[]{:S(2)}) async-start(bf16[8,128,1024]{2,1,0:T(8,128)(2,1)} %fusion.1), calls=%async_computation.2 | async-start | bytes 4194304 | tf_op jit(solution)/shard_map/all_to_all | solution.py:1056
  607.8 5.1 copy-start.16
  607.8 5.1 copy-start.18
  612.9 5.8 copy-start.22
  623.6 4.6 copy-start.23
  623.6 4.5 copy-start.35
  623.6 4.5 copy-start.37
  623.6 4.5 copy-start.39
  623.6 4.5 copy-start.41
  628.1 2.9 copy-start.24
  658.1 11.3 %copy-start.14 = (bf16[8,2,128,384]{3,2,1,0:T(8,128)(2,1)S(1)}, bf16[8,2,128,384]{3,2,1,0:T(8,128)(2,1)}, u32[]{:S(2)}) copy-start(bf16[8,2,128,384]{3,2,1,0:T(8,128)(2,1)} %copy-done.13) | copy-start | bytes 4718596
  663.7 28.4 %all-to-all-start.3 = ((bf16[8,256,256]{2,1,0:T(8,128)(2,1)}), bf16[8,256,256]{2,1,0:T(8,128)(2,1)S(1)}, u32[]{:S(2)}, u32[]{:S(2)}) async-start(bf16[8,256,256]{2,1,0:T(8,128)(2,1)} %bitcast.235), calls=%async_computation.3 | async-start | bytes 2097152 | tf_op jit(solution)/shard_map/all_to_all | solution.py:1056
  669.4 11.5 %copy-start.29 = (bf16[2048,128]{1,0:T(8,128)(2,1)S(1)}, bf16[2048,128]{1,0:T(8,128)(2,1)}, u32[]{:S(2)}) copy-start(bf16[2048,128]{1,0:T(8,128)(2,1)} %get-tuple-element.95) | copy-start | bytes 1572868
  669.4 11.5 %copy-start.30 = (bf16[2048,128]{1,0:T(8,128)(2,1)S(1)}, bf16[2048,128]{1,0:T(8,128)(2,1)}, u32[]{:S(2)}) copy-start(bf16[2048,128]{1,0:T(8,128)(2,1)} %get-tuple-element.96) | copy-start | bytes 1572868
  669.4 11.5 %copy-start.33 = (bf16[8,256,1,128]{3,1,0,2:T(8,128)(2,1)S(1)}, bf16[8,256,1,128]{3,1,0,2:T(8,128)(2,1)}, u32[]{:S(2)}) copy-start(bf16[8,256,1,128]{3,1,0,2:T(8,128)(2,1)} %copy.101) | copy-start | bytes 1572868
  677.7 130.6 %collective-permute-start.3 = (bf16[8,128,1024]{2,1,0:T(8,128)(2,1)}, bf16[8,128,1024]{2,1,0:T(8,128)(2,1)}, u32[]{:S(2)}, u32[]{:S(2)}) collective-permute-start(bf16[8,128,1024]{2,1,0:T(8,128)(2,1)} %all-to-all-done.2), channel_id=1, source_target_pairs={{0,2},{2,0},{1,3},{3,1},{4,6},{6,4},{5,7},{7,5},{8,10},{10,8},{9,1... | collective-permute-start | bytes 6291464 | tf_op jit(solution)/shard_map/ppermute | solution.py:1062
  692.1 1.2 copy-start.3
  801.5 0.8 copy-start.11
  802.3 5.0 copy-start.12
  807.3 9.7 %copy-start.5 = (bf16[256,2048]{1,0:T(8,128)(2,1)S(1)}, bf16[256,2048]{1,0:T(8,128)(2,1)}, u32[]{:S(2)}) copy-start(bf16[256,2048]{1,0:T(8,128)(2,1)} %copy-done.4) | copy-start | bytes 3145732
  808.4 12.8 %copy-start.1 = (bf16[256,2048]{1,0:T(8,128)(2,1)S(1)}, bf16[256,2048]{1,0:T(8,128)(2,1)}, u32[]{:S(2)}) copy-start(bf16[256,2048]{1,0:T(8,128)(2,1)} %param.14) | copy-start | bytes 3145732

commit v5 on v4

--- a/solution.py
+++ b/solution.py
@@ -185,7 +185,7 @@
     ]
 
 
-def reduce_phase(place, sender, partial, scratch, between=None):
+def reduce_phase(place, sender, partial, scratch, between=None, idle=None):
     mine, core_in, y_in, line_in, total, local_sem, core_sem, y_sem, line_sem = scratch
     rows = total.shape[0]
     z, y, core = place.z, place.y, place.core
@@ -263,6 +263,8 @@
     for number, block in enumerate(order[:-1]):
         if number == LINE - 2 and between is not None:
             between()
+        if number < 2 and idle is not None:
+            idle(number)
         slot = 2 * block + y
         fetch(slot).wait()
         to_core(slot).wait_recv()
@@ -322,7 +324,7 @@
     ]
 
 
-def gather_phase(place, sender, gathered, scratch, between=None, later=None):
+def gather_phase(place, sender, gathered, scratch, between=None, later=None, last=None):
     own, local_sem, core_sem, y_sem, line_sem = scratch
     rows = own.shape[0]
     z, y, core = place.z, place.y, place.core
@@ -400,6 +402,8 @@
             across(z + distance - 1 < LINE, z + distance - 1)
         if distance == 1 and later is not None:
             later()
+        if distance == LINE - 1 and last is not None:
+            last()
 
     keep.wait()
     for block in range(LINE):
@@ -575,6 +579,7 @@
 
 REDUCE = 9
 GATHER = 5
+PIECES = 8
 
 
 def first_kernel(
@@ -673,34 +678,123 @@
     sender.drain()
 
 
+class WeightGrads:
+    def __init__(self, place, arrays, outs, scratch):
+        self.place = place
+        self.inner, self.grad_mlp, self.hidden, self.grad_pair = arrays
+        self.outs = outs
+        self.tall, self.turned, self.inner_turned = scratch[:3]
+        self.fulls, self.others = scratch[3:5], scratch[5:7]
+        self.fetch_sem, self.side_sem = scratch[7:]
+        self.piece = self.tall.shape[3]
+
+    def fetch(self, number, slot):
+        columns = pl.ds(pl.multiple_of(number * self.piece, self.piece), self.piece)
+        return [
+            pltpu.make_async_copy(
+                array.at[:, columns], self.tall.at[slot, index], self.fetch_sem.at[slot, index]
+            )
+            for index, array in enumerate((self.hidden, self.grad_mlp))
+        ]
+
+    def side_of(self, index, number, side):
+        if index == 0:
+            return self.fulls[0].at[number, :, side]
+        return self.fulls[1].at[number, side]
+
+    def crossing(self, number, index):
+        return remote(
+            self.side_of(index, number, 1 - self.place.side),
+            self.others[index].at[number],
+            self.side_sem.at[0, index, number],
+            self.side_sem.at[1, index, number],
+            self.place.across(),
+        )
+
+    def start(self):
+        for copy in self.fetch(0, 0):
+            copy.start()
+        self.inner_turned[...] = self.inner[...].T
+
+    def one(self, number, carry):
+        slot = lax.rem(number, 2)
+        for copy in self.fetch(number, slot):
+            copy.wait()
+
+        @pl.when(number < PIECES - 1)
+        def _():
+            for copy in self.fetch(number + 1, 1 - slot):
+                copy.start()
+
+        full, low = self.fulls
+        self.turned[...] = self.tall[slot, 0].T
+        columns = self.grad_pair.shape[1]
+        step = columns // 4
+
+        def columns_step(index, carry):
+            at = pl.ds(pl.multiple_of(index * step, step), step)
+            value = product(self.turned[...], self.grad_pair[:, at]).astype(BF)
+            full[number, :, :, :, at] = value.reshape(full.shape[1:4] + (step,))
+            return carry
+
+        lax.fori_loop(0, 4, columns_step, 0)
+        value = product(self.inner_turned[...], self.tall[slot, 1]).astype(BF)
+        low[number] = value.reshape(low.shape[1:])
+        for index in range(2):
+            self.crossing(number, index).start()
+        return carry
+
+    def some(self, which):
+        half = PIECES // 2
+        lax.fori_loop(which * half, which * half + half, self.one, 0)
+
+    def add(self):
+        def step(number, carry):
+            for index in range(2):
+                self.crossing(number, index).wait_recv()
+                own = self.side_of(index, number, self.place.side)[...].astype(F32)
+                other = self.others[index][number].astype(F32)
+                self.outs[index][number] = (own + other).astype(BF)
+            return carry
+
+        lax.fori_loop(0, PIECES, step, 0)
+
+    def finish(self):
+        def step(number, carry):
+            for index in range(2):
+                self.crossing(number, index).wait_send()
+            return carry
+
+        lax.fori_loop(0, PIECES, step, 0)
+
+
 def branch_kernel(
     partial,
     branch,
     cotangent,
     gain,
-    pair_grad,
-    down_grad,
+    inner_low,
+    grad_mlp,
+    hidden_low,
+    grad_pair,
     gathered,
     grad_hidden,
     gain_grad,
-    pair_other,
-    down_other,
+    pair_mine,
+    down_mine,
     *scratch,
 ):
     place = Place()
     sender = Sender()
     greet(place, True)
-    (side_sem,) = scratch[REDUCE + GATHER :]
-    count = down_other.shape[0]
-    rows_out = pl.ds(pl.multiple_of((1 - place.side) * count, count), count)
-    sources = (pair_grad.at[:, 1 - place.side], down_grad.at[rows_out])
-    crossings = [
-        remote(source, target, side_sem.at[0, index], side_sem.at[1, index], place.across())
-        for index, (source, target) in enumerate(zip(sources, (pair_other, down_other)))
-    ]
-    for crossing in crossings:
-        crossing.start()
-    reduce_phase(place, sender, partial, scratch[:REDUCE])
+    grads = WeightGrads(
+        place,
+        (inner_low, grad_mlp, hidden_low, grad_pair),
+        (pair_mine, down_mine),
+        scratch[REDUCE + GATHER :],
+    )
+    grads.start()
+    reduce_phase(place, sender, partial, scratch[:REDUCE], idle=grads.some)
     total, own = scratch[4], scratch[REDUCE]
     rows, width = total.shape
     gain_grad[...] = jnp.zeros_like(gain_grad)
@@ -717,9 +811,10 @@
         own[at] = (scale * (gained - normed * (inner / width))).astype(BF)
 
     by_rows(rows, body)
-    gather_phase(place, sender, gathered, scratch[REDUCE : REDUCE + GATHER])
-    for crossing in crossings:
-        crossing.wait()
+    gather_phase(
+        place, sender, gathered, scratch[REDUCE : REDUCE + GATHER], last=grads.add
+    )
+    grads.finish()
     sender.drain()
 
 
@@ -992,18 +1087,58 @@
             100,
         )(partial, hidden, cotangent, gain)
 
-    def branch(self, partial, branch, cotangent, gain, pair_grad, down_grad):
-        shape = pair_grad.shape
-        pair_other = jax.ShapeDtypeStruct((shape[0],) + shape[2:], BF)
-        down_other = jax.ShapeDtypeStruct((down_grad.shape[0] // 2, down_grad.shape[1]), BF)
-        return talk(
+    def branch(self, partial, branch, cotangent, gain, inner, grad_mlp, hidden, grad_pair):
+        team_rows, units = inner.shape
+        columns = grad_pair.shape[1]
+        piece = self.width // PIECES
+        count = self.fsdp // PIECES
+        half = self.width // self.fsdp // 2
+        pair_shape = (PIECES, count, half, columns)
+        down_shape = (PIECES, units // 2, piece)
+
+        def both(shape):
+            return pltpu.VMEM((shape[0], 2) + shape[1:], BF)
+
+        def sides_inside(shape):
+            return pltpu.VMEM((shape[0], shape[1], 2) + shape[2:], BF)
+
+        gathered, grad_hidden, gain_grad, pair_mine, down_mine = talk(
             branch_kernel,
             3,
-            (self.all_low, self.own_wide, self.line_wide, pair_other, down_other),
-            ([HBM, VMEM, VMEM, VMEM, HBM, HBM], (HBM, VMEM, VMEM, HBM, HBM)),
-            self.reduces + self.gathers + [DMA((2, 2))],
+            (
+                self.all_low,
+                self.own_wide,
+                self.line_wide,
+                jax.ShapeDtypeStruct(pair_shape, BF),
+                jax.ShapeDtypeStruct(down_shape, BF),
+            ),
+            (
+                [HBM, VMEM, VMEM, VMEM, VMEM, HBM, HBM, VMEM],
+                (HBM, VMEM, VMEM, VMEM, VMEM),
+            ),
+            self.reduces
+            + self.gathers
+            + [
+                pltpu.VMEM((2, 2, team_rows, piece), BF),
+                pltpu.VMEM((piece, team_rows), BF),
+                pltpu.VMEM((units, team_rows), BF),
+                sides_inside(pair_shape),
+                both(down_shape),
+                pltpu.VMEM(pair_shape, BF),
+                pltpu.VMEM(down_shape, BF),
+                DMA((2, 2)),
+                DMA((2, 2, PIECES)),
+            ],
             100,
-        )(partial, branch, cotangent, gain, pair_grad, down_grad)
+        )(partial, branch, cotangent, gain, inner, grad_mlp, hidden, grad_pair)
+        down_mine = down_mine.reshape(PIECES, units // 2, count, piece // count)
+        return (
+            gathered,
+            grad_hidden,
+            gain_grad,
+            pair_mine.reshape(self.fsdp, half, columns),
+            down_mine.transpose(0, 2, 1, 3).reshape(self.fsdp, units // 2, piece // count),
+        )
 
     def last(self, partial, grad_hidden, qkv, out, small, down):
         both = jax.ShapeDtypeStruct((2 * self.rows, self.width), F32)
@@ -1058,8 +1193,7 @@
     def repeat(self, pieces):
         return jnp.concatenate([pieces] * self.teams, axis=0) if self.teams > 1 else pieces
 
-    def unpack(self, own, down):
-        other = lax.ppermute(own, "context", [(0, 1), (1, 0)])
+    def unpack(self, own, other, down):
         half, columns = own.shape[1], own.shape[2] // 2
         rows, down_columns = 2 * down.shape[2], down.shape[3]
 
@@ -1246,24 +1380,20 @@
     grad_mlp_all, outputs, grad_mlp_gain = team.turn(
         product(inner_low, down_w).astype(BF), hidden, grad_out, gain_mlp
     )
-    down_grad = product_left(inner_low, grad_mlp_all).astype(BF)
     grad_inner = product_right(grad_mlp_all, down_w)
     grad_gate_low = (grad_inner * upward * sigma * (1.0 + gate * (1.0 - sigma))).astype(BF)
     grad_up_low = (grad_inner * gate * sigma).astype(BF)
     grad_pair = jnp.concatenate([grad_gate_low, grad_up_low], axis=1)
-    pair_grad = team.of_columns(product_left(hidden_all, grad_pair))
-    grad_branch_all, grad_hidden, grad_attn_gain, pair_other, down_other = team.branch(
+    grad_branch_all, grad_hidden, grad_attn_gain, pair_mine, down_mine = team.branch(
         product_right(grad_pair, pair_w).astype(BF),
         attn_sum,
         grad_out,
         gain_attn,
-        pair_grad,
-        down_grad,
-    )
-    pair_mine = lax.dynamic_index_in_dim(pair_grad, team.context, 1, keepdims=False)
-    pair_mine = (pair_mine.astype(F32) + pair_other.astype(F32)).astype(BF)
-    down_mine = (team.half(down_grad, 0).astype(F32) + down_other.astype(F32)).astype(BF)
-    down_mine = down_mine.reshape(down_mine.shape[0], fsdp, -1).transpose(1, 0, 2)
+        inner_low,
+        grad_mlp_all,
+        hidden_all,
+        grad_pair,
+    )
     pair_came = team.swap(pair_mine)
     output_grad = team.of_rows(product_left(attended_low, grad_branch_all))
     grad_attended = product_right(grad_branch_all, output_w).astype(BF).reshape(by_head)
@@ -1288,14 +1418,15 @@
     grad_key_norm = rotate_back(grad_key_rot, cosine, sine).reshape(team_rows, -1)
     grad_query_gain = jnp.sum(grad_query_norm * query_raw * scale_query, axis=0)
     grad_key_gain = jnp.sum(grad_key_norm * key_raw * scale_key, axis=0)
-    totals = team.total(
-        jnp.stack(
-            [
-                jnp.sum(query_raw * flat_query * grad_query_norm, axis=1),
-                jnp.sum(key_raw * flat_key * grad_key_norm, axis=1),
-            ]
-        )
-    )
+    inner_sums = jnp.stack(
+        [
+            jnp.sum(query_raw * flat_query * grad_query_norm, axis=1),
+            jnp.sum(key_raw * flat_key * grad_key_norm, axis=1),
+        ]
+    )
+    inner_sums, pair_came = lax.optimization_barrier((inner_sums, pair_came))
+    pair_other = lax.ppermute(pair_came, "context", [(0, 1), (1, 0)])
+    totals = team.total(inner_sums)
     down_mine, totals = lax.optimization_barrier((down_mine, totals))
     down_came = team.swap(down_mine)
     grad_query_low = norm_back(
@@ -1315,8 +1446,8 @@
     ]
     used = 2 * share + 2 * heads * head_share
     small = jnp.concatenate(small + [jnp.zeros((fsdp, 8 * 128 - used), F32)], axis=1)
-    partial, pair_came = lax.optimization_barrier(
-        (product_right(grad_qkv, qkv_w).astype(BF), pair_came)
+    partial, pair_other = lax.optimization_barrier(
+        (product_right(grad_qkv, qkv_w).astype(BF), pair_other)
     )
     input_grad, qkv_came, output_came, small_came, down_came = team.last(
         partial,
@@ -1327,7 +1458,7 @@
         down_came,
     )
     grad_w_query, grad_w_key, grad_w_value = team.columns_out(qkv_came, 3)
-    grad_w_gate, grad_w_up, grad_w_down = team.unpack(pair_came, down_came)
+    grad_w_gate, grad_w_up, grad_w_down = team.unpack(pair_came, pair_other, down_came)
     grad_w_output = team.rows_out(output_came)
     came = jnp.sum(small_came, axis=1).reshape(fsdp, -1)
     row_gains = jnp.sum(came[:, : 2 * share], axis=0).reshape(2, share)

time: 831 us -> 800 us (0.963)
  matrix products: 130 us -> 106 us
  waiting for transfers between devices: 3.99 us -> 25.3 us
  Pallas kernels: 545 us -> 527 us
    dot_general x4 -> x2, matrix products: 35.4 us -> 13.8 us  [product_left(): return jnp.einsum('rd,rf->df', left, right, preferred_element_type=F32)]
    ppermute x1, waiting for transfers between devices: 0.01 us -> 19.9 us  [local(): pair_other = lax.ppermute(pair_came, 'context', [(0, 1), (1, 0)])]
    pallas_call x7, Pallas kernels: 530 us -> 512 us  [call(): pl.pallas_call(kernel, out_shape=shapes, in_specs=specs[0], out_specs=spe...]
  transfers between devices with their start and end apart: 8 -> 8, of which waited for: 2 -> 3; matrix products, arithmetic and copies ran while one was open for 15% -> 14% of each run, Pallas kernels for 18% -> 2%
where the time goes in v5:
time: 800 us; the launch traced here: 792 us
  Pallas kernels  527 us (66%)
  matrix products  106 us (13%)
  other arithmetic  56.3 us (7%)
  starting transfers between devices  43.6 us (5%)
  local copies, waits for them, and re-layouts  31.2 us (4%)
  waiting for transfers between devices  25.3 us (3%)
    pallas_call x7, Pallas kernels, call(): pl.pallas_call(kernel, out_shape=shapes, in_specs=specs[0], out_specs=spe...  512 us
    all_to_all x4, starting transfers between devices, swap(): lax.all_to_all(pieces, 'fsdp', split_axis=0, concat_axis=0, tiled=True)  36.1 us
    dot_general x4, matrix products, product(): return jnp.dot(left, right, preferred_element_type=F32)  35.9 us
    dot_general x4, matrix products, product_right(): return jnp.einsum('rf,df->rd', left, right, preferred_element_type=F32)  35.2 us
    ppermute x1, waiting for transfers between devices, local(): pair_other = lax.ppermute(pair_came, 'context', [(0, 1), (1, 0)])  19.9 us
    unnamed x86, local copies, waits for them, and re-layouts  16.5 us
  transfers between devices with their start and end apart: 8, of which 3 were waited for; matrix products, arithmetic and copies ran while one was open for 14% of the time, Pallas kernels for 2%

profile of v5, /device:TPU:16, one launch (start us, length us, event | category | flops | bytes accessed | tf_op | source)
XLA Modules:
  0.0 791.8 jit_solution(236119323855086575)
XLA Ops:
  4.5 6.3 pack_kernel.1
  10.8 65.9 %first_kernel.1 = (bf16[2048,2048]{1,0:T(8,128)(2,1)}, bf16[8,2,128,384]{3,2,1,0:T(8,128)(2,1)S(1)}, bf16[8,2,64,256]{3,2,1,0:T(8,128)(2,1)S(1)}, f32[8,2,8,128]{3,2,1,0:T(8,128)S(1)}) custom-call(bf16[128,2048]{1,0:T(8,128)(2,1)S(1)} %constant_dynamic-slice_fusion.3.own_ref.tokens, bf16[256,1024]{1,0:T(8,128)(2,1)S(1)} %copy-done.6, ...), custom_call_target="tpu_custom_call" | custom-call | bytes 240000000 | tf_op jit(solution)/shard_map/first_kernel/pallas_call | solution.py:974
  76.7 1.2 copy-done.12
  77.9 17.3 %all-to-all-start.1 = ((bf16[8,256,256]{2,1,0:T(8,128)(2,1)}), bf16[8,256,256]{2,1,0:T(8,128)(2,1)S(1)}, u32[]{:S(2)}, u32[]{:S(2)}) async-start(bf16[8,256,256]{2,1,0:T(8,128)(2,1)} %get-tuple-element.61), calls=%async_computation.1 | async-start | bytes 2097152 | tf_op jit(solution)/shard_map/all_to_all | solution.py:1191
  95.3 10.0 %fusion.57 = f32[2048,384]{1,0:T(8,128)} fusion(bf16[2048,2048]{1,0:T(8,128)(2,1)} %get-tuple-element.54, bf16[2048,384]{1,0:T(8,128)(2,1)} %bitcast.214), kind=kOutput, calls=%fused_computation.152 | convolution fusion | flops 3221225472 | bytes 13107200 | tf_op jit(solution)/shard_map/dot_general | solution.py:18
  105.3 2.2 multiply_reduce_fusion.2
  107.6 1.3 split.54.rest_0_
  109.4 15.0 %sum_kernel.2 = (f32[32,128]{1,0:T(8,128)S(1)}, bf16[2048,128]{1,0:T(8,128)(2,1)S(1)}) custom-call(f32[32,128]{1,0:T(8,128)S(1)} %reshape.506.value, bf16[2048,128]{1,0:T(8,128)(2,1)S(1)} %split.54.rest_0_), custom_call_target="tpu_custom_call" | custom-call | bytes 30000000 | tf_op jit(solution)/shard_map/sum_kernel/pallas_call | solution.py:974
  124.6 2.7 multiply_multiply_fusion
  128.3 1.7 slice_negate_fusion.2
  129.9 6.6 all-to-all-start
  136.6 1.3 fusion.35
  138.9 6.2 fusion.15
  145.1 3.4 collective-permute-start
  148.7 1.7 fusion.11
  153.6 1.1 constant_dynamic-slice_fusion.1.cotangent
  154.7 6.4 fusion.13
  161.2 5.3 fusion.56
  166.5 4.2 fusion.9
  170.7 1.3 copy.95
  172.0 6.7 convolution_convert_fusion.3.partial
  178.6 2.6 all-to-all-done.pair
  181.2 108.8 %hidden_kernel.1 = (bf16[2048,2048]{1,0:T(8,128)(2,1)}, f32[128,2048]{1,0:T(8,128)S(1)}, f32[128,2048]{1,0:T(8,128)S(1)}, bf16[8,2,128,1024]{3,2,1,0:T(8,128)(2,1)}, bf16[8,2,256,256]{3,2,1,0:T(8,128)(2,1)S(1)}) custom-call(bf16[2048,2048]{1,0:T(8,128)(2,1)} %convolution_convert_fusion.3.partial, ...), custom_call_target="tpu_custom_call" | custom-call | bytes 300000000 | tf_op jit(solution)/shard_map/hidden_kernel/pallas_call | solution.py:974
  290.1 12.5 %fusion.58 = f32[2048,1024]{1,0:T(8,128)S(1)} fusion(bf16[2048,2048]{1,0:T(8,128)(2,1)} %get-tuple-element.62.hidden_low, bf16[2048,1024]{1,0:T(8,128)(2,1)} %bitcast.253), kind=kOutput, calls=%fused_computation.153 | convolution fusion | flops 8589934592 | bytes 20971520 | tf_op jit(solution)/shard_map/dot_general | solution.py:18
  302.5 1.5 multiply_convert_fusion.3.inner_low
  304.0 1.8 copy-done.25
  305.8 1.2 copy.99
  307.7 6.8 convolution_convert_fusion.2.partial
  314.5 104.1 %turn_kernel.1 = (bf16[2048,2048]{1,0:T(8,128)(2,1)}, bf16[256,2048]{1,0:T(8,128)(2,1)S(1)}, f32[1,2048]{1,0:T(1,128)S(1)}) custom-call(bf16[2048,2048]{1,0:T(8,128)(2,1)} %convolution_convert_fusion.2.partial, f32[128,2048]{1,0:T(8,128)S(1)} %get-tuple-element.65.hidden, bf16[128,2048]{1,0:T(8,128)(2,1)S(1)} %constant_dynamic-slice_fusion.1.cotangent, ...), custom_call_target="tpu_custom_call" | custom-call | bytes 300000000 | tf_op jit(solution)/shard_map/turn_kernel/pallas_call | solution.py:974
  418.6 11.2 %multiply_convert_fusion.2 = (bf16[2048,512]{1,0:T(8,128)(2,1)S(1)}, bf16[2048,512]{1,0:T(8,128)(2,1)S(1)}) fusion(f32[2048,1024]{1,0:T(8,128)} %copy-done.25, bf16[2048,2048]{1,0:T(8,128)(2,1)} %get-tuple-element.67.grad_mlp, bf16[512,2048]{1,0:T(8,128)(2,1)S(1)} %bitcast.226), kind=kOutput, calls=%fused_computation.9 | convolution fusion | flops 4308598784 | bytes 23068672 | tf_op jit(solution)/shard_map/rf,df->rd/dot_general | solution.py:26
  429.9 2.8 pad_maximum_fusion.grad_pair
  433.5 10.9 %convolution_convert_fusion.1.partial = bf16[2048,2048]{1,0:T(8,128)(2,1)} fusion(bf16[2048,1024]{1,0:T(8,128)(2,1)S(1)} %bitcast.254, bf16[2048,512]{1,0:T(8,128)(2,1)S(1)} %get-tuple-element.98, bf16[2048,512]{1,0:T(8,128)(2,1)S(1)} %get-tuple-element.97), kind=kOutput, calls=%fused_computation.2 | convolution fusion | flops 8602517504 | bytes 16777216 | tf_op jit(solution)/shard_map/rf,df->rd/dot_general | solution.py:26
  444.5 112.3 %branch_kernel.1 = (bf16[2048,2048]{1,0:T(8,128)(2,1)}, f32[128,2048]{1,0:T(8,128)S(1)}, f32[1,2048]{1,0:T(1,128)S(1)}, bf16[8,1,128,1024]{3,2,1,0:T(8,128)(2,1)}, bf16[8,256,256]{2,1,0:T(8,128)(2,1)}) custom-call(bf16[2048,2048]{1,0:T(8,128)(2,1)} %convolution_convert_fusion.1.partial, f32[128,2048]{1,0:T(8,128)S(1)} %get-tuple-element.68.branch, ...), custom_call_target="tpu_custom_call" | custom-call | bytes 300000000 | tf_op jit(solution)/shard_map/branch_kernel/pallas_call | solution.py:974
  556.8 6.1 convolution_convert_fusion.6
  563.0 2.5 multiply_reduce_fusion
  565.5 5.7 all-to-all-start.2
  571.2 3.9 multiply_convert_fusion
  575.1 1.3 copy-done.16
  577.3 1.4 copy-done.20
  579.6 1.3 collective-permute-start.1
  582.7 3.1 convolution_bitcast_fusion
  586.8 1.8 collective-permute-start.2
  588.6 4.7 convolution_convert_fusion.5
  593.5 5.4 fusion.33
  599.3 4.8 maximum_add_fusion
  604.5 4.1 maximum_add_fusion.1
  608.6 2.9 fusion.20
  611.8 1.5 fusion.10
  614.3 2.7 all-to-all-done.2
  617.1 10.6 %sum_kernel.3 = f32[32,128]{1,0:T(8,128)S(1)} custom-call(f32[32,128]{1,0:T(8,128)S(1)} %reshape.527.value), custom_call_target="tpu_custom_call" | custom-call | bytes 30000000 | tf_op jit(solution)/shard_map/sum_kernel/pallas_call | solution.py:974
  627.8 1.0 collective-permute-start.3
  628.8 6.4 all-to-all-start.3
  635.2 3.7 fusion.22
  639.0 6.9 convolution_convert_fusion.partial
  645.9 9.1 %convolution_convert_fusion.4 = bf16[2048,384]{1,0:T(8,128)(2,1)} fusion(bf16[2048,2048]{1,0:T(8,128)(2,1)} %get-tuple-element.54, bf16[2048,128]{1,0:T(8,128)(2,1)S(1)} %bitcast.233, bf16[2048,128]{1,0:T(8,128)(2,1)S(1)} %get-tuple-element.100, bf16[2048,128]{1,0:T(8,128)(2,1)S(1)} %get-tuple-element.99), kind=kOutput, calls=%fused_computation.14 | convolution fusion | flops 3226730496 | bytes 11534336 | tf_op jit(solution)/shard_map/rd,rf->df/dot_general | solution.py:22
  655.0 19.9 %collective-permute-done.3 = bf16[8,128,1024]{2,1,0:T(8,128)(2,1)} collective-permute-done((bf16[8,128,1024]{2,1,0:T(8,128)(2,1)}, bf16[8,128,1024]{2,1,0:T(8,128)(2,1)}, u32[]{:S(2)}, u32[]{:S(2)}) %collective-permute-start.3) | collective-permute-done | bytes 2097184 | tf_op jit(solution)/shard_map/ppermute | solution.py:1428
  674.9 1.2 copy-done.3
  676.2 95.5 %last_kernel.1 = (f32[256,2048]{1,0:T(8,128)}, bf16[8,2,128,384]{3,2,1,0:T(8,128)(2,1)S(1)}, bf16[8,2,64,256]{3,2,1,0:T(8,128)(2,1)S(1)}, f32[8,2,8,128]{3,2,1,0:T(8,128)S(1)}, bf16[8,2,256,256]{3,2,1,0:T(8,128)(2,1)}) custom-call(bf16[2048,2048]{1,0:T(8,128)(2,1)} %convolution_convert_fusion.partial, f32[128,2048]{1,0:T(8,128)S(1)} %copy-done.3, ...), custom_call_target="tpu_custom_call" | custom-call | bytes 240000000 | tf_op jit(solution)/shard_map/last_kernel/pallas_call | solution.py:974
  772.8 1.1 copy_bitcast_fusion
  773.9 1.1 copy_bitcast_fusion.1
  775.0 1.1 copy_bitcast_fusion.2
  776.2 1.1 bitcast_convert_fusion
  778.5 8.6 %unpack_kernel.1 = (f32[256,4096]{1,0:T(8,128)}, f32[256,4096]{1,0:T(8,128)}, f32[4096,256]{1,0:T(8,128)}) custom-call(s32[1]{0:T(128)} %bitcast.side, bf16[1,8,128,1024]{3,2,1,0:T(8,128)(2,1)} %bitcast.58.own, bf16[1,8,128,1024]{3,2,1,0:T(8,128)(2,1)} %bitcast.59.other, bf16[1,8,512,256]{3,2,1,0:T(8,128)(2,1)} %bitcast.223), custom_call_target="tpu_custom_call" | custom-call | tf_op jit(solution)/shard_map/unpack_kernel/pallas_call | solution.py:1208
  788.1 3.1 copy.155
  (149 shorter events, 21.8 us)
Async XLA Ops:
  0.6 3.8 copy-start
  0.7 10.1 %copy-start.6 = (bf16[256,1024]{1,0:T(8,128)(2,1)S(1)}, bf16[256,1024]{1,0:T(8,128)(2,1)}, u32[]{:S(2)}) copy-start(bf16[256,1024]{1,0:T(8,128)(2,1)} %query.1) | copy-start | bytes 1572868
  0.7 10.1 %copy-start.7 = (bf16[256,1024]{1,0:T(8,128)(2,1)S(1)}, bf16[256,1024]{1,0:T(8,128)(2,1)}, u32[]{:S(2)}) copy-start(bf16[256,1024]{1,0:T(8,128)(2,1)} %key.1) | copy-start | bytes 1572868
  0.7 10.1 %copy-start.8 = (bf16[256,1024]{1,0:T(8,128)(2,1)S(1)}, bf16[256,1024]{1,0:T(8,128)(2,1)}, u32[]{:S(2)}) copy-start(bf16[256,1024]{1,0:T(8,128)(2,1)} %value.1) | copy-start | bytes 1572868
  4.5 6.3 copy-start.9
  76.7 1.2 copy-start.12
  77.9 52.0 %all-to-all-start.1 = ((bf16[8,256,256]{2,1,0:T(8,128)(2,1)}), bf16[8,256,256]{2,1,0:T(8,128)(2,1)S(1)}, u32[]{:S(2)}, u32[]{:S(2)}) async-start(bf16[8,256,256]{2,1,0:T(8,128)(2,1)} %get-tuple-element.61), calls=%async_computation.1 | async-start | bytes 2097152 | tf_op jit(solution)/shard_map/all_to_all | solution.py:1191
  127.3 1.0 copy-start.19
  129.9 51.3 %all-to-all-start = ((bf16[8,128,1024]{2,1,0:T(8,128)(2,1)}), bf16[8,128,1024]{2,1,0:T(8,128)(2,1)}, u32[]{:S(2)}, u32[]{:S(2)}) async-start(bf16[8,128,1024]{2,1,0:T(8,128)(2,1)} %get-tuple-element.60), calls=%async_computation | async-start | bytes 4194304 | tf_op jit(solution)/shard_map/all_to_all | solution.py:1191
  136.6 12.1 %copy-start.18 = (f32[2048,128]{1,0:T(8,128)S(1)}, f32[2048,128]{1,0:T(8,128)}, u32[]{:S(2)}) copy-start(f32[2048,128]{1,0:T(8,128)} %get-tuple-element.102) | copy-start | bytes 3145732
  137.9 1.0 copy-start.14
  145.1 16.0 %collective-permute-start = (bf16[8,256,1,128]{3,1,0,2:T(8,128)(2,1)}, bf16[8,256,1,128]{3,1,0,2:T(8,128)(2,1)}, u32[]{:S(2)}, u32[]{:S(2)}) collective-permute-start(bf16[8,256,1,128]{3,1,0,2:T(8,128)(2,1)} %fusion.15), channel_id=1, source_target_pairs={{0,2},{1,3},{4,6},{5,7},{8,10},{9,11},{12,14},{13,15},{16,18},{17,... | collective-permute-start | bytes 1572872 | tf_op jit(solution)/shard_map/ppermute | solution.py:1348
  161.1 5.3 copy-start.27
  302.5 3.3 copy-start.25
  305.8 1.9 copy-start.24
  418.6 11.3 %copy-start.4 = (bf16[256,2048]{1,0:T(8,128)(2,1)}, bf16[256,2048]{1,0:T(8,128)(2,1)S(1)}, u32[]{:S(2)}) copy-start(bf16[256,2048]{1,0:T(8,128)(2,1)S(1)} %get-tuple-element.151) | copy-start | bytes 3145732
  429.9 3.6 copy-start.34
  444.5 112.3 %copy-start.29 = (bf16[16,8,8,256]{3,1,2,0:T(8,128)(2,1)S(1)}, bf16[16,8,8,256]{3,1,2,0:T(8,128)(2,1)}, u32[]{:S(2)}) copy-start(bf16[16,8,8,256]{3,1,2,0:T(8,128)(2,1)} %copy.125) | copy-start | bytes 1572868
  556.8 6.2 copy-start.2
  556.8 6.2 copy-start.26
  556.8 6.2 copy-start.31
  556.8 6.2 copy-start.32
  563.0 2.5 copy-start.35
  565.5 51.6 %all-to-all-start.2 = ((bf16[8,128,1024]{2,1,0:T(8,128)(2,1)}), bf16[8,128,1024]{2,1,0:T(8,128)(2,1)}, u32[]{:S(2)}, u32[]{:S(2)}) async-start(bf16[8,128,1024]{2,1,0:T(8,128)(2,1)} %bitcast.39), calls=%async_computation.2 | async-start | bytes 4194304 | tf_op jit(solution)/shard_map/all_to_all | solution.py:1191
  571.2 5.2 copy-start.28
  575.1 1.3 copy-start.16
  577.3 1.4 copy-start.20
  579.6 19.8 %collective-permute-start.1 = (bf16[8,256,1,128]{3,1,0,2:T(8,128)(2,1)}, bf16[8,256,1,128]{3,1,0,2:T(8,128)(2,1)S(1)}, u32[]{:S(2)}, u32[]{:S(2)}) collective-permute-start(bf16[8,256,1,128]{3,1,0,2:T(8,128)(2,1)} %slice.170), channel_id=1, source_target_pairs={{2,0},{3,1},{6,4},{7,5},{10,8},{11,9},{14,12},{15,13},{18,16},{19,... | collective-permute-start | bytes 1572872 | tf_op jit(solution)/shard_map/ppermute | solution.py:1412
  585.9 7.4 copy-start.30
  586.8 6.7 copy-start.15
  586.8 6.7 copy-start.17
  586.8 25.0 %collective-permute-start.2 = (bf16[8,256,1,128]{1,3,0,2:T(8,128)(2,1)}, bf16[8,256,1,128]{1,3,0,2:T(8,128)(2,1)}, u32[]{:S(2)}, u32[]{:S(2)}) collective-permute-start(bf16[8,256,1,128]{1,3,0,2:T(8,128)(2,1)} %slice.169), channel_id=1, source_target_pairs={{2,0},{3,1},{6,4},{7,5},{10,8},{11,9},{14,12},{15,13},{18,16},{19,... | collective-permute-start | bytes 1572872 | tf_op jit(solution)/shard_map/ppermute | solution.py:1411
  593.5 5.8 copy-start.21
  604.1 4.5 copy-start.22
  608.6 2.9 copy-start.23
  613.3 25.7 %copy-start.13 = (bf16[8,2,128,384]{3,2,1,0:T(8,128)(2,1)S(1)}, bf16[8,2,128,384]{3,2,1,0:T(8,128)(2,1)}, u32[]{:S(2)}) copy-start(bf16[8,2,128,384]{3,2,1,0:T(8,128)(2,1)} %copy-done.12) | copy-start | bytes 4718596
  627.8 47.2 %collective-permute-start.3 = (bf16[8,128,1024]{2,1,0:T(8,128)(2,1)}, bf16[8,128,1024]{2,1,0:T(8,128)(2,1)}, u32[]{:S(2)}, u32[]{:S(2)}) collective-permute-start(bf16[8,128,1024]{2,1,0:T(8,128)(2,1)} %all-to-all-done.2), channel_id=1, source_target_pairs={{0,2},{2,0},{1,3},{3,1},{4,6},{6,4},{5,7},{7,5},{8,10},{10,8},{9,1... | collective-permute-start | bytes 6291464 | tf_op jit(solution)/shard_map/ppermute | solution.py:1428
  628.8 46.1 %all-to-all-start.3 = ((bf16[8,256,256]{2,1,0:T(8,128)(2,1)}), bf16[8,256,256]{2,1,0:T(8,128)(2,1)S(1)}, u32[]{:S(2)}, u32[]{:S(2)}) async-start(bf16[8,256,256]{2,1,0:T(8,128)(2,1)} %get-tuple-element.79), calls=%async_computation.3 | async-start | bytes 2097152 | tf_op jit(solution)/shard_map/all_to_all | solution.py:1191
  635.2 3.8 copy-start.33
  674.9 1.2 copy-start.3
  771.6 0.8 copy-start.10
  772.4 3.7 copy-start.11
  776.2 11.0 %copy-start.5 = (bf16[256,2048]{1,0:T(8,128)(2,1)S(1)}, bf16[256,2048]{1,0:T(8,128)(2,1)}, u32[]{:S(2)}) copy-start(bf16[256,2048]{1,0:T(8,128)(2,1)} %copy-done.4) | copy-start | bytes 3145732
  778.5 12.8 %copy-start.1 = (bf16[256,2048]{1,0:T(8,128)(2,1)S(1)}, bf16[256,2048]{1,0:T(8,128)(2,1)}, u32[]{:S(2)}) copy-start(bf16[256,2048]{1,0:T(8,128)(2,1)} %param.14) | copy-start | bytes 3145732

commit v6 on v5

--- a/solution.py
+++ b/solution.py
@@ -173,41 +173,54 @@
 
 def reduce_scratch(rows, width):
     return [
-        pltpu.VMEM((2 * LINE, rows, width), BF),
+        pltpu.VMEM((2 * LINE, 2, rows, width), BF),
         pltpu.VMEM((2 * LINE, rows, width), BF),
         pltpu.VMEM((LINE, rows, width), BF),
         pltpu.VMEM((LINE + 1, rows, width), BF),
         pltpu.VMEM((rows, width), F32),
-        DMA((2 * LINE,)),
         DMA((2, 2 * LINE)),
         DMA((2, LINE)),
         DMA((2, LINE + 1)),
     ]
 
 
-def reduce_phase(place, sender, partial, scratch, between=None, idle=None):
-    mine, core_in, y_in, line_in, total, local_sem, core_sem, y_sem, line_sem = scratch
+def rows_product(left, right, turned):
+    def make(slot, made):
+        rows, width = made.shape[2:]
+        values = left[pl.ds(pl.multiple_of(slot * 2 * rows, 2 * rows), 2 * rows)]
+        step = width // 4
+
+        def some(index, carry):
+            at = pl.ds(pl.multiple_of(index * step, step), step)
+            if turned:
+                value = product_right(values, right[at])
+            else:
+                value = product(values, right[:, at])
+            made[slot, :, :, at] = value.astype(BF).reshape(2, rows, step)
+            return carry
+
+        lax.fori_loop(0, 4, some, 0)
+
+    return make
+
+
+def reduce_phase(place, sender, make, scratch, between=None, idle=None):
+    made, core_in, y_in, line_in, total, core_sem, y_sem, line_sem = scratch
     rows = total.shape[0]
     z, y, core = place.z, place.y, place.core
     low = z < LINE // 2
-    order = []
-    for k in range(LINE - 1):
+
+    def turn_of(k):
         down = LINE - 1 - k
         down = jnp.where(down <= z, down - 1, down)
         up = jnp.where(k >= z, k + 1, k)
-        order.append(jnp.where(low, down, up))
-    order.append(z)
-
-    def fetch(slot):
-        half = lax.rem(slot, 2)
-        return pltpu.make_async_copy(
-            partial.at[place.rows(slot // 2, half, core, rows)], mine.at[slot], local_sem.at[slot]
-        )
+        return jnp.where(k == LINE - 1, z, jnp.where(low, down, up))
+
+    order = [turn_of(jnp.int32(k)) for k in range(LINE)]
 
     def to_core(slot):
-        half = lax.rem(slot, 2)
         return remote(
-            partial.at[place.rows(slot // 2, half, 1 - core, rows)],
+            made.at[slot, 1 - core],
             core_in.at[slot],
             core_sem.at[0, slot],
             core_sem.at[1, slot],
@@ -216,7 +229,7 @@
 
     def to_y(block):
         return remote(
-            mine.at[2 * block + 1 - y],
+            made.at[2 * block + 1 - y, core],
             y_in.at[block],
             y_sem.at[0, block],
             y_sem.at[1, block],
@@ -227,7 +240,7 @@
         step = jnp.where(block > z, 1, -1)
         slot = jnp.where((step < 0) & (block == z - 1), LINE, block)
         return remote(
-            mine.at[2 * block + y],
+            made.at[2 * block + y, core],
             line_in.at[slot],
             line_sem.at[0, block],
             line_sem.at[1, slot],
@@ -236,29 +249,46 @@
 
     def from_line(slot):
         return remote(
-            mine.at[0],
+            made.at[0, core],
             line_in.at[slot],
             line_sem.at[0, 0],
             line_sem.at[1, slot],
             place.at(z, y, 1 - core),
         )
 
-    for half in (1 - y, y):
-        for block in order:
-            sender(None, functools.partial(to_core, 2 * block + half))
-            fetch(2 * block + half).start()
-
-    for block in order:
+    def produce(slot):
+        make(slot, made)
+        to_core(slot).start()
+
+    def pass_y(block):
         slot = 2 * block + 1 - y
-        fetch(slot).wait()
         to_core(slot).wait_recv()
 
-        def add(at, slot=slot):
-            value = mine[slot, at].astype(F32) + core_in[slot, at].astype(F32)
-            mine[slot, at] = value.astype(BF)
+        def add(at):
+            value = made[slot, core, at].astype(F32) + core_in[slot, at].astype(F32)
+            made[slot, core, at] = value.astype(BF)
 
         by_rows(rows, add)
-        sender(None, functools.partial(to_y, block))
+        to_y(block).start()
+
+    def first_half(k, carry):
+        produce(2 * turn_of(k) + 1 - y)
+
+        @pl.when(k > 0)
+        def _():
+            pass_y(turn_of(k - 1))
+
+        return carry
+
+    def second_half(k, carry):
+        produce(2 * turn_of(k) + y)
+        return carry
+
+    lax.fori_loop(0, LINE, first_half, 0)
+    pass_y(order[LINE - 1])
+    lax.fori_loop(0, LINE, second_half, 0)
+    sender.sent += [(None, functools.partial(to_core, slot)) for slot in range(2 * LINE)]
+    sender.sent += [(None, functools.partial(to_y, block)) for block in range(LINE)]
 
     for number, block in enumerate(order[:-1]):
         if number == LINE - 2 and between is not None:
@@ -266,7 +296,6 @@
         if number < 2 and idle is not None:
             idle(number)
         slot = 2 * block + y
-        fetch(slot).wait()
         to_core(slot).wait_recv()
         to_y(block).wait_recv()
         inner = jnp.where(block > z, z > 0, z < LINE - 1)
@@ -276,29 +305,28 @@
             from_line(block).wait_recv()
 
             def add(at):
-                value = mine[slot, at].astype(F32) + core_in[slot, at].astype(F32)
+                value = made[slot, core, at].astype(F32) + core_in[slot, at].astype(F32)
                 value = value + y_in[block, at].astype(F32)
-                mine[slot, at] = (value + line_in[block, at].astype(F32)).astype(BF)
+                made[slot, core, at] = (value + line_in[block, at].astype(F32)).astype(BF)
 
             by_rows(rows, add)
 
         @pl.when(jnp.logical_not(inner))
         def _(block=block, slot=slot):
             def add(at):
-                value = mine[slot, at].astype(F32) + core_in[slot, at].astype(F32)
-                mine[slot, at] = (value + y_in[block, at].astype(F32)).astype(BF)
+                value = made[slot, core, at].astype(F32) + core_in[slot, at].astype(F32)
+                made[slot, core, at] = (value + y_in[block, at].astype(F32)).astype(BF)
 
             by_rows(rows, add)
 
         sender(None, functools.partial(to_line, block))
 
     slot = 2 * z + y
-    fetch(slot).wait()
     to_core(slot).wait_recv()
     to_y(z).wait_recv()
 
     def start(at):
-        value = mine[slot, at].astype(F32) + core_in[slot, at].astype(F32)
+        value = made[slot, core, at].astype(F32) + core_in[slot, at].astype(F32)
         total[at] = value + y_in[z, at].astype(F32)
 
     by_rows(rows, start)
@@ -577,7 +605,7 @@
             self.copy(index, self.place.side).wait_send()
 
 
-REDUCE = 9
+REDUCE = 8
 GATHER = 5
 PIECES = 8
 
@@ -625,14 +653,14 @@
 
 
 def hidden_kernel(
-    partial, tokens, gain, pair, down, gathered, branch, hidden, pair_all, down_all, *scratch
+    left, right, tokens, gain, pair, down, gathered, branch, hidden, pair_all, down_all, *scratch
 ):
     place = Place()
     sender = Sender()
     greet(place, True)
     halves = Halves(place, (pair, down), (pair_all, down_all), scratch[REDUCE + GATHER :])
     halves.start()
-    reduce_phase(place, sender, partial, scratch[:REDUCE])
+    reduce_phase(place, sender, rows_product(left, right, False), scratch[:REDUCE])
     total, own = scratch[4], scratch[REDUCE]
     rows, width = total.shape
 
@@ -650,11 +678,11 @@
     sender.drain()
 
 
-def turn_kernel(partial, hidden, cotangent, gain, gathered, outputs, gain_grad, *scratch):
+def turn_kernel(left, right, hidden, cotangent, gain, gathered, outputs, gain_grad, *scratch):
     place = Place()
     sender = Sender()
     greet(place)
-    reduce_phase(place, sender, partial, scratch[:REDUCE])
+    reduce_phase(place, sender, rows_product(left, right, False), scratch[:REDUCE])
     total, own = scratch[4], scratch[REDUCE]
     out_own = scratch[REDUCE + GATHER]
     rows, width = total.shape
@@ -769,7 +797,7 @@
 
 
 def branch_kernel(
-    partial,
+    weights,
     branch,
     cotangent,
     gain,
@@ -794,7 +822,8 @@
         scratch[REDUCE + GATHER :],
     )
     grads.start()
-    reduce_phase(place, sender, partial, scratch[:REDUCE], idle=grads.some)
+    make = rows_product(grad_pair, weights, True)
+    reduce_phase(place, sender, make, scratch[:REDUCE], idle=grads.some)
     total, own = scratch[4], scratch[REDUCE]
     rows, width = total.shape
     gain_grad[...] = jnp.zeros_like(gain_grad)
@@ -819,24 +848,32 @@
 
 
 def last_kernel(
-    partial,
+    left,
+    right,
     grad_hidden,
     qkv,
     out,
     small,
     down,
+    pair,
     result,
     qkv_all,
     out_all,
     small_all,
     down_all,
+    pair_rest,
     *scratch,
 ):
     place = Place()
     sender = Sender()
     parts = scratch[REDUCE + 1 :]
     swap_sems, halves_sems, parts = parts[:3], parts[3:4], parts[4:]
-    qkv_own, qkv_other, out_own, out_other, small_own, small_other, fetch_sem, side_sem = parts
+    qkv_own, qkv_other, out_own, out_other, small_own, small_other = parts[:6]
+    fetch_sem, side_sem, rest_sem = parts[6:]
+    rest = pair_rest.shape[1]
+    resting = remote(
+        pair.at[:, pl.ds(rest, rest)], pair_rest, rest_sem.at[0], rest_sem.at[1], place.across()
+    )
     greet_all(place)
     fetches, crossings = [], []
     for index, (grad, own, other) in enumerate(
@@ -868,7 +905,7 @@
     pairs = ((small_own, small_all), (qkv_own, qkv_all), (out_own, out_all))
     swap = Swap(place, [whole_pair(*pair) for pair in pairs], swap_sems)
     halves = Halves(place, (down,), (down_all,), halves_sems)
-    shared_rows = 2 * partial.shape[1] // place.count // 128
+    shared_rows = 2 * right.shape[0] // place.count // 128
 
     def between():
         for fetch in fetches:
@@ -890,8 +927,9 @@
         lax.fori_loop(0, place.count, one, 0)
         swap.start()
         halves.start()
-
-    reduce_phase(place, sender, partial, scratch[:REDUCE], between)
+        resting.start()
+
+    reduce_phase(place, sender, rows_product(left, right, True), scratch[:REDUCE], between)
     total = scratch[4]
 
     def body(at):
@@ -902,6 +940,7 @@
     swap.pass_on()
     finish()
     halves.finish()
+    resting.wait()
     swap.finish()
     sender.drain()
 
@@ -959,11 +998,14 @@
     down_out[0] = down[...]
 
 
-def unpack_kernel(side, own, other, down, gate_out, up_out, down_out):
+def unpack_kernel(side, own, other, rest, down, gate_out, up_out, down_out):
     half, columns = own.shape[2], gate_out.shape[1]
-    for part, start in ((own, side[0]), (other, 1 - side[0])):
+    quarter = half // 2
+    other_start = (1 - side[0]) * half
+    parts = ((own, side[0] * half), (other, other_start), (rest, other_start + quarter))
+    for part, start in parts:
         value = jnp.sum(part[:, 0].astype(F32), axis=0)
-        rows = pl.ds(pl.multiple_of(start * half, half), half)
+        rows = pl.ds(pl.multiple_of(start, quarter), part.shape[2])
         gate_out[rows] = value[:, :columns]
         up_out[rows] = value[:, columns:]
     down_out[...] = jnp.sum(down[:, 0].astype(F32), axis=0)
@@ -978,7 +1020,7 @@
             out_specs=specs[1],
             scratch_shapes=scratch,
             compiler_params=pltpu.CompilerParams(
-                collective_id=which, has_side_effects=True, vmem_limit_bytes=48 << 20
+                collective_id=which, has_side_effects=True, vmem_limit_bytes=56 << 20
             ),
             cost_estimate=pl.CostEstimate(
                 flops=0, bytes_accessed=int(microseconds * 3.0e6), transcendentals=0
@@ -1066,28 +1108,28 @@
         )(self.context.reshape(1).astype(jnp.int32), gate, up, down)
         return self.repeat(pair), self.repeat(low)
 
-    def hidden(self, partial, tokens, gain, pair, down):
+    def hidden(self, left, right, tokens, gain, pair, down):
         return talk(
             hidden_kernel,
             1,
             (self.all_low, self.own_wide, self.own_wide, self.whole(pair), self.whole(down)),
-            ([HBM, VMEM, VMEM, VMEM, VMEM], (HBM, VMEM, VMEM, HBM, HBM)),
+            ([VMEM] * 6, (HBM, VMEM, VMEM, HBM, HBM)),
             self.reduces + self.gathers + halves_scratch(2),
             100,
-        )(partial, tokens, gain, pair, down)
-
-    def turn(self, partial, hidden, cotangent, gain):
+        )(left, right, tokens, gain, pair, down)
+
+    def turn(self, left, right, hidden, cotangent, gain):
         pair = jax.ShapeDtypeStruct((2 * self.rows, self.width), BF)
         return talk(
             turn_kernel,
             2,
             (self.all_low, pair, self.line_wide),
-            ([HBM, VMEM, VMEM, VMEM], (HBM, HBM, VMEM)),
+            ([VMEM] * 5, (HBM, HBM, VMEM)),
             self.reduces + self.gathers + [pltpu.VMEM((self.rows, self.width), BF)] + pair_scratch(),
             100,
-        )(partial, hidden, cotangent, gain)
-
-    def branch(self, partial, branch, cotangent, gain, inner, grad_mlp, hidden, grad_pair):
+        )(left, right, hidden, cotangent, gain)
+
+    def branch(self, weights, branch, cotangent, gain, inner, grad_mlp, hidden, grad_pair):
         team_rows, units = inner.shape
         columns = grad_pair.shape[1]
         piece = self.width // PIECES
@@ -1113,7 +1155,7 @@
                 jax.ShapeDtypeStruct(down_shape, BF),
             ),
             (
-                [HBM, VMEM, VMEM, VMEM, VMEM, HBM, HBM, VMEM],
+                [VMEM, VMEM, VMEM, VMEM, VMEM, HBM, HBM, VMEM],
                 (HBM, VMEM, VMEM, VMEM, VMEM),
             ),
             self.reduces
@@ -1130,7 +1172,7 @@
                 DMA((2, 2, PIECES)),
             ],
             100,
-        )(partial, branch, cotangent, gain, inner, grad_mlp, hidden, grad_pair)
+        )(weights, branch, cotangent, gain, inner, grad_mlp, hidden, grad_pair)
         down_mine = down_mine.reshape(PIECES, units // 2, count, piece // count)
         return (
             gathered,
@@ -1140,7 +1182,7 @@
             down_mine.transpose(0, 2, 1, 3).reshape(self.fsdp, units // 2, piece // count),
         )
 
-    def last(self, partial, grad_hidden, qkv, out, small, down):
+    def last(self, left, right, grad_hidden, qkv, out, small, down, pair):
         both = jax.ShapeDtypeStruct((2 * self.rows, self.width), F32)
 
         def same(array):
@@ -1153,15 +1195,23 @@
         return talk(
             last_kernel,
             4,
-            (both, same(qkv), same(out), self.whole(small), self.whole(down)),
-            ([HBM, VMEM, HBM, HBM, VMEM, VMEM], (HBM,) * 5),
+            (
+                both,
+                same(qkv),
+                same(out),
+                self.whole(small),
+                self.whole(down),
+                jax.ShapeDtypeStruct((pair.shape[0], pair.shape[1] // 2, pair.shape[2]), BF),
+            ),
+            ([VMEM, VMEM, VMEM, HBM, HBM, VMEM, VMEM, HBM], (HBM,) * 6),
             self.reduces
             + pair_scratch()
             + swap_scratch(self.fsdp, 3)
             + halves_scratch(1)
-            + [half(qkv), half(qkv), half(out), half(out), held, held, DMA((2,)), DMA((2, 3))],
+            + [half(qkv), half(qkv), half(out), half(out), held, held]
+            + [DMA((2,)), DMA((2, 3)), DMA((2,))],
             80,
-        )(partial, grad_hidden, qkv, out, small, down)
+        )(left, right, grad_hidden, qkv, out, small, down, pair)
 
     def total(self, values, moved=None):
         flat = values.reshape(-1, 128)
@@ -1193,7 +1243,7 @@
     def repeat(self, pieces):
         return jnp.concatenate([pieces] * self.teams, axis=0) if self.teams > 1 else pieces
 
-    def unpack(self, own, other, down):
+    def unpack(self, own, other, rest, down):
         half, columns = own.shape[1], own.shape[2] // 2
         rows, down_columns = 2 * down.shape[2], down.shape[3]
 
@@ -1210,7 +1260,9 @@
             grid_spec=pltpu.PrefetchScalarGridSpec(
                 num_scalar_prefetch=1,
                 grid=(self.size,),
-                in_specs=[piece_spec(half, 2 * columns)] * 2 + [piece_spec(rows, down_columns)],
+                in_specs=[piece_spec(half, 2 * columns)]
+                + [piece_spec(half // 2, 2 * columns)] * 2
+                + [piece_spec(rows, down_columns)],
                 out_specs=[wide, wide, pl.BlockSpec((rows, down_columns), lambda d, side: (d, 0))],
             ),
             out_shape=[
@@ -1222,7 +1274,8 @@
         )(
             self.context.reshape(1).astype(jnp.int32),
             cut(own, half, 2 * columns),
-            cut(other, half, 2 * columns),
+            cut(other, half // 2, 2 * columns),
+            cut(rest, half // 2, 2 * columns),
             cut(down, rows, down_columns),
         )
 
@@ -1369,7 +1422,7 @@
     mixed = jnp.einsum("ghqk,gkhd->gqhd", probs_low, values_all, preferred_element_type=F32)
     attended_low = mixed.reshape(team_rows, heads * head_size).astype(BF)
     hidden_all, attn_sum, hidden, pair_came, down_came = team.hidden(
-        product(attended_low, output_w).astype(BF), tokens_own, gain_attn, pair_came, down_came
+        attended_low, output_w, tokens_own, gain_attn, pair_came, down_came
     )
     pair_w = team.columns_whole(pair_came)
     down_w = team.rows_whole(down_came)
@@ -1378,14 +1431,14 @@
     sigma = jax.nn.sigmoid(gate)
     inner_low = (gate * sigma * upward).astype(BF)
     grad_mlp_all, outputs, grad_mlp_gain = team.turn(
-        product(inner_low, down_w).astype(BF), hidden, grad_out, gain_mlp
+        inner_low, down_w, hidden, grad_out, gain_mlp
     )
     grad_inner = product_right(grad_mlp_all, down_w)
     grad_gate_low = (grad_inner * upward * sigma * (1.0 + gate * (1.0 - sigma))).astype(BF)
     grad_up_low = (grad_inner * gate * sigma).astype(BF)
     grad_pair = jnp.concatenate([grad_gate_low, grad_up_low], axis=1)
     grad_branch_all, grad_hidden, grad_attn_gain, pair_mine, down_mine = team.branch(
-        product_right(grad_pair, pair_w).astype(BF),
+        pair_w,
         attn_sum,
         grad_out,
         gain_attn,
@@ -1425,7 +1478,9 @@
         ]
     )
     inner_sums, pair_came = lax.optimization_barrier((inner_sums, pair_came))
-    pair_other = lax.ppermute(pair_came, "context", [(0, 1), (1, 0)])
+    pair_other = lax.ppermute(
+        pair_came[:, : pair_came.shape[1] // 2], "context", [(0, 1), (1, 0)]
+    )
     totals = team.total(inner_sums)
     down_mine, totals = lax.optimization_barrier((down_mine, totals))
     down_came = team.swap(down_mine)
@@ -1446,19 +1501,21 @@
     ]
     used = 2 * share + 2 * heads * head_share
     small = jnp.concatenate(small + [jnp.zeros((fsdp, 8 * 128 - used), F32)], axis=1)
-    partial, pair_other = lax.optimization_barrier(
-        (product_right(grad_qkv, qkv_w).astype(BF), pair_other)
-    )
-    input_grad, qkv_came, output_came, small_came, down_came = team.last(
-        partial,
+    grad_qkv, pair_other = lax.optimization_barrier((grad_qkv, pair_other))
+    input_grad, qkv_came, output_came, small_came, down_came, pair_rest = team.last(
+        grad_qkv,
+        qkv_w,
         grad_hidden,
         qkv_grad,
         output_grad,
         small.reshape(fsdp, 8, 128),
         down_came,
+        pair_came,
     )
     grad_w_query, grad_w_key, grad_w_value = team.columns_out(qkv_came, 3)
-    grad_w_gate, grad_w_up, grad_w_down = team.unpack(pair_came, pair_other, down_came)
+    grad_w_gate, grad_w_up, grad_w_down = team.unpack(
+        pair_came, pair_other, pair_rest, down_came
+    )
     grad_w_output = team.rows_out(output_came)
     came = jnp.sum(small_came, axis=1).reshape(fsdp, -1)
     row_gains = jnp.sum(came[:, : 2 * share], axis=0).reshape(2, share)

time: 800 us -> 818 us (1.022)
  Pallas kernels: 527 us -> 580 us
  matrix products: 106 us -> 68.8 us
    pallas_call x7, Pallas kernels: 512 us -> 565 us  [call(): pl.pallas_call(kernel, out_shape=shapes, in_specs=specs[0], out_specs=spe...]
    dot_general x4 -> x2, matrix products: 35.2 us -> 16.8 us  [product_right(): return jnp.einsum('rf,df->rd', left, right, preferred_element_type=F32)]
    ppermute x1, waiting for transfers between devices: 19.9 us -> 3.36 us  [local(): lax.ppermute(pair_came[:, :pair_came.shape[1] // 2], 'context', [(0, 1),...]
    dot_general x4 -> x2, matrix products: 35.9 us -> 19.8 us  [product(): return jnp.dot(left, right, preferred_element_type=F32)]
    all_to_all x4, waiting for transfers between devices: 5.33 us -> 14.2 us  [swap(): lax.all_to_all(pieces, 'fsdp', split_axis=0, concat_axis=0, tiled=True)]
    unnamed x86 -> x84, local copies, waits for them, and re-layouts: 16.5 us -> 14.6 us
  transfers between devices with their start and end apart: 8 -> 8, of which waited for: 3 -> 3; matrix products, arithmetic and copies ran while one was open for 14% -> 12% of each run, Pallas kernels for 2% -> 2%
where the time goes in v6:
time: 818 us; the launch traced here: 808 us
  Pallas kernels  580 us (71%)
  matrix products  68.8 us (8%)
  other arithmetic  57.4 us (7%)
  starting transfers between devices  43.4 us (5%)
  local copies, waits for them, and re-layouts  38.9 us (5%)
  waiting for transfers between devices  17.5 us (2%)
    pallas_call x7, Pallas kernels, call(): pl.pallas_call(kernel, out_shape=shapes, in_specs=specs[0], out_specs=spe...  565 us
    all_to_all x4, starting transfers between devices, swap(): lax.all_to_all(pieces, 'fsdp', split_axis=0, concat_axis=0, tiled=True)  35.2 us
    dot_general x2, matrix products, product(): return jnp.dot(left, right, preferred_element_type=F32)  19.8 us
    dot_general x2, matrix products, product_right(): return jnp.einsum('rf,df->rd', left, right, preferred_element_type=F32)  16.8 us
  transfers between devices with their start and end apart: 8, of which 3 were waited for; matrix products, arithmetic and copies ran while one was open for 12% of the time, Pallas kernels for 2%

profile of v6, /device:TPU:16, one launch (start us, length us, event | category | flops | bytes accessed | tf_op | source)
XLA Modules:
  0.0 808.0 jit_solution(16098524106199473124)
XLA Ops:
  5.8 6.2 pack_kernel.1
  11.9 67.6 %first_kernel.1 = (bf16[2048,2048]{1,0:T(8,128)(2,1)}, bf16[8,2,128,384]{3,2,1,0:T(8,128)(2,1)}, bf16[8,2,64,256]{3,2,1,0:T(8,128)(2,1)}, f32[8,2,8,128]{3,2,1,0:T(8,128)}) custom-call(bf16[128,2048]{1,0:T(8,128)(2,1)} %constant_dynamic-slice_fusion.3.own_ref.tokens, bf16[256,1024]{1,0:T(8,128)(2,1)} %query.1, bf16[256,1024]{1,0:T(8,128)(2,1)} %key.1, ...), custom_call_target="tpu_custom_call" | custom-call | bytes 240000000 | tf_op jit(solution)/shard_map/first_kernel/pallas_call | solution.py:1016
  79.6 17.3 %all-to-all-start.1 = ((bf16[8,256,256]{2,1,0:T(8,128)(2,1)}), bf16[8,256,256]{2,1,0:T(8,128)(2,1)S(1)}, u32[]{:S(2)}, u32[]{:S(2)}) async-start(bf16[8,256,256]{2,1,0:T(8,128)(2,1)} %get-tuple-element.62), calls=%async_computation.1 | async-start | bytes 2097152 | tf_op jit(solution)/shard_map/all_to_all | solution.py:1241
  96.9 7.4 fusion.55
  104.9 1.0 copy-done.3
  108.1 16.8 %sum_kernel.2 = (f32[32,128]{1,0:T(8,128)}, bf16[2048,128]{1,0:T(8,128)(2,1)}) custom-call(f32[32,128]{1,0:T(8,128)} %reshape.507.value, bf16[2048,128]{1,0:T(8,128)(2,1)} %split.54.rest_0_), custom_call_target="tpu_custom_call" | custom-call | bytes 30000000 | tf_op jit(solution)/shard_map/sum_kernel/pallas_call | solution.py:1016
  125.9 1.9 multiply_multiply_fusion
  128.8 6.6 all-to-all-start
  135.4 1.3 fusion.35
  137.1 5.1 fusion.15
  142.1 2.6 collective-permute-start
  144.9 1.7 fusion.11
  146.5 2.0 copy.92
  148.6 1.0 copy.93
  150.2 1.3 copy.99
  153.1 1.9 constant_dynamic-slice_fusion.1.cotangent
  155.0 5.9 fusion.13
  160.9 5.4 fusion.54
  166.3 3.1 fusion.9
  170.4 9.6 %all-to-all-done.pair = bf16[8,128,1024]{2,1,0:T(8,128)(2,1)} async-done(((bf16[8,128,1024]{2,1,0:T(8,128)(2,1)}), bf16[8,128,1024]{2,1,0:T(8,128)(2,1)}, u32[]{:S(2)}, u32[]{:S(2)}) %all-to-all-start) | async-done | bytes 2097184 | tf_op jit(solution)/shard_map/all_to_all | solution.py:1241
  180.0 112.0 %hidden_kernel.1 = (bf16[2048,2048]{1,0:T(8,128)(2,1)}, f32[128,2048]{1,0:T(8,128)}, f32[128,2048]{1,0:T(8,128)}, bf16[8,2,128,1024]{3,2,1,0:T(8,128)(2,1)}, bf16[8,2,256,256]{3,2,1,0:T(8,128)(2,1)}) custom-call(bf16[2048,128]{1,0:T(8,128)(2,1)} %bitcast.208, bf16[128,2048]{1,0:T(8,128)(2,1)} %bitcast.215, ...), custom_call_target="tpu_custom_call" | custom-call | bytes 300000000 | tf_op jit(solution)/shard_map/hidden_kernel/pallas_call | solution.py:1016
  292.1 12.5 %fusion.56 = f32[2048,1024]{1,0:T(8,128)S(1)} fusion(bf16[2048,2048]{1,0:T(8,128)(2,1)} %get-tuple-element.63.hidden_low, bf16[2048,1024]{1,0:T(8,128)(2,1)} %bitcast.211), kind=kOutput, calls=%fused_computation.147 | convolution fusion | flops 8589934592 | bytes 20971520 | tf_op jit(solution)/shard_map/dot_general | solution.py:18
  304.6 2.8 multiply_convert_fusion.3.left.inner_low
  307.4 1.3 copy-done.12
  308.7 1.2 copy.102
  309.9 2.0 copy.130
  311.9 110.5 %turn_kernel.1 = (bf16[2048,2048]{1,0:T(8,128)(2,1)}, bf16[256,2048]{1,0:T(8,128)(2,1)}, f32[1,2048]{1,0:T(1,128)}) custom-call(bf16[2048,512]{1,0:T(8,128)(2,1)} %multiply_convert_fusion.3.left.inner_low, bf16[512,2048]{1,0:T(8,128)(2,1)} %bitcast.205, f32[128,2048]{1,0:T(8,128)} %get-tuple-element.66.hidden, ...), custom_call_target="tpu_custom_call" | custom-call | bytes 300000000 | tf_op jit(solution)/shard_map/turn_kernel/pallas_call | solution.py:1016
  422.5 10.9 %multiply_convert_fusion.2 = (bf16[2048,512]{1,0:T(8,128)(2,1)S(1)}, bf16[2048,512]{1,0:T(8,128)(2,1)S(1)}) fusion(f32[2048,1024]{1,0:T(8,128)} %copy-done.12, bf16[2048,2048]{1,0:T(8,128)(2,1)} %get-tuple-element.69.grad_mlp, bf16[512,2048]{1,0:T(8,128)(2,1)S(1)} %bitcast.206), kind=kOutput, calls=%fused_computation.5 | convolution fusion | flops 4308598784 | bytes 23068672 | tf_op jit(solution)/shard_map/rf,df->rd/dot_general | solution.py:26
  433.4 2.5 pad_maximum_fusion.grad_pair
  435.9 127.7 %branch_kernel.1 = (bf16[2048,2048]{1,0:T(8,128)(2,1)}, f32[128,2048]{1,0:T(8,128)}, f32[1,2048]{1,0:T(1,128)}, bf16[8,1,128,1024]{3,2,1,0:T(8,128)(2,1)}, bf16[8,256,256]{2,1,0:T(8,128)(2,1)}) custom-call(bf16[2048,1024]{1,0:T(8,128)(2,1)} %bitcast.212, f32[128,2048]{1,0:T(8,128)} %get-tuple-element.68.branch, ...), custom_call_target="tpu_custom_call" | custom-call | bytes 300000000 | tf_op jit(solution)/shard_map/branch_kernel/pallas_call | solution.py:1016
  563.7 5.9 convolution_convert_fusion.2
  569.6 2.5 multiply_reduce_fusion
  572.0 5.8 all-to-all-start.2
  577.9 3.9 multiply_convert_fusion
  581.8 1.3 copy-done.5
  584.0 1.3 copy-done.7
  586.1 1.3 collective-permute-start.1
  589.3 5.0 convolution_convert_fusion.1
  595.3 1.0 convolution_bitcast_fusion
  597.4 1.3 collective-permute-start.2
  598.7 5.3 fusion.33
  604.4 6.4 maximum_add_fusion
  611.1 5.6 maximum_add_fusion.1
  616.8 1.5 fusion.20
  619.1 2.3 fusion.10
  621.4 2.0 copy.111
  624.2 11.7 %sum_kernel.3 = f32[32,128]{1,0:T(8,128)} custom-call(f32[32,128]{1,0:T(8,128)} %reshape.528.value), custom_call_target="tpu_custom_call" | custom-call | bytes 30000000 | tf_op jit(solution)/shard_map/sum_kernel/pallas_call | solution.py:1016
  636.7 1.1 slice.117
  637.8 3.0 collective-permute-start.3
  640.7 5.5 all-to-all-start.3
  646.3 3.5 fusion.22
  649.9 1.3 pad_maximum_fusion.1.left
  651.2 9.1 %convolution_convert_fusion = bf16[2048,384]{1,0:T(8,128)(2,1)} fusion(bf16[2048,2048]{1,0:T(8,128)(2,1)} %get-tuple-element.55, bf16[2048,128]{1,0:T(8,128)(2,1)S(1)} %bitcast.223, bf16[2048,128]{1,0:T(8,128)(2,1)S(1)} %get-tuple-element.102, bf16[2048,128]{1,0:T(8,128)(2,1)S(1)} %get-tuple-element.101), kind=kOutput, calls=%fused_computation.10 | convolution fusion | flops 3226730496 | bytes 11534336 | tf_op jit(solution)/shard_map/rd,rf->df/dot_general | solution.py:22
  660.3 3.4 collective-permute-done.3
  663.7 4.6 all-to-all-done.3.down
  668.2 118.6 %last_kernel.1 = (f32[256,2048]{1,0:T(8,128)}, bf16[8,2,128,384]{3,2,1,0:T(8,128)(2,1)}, bf16[8,2,64,256]{3,2,1,0:T(8,128)(2,1)}, f32[8,2,8,128]{3,2,1,0:T(8,128...) custom-call(bf16[2048,384]{1,0:T(8,128)(2,1)} %pad_maximum_fusion.1.left, bf16[2048,384]{1,0:T(8,128)(2,1)} %bitcast.225, ...), custom_call_target="tpu_custom_call" | custom-call | bytes 240000000 | tf_op jit(solution)/shard_map/last_kernel/pallas_call | solution.py:1016
  787.8 1.5 fusion.48
  789.3 1.1 copy_bitcast_fusion
  790.5 1.1 copy_bitcast_fusion.1
  791.6 1.1 copy_bitcast_fusion.2
  792.7 1.1 bitcast_convert_fusion
  795.1 9.1 %unpack_kernel.1 = (f32[256,4096]{1,0:T(8,128)}, f32[256,4096]{1,0:T(8,128)}, f32[4096,256]{1,0:T(8,128)}) custom-call(s32[1]{0:T(128)} %bitcast.side, bf16[1,8,128,1024]{3,2,1,0:T(8,128)(2,1)} %bitcast.200, bf16[1,8,64,1024]{3,2,1,0:T(8,128)(2,1)} %bitcast.59.other, bf16[1,8,64,1024]{3,2,1,0:T(8,128)(2,1)} %bitcast.227, bf16[1,8,512,256]{3,2,1,0:T(8,128)(2,1)} %bitcast.213), custom_call_target="tpu_custom_call" | custom-call | tf_op jit(solution)/shard_map/unpack_kernel/pallas_call | solution.py:1258
  804.1 2.3 copy.157
  806.4 1.3 copy.158
  (145 shorter events, 24.2 us)
Async XLA Ops:
  0.6 4.3 copy-start
  79.6 48.2 %all-to-all-start.1 = ((bf16[8,256,256]{2,1,0:T(8,128)(2,1)}), bf16[8,256,256]{2,1,0:T(8,128)(2,1)S(1)}, u32[]{:S(2)}, u32[]{:S(2)}) async-start(bf16[8,256,256]{2,1,0:T(8,128)(2,1)} %get-tuple-element.62), calls=%async_computation.1 | async-start | bytes 2097152 | tf_op jit(solution)/shard_map/all_to_all | solution.py:1241
  96.9 10.5 %copy-start.30 = (f32[8,2,8,128]{3,2,1,0:T(8,128)S(1)}, f32[8,2,8,128]{3,2,1,0:T(8,128)}, u32[]{:S(2)}) copy-start(f32[8,2,8,128]{3,2,1,0:T(8,128)} %get-tuple-element.58) | copy-start | bytes 196612
  104.2 1.7 copy-start.3
  127.8 1.0 copy-start.17
  128.8 51.3 %all-to-all-start = ((bf16[8,128,1024]{2,1,0:T(8,128)(2,1)}), bf16[8,128,1024]{2,1,0:T(8,128)(2,1)}, u32[]{:S(2)}, u32[]{:S(2)}) async-start(bf16[8,128,1024]{2,1,0:T(8,128)(2,1)} %get-tuple-element.61), calls=%async_computation | async-start | bytes 4194304 | tf_op jit(solution)/shard_map/all_to_all | solution.py:1241
  142.1 6.5 copy-start.14
  142.1 18.8 %collective-permute-start = (bf16[8,256,1,128]{3,1,0,2:T(8,128)(2,1)}, bf16[8,256,1,128]{3,1,0,2:T(8,128)(2,1)S(1)}, u32[]{:S(2)}, u32[]{:S(2)}) collective-permute-start(bf16[8,256,1,128]{3,1,0,2:T(8,128)(2,1)} %fusion.15), channel_id=1, source_target_pairs={{0,2},{1,3},{4,6},{5,7},{8,10},{9,11},{12,14},{13,15},{16,18},{17,... | collective-permute-start | bytes 1572872 | tf_op jit(solution)/shard_map/ppermute | solution.py:1401
  160.9 5.4 copy-start.18
  160.9 5.4 copy-start.28
  160.9 5.4 copy-start.29
  160.9 5.4 copy-start.25
  304.5 4.2 copy-start.12
  304.6 4.2 copy-start.22
  311.9 110.6 %copy-start.13 = (bf16[64,8,8,256]{3,1,2,0:T(8,128)(2,1)S(1)}, bf16[64,8,8,256]{3,1,2,0:T(8,128)(2,1)}, u32[]{:S(2)}) copy-start(bf16[64,8,8,256]{3,1,2,0:T(8,128)(2,1)} %copy.130) | copy-start | bytes 6291460
  435.9 127.7 %copy-start.20 = (bf16[16,8,8,256]{3,1,2,0:T(8,128)(2,1)S(1)}, bf16[16,8,8,256]{3,1,2,0:T(8,128)(2,1)}, u32[]{:S(2)}) copy-start(bf16[16,8,8,256]{3,1,2,0:T(8,128)(2,1)} %copy.128) | copy-start | bytes 1572868
  563.6 5.9 copy-start.15
  569.5 2.5 copy-start.33
  572.0 51.4 %all-to-all-start.2 = ((bf16[8,128,1024]{2,1,0:T(8,128)(2,1)}), bf16[8,128,1024]{2,1,0:T(8,128)(2,1)S(1)}, u32[]{:S(2)}, u32[]{:S(2)}) async-start(bf16[8,128,1024]{2,1,0:T(8,128)(2,1)} %bitcast.218), calls=%async_computation.2 | async-start | bytes 4194304 | tf_op jit(solution)/shard_map/all_to_all | solution.py:1241
  577.8 5.3 copy-start.19
  581.8 1.3 copy-start.5
  583.1 4.8 copy-start.32
  583.1 5.5 copy-start.31
  584.0 1.3 copy-start.7
  586.1 18.2 %collective-permute-start.1 = (bf16[8,256,1,128]{3,1,0,2:T(8,128)(2,1)}, bf16[8,256,1,128]{3,1,0,2:T(8,128)(2,1)}, u32[]{:S(2)}, u32[]{:S(2)}) collective-permute-start(bf16[8,256,1,128]{3,1,0,2:T(8,128)(2,1)} %slice.174), channel_id=1, source_target_pairs={{2,0},{3,1},{6,4},{7,5},{10,8},{11,9},{14,12},{15,13},{18,16},{19,... | collective-permute-start | bytes 1572872 | tf_op jit(solution)/shard_map/ppermute | solution.py:1465
  589.3 6.0 copy-start.16
  589.3 6.0 copy-start.34
  595.3 3.3 copy-start.6
  595.3 3.3 copy-start.26
  596.4 8.0 copy-start.24
  597.4 21.8 %collective-permute-start.2 = (bf16[8,256,1,128]{1,3,0,2:T(8,128)(2,1)}, bf16[8,256,1,128]{1,3,0,2:T(8,128)(2,1)}, u32[]{:S(2)}, u32[]{:S(2)}) collective-permute-start(bf16[8,256,1,128]{1,3,0,2:T(8,128)(2,1)} %slice.173), channel_id=1, source_target_pairs={{2,0},{3,1},{6,4},{7,5},{10,8},{11,9},{14,12},{15,13},{18,16},{19,... | collective-permute-start | bytes 1572872 | tf_op jit(solution)/shard_map/ppermute | solution.py:1464
  598.7 5.7 copy-start.8
  610.7 6.0 copy-start.9
  610.8 6.0 copy-start.4
  616.7 1.5 copy-start.11
  618.3 28.0 %copy-start.10 = (f32[8,256,1,128]{3,1,0,2:T(8,128)S(1)}, f32[8,256,1,128]{3,1,0,2:T(8,128)}, u32[]{:S(2)}) copy-start(f32[8,256,1,128]{3,1,0,2:T(8,128)} %copy-done.9) | copy-start | bytes 3145732
  623.5 26.4 %copy-start.2 = (bf16[8,128,1024]{2,1,0:T(8,128)(2,1)}, bf16[8,128,1024]{2,1,0:T(8,128)(2,1)S(1)}, u32[]{:S(2)}) copy-start(bf16[8,128,1024]{2,1,0:T(8,128)(2,1)S(1)} %all-to-all-done.2.pair) | copy-start | bytes 6291460
  637.8 25.9 %collective-permute-start.3 = (bf16[8,64,1024]{2,1,0:T(8,128)(2,1)}, bf16[8,64,1024]{2,1,0:T(8,128)(2,1)}, u32[]{:S(2)}, u32[]{:S(2)}) collective-permute-start(bf16[8,64,1024]{2,1,0:T(8,128)(2,1)} %slice.117), channel_id=1, source_target_pairs={{0,2},{2,0},{1,3},{3,1},{4,6},{6,4},{5,7},{7,5},{8,10},{10,8},{9,1... | collective-permute-start | bytes 3145736 | tf_op jit(solution)/shard_map/ppermute | solution.py:1481
  640.7 27.5 %all-to-all-start.3 = ((bf16[8,256,256]{2,1,0:T(8,128)(2,1)}), bf16[8,256,256]{2,1,0:T(8,128)(2,1)}, u32[]{:S(2)}, u32[]{:S(2)}) async-start(bf16[8,256,256]{2,1,0:T(8,128)(2,1)} %get-tuple-element.80), calls=%async_computation.3 | async-start | bytes 2097152 | tf_op jit(solution)/shard_map/all_to_all | solution.py:1241
  646.3 3.6 copy-start.23
  786.9 5.9 copy-start.27
  795.1 11.4 %copy-start.21 = (f32[256,2048]{1,0:T(8,128)S(1)}, f32[256,2048]{1,0:T(8,128)}, u32[]{:S(2)}) copy-start(f32[256,2048]{1,0:T(8,128)} %get-tuple-element.154) | copy-start | bytes 6291460
  795.1 12.7 %copy-start.1 = (bf16[256,2048]{1,0:T(8,128)(2,1)S(1)}, bf16[256,2048]{1,0:T(8,128)(2,1)}, u32[]{:S(2)}) copy-start(bf16[256,2048]{1,0:T(8,128)(2,1)} %param.14) | copy-start | bytes 3145732

commit v7 on v6

--- a/solution.py
+++ b/solution.py
@@ -184,7 +184,7 @@
     ]
 
 
-def rows_product(left, right, turned):
+def rows_product(left, right):
     def make(slot, made):
         rows, width = made.shape[2:]
         values = left[pl.ds(pl.multiple_of(slot * 2 * rows, 2 * rows), 2 * rows)]
@@ -192,16 +192,21 @@
 
         def some(index, carry):
             at = pl.ds(pl.multiple_of(index * step, step), step)
-            if turned:
-                value = product_right(values, right[at])
-            else:
-                value = product(values, right[:, at])
+            value = product(values, right[:, at])
             made[slot, :, :, at] = value.astype(BF).reshape(2, rows, step)
             return carry
 
         lax.fori_loop(0, 4, some, 0)
 
     return make
+
+
+def rows_fetch(partial, made, sem):
+    def fetch(slot):
+        return pltpu.make_async_copy(partial.at[slot], made.at[slot], sem.at[slot])
+
+    lax.fori_loop(0, 2 * LINE, lambda slot, carry: (fetch(slot).start(), carry)[1], 0)
+    return lambda slot, made: fetch(slot).wait()
 
 
 def reduce_phase(place, sender, make, scratch, between=None, idle=None):
@@ -660,7 +665,7 @@
     greet(place, True)
     halves = Halves(place, (pair, down), (pair_all, down_all), scratch[REDUCE + GATHER :])
     halves.start()
-    reduce_phase(place, sender, rows_product(left, right, False), scratch[:REDUCE])
+    reduce_phase(place, sender, rows_product(left, right), scratch[:REDUCE])
     total, own = scratch[4], scratch[REDUCE]
     rows, width = total.shape
 
@@ -682,7 +687,7 @@
     place = Place()
     sender = Sender()
     greet(place)
-    reduce_phase(place, sender, rows_product(left, right, False), scratch[:REDUCE])
+    reduce_phase(place, sender, rows_product(left, right), scratch[:REDUCE])
     total, own = scratch[4], scratch[REDUCE]
     out_own = scratch[REDUCE + GATHER]
     rows, width = total.shape
@@ -797,7 +802,7 @@
 
 
 def branch_kernel(
-    weights,
+    partial,
     branch,
     cotangent,
     gain,
@@ -819,10 +824,11 @@
         place,
         (inner_low, grad_mlp, hidden_low, grad_pair),
         (pair_mine, down_mine),
-        scratch[REDUCE + GATHER :],
-    )
+        scratch[REDUCE + GATHER : -1],
+    )
+    rows_sem = scratch[-1]
     grads.start()
-    make = rows_product(grad_pair, weights, True)
+    make = rows_fetch(partial, scratch[0], rows_sem)
     reduce_phase(place, sender, make, scratch[:REDUCE], idle=grads.some)
     total, own = scratch[4], scratch[REDUCE]
     rows, width = total.shape
@@ -848,8 +854,7 @@
 
 
 def last_kernel(
-    left,
-    right,
+    partial,
     grad_hidden,
     qkv,
     out,
@@ -869,7 +874,7 @@
     parts = scratch[REDUCE + 1 :]
     swap_sems, halves_sems, parts = parts[:3], parts[3:4], parts[4:]
     qkv_own, qkv_other, out_own, out_other, small_own, small_other = parts[:6]
-    fetch_sem, side_sem, rest_sem = parts[6:]
+    fetch_sem, side_sem, rest_sem, rows_sem = parts[6:]
     rest = pair_rest.shape[1]
     resting = remote(
         pair.at[:, pl.ds(rest, rest)], pair_rest, rest_sem.at[0], rest_sem.at[1], place.across()
@@ -905,7 +910,7 @@
     pairs = ((small_own, small_all), (qkv_own, qkv_all), (out_own, out_all))
     swap = Swap(place, [whole_pair(*pair) for pair in pairs], swap_sems)
     halves = Halves(place, (down,), (down_all,), halves_sems)
-    shared_rows = 2 * right.shape[0] // place.count // 128
+    shared_rows = 2 * partial.shape[3] // place.count // 128
 
     def between():
         for fetch in fetches:
@@ -929,7 +934,8 @@
         halves.start()
         resting.start()
 
-    reduce_phase(place, sender, rows_product(left, right, True), scratch[:REDUCE], between)
+    make = rows_fetch(partial, scratch[0], rows_sem)
+    reduce_phase(place, sender, make, scratch[:REDUCE], between)
     total = scratch[4]
 
     def body(at):
@@ -1076,6 +1082,9 @@
             80,
         )(own, *weights, out, small)
 
+    def cut(self, partial):
+        return partial.reshape(self.size, 2, self.rows, self.width)
+
     def pack(self, gate, up, down):
         rows, columns = gate.shape
         rows, columns = rows // 2, columns // self.size
@@ -1129,7 +1138,7 @@
             100,
         )(left, right, hidden, cotangent, gain)
 
-    def branch(self, weights, branch, cotangent, gain, inner, grad_mlp, hidden, grad_pair):
+    def branch(self, partial, branch, cotangent, gain, inner, grad_mlp, hidden, grad_pair):
         team_rows, units = inner.shape
         columns = grad_pair.shape[1]
         piece = self.width // PIECES
@@ -1155,7 +1164,7 @@
                 jax.ShapeDtypeStruct(down_shape, BF),
             ),
             (
-                [VMEM, VMEM, VMEM, VMEM, VMEM, HBM, HBM, VMEM],
+                [HBM, VMEM, VMEM, VMEM, VMEM, HBM, HBM, VMEM],
                 (HBM, VMEM, VMEM, VMEM, VMEM),
             ),
             self.reduces
@@ -1170,9 +1179,10 @@
                 pltpu.VMEM(down_shape, BF),
                 DMA((2, 2)),
                 DMA((2, 2, PIECES)),
+                DMA((2 * LINE,)),
             ],
             100,
-        )(weights, branch, cotangent, gain, inner, grad_mlp, hidden, grad_pair)
+        )(self.cut(partial), branch, cotangent, gain, inner, grad_mlp, hidden, grad_pair)
         down_mine = down_mine.reshape(PIECES, units // 2, count, piece // count)
         return (
             gathered,
@@ -1182,7 +1192,7 @@
             down_mine.transpose(0, 2, 1, 3).reshape(self.fsdp, units // 2, piece // count),
         )
 
-    def last(self, left, right, grad_hidden, qkv, out, small, down, pair):
+    def last(self, partial, grad_hidden, qkv, out, small, down, pair):
         both = jax.ShapeDtypeStruct((2 * self.rows, self.width), F32)
 
         def same(array):
@@ -1203,15 +1213,15 @@
                 self.whole(down),
                 jax.ShapeDtypeStruct((pair.shape[0], pair.shape[1] // 2, pair.shape[2]), BF),
             ),
-            ([VMEM, VMEM, VMEM, HBM, HBM, VMEM, VMEM, HBM], (HBM,) * 6),
+            ([HBM, VMEM, HBM, HBM, VMEM, VMEM, HBM], (HBM,) * 6),
             self.reduces
             + pair_scratch()
             + swap_scratch(self.fsdp, 3)
             + halves_scratch(1)
             + [half(qkv), half(qkv), half(out), half(out), held, held]
-            + [DMA((2,)), DMA((2, 3)), DMA((2,))],
+            + [DMA((2,)), DMA((2, 3)), DMA((2,)), DMA((2 * LINE,))],
             80,
-        )(left, right, grad_hidden, qkv, out, small, down, pair)
+        )(self.cut(partial), grad_hidden, qkv, out, small, down, pair)
 
     def total(self, values, moved=None):
         flat = values.reshape(-1, 128)
@@ -1438,7 +1448,7 @@
     grad_up_low = (grad_inner * gate * sigma).astype(BF)
     grad_pair = jnp.concatenate([grad_gate_low, grad_up_low], axis=1)
     grad_branch_all, grad_hidden, grad_attn_gain, pair_mine, down_mine = team.branch(
-        pair_w,
+        product_right(grad_pair, pair_w).astype(BF),
         attn_sum,
         grad_out,
         gain_attn,
@@ -1501,10 +1511,11 @@
     ]
     used = 2 * share + 2 * heads * head_share
     small = jnp.concatenate(small + [jnp.zeros((fsdp, 8 * 128 - used), F32)], axis=1)
-    grad_qkv, pair_other = lax.optimization_barrier((grad_qkv, pair_other))
+    partial, pair_other = lax.optimization_barrier(
+        (product_right(grad_qkv, qkv_w).astype(BF), pair_other)
+    )
     input_grad, qkv_came, output_came, small_came, down_came, pair_rest = team.last(
-        grad_qkv,
-        qkv_w,
+        partial,
         grad_hidden,
         qkv_grad,
         output_grad,

time: 818 us -> 825 us (level)
  matrix products: 68.8 us -> 84.9 us
  Pallas kernels: 580 us -> 566 us
    dot_general x2 -> x4, matrix products: 16.8 us -> 34.5 us  [product_right(): return jnp.einsum('rf,df->rd', left, right, preferred_element_type=F32)]
    pallas_call x7, Pallas kernels: 565 us -> 551 us  [call(): pl.pallas_call(kernel, out_shape=shapes, in_specs=specs[0], out_specs=spe...]
    unnamed x84 -> x90, local copies, waits for them, and re-layouts: 14.6 us -> 16.8 us
  transfers between devices with their start and end apart: 8 -> 8, of which waited for: 3 -> 3; matrix products, arithmetic and copies ran while one was open for 12% -> 13% of each run, Pallas kernels for 2% -> 2%
where the time goes in v7:
time: 825 us; the launch traced here: 811 us
  Pallas kernels  566 us (69%)
  matrix products  84.9 us (10%)
  other arithmetic  56.8 us (7%)
  starting transfers between devices  45.5 us (6%)
  local copies, waits for them, and re-layouts  41 us (5%)
  waiting for transfers between devices  15 us (2%)
    pallas_call x7, Pallas kernels, call(): pl.pallas_call(kernel, out_shape=shapes, in_specs=specs[0], out_specs=spe...  551 us
    all_to_all x4, starting transfers between devices, swap(): lax.all_to_all(pieces, 'fsdp', split_axis=0, concat_axis=0, tiled=True)  35.9 us
    dot_general x4, matrix products, product_right(): return jnp.einsum('rf,df->rd', left, right, preferred_element_type=F32)  34.5 us
    dot_general x2, matrix products, product(): return jnp.dot(left, right, preferred_element_type=F32)  19.8 us
    unnamed x90, local copies, waits for them, and re-layouts  16.8 us
  transfers between devices with their start and end apart: 8, of which 3 were waited for; matrix products, arithmetic and copies ran while one was open for 13% of the time, Pallas kernels for 2%

profile of v7, /device:TPU:16, one launch (start us, length us, event | category | flops | bytes accessed | tf_op | source)
XLA Modules:
  0.0 811.3 jit_solution(16102136453880200)
XLA Ops:
  5.8 6.2 pack_kernel.1
  11.9 67.6 %first_kernel.1 = (bf16[2048,2048]{1,0:T(8,128)(2,1)}, bf16[8,2,128,384]{3,2,1,0:T(8,128)(2,1)}, bf16[8,2,64,256]{3,2,1,0:T(8,128)(2,1)}, f32[8,2,8,128]{3,2,1,0:T(8,128)}) custom-call(bf16[128,2048]{1,0:T(8,128)(2,1)} %constant_dynamic-slice_fusion.3.own_ref.tokens, bf16[256,1024]{1,0:T(8,128)(2,1)} %query.1, bf16[256,1024]{1,0:T(8,128)(2,1)} %key.1, ...), custom_call_target="tpu_custom_call" | custom-call | bytes 240000000 | tf_op jit(solution)/shard_map/first_kernel/pallas_call | solution.py:1022
  79.6 17.3 %all-to-all-start.1 = ((bf16[8,256,256]{2,1,0:T(8,128)(2,1)}), bf16[8,256,256]{2,1,0:T(8,128)(2,1)S(1)}, u32[]{:S(2)}, u32[]{:S(2)}) async-start(bf16[8,256,256]{2,1,0:T(8,128)(2,1)} %get-tuple-element.62), calls=%async_computation.1 | async-start | bytes 2097152 | tf_op jit(solution)/shard_map/all_to_all | solution.py:1251
  96.9 7.4 fusion.57
  104.9 1.0 copy-done.3
  108.1 16.8 %sum_kernel.2 = (f32[32,128]{1,0:T(8,128)}, bf16[2048,128]{1,0:T(8,128)(2,1)}) custom-call(f32[32,128]{1,0:T(8,128)} %reshape.513.value, bf16[2048,128]{1,0:T(8,128)(2,1)} %split.54.rest_0_), custom_call_target="tpu_custom_call" | custom-call | bytes 30000000 | tf_op jit(solution)/shard_map/sum_kernel/pallas_call | solution.py:1022
  125.9 1.9 multiply_multiply_fusion
  128.8 6.6 all-to-all-start
  135.4 1.3 fusion.35
  137.1 5.0 fusion.15
  142.1 2.6 collective-permute-start
  144.9 1.7 fusion.11
  146.5 2.0 copy.92
  150.2 1.3 copy.99
  153.0 1.9 constant_dynamic-slice_fusion.1.cotangent
  154.9 5.8 fusion.13
  160.8 5.4 fusion.56
  166.2 3.1 fusion.9
  170.3 9.7 %all-to-all-done.pair = bf16[8,128,1024]{2,1,0:T(8,128)(2,1)} async-done(((bf16[8,128,1024]{2,1,0:T(8,128)(2,1)}), bf16[8,128,1024]{2,1,0:T(8,128)(2,1)}, u32[]{:S(2)}, u32[]{:S(2)}) %all-to-all-start) | async-done | bytes 2097184 | tf_op jit(solution)/shard_map/all_to_all | solution.py:1251
  180.0 112.0 %hidden_kernel.1 = (bf16[2048,2048]{1,0:T(8,128)(2,1)}, f32[128,2048]{1,0:T(8,128)}, f32[128,2048]{1,0:T(8,128)}, bf16[8,2,128,1024]{3,2,1,0:T(8,128)(2,1)}, bf16[8,2,256,256]{3,2,1,0:T(8,128)(2,1)}) custom-call(bf16[2048,128]{1,0:T(8,128)(2,1)} %bitcast.214, bf16[128,2048]{1,0:T(8,128)(2,1)} %bitcast.219, ...), custom_call_target="tpu_custom_call" | custom-call | bytes 300000000 | tf_op jit(solution)/shard_map/hidden_kernel/pallas_call | solution.py:1022
  292.0 12.5 %fusion.58 = f32[2048,1024]{1,0:T(8,128)S(1)} fusion(bf16[2048,2048]{1,0:T(8,128)(2,1)} %get-tuple-element.63.hidden_low, bf16[2048,1024]{1,0:T(8,128)(2,1)} %bitcast.257), kind=kOutput, calls=%fused_computation.151 | convolution fusion | flops 8589934592 | bytes 20971520 | tf_op jit(solution)/shard_map/dot_general | solution.py:18
  304.5 2.8 multiply_convert_fusion.3.left.inner_low
  307.4 1.3 copy-done.12
  308.7 1.2 copy.102
  309.9 2.0 copy.130
  311.9 110.2 %turn_kernel.1 = (bf16[2048,2048]{1,0:T(8,128)(2,1)}, bf16[256,2048]{1,0:T(8,128)(2,1)}, f32[1,2048]{1,0:T(1,128)}) custom-call(bf16[2048,512]{1,0:T(8,128)(2,1)} %multiply_convert_fusion.3.left.inner_low, bf16[512,2048]{1,0:T(8,128)(2,1)} %bitcast.211, f32[128,2048]{1,0:T(8,128)} %get-tuple-element.66.hidden, ...), custom_call_target="tpu_custom_call" | custom-call | bytes 300000000 | tf_op jit(solution)/shard_map/turn_kernel/pallas_call | solution.py:1022
  422.2 10.9 %multiply_convert_fusion.2 = (bf16[2048,512]{1,0:T(8,128)(2,1)S(1)}, bf16[2048,512]{1,0:T(8,128)(2,1)S(1)}) fusion(f32[2048,1024]{1,0:T(8,128)} %copy-done.12, bf16[2048,2048]{1,0:T(8,128)(2,1)} %get-tuple-element.68.grad_mlp, bf16[512,2048]{1,0:T(8,128)(2,1)S(1)} %bitcast.212), kind=kOutput, calls=%fused_computation.7 | convolution fusion | flops 4308598784 | bytes 23068672 | tf_op jit(solution)/shard_map/rf,df->rd/dot_general | solution.py:26
  433.0 2.8 pad_maximum_fusion.grad_pair
  436.7 10.9 %convolution_convert_fusion.1 = bf16[2048,2048]{1,0:T(8,128)(2,1)} fusion(bf16[2048,1024]{1,0:T(8,128)(2,1)S(1)} %bitcast.258, bf16[2048,512]{1,0:T(8,128)(2,1)S(1)} %get-tuple-element.100, bf16[2048,512]{1,0:T(8,128)(2,1)S(1)} %get-tuple-element.99), kind=kOutput, calls=%fused_computation.2 | convolution fusion | flops 8602517504 | bytes 16777216 | tf_op jit(solution)/shard_map/rf,df->rd/dot_general | solution.py:26
  447.6 116.2 %branch_kernel.1 = (bf16[2048,2048]{1,0:T(8,128)(2,1)}, f32[128,2048]{1,0:T(8,128)}, f32[1,2048]{1,0:T(1,128)}, bf16[8,1,128,1024]{3,2,1,0:T(8,128)(2,1)}, bf16[8,256,256]{2,1,0:T(8,128)(2,1)}) custom-call(bf16[8,2,128,2048]{3,2,1,0:T(8,128)(2,1)} %bitcast.209, f32[128,2048]{1,0:T(8,128)} %get-tuple-element.69.branch, ...), custom_call_target="tpu_custom_call" | custom-call | bytes 300000000 | tf_op jit(solution)/shard_map/branch_kernel/pallas_call | solution.py:1022
  563.8 5.9 convolution_convert_fusion.4
  569.7 2.5 multiply_reduce_fusion
  572.2 6.7 all-to-all-start.2
  578.9 3.9 multiply_convert_fusion
  582.8 1.3 copy-done.5
  585.0 1.3 copy-done.7
  587.2 1.3 collective-permute-start.1
  590.4 3.2 convolution_bitcast_fusion
  593.6 1.3 copy-done.23
  595.7 1.7 collective-permute-start.2
  597.5 4.7 convolution_convert_fusion.3
  603.2 5.3 fusion.33
  608.9 6.4 maximum_add_fusion
  615.6 5.6 maximum_add_fusion.1
  621.3 1.5 fusion.20
  623.6 2.3 fusion.10
  625.9 2.0 copy.111
  628.7 10.7 %sum_kernel.3 = f32[32,128]{1,0:T(8,128)} custom-call(f32[32,128]{1,0:T(8,128)} %reshape.535.value), custom_call_target="tpu_custom_call" | custom-call | bytes 30000000 | tf_op jit(solution)/shard_map/sum_kernel/pallas_call | solution.py:1022
  640.1 1.1 slice.117
  641.2 4.0 collective-permute-start.3
  645.2 5.3 all-to-all-start.3
  650.5 4.2 fusion.22
  654.8 6.9 convolution_convert_fusion
  661.7 5.6 convolution_convert_fusion.2
  668.2 4.3 all-to-all-done.3.down
  672.5 117.7 %last_kernel.1 = (f32[256,2048]{1,0:T(8,128)}, bf16[8,2,128,384]{3,2,1,0:T(8,128)(2,1)}, bf16[8,2,64,256]{3,2,1,0:T(8,128)(2,1)}, f32[8,2,8,128]{3,2,1,0:T(8,128...) custom-call(bf16[8,2,128,2048]{3,2,1,0:T(8,128)(2,1)} %bitcast.210, ...), custom_call_target="tpu_custom_call" | custom-call | bytes 240000000 | tf_op jit(solution)/shard_map/last_kernel/pallas_call | solution.py:1022
  791.2 1.5 fusion.50
  792.7 1.1 copy_bitcast_fusion
  793.9 1.1 copy_bitcast_fusion.1
  795.0 1.1 copy_bitcast_fusion.2
  796.1 1.1 bitcast_convert_fusion
  798.5 9.1 %unpack_kernel.1 = (f32[256,4096]{1,0:T(8,128)}, f32[256,4096]{1,0:T(8,128)}, f32[4096,256]{1,0:T(8,128)}) custom-call(s32[1]{0:T(128)} %bitcast.side, bf16[1,8,128,1024]{3,2,1,0:T(8,128)(2,1)} %bitcast.204, bf16[1,8,64,1024]{3,2,1,0:T(8,128)(2,1)} %bitcast.61.other, bf16[1,8,64,1024]{3,2,1,0:T(8,128)(2,1)} %bitcast.227, bf16[1,8,512,256]{3,2,1,0:T(8,128)(2,1)} %bitcast.217), custom_call_target="tpu_custom_call" | custom-call | tf_op jit(solution)/shard_map/unpack_kernel/pallas_call | solution.py:1268
  807.5 2.3 copy.157
  809.8 1.3 copy.158
  (153 shorter events, 26.9 us)
Async XLA Ops:
  0.6 4.3 copy-start
  79.6 48.2 %all-to-all-start.1 = ((bf16[8,256,256]{2,1,0:T(8,128)(2,1)}), bf16[8,256,256]{2,1,0:T(8,128)(2,1)S(1)}, u32[]{:S(2)}, u32[]{:S(2)}) async-start(bf16[8,256,256]{2,1,0:T(8,128)(2,1)} %get-tuple-element.62), calls=%async_computation.1 | async-start | bytes 2097152 | tf_op jit(solution)/shard_map/all_to_all | solution.py:1251
  96.9 10.5 %copy-start.30 = (f32[8,2,8,128]{3,2,1,0:T(8,128)S(1)}, f32[8,2,8,128]{3,2,1,0:T(8,128)}, u32[]{:S(2)}) copy-start(f32[8,2,8,128]{3,2,1,0:T(8,128)} %get-tuple-element.58) | copy-start | bytes 196612
  104.2 1.7 copy-start.3
  127.8 1.0 copy-start.17
  128.8 51.3 %all-to-all-start = ((bf16[8,128,1024]{2,1,0:T(8,128)(2,1)}), bf16[8,128,1024]{2,1,0:T(8,128)(2,1)}, u32[]{:S(2)}, u32[]{:S(2)}) async-start(bf16[8,128,1024]{2,1,0:T(8,128)(2,1)} %get-tuple-element.61), calls=%async_computation | async-start | bytes 4194304 | tf_op jit(solution)/shard_map/all_to_all | solution.py:1251
  142.1 6.5 copy-start.15
  142.1 18.7 %collective-permute-start = (bf16[8,256,1,128]{3,1,0,2:T(8,128)(2,1)}, bf16[8,256,1,128]{3,1,0,2:T(8,128)(2,1)S(1)}, u32[]{:S(2)}, u32[]{:S(2)}) collective-permute-start(bf16[8,256,1,128]{3,1,0,2:T(8,128)(2,1)} %fusion.15), channel_id=1, source_target_pairs={{0,2},{1,3},{4,6},{5,7},{8,10},{9,11},{12,14},{13,15},{16,18},{17,... | collective-permute-start | bytes 1572872 | tf_op jit(solution)/shard_map/ppermute | solution.py:1411
  160.8 5.4 copy-start.18
  160.8 5.4 copy-start.27
  160.8 5.4 copy-start.28
  160.8 5.4 copy-start.24
  304.5 4.2 copy-start.12
  304.5 4.2 copy-start.22
  311.9 110.2 %copy-start.13 = (bf16[64,8,8,256]{3,1,2,0:T(8,128)(2,1)S(1)}, bf16[64,8,8,256]{3,1,2,0:T(8,128)(2,1)}, u32[]{:S(2)}) copy-start(bf16[64,8,8,256]{3,1,2,0:T(8,128)(2,1)} %copy.130) | copy-start | bytes 6291460
  433.0 3.6 copy-start.33
  447.6 116.2 %copy-start.20 = (bf16[16,8,8,256]{3,1,2,0:T(8,128)(2,1)S(1)}, bf16[16,8,8,256]{3,1,2,0:T(8,128)(2,1)}, u32[]{:S(2)}) copy-start(bf16[16,8,8,256]{3,1,2,0:T(8,128)(2,1)} %copy.128) | copy-start | bytes 1572868
  563.8 5.9 copy-start.16
  569.7 2.5 copy-start.35
  572.2 55.8 %all-to-all-start.2 = ((bf16[8,128,1024]{2,1,0:T(8,128)(2,1)}), bf16[8,128,1024]{2,1,0:T(8,128)(2,1)S(1)}, u32[]{:S(2)}, u32[]{:S(2)}) async-start(bf16[8,128,1024]{2,1,0:T(8,128)(2,1)} %bitcast.222), calls=%async_computation.2 | async-start | bytes 4194304 | tf_op jit(solution)/shard_map/all_to_all | solution.py:1251
  578.9 5.2 copy-start.19
  582.8 1.3 copy-start.5
  584.2 4.8 copy-start.32
  584.2 5.5 copy-start.31
  585.0 1.3 copy-start.7
  587.2 21.7 %collective-permute-start.1 = (bf16[8,256,1,128]{3,1,0,2:T(8,128)(2,1)}, bf16[8,256,1,128]{3,1,0,2:T(8,128)(2,1)}, u32[]{:S(2)}, u32[]{:S(2)}) collective-permute-start(bf16[8,256,1,128]{3,1,0,2:T(8,128)(2,1)} %slice.174), channel_id=1, source_target_pairs={{2,0},{3,1},{6,4},{7,5},{10,8},{11,9},{14,12},{15,13},{18,16},{19,... | collective-permute-start | bytes 1572872 | tf_op jit(solution)/shard_map/ppermute | solution.py:1475
  590.4 7.1 copy-start.14
  593.5 1.3 copy-start.23
  595.7 7.4 copy-start.6
  595.7 7.4 copy-start.25
  595.7 27.9 %collective-permute-start.2 = (bf16[8,256,1,128]{1,3,0,2:T(8,128)(2,1)}, bf16[8,256,1,128]{1,3,0,2:T(8,128)(2,1)}, u32[]{:S(2)}, u32[]{:S(2)}) collective-permute-start(bf16[8,256,1,128]{1,3,0,2:T(8,128)(2,1)} %slice.173), channel_id=1, source_target_pairs={{2,0},{3,1},{6,4},{7,5},{10,8},{11,9},{14,12},{15,13},{18,16},{19,... | collective-permute-start | bytes 1572872 | tf_op jit(solution)/shard_map/ppermute | solution.py:1474
  603.2 5.7 copy-start.8
  615.2 6.0 copy-start.9
  615.3 6.0 copy-start.4
  621.2 1.5 copy-start.11
  622.8 27.8 %copy-start.10 = (f32[8,256,1,128]{3,1,0,2:T(8,128)S(1)}, f32[8,256,1,128]{3,1,0,2:T(8,128)}, u32[]{:S(2)}) copy-start(f32[8,256,1,128]{3,1,0,2:T(8,128)} %copy-done.9) | copy-start | bytes 3145732
  628.0 26.8 %copy-start.2 = (bf16[8,128,1024]{2,1,0:T(8,128)(2,1)}, bf16[8,128,1024]{2,1,0:T(8,128)(2,1)S(1)}, u32[]{:S(2)}) copy-start(bf16[8,128,1024]{2,1,0:T(8,128)(2,1)S(1)} %all-to-all-done.2.pair) | copy-start | bytes 6291460
  641.2 27.0 %collective-permute-start.3 = (bf16[8,64,1024]{2,1,0:T(8,128)(2,1)}, bf16[8,64,1024]{2,1,0:T(8,128)(2,1)}, u32[]{:S(2)}, u32[]{:S(2)}) collective-permute-start(bf16[8,64,1024]{2,1,0:T(8,128)(2,1)} %slice.117), channel_id=1, source_target_pairs={{0,2},{2,0},{1,3},{3,1},{4,6},{6,4},{5,7},{7,5},{8,10},{10,8},{9,1... | collective-permute-start | bytes 3145736 | tf_op jit(solution)/shard_map/ppermute | solution.py:1491
  645.2 27.3 %all-to-all-start.3 = ((bf16[8,256,256]{2,1,0:T(8,128)(2,1)}), bf16[8,256,256]{2,1,0:T(8,128)(2,1)}, u32[]{:S(2)}, u32[]{:S(2)}) async-start(bf16[8,256,256]{2,1,0:T(8,128)(2,1)} %get-tuple-element.80), calls=%async_computation.3 | async-start | bytes 2097152 | tf_op jit(solution)/shard_map/all_to_all | solution.py:1251
  650.5 4.3 copy-start.29
  650.5 4.3 copy-start.34
  650.5 11.1 %slice-start = ((s8[8388608]{0:T(1024)(128)(4,1)}), s8[4194304]{0:T(1024)(128)(4,1)S(1)}, s32[]{:S(2)}) async-start(s8[8388608]{0:T(1024)(128)(4,1)} %bitcast.255), calls=%async_computation.4 | async-start | bytes 8388608
  654.8 6.9 slice-start.1
  790.2 5.9 copy-start.26
  798.5 11.4 %copy-start.21 = (f32[256,2048]{1,0:T(8,128)S(1)}, f32[256,2048]{1,0:T(8,128)}, u32[]{:S(2)}) copy-start(f32[256,2048]{1,0:T(8,128)} %get-tuple-element.154) | copy-start | bytes 6291460
  798.5 12.7 %copy-start.1 = (bf16[256,2048]{1,0:T(8,128)(2,1)S(1)}, bf16[256,2048]{1,0:T(8,128)(2,1)}, u32[]{:S(2)}) copy-start(bf16[256,2048]{1,0:T(8,128)(2,1)} %param.14) | copy-start | bytes 3145732

commit v8 on v5

--- a/solution.py
+++ b/solution.py
@@ -185,7 +185,7 @@
     ]
 
 
-def reduce_phase(place, sender, partial, scratch, between=None, idle=None):
+def reduce_phase(place, sender, partial, scratch, between=None, idle=None, late=None):
     mine, core_in, y_in, line_in, total, local_sem, core_sem, y_sem, line_sem = scratch
     rows = total.shape[0]
     z, y, core = place.z, place.y, place.core
@@ -292,6 +292,8 @@
 
         sender(None, functools.partial(to_line, block))
 
+    if late is not None:
+        late()
     slot = 2 * z + y
     fetch(slot).wait()
     to_core(slot).wait_recv()
@@ -891,7 +893,7 @@
         swap.start()
         halves.start()
 
-    reduce_phase(place, sender, partial, scratch[:REDUCE], between)
+    reduce_phase(place, sender, partial, scratch[:REDUCE], between, late=swap.pass_on)
     total = scratch[4]
 
     def body(at):
@@ -899,7 +901,6 @@
 
     by_rows(total.shape[0], body)
     finish = pair_phase(place, sender, total, result, scratch[REDUCE : REDUCE + 1])
-    swap.pass_on()
     finish()
     halves.finish()
     swap.finish()
@@ -959,11 +960,14 @@
     down_out[0] = down[...]
 
 
-def unpack_kernel(side, own, other, down, gate_out, up_out, down_out):
+def unpack_kernel(side, own, other, rest, down, gate_out, up_out, down_out):
     half, columns = own.shape[2], gate_out.shape[1]
-    for part, start in ((own, side[0]), (other, 1 - side[0])):
+    first = other.shape[2]
+    other_start = (1 - side[0]) * half
+    parts = ((own, side[0] * half), (other, other_start), (rest, other_start + first))
+    for part, start in parts:
         value = jnp.sum(part[:, 0].astype(F32), axis=0)
-        rows = pl.ds(pl.multiple_of(start * half, half), half)
+        rows = pl.ds(pl.multiple_of(start, first), part.shape[2])
         gate_out[rows] = value[:, :columns]
         up_out[rows] = value[:, columns:]
     down_out[...] = jnp.sum(down[:, 0].astype(F32), axis=0)
@@ -1193,7 +1197,7 @@
     def repeat(self, pieces):
         return jnp.concatenate([pieces] * self.teams, axis=0) if self.teams > 1 else pieces
 
-    def unpack(self, own, other, down):
+    def unpack(self, own, other, rest, down):
         half, columns = own.shape[1], own.shape[2] // 2
         rows, down_columns = 2 * down.shape[2], down.shape[3]
 
@@ -1210,7 +1214,12 @@
             grid_spec=pltpu.PrefetchScalarGridSpec(
                 num_scalar_prefetch=1,
                 grid=(self.size,),
-                in_specs=[piece_spec(half, 2 * columns)] * 2 + [piece_spec(rows, down_columns)],
+                in_specs=[
+                    piece_spec(half, 2 * columns),
+                    piece_spec(other.shape[1], 2 * columns),
+                    piece_spec(rest.shape[1], 2 * columns),
+                    piece_spec(rows, down_columns),
+                ],
                 out_specs=[wide, wide, pl.BlockSpec((rows, down_columns), lambda d, side: (d, 0))],
             ),
             out_shape=[
@@ -1222,7 +1231,8 @@
         )(
             self.context.reshape(1).astype(jnp.int32),
             cut(own, half, 2 * columns),
-            cut(other, half, 2 * columns),
+            cut(other, other.shape[1], 2 * columns),
+            cut(rest, rest.shape[1], 2 * columns),
             cut(down, rows, down_columns),
         )
 
@@ -1425,8 +1435,9 @@
         ]
     )
     inner_sums, pair_came = lax.optimization_barrier((inner_sums, pair_came))
-    pair_other = lax.ppermute(pair_came, "context", [(0, 1), (1, 0)])
-    totals = team.total(inner_sums)
+    first = pair_came.shape[1] // 4
+    pair_rest = lax.ppermute(pair_came[:, first:], "context", [(0, 1), (1, 0)])
+    totals, pair_other = team.total(inner_sums, pair_came[:, :first])
     down_mine, totals = lax.optimization_barrier((down_mine, totals))
     down_came = team.swap(down_mine)
     grad_query_low = norm_back(
@@ -1446,8 +1457,8 @@
     ]
     used = 2 * share + 2 * heads * head_share
     small = jnp.concatenate(small + [jnp.zeros((fsdp, 8 * 128 - used), F32)], axis=1)
-    partial, pair_other = lax.optimization_barrier(
-        (product_right(grad_qkv, qkv_w).astype(BF), pair_other)
+    partial, pair_rest = lax.optimization_barrier(
+        (product_right(grad_qkv, qkv_w).astype(BF), pair_rest)
     )
     input_grad, qkv_came, output_came, small_came, down_came = team.last(
         partial,
@@ -1458,7 +1469,9 @@
         down_came,
     )
     grad_w_query, grad_w_key, grad_w_value = team.columns_out(qkv_came, 3)
-    grad_w_gate, grad_w_up, grad_w_down = team.unpack(pair_came, pair_other, down_came)
+    grad_w_gate, grad_w_up, grad_w_down = team.unpack(
+        pair_came, pair_other, pair_rest, down_came
+    )
     grad_w_output = team.rows_out(output_came)
     came = jnp.sum(small_came, axis=1).reshape(fsdp, -1)
     row_gains = jnp.sum(came[:, : 2 * share], axis=0).reshape(2, share)

time: 800 us -> 797 us (level)
  waiting for transfers between devices: 25.3 us -> 14.2 us
    ppermute x1, waiting for transfers between devices: 19.9 us -> 8.89 us  [local(): pair_rest = lax.ppermute(pair_came[:, first:], 'context', [(0, 1), (1, 0)])]
    unnamed x86 -> x88, local copies, waits for them, and re-layouts: 16.5 us -> 17.2 us
where the time goes in v8:
time: 797 us; the launch traced here: 789 us
  Pallas kernels  531 us (67%)
  matrix products  106 us (13%)
  other arithmetic  56.4 us (7%)
  starting transfers between devices  43.3 us (5%)
  local copies, waits for them, and re-layouts  35.7 us (4%)
  waiting for transfers between devices  14.2 us (2%)
    pallas_call x7, Pallas kernels, call(): pl.pallas_call(kernel, out_shape=shapes, in_specs=specs[0], out_specs=spe...  516 us
    dot_general x4, matrix products, product(): return jnp.dot(left, right, preferred_element_type=F32)  35.9 us
    all_to_all x4, starting transfers between devices, swap(): lax.all_to_all(pieces, 'fsdp', split_axis=0, concat_axis=0, tiled=True)  35.8 us
    dot_general x4, matrix products, product_right(): return jnp.einsum('rf,df->rd', left, right, preferred_element_type=F32)  35.2 us
    unnamed x88, local copies, waits for them, and re-layouts  17.2 us
  transfers between devices with their start and end apart: 8, of which 3 were waited for; matrix products, arithmetic and copies ran while one was open for 14% of the time, Pallas kernels for 2%

profile of v8, /device:TPU:16, one launch (start us, length us, event | category | flops | bytes accessed | tf_op | source)
XLA Modules:
  0.0 788.8 jit_solution(1073384238059934410)
XLA Ops:
  4.5 6.3 pack_kernel.1
  10.8 65.9 %first_kernel.1 = (bf16[2048,2048]{1,0:T(8,128)(2,1)}, bf16[8,2,128,384]{3,2,1,0:T(8,128)(2,1)S(1)}, bf16[8,2,64,256]{3,2,1,0:T(8,128)(2,1)S(1)}, f32[8,2,8,128]{3,2,1,0:T(8,128)S(1)}) custom-call(bf16[128,2048]{1,0:T(8,128)(2,1)S(1)} %constant_dynamic-slice_fusion.3.own_ref.tokens, bf16[256,1024]{1,0:T(8,128)(2,1)S(1)} %copy-done.6, ...), custom_call_target="tpu_custom_call" | custom-call | bytes 240000000 | tf_op jit(solution)/shard_map/first_kernel/pallas_call | solution.py:978
  76.7 1.2 copy-done.13
  77.9 17.3 %all-to-all-start.1 = ((bf16[8,256,256]{2,1,0:T(8,128)(2,1)}), bf16[8,256,256]{2,1,0:T(8,128)(2,1)S(1)}, u32[]{:S(2)}, u32[]{:S(2)}) async-start(bf16[8,256,256]{2,1,0:T(8,128)(2,1)} %get-tuple-element.63), calls=%async_computation.1 | async-start | bytes 2097152 | tf_op jit(solution)/shard_map/all_to_all | solution.py:1195
  95.3 10.0 %fusion.57 = f32[2048,384]{1,0:T(8,128)} fusion(bf16[2048,2048]{1,0:T(8,128)(2,1)} %get-tuple-element.56, bf16[2048,384]{1,0:T(8,128)(2,1)} %bitcast.216), kind=kOutput, calls=%fused_computation.152 | convolution fusion | flops 3221225472 | bytes 13107200 | tf_op jit(solution)/shard_map/dot_general | solution.py:18
  105.3 2.2 multiply_reduce_fusion.2
  107.6 1.3 split.54.rest_0_
  109.4 15.0 %sum_kernel.2 = (f32[32,128]{1,0:T(8,128)S(1)}, bf16[2048,128]{1,0:T(8,128)(2,1)S(1)}) custom-call(f32[32,128]{1,0:T(8,128)S(1)} %reshape.509.value, bf16[2048,128]{1,0:T(8,128)(2,1)S(1)} %split.54.rest_0_), custom_call_target="tpu_custom_call" | custom-call | bytes 30000000 | tf_op jit(solution)/shard_map/sum_kernel/pallas_call | solution.py:978
  124.6 2.7 multiply_multiply_fusion
  128.3 1.7 slice_negate_fusion.2
  129.9 6.6 all-to-all-start
  136.6 1.3 fusion.35
  138.9 6.2 fusion.15
  145.1 3.4 collective-permute-start
  148.7 1.7 fusion.11
  153.7 1.1 constant_dynamic-slice_fusion.1.cotangent
  154.8 6.4 fusion.13
  161.2 5.3 fusion.56
  166.5 4.2 fusion.9
  170.7 1.3 copy.95
  172.0 6.6 convolution_convert_fusion.3.partial
  178.7 2.6 all-to-all-done.pair
  181.2 108.8 %hidden_kernel.1 = (bf16[2048,2048]{1,0:T(8,128)(2,1)}, f32[128,2048]{1,0:T(8,128)S(1)}, f32[128,2048]{1,0:T(8,128)S(1)}, bf16[8,2,128,1024]{3,2,1,0:T(8,128)(2,1)}, bf16[8,2,256,256]{3,2,1,0:T(8,128)(2,1)S(1)}) custom-call(bf16[2048,2048]{1,0:T(8,128)(2,1)} %convolution_convert_fusion.3.partial, ...), custom_call_target="tpu_custom_call" | custom-call | bytes 300000000 | tf_op jit(solution)/shard_map/hidden_kernel/pallas_call | solution.py:978
  290.0 12.5 %fusion.58 = f32[2048,1024]{1,0:T(8,128)S(1)} fusion(bf16[2048,2048]{1,0:T(8,128)(2,1)} %get-tuple-element.64.hidden_low, bf16[2048,1024]{1,0:T(8,128)(2,1)} %bitcast.255), kind=kOutput, calls=%fused_computation.153 | convolution fusion | flops 8589934592 | bytes 20971520 | tf_op jit(solution)/shard_map/dot_general | solution.py:18
  302.5 1.5 multiply_convert_fusion.3.inner_low
  304.0 1.8 copy-done.26
  305.8 1.2 copy.99
  307.7 6.8 convolution_convert_fusion.2.partial
  314.5 104.1 %turn_kernel.1 = (bf16[2048,2048]{1,0:T(8,128)(2,1)}, bf16[256,2048]{1,0:T(8,128)(2,1)S(1)}, f32[1,2048]{1,0:T(1,128)S(1)}) custom-call(bf16[2048,2048]{1,0:T(8,128)(2,1)} %convolution_convert_fusion.2.partial, f32[128,2048]{1,0:T(8,128)S(1)} %get-tuple-element.67.hidden, bf16[128,2048]{1,0:T(8,128)(2,1)S(1)} %constant_dynamic-slice_fusion.1.cotangent, ...), custom_call_target="tpu_custom_call" | custom-call | bytes 300000000 | tf_op jit(solution)/shard_map/turn_kernel/pallas_call | solution.py:978
  418.6 11.2 %multiply_convert_fusion.2 = (bf16[2048,512]{1,0:T(8,128)(2,1)S(1)}, bf16[2048,512]{1,0:T(8,128)(2,1)S(1)}) fusion(f32[2048,1024]{1,0:T(8,128)} %copy-done.26, bf16[2048,2048]{1,0:T(8,128)(2,1)} %get-tuple-element.69.grad_mlp, bf16[512,2048]{1,0:T(8,128)(2,1)S(1)} %bitcast.228), kind=kOutput, calls=%fused_computation.9 | convolution fusion | flops 4308598784 | bytes 23068672 | tf_op jit(solution)/shard_map/rf,df->rd/dot_general | solution.py:26
  429.9 2.8 pad_maximum_fusion.grad_pair
  433.5 10.9 %convolution_convert_fusion.1.partial = bf16[2048,2048]{1,0:T(8,128)(2,1)} fusion(bf16[2048,1024]{1,0:T(8,128)(2,1)S(1)} %bitcast.256, bf16[2048,512]{1,0:T(8,128)(2,1)S(1)} %get-tuple-element.102, bf16[2048,512]{1,0:T(8,128)(2,1)S(1)} %get-tuple-element.101), kind=kOutput, calls=%fused_computation.2 | convolution fusion | flops 8602517504 | bytes 16777216 | tf_op jit(solution)/shard_map/rf,df->rd/dot_general | solution.py:26
  444.4 112.4 %branch_kernel.1 = (bf16[2048,2048]{1,0:T(8,128)(2,1)}, f32[128,2048]{1,0:T(8,128)S(1)}, f32[1,2048]{1,0:T(1,128)S(1)}, bf16[8,1,128,1024]{3,2,1,0:T(8,128)(2,1)}, bf16[8,256,256]{2,1,0:T(8,128)(2,1)}) custom-call(bf16[2048,2048]{1,0:T(8,128)(2,1)} %convolution_convert_fusion.1.partial, f32[128,2048]{1,0:T(8,128)S(1)} %get-tuple-element.70.branch, ...), custom_call_target="tpu_custom_call" | custom-call | bytes 300000000 | tf_op jit(solution)/shard_map/branch_kernel/pallas_call | solution.py:978
  556.9 6.1 convolution_convert_fusion.6
  563.1 2.5 multiply_reduce_fusion
  565.6 5.7 all-to-all-start.2
  571.3 3.9 multiply_convert_fusion
  575.2 1.3 copy-done.17
  577.4 1.4 copy-done.21
  579.7 1.3 collective-permute-start.1
  582.8 3.1 convolution_bitcast_fusion
  586.9 1.8 collective-permute-start.2
  588.7 4.7 convolution_convert_fusion.5
  593.6 5.4 fusion.33
  599.4 4.8 maximum_add_fusion
  604.6 4.1 maximum_add_fusion.1
  608.7 2.9 fusion.20
  611.9 1.5 fusion.10
  614.4 2.8 all-to-all-done.2
  617.2 1.1 slice.116.rest_0_
  618.3 2.7 slice.121
  620.9 16.4 %sum_kernel.3 = (f32[32,128]{1,0:T(8,128)S(1)}, bf16[8,32,1024]{2,1,0:T(8,128)(2,1)S(1)}) custom-call(f32[32,128]{1,0:T(8,128)S(1)} %reshape.530.value, bf16[8,32,1024]{2,1,0:T(8,128)(2,1)S(1)} %slice.116.rest_0_), custom_call_target="tpu_custom_call" | custom-call | bytes 30000000 | tf_op jit(solution)/shard_map/sum_kernel/pallas_call | solution.py:978
  639.2 6.1 all-to-all-start.3
  645.4 3.7 fusion.22
  649.1 6.9 convolution_convert_fusion.partial
  656.0 9.1 %convolution_convert_fusion.4 = bf16[2048,384]{1,0:T(8,128)(2,1)} fusion(bf16[2048,2048]{1,0:T(8,128)(2,1)} %get-tuple-element.56, bf16[2048,128]{1,0:T(8,128)(2,1)S(1)} %bitcast.235, bf16[2048,128]{1,0:T(8,128)(2,1)S(1)} %get-tuple-element.104, bf16[2048,128]{1,0:T(8,128)(2,1)S(1)} %get-tuple-element.103), kind=kOutput, calls=%fused_computation.14 | convolution fusion | flops 3226730496 | bytes 11534336 | tf_op jit(solution)/shard_map/rd,rf->df/dot_general | solution.py:22
  665.1 8.9 %collective-permute-done.3 = bf16[8,96,1024]{2,1,0:T(8,128)(2,1)} collective-permute-done((bf16[8,96,1024]{2,1,0:T(8,128)(2,1)}, bf16[8,96,1024]{2,1,0:T(8,128)(2,1)}, u32[]{:S(2)}, u32[]{:S(2)}) %collective-permute-start.3) | collective-permute-done | bytes 1572896 | tf_op jit(solution)/shard_map/ppermute | solution.py:1439
  674.0 1.2 copy-done.3
  675.2 93.2 %last_kernel.1 = (f32[256,2048]{1,0:T(8,128)}, bf16[8,2,128,384]{3,2,1,0:T(8,128)(2,1)S(1)}, bf16[8,2,64,256]{3,2,1,0:T(8,128)(2,1)S(1)}, f32[8,2,8,128]{3,2,1,0:T(8,128)S(1)}, bf16[8,2,256,256]{3,2,1,0:T(8,128)(2,1)}) custom-call(bf16[2048,2048]{1,0:T(8,128)(2,1)} %convolution_convert_fusion.partial, f32[128,2048]{1,0:T(8,128)S(1)} %copy-done.3, ...), custom_call_target="tpu_custom_call" | custom-call | bytes 240000000 | tf_op jit(solution)/shard_map/last_kernel/pallas_call | solution.py:978
  769.6 1.1 copy_bitcast_fusion
  770.7 1.1 copy_bitcast_fusion.1
  771.9 1.1 copy_bitcast_fusion.2
  775.3 8.8 %unpack_kernel.1 = (f32[256,4096]{1,0:T(8,128)}, f32[256,4096]{1,0:T(8,128)}, f32[4096,256]{1,0:T(8,128)}) custom-call(s32[1]{0:T(128)} %bitcast.side, bf16[1,8,128,1024]{3,2,1,0:T(8,128)(2,1)} %bitcast.58.own, bf16[1,8,32,1024]{3,2,1,0:T(8,128)(2,1)} %bitcast.209, bf16[1,8,96,1024]{3,2,1,0:T(8,128)(2,1)} %bitcast.60.rest, bf16[1,8,512,256]{3,2,1,0:T(8,128)(2,1)} %bitcast.225), custom_call_target="tpu_custom_call" | custom-call | tf_op jit(solution)/shard_map/unpack_kernel/pallas_call | solution.py:1212
  785.1 3.1 copy.155
  (153 shorter events, 24.6 us)
Async XLA Ops:
  0.6 3.8 copy-start
  0.7 10.1 %copy-start.6 = (bf16[256,1024]{1,0:T(8,128)(2,1)S(1)}, bf16[256,1024]{1,0:T(8,128)(2,1)}, u32[]{:S(2)}) copy-start(bf16[256,1024]{1,0:T(8,128)(2,1)} %query.1) | copy-start | bytes 1572868
  0.7 10.1 %copy-start.7 = (bf16[256,1024]{1,0:T(8,128)(2,1)S(1)}, bf16[256,1024]{1,0:T(8,128)(2,1)}, u32[]{:S(2)}) copy-start(bf16[256,1024]{1,0:T(8,128)(2,1)} %key.1) | copy-start | bytes 1572868
  0.7 10.1 %copy-start.8 = (bf16[256,1024]{1,0:T(8,128)(2,1)S(1)}, bf16[256,1024]{1,0:T(8,128)(2,1)}, u32[]{:S(2)}) copy-start(bf16[256,1024]{1,0:T(8,128)(2,1)} %value.1) | copy-start | bytes 1572868
  4.5 6.3 copy-start.9
  76.7 1.2 copy-start.13
  77.9 52.0 %all-to-all-start.1 = ((bf16[8,256,256]{2,1,0:T(8,128)(2,1)}), bf16[8,256,256]{2,1,0:T(8,128)(2,1)S(1)}, u32[]{:S(2)}, u32[]{:S(2)}) async-start(bf16[8,256,256]{2,1,0:T(8,128)(2,1)} %get-tuple-element.63), calls=%async_computation.1 | async-start | bytes 2097152 | tf_op jit(solution)/shard_map/all_to_all | solution.py:1195
  127.3 1.0 copy-start.20
  129.9 51.3 %all-to-all-start = ((bf16[8,128,1024]{2,1,0:T(8,128)(2,1)}), bf16[8,128,1024]{2,1,0:T(8,128)(2,1)}, u32[]{:S(2)}, u32[]{:S(2)}) async-start(bf16[8,128,1024]{2,1,0:T(8,128)(2,1)} %get-tuple-element.62), calls=%async_computation | async-start | bytes 4194304 | tf_op jit(solution)/shard_map/all_to_all | solution.py:1195
  136.6 12.1 %copy-start.19 = (f32[2048,128]{1,0:T(8,128)S(1)}, f32[2048,128]{1,0:T(8,128)}, u32[]{:S(2)}) copy-start(f32[2048,128]{1,0:T(8,128)} %get-tuple-element.106) | copy-start | bytes 3145732
  137.9 1.0 copy-start.15
  145.1 16.1 %collective-permute-start = (bf16[8,256,1,128]{3,1,0,2:T(8,128)(2,1)}, bf16[8,256,1,128]{3,1,0,2:T(8,128)(2,1)}, u32[]{:S(2)}, u32[]{:S(2)}) collective-permute-start(bf16[8,256,1,128]{3,1,0,2:T(8,128)(2,1)} %fusion.15), channel_id=1, source_target_pairs={{0,2},{1,3},{4,6},{5,7},{8,10},{9,11},{12,14},{13,15},{16,18},{17,... | collective-permute-start | bytes 1572872 | tf_op jit(solution)/shard_map/ppermute | solution.py:1358
  161.2 5.3 copy-start.28
  302.5 3.3 copy-start.26
  305.8 1.9 copy-start.25
  418.6 11.3 %copy-start.4 = (bf16[256,2048]{1,0:T(8,128)(2,1)}, bf16[256,2048]{1,0:T(8,128)(2,1)S(1)}, u32[]{:S(2)}) copy-start(bf16[256,2048]{1,0:T(8,128)(2,1)S(1)} %get-tuple-element.155) | copy-start | bytes 3145732
  429.9 3.6 copy-start.35
  444.4 112.5 %copy-start.30 = (bf16[16,8,8,256]{3,1,2,0:T(8,128)(2,1)S(1)}, bf16[16,8,8,256]{3,1,2,0:T(8,128)(2,1)}, u32[]{:S(2)}) copy-start(bf16[16,8,8,256]{3,1,2,0:T(8,128)(2,1)} %copy.125) | copy-start | bytes 1572868
  556.9 6.2 copy-start.2
  556.9 6.2 copy-start.27
  556.9 6.2 copy-start.32
  556.9 6.2 copy-start.33
  563.1 2.5 copy-start.36
  565.6 51.6 %all-to-all-start.2 = ((bf16[8,128,1024]{2,1,0:T(8,128)(2,1)}), bf16[8,128,1024]{2,1,0:T(8,128)(2,1)}, u32[]{:S(2)}, u32[]{:S(2)}) async-start(bf16[8,128,1024]{2,1,0:T(8,128)(2,1)} %bitcast.39), calls=%async_computation.2 | async-start | bytes 4194304 | tf_op jit(solution)/shard_map/all_to_all | solution.py:1195
  571.3 5.2 copy-start.29
  575.2 1.3 copy-start.17
  577.4 1.4 copy-start.21
  579.7 19.8 %collective-permute-start.1 = (bf16[8,256,1,128]{3,1,0,2:T(8,128)(2,1)}, bf16[8,256,1,128]{3,1,0,2:T(8,128)(2,1)S(1)}, u32[]{:S(2)}, u32[]{:S(2)}) collective-permute-start(bf16[8,256,1,128]{3,1,0,2:T(8,128)(2,1)} %slice.178), channel_id=1, source_target_pairs={{2,0},{3,1},{6,4},{7,5},{10,8},{11,9},{14,12},{15,13},{18,16},{19,... | collective-permute-start | bytes 1572872 | tf_op jit(solution)/shard_map/ppermute | solution.py:1422
  585.9 7.4 copy-start.31
  586.9 6.7 copy-start.16
  586.9 6.7 copy-start.18
  586.9 25.0 %collective-permute-start.2 = (bf16[8,256,1,128]{1,3,0,2:T(8,128)(2,1)}, bf16[8,256,1,128]{1,3,0,2:T(8,128)(2,1)}, u32[]{:S(2)}, u32[]{:S(2)}) collective-permute-start(bf16[8,256,1,128]{1,3,0,2:T(8,128)(2,1)} %slice.177), channel_id=1, source_target_pairs={{2,0},{3,1},{6,4},{7,5},{10,8},{11,9},{14,12},{15,13},{18,16},{19,... | collective-permute-start | bytes 1572872 | tf_op jit(solution)/shard_map/ppermute | solution.py:1421
  593.6 5.8 copy-start.22
  604.2 4.5 copy-start.23
  608.7 2.9 copy-start.24
  620.9 28.2 %copy-start.14 = (bf16[8,2,128,384]{3,2,1,0:T(8,128)(2,1)S(1)}, bf16[8,2,128,384]{3,2,1,0:T(8,128)(2,1)}, u32[]{:S(2)}) copy-start(bf16[8,2,128,384]{3,2,1,0:T(8,128)(2,1)} %copy-done.13) | copy-start | bytes 4718596
  637.4 0.8 copy-start.10
  638.2 35.8 %collective-permute-start.3 = (bf16[8,96,1024]{2,1,0:T(8,128)(2,1)}, bf16[8,96,1024]{2,1,0:T(8,128)(2,1)}, u32[]{:S(2)}, u32[]{:S(2)}) collective-permute-start(bf16[8,96,1024]{2,1,0:T(8,128)(2,1)} %slice.121), channel_id=1, source_target_pairs={{0,2},{2,0},{1,3},{3,1},{4,6},{6,4},{5,7},{7,5},{8,10},{10,8},{9,1... | collective-permute-start | bytes 4718600 | tf_op jit(solution)/shard_map/ppermute | solution.py:1439
  639.2 34.8 %all-to-all-start.3 = ((bf16[8,256,256]{2,1,0:T(8,128)(2,1)}), bf16[8,256,256]{2,1,0:T(8,128)(2,1)S(1)}, u32[]{:S(2)}, u32[]{:S(2)}) async-start(bf16[8,256,256]{2,1,0:T(8,128)(2,1)} %get-tuple-element.82), calls=%async_computation.3 | async-start | bytes 2097152 | tf_op jit(solution)/shard_map/all_to_all | solution.py:1195
  645.4 3.8 copy-start.34
  674.0 1.2 copy-start.3
  768.5 0.8 copy-start.11
  769.3 3.7 copy-start.12
  773.0 11.2 %copy-start.5 = (bf16[256,2048]{1,0:T(8,128)(2,1)S(1)}, bf16[256,2048]{1,0:T(8,128)(2,1)}, u32[]{:S(2)}) copy-start(bf16[256,2048]{1,0:T(8,128)(2,1)} %copy-done.4) | copy-start | bytes 3145732
  775.3 12.9 %copy-start.1 = (bf16[256,2048]{1,0:T(8,128)(2,1)S(1)}, bf16[256,2048]{1,0:T(8,128)(2,1)}, u32[]{:S(2)}) copy-start(bf16[256,2048]{1,0:T(8,128)(2,1)} %param.14) | copy-start | bytes 3145732

commit v9 on v8

--- a/solution.py
+++ b/solution.py
@@ -63,6 +63,7 @@
 
 LINE = 4
 CHUNK = 16
+FEW = 8
 MESH_ID = pl.DeviceIdType.MESH
 HBM = pl.BlockSpec(memory_space=pl.ANY)
 VMEM = pl.BlockSpec(memory_space=pltpu.VMEM)
@@ -163,12 +164,12 @@
     )
 
 
-def by_rows(rows, body):
+def by_rows(rows, body, first=0):
     def step(index, carry):
         body(pl.ds(pl.multiple_of(index * CHUNK, CHUNK), CHUNK))
         return carry
 
-    lax.fori_loop(0, rows // CHUNK, step, 0)
+    lax.fori_loop(first // CHUNK, rows // CHUNK, step, 0)
 
 
 def reduce_scratch(rows, width):
@@ -182,12 +183,16 @@
         DMA((2, 2 * LINE)),
         DMA((2, LINE)),
         DMA((2, LINE + 1)),
+        pltpu.VMEM((LINE + 1, rows // FEW, width), BF),
+        DMA((2, LINE + 1)),
     ]
 
 
 def reduce_phase(place, sender, partial, scratch, between=None, idle=None, late=None):
-    mine, core_in, y_in, line_in, total, local_sem, core_sem, y_sem, line_sem = scratch
+    mine, core_in, y_in, line_in, total, local_sem, core_sem, y_sem, line_sem = scratch[:9]
+    few_in, few_sem = scratch[9:]
     rows = total.shape[0]
+    few = rows // FEW
     z, y, core = place.z, place.y, place.core
     low = z < LINE // 2
     order = []
@@ -214,14 +219,41 @@
             place.at(z, y, 1 - core),
         )
 
-    def to_y(block):
+    def to_y(block, first):
+        at = pl.ds(first, rows - first)
         return remote(
-            mine.at[2 * block + 1 - y],
-            y_in.at[block],
+            mine.at[2 * block + 1 - y, at],
+            y_in.at[block, at],
             y_sem.at[0, block],
             y_sem.at[1, block],
             place.at(z, 1 - y, core),
         )
+
+    def few_along(block):
+        step = jnp.where(block > z, 1, -1)
+        slot = jnp.where((step < 0) & (block == z - 1), LINE, block)
+        return remote(
+            mine.at[2 * block + 1 - y, pl.ds(0, few)],
+            few_in.at[slot],
+            few_sem.at[0, block],
+            few_sem.at[1, slot],
+            place.at(z + step, y, core),
+        )
+
+    def add_few(slot, source):
+        remote(
+            mine.at[0, pl.ds(0, few)],
+            few_in.at[source],
+            few_sem.at[0, 0],
+            few_sem.at[1, source],
+            place.at(z, y, 1 - core),
+        ).wait_recv()
+
+        def add(at):
+            value = mine[slot, at].astype(F32) + few_in[source, at].astype(F32)
+            mine[slot, at] = value.astype(BF)
+
+        by_rows(few, add)
 
     def to_line(block):
         step = jnp.where(block > z, 1, -1)
@@ -248,7 +280,7 @@
             sender(None, functools.partial(to_core, 2 * block + half))
             fetch(2 * block + half).start()
 
-    for block in order:
+    for number, block in enumerate(order):
         slot = 2 * block + 1 - y
         fetch(slot).wait()
         to_core(slot).wait_recv()
@@ -258,7 +290,15 @@
             mine[slot, at] = value.astype(BF)
 
         by_rows(rows, add)
-        sender(None, functools.partial(to_y, block))
+        if number == LINE - 1:
+            pl.when(z > 0)(functools.partial(add_few, slot, z))
+            pl.when(z < LINE - 1)(functools.partial(add_few, slot, LINE))
+            sender(None, functools.partial(to_y, block, 0))
+        else:
+            sender(None, functools.partial(to_y, block, few))
+            inner = jnp.where(block > z, z > 0, z < LINE - 1)
+            pl.when(inner)(functools.partial(add_few, slot, block))
+            sender(None, functools.partial(few_along, block))
 
     for number, block in enumerate(order[:-1]):
         if number == LINE - 2 and between is not None:
@@ -268,27 +308,37 @@
         slot = 2 * block + y
         fetch(slot).wait()
         to_core(slot).wait_recv()
-        to_y(block).wait_recv()
+        to_y(block, few).wait_recv()
         inner = jnp.where(block > z, z > 0, z < LINE - 1)
 
         @pl.when(inner)
         def _(block=block, slot=slot):
             from_line(block).wait_recv()
+
+            def add_first(at):
+                value = mine[slot, at].astype(F32) + core_in[slot, at].astype(F32)
+                mine[slot, at] = (value + line_in[block, at].astype(F32)).astype(BF)
 
             def add(at):
                 value = mine[slot, at].astype(F32) + core_in[slot, at].astype(F32)
                 value = value + y_in[block, at].astype(F32)
                 mine[slot, at] = (value + line_in[block, at].astype(F32)).astype(BF)
 
-            by_rows(rows, add)
+            by_rows(few, add_first)
+            by_rows(rows, add, few)
 
         @pl.when(jnp.logical_not(inner))
         def _(block=block, slot=slot):
+            def add_first(at):
+                value = mine[slot, at].astype(F32) + core_in[slot, at].astype(F32)
+                mine[slot, at] = value.astype(BF)
+
             def add(at):
                 value = mine[slot, at].astype(F32) + core_in[slot, at].astype(F32)
                 mine[slot, at] = (value + y_in[block, at].astype(F32)).astype(BF)
 
-            by_rows(rows, add)
+            by_rows(few, add_first)
+            by_rows(rows, add, few)
 
         sender(None, functools.partial(to_line, block))
 
@@ -297,7 +347,7 @@
     slot = 2 * z + y
     fetch(slot).wait()
     to_core(slot).wait_recv()
-    to_y(z).wait_recv()
+    to_y(z, 0).wait_recv()
 
     def start(at):
         value = mine[slot, at].astype(F32) + core_in[slot, at].astype(F32)
@@ -323,12 +373,14 @@
         DMA((2, 2 * LINE)),
         DMA((2, LINE)),
         DMA((2, LINE + 2)),
+        DMA((2, LINE + 2)),
     ]
 
 
 def gather_phase(place, sender, gathered, scratch, between=None, later=None, last=None):
-    own, local_sem, core_sem, y_sem, line_sem = scratch
+    own, local_sem, core_sem, y_sem, line_sem, few_sem = scratch
     rows = own.shape[0]
+    few = rows // FEW
     z, y, core = place.z, place.y, place.core
 
     def spot(block, half):
@@ -358,6 +410,28 @@
             spot(block, y),
             line_sem.at[0, index],
             line_sem.at[1, block],
+            place.at(z + step, y, core),
+        )
+
+    def some(block, half, first, count):
+        start = ((2 * block + half) * 2 + core) * rows + first
+        return gathered.at[pl.ds(pl.multiple_of(start, few), count)]
+
+    def rest_to_y(half, block):
+        return remote(
+            some(block, half, few, rows - few),
+            some(block, half, few, rows - few),
+            y_sem.at[0, block],
+            y_sem.at[1, block],
+            place.at(z, 1 - y, core),
+        )
+
+    def few_along(block, step, index):
+        return remote(
+            some(block, 1 - y, 0, few),
+            some(block, 1 - y, 0, few),
+            few_sem.at[0, index],
+            few_sem.at[1, block],
             place.at(z + step, y, core),
         )
 
@@ -379,8 +453,17 @@
             place.at(z, 1 - y, core),
         ).wait_recv()
 
-    def across(condition, block):
-        guarded(condition, functools.partial(took_y, block))
+    def across_own():
+        took_y(z)
+        sender(z < LINE - 1, functools.partial(few_along, z, 1, LINE))
+        sender(z > 0, functools.partial(few_along, z, -1, LINE + 1))
+        sender(None, lambda: to_core(spot(z, 1 - y), z, 1 - y))
+
+    def across(condition, block, step):
+        guarded(condition, lambda: few_along(block, step, block).wait_recv())
+        onward = condition & ((z < LINE - 1) if step > 0 else (z > 0))
+        sender(onward, functools.partial(few_along, block, step, block))
+        guarded(condition, lambda: rest_to_y(1 - y, block).wait_recv())
         sender(condition, lambda: to_core(spot(block, 1 - y), block, 1 - y))
 
     def along(condition, block, step):
@@ -390,7 +473,7 @@
         guarded(condition, took)
         onward = condition & ((z < LINE - 1) if step > 0 else (z > 0))
         sender(onward, lambda: to_line(spot(block, y), block, step, block))
-        sender(condition, lambda: to_y(spot(block, y), block))
+        sender(condition, lambda: rest_to_y(y, block))
         sender(condition, lambda: to_core(spot(block, y), block, y))
 
     for distance in range(1, LINE + 1):
@@ -398,10 +481,10 @@
             along(z >= distance, z - distance, 1)
             along(z + distance < LINE, z + distance, -1)
         if distance == 1:
-            across(None, z)
+            across_own()
         else:
-            across(z >= distance - 1, z - distance + 1)
-            across(z + distance - 1 < LINE, z + distance - 1)
+            across(z >= distance - 1, z - distance + 1, 1)
+            across(z + distance - 1 < LINE, z + distance - 1, -1)
         if distance == 1 and later is not None:
             later()
         if distance == LINE - 1 and last is not None:
@@ -579,8 +662,8 @@
             self.copy(index, self.place.side).wait_send()
 
 
-REDUCE = 9
-GATHER = 5
+REDUCE = 11
+GATHER = 6
 PIECES = 8
 
 

time: 797 us -> 791 us (level)
  Pallas kernels: 531 us -> 523 us
    pallas_call x7, Pallas kernels: 516 us -> 508 us  [call(): pl.pallas_call(kernel, out_shape=shapes, in_specs=specs[0], out_specs=spe...]
where the time goes in v9:
time: 791 us; the launch traced here: 783 us
  Pallas kernels  523 us (66%)
  matrix products  106 us (13%)
  other arithmetic  56.4 us (7%)
  starting transfers between devices  46 us (6%)
  local copies, waits for them, and re-layouts  35.7 us (5%)
  waiting for transfers between devices  13.9 us (2%)
    pallas_call x7, Pallas kernels, call(): pl.pallas_call(kernel, out_shape=shapes, in_specs=specs[0], out_specs=spe...  508 us
    all_to_all x4, starting transfers between devices, swap(): lax.all_to_all(pieces, 'fsdp', split_axis=0, concat_axis=0, tiled=True)  38.1 us
    dot_general x4, matrix products, product(): return jnp.dot(left, right, preferred_element_type=F32)  35.9 us
    dot_general x4, matrix products, product_right(): return jnp.einsum('rf,df->rd', left, right, preferred_element_type=F32)  35.2 us
    unnamed x88, local copies, waits for them, and re-layouts  17.2 us
  transfers between devices with their start and end apart: 8, of which 3 were waited for; matrix products, arithmetic and copies ran while one was open for 14% of the time, Pallas kernels for 2%

profile of v9, /device:TPU:16, one launch (start us, length us, event | category | flops | bytes accessed | tf_op | source)
XLA Modules:
  0.0 783.0 jit_solution(10430996380955747651)
XLA Ops:
  4.5 6.3 pack_kernel.1
  10.8 65.9 %first_kernel.1 = (bf16[2048,2048]{1,0:T(8,128)(2,1)}, bf16[8,2,128,384]{3,2,1,0:T(8,128)(2,1)S(1)}, bf16[8,2,64,256]{3,2,1,0:T(8,128)(2,1)S(1)}, f32[8,2,8,128]{3,2,1,0:T(8,128)S(1)}) custom-call(bf16[128,2048]{1,0:T(8,128)(2,1)S(1)} %constant_dynamic-slice_fusion.3.own_ref.tokens, bf16[256,1024]{1,0:T(8,128)(2,1)S(1)} %copy-done.6, ...), custom_call_target="tpu_custom_call" | custom-call | bytes 240000000 | tf_op jit(solution)/shard_map/first_kernel/pallas_call | solution.py:1061
  76.7 1.2 copy-done.13
  77.9 15.3 %all-to-all-start.1 = ((bf16[8,256,256]{2,1,0:T(8,128)(2,1)}), bf16[8,256,256]{2,1,0:T(8,128)(2,1)S(1)}, u32[]{:S(2)}, u32[]{:S(2)}) async-start(bf16[8,256,256]{2,1,0:T(8,128)(2,1)} %get-tuple-element.63), calls=%async_computation.1 | async-start | bytes 2097152 | tf_op jit(solution)/shard_map/all_to_all | solution.py:1278
  93.3 10.0 %fusion.57 = f32[2048,384]{1,0:T(8,128)} fusion(bf16[2048,2048]{1,0:T(8,128)(2,1)} %get-tuple-element.56, bf16[2048,384]{1,0:T(8,128)(2,1)} %bitcast.216), kind=kOutput, calls=%fused_computation.152 | convolution fusion | flops 3221225472 | bytes 13107200 | tf_op jit(solution)/shard_map/dot_general | solution.py:18
  103.2 2.2 multiply_reduce_fusion.2
  105.6 1.3 split.54.rest_0_
  107.4 15.0 %sum_kernel.2 = (f32[32,128]{1,0:T(8,128)S(1)}, bf16[2048,128]{1,0:T(8,128)(2,1)S(1)}) custom-call(f32[32,128]{1,0:T(8,128)S(1)} %reshape.509.value, bf16[2048,128]{1,0:T(8,128)(2,1)S(1)} %split.54.rest_0_), custom_call_target="tpu_custom_call" | custom-call | bytes 30000000 | tf_op jit(solution)/shard_map/sum_kernel/pallas_call | solution.py:1061
  122.6 2.7 multiply_multiply_fusion
  126.3 1.7 slice_negate_fusion.2
  128.0 6.6 all-to-all-start
  134.6 1.3 fusion.35
  136.9 6.2 fusion.15
  143.1 3.4 collective-permute-start
  146.7 1.7 fusion.11
  152.8 6.4 fusion.13
  159.2 5.3 fusion.56
  164.5 4.2 fusion.9
  168.7 1.3 copy.95
  170.0 6.6 convolution_convert_fusion.3.partial
  176.7 2.6 all-to-all-done.pair
  179.2 102.9 %hidden_kernel.1 = (bf16[2048,2048]{1,0:T(8,128)(2,1)}, f32[128,2048]{1,0:T(8,128)S(1)}, f32[128,2048]{1,0:T(8,128)S(1)}, bf16[8,2,128,1024]{3,2,1,0:T(8,128)(2,1)}, bf16[8,2,256,256]{3,2,1,0:T(8,128)(2,1)S(1)}) custom-call(bf16[2048,2048]{1,0:T(8,128)(2,1)} %convolution_convert_fusion.3.partial, ...), custom_call_target="tpu_custom_call" | custom-call | bytes 300000000 | tf_op jit(solution)/shard_map/hidden_kernel/pallas_call | solution.py:1061
  282.2 12.5 %fusion.58 = f32[2048,1024]{1,0:T(8,128)S(1)} fusion(bf16[2048,2048]{1,0:T(8,128)(2,1)} %get-tuple-element.64.hidden_low, bf16[2048,1024]{1,0:T(8,128)(2,1)} %bitcast.255), kind=kOutput, calls=%fused_computation.153 | convolution fusion | flops 8589934592 | bytes 20971520 | tf_op jit(solution)/shard_map/dot_general | solution.py:18
  294.6 1.5 multiply_convert_fusion.3.inner_low
  296.1 1.8 copy-done.26
  297.9 1.2 copy.99
  299.8 6.8 convolution_convert_fusion.2.partial
  306.6 101.8 %turn_kernel.1 = (bf16[2048,2048]{1,0:T(8,128)(2,1)}, bf16[256,2048]{1,0:T(8,128)(2,1)S(1)}, f32[1,2048]{1,0:T(1,128)S(1)}) custom-call(bf16[2048,2048]{1,0:T(8,128)(2,1)} %convolution_convert_fusion.2.partial, f32[128,2048]{1,0:T(8,128)S(1)} %get-tuple-element.67.hidden, bf16[128,2048]{1,0:T(8,128)(2,1)S(1)} %constant_dynamic-slice_fusion.1.cotangent, ...), custom_call_target="tpu_custom_call" | custom-call | bytes 300000000 | tf_op jit(solution)/shard_map/turn_kernel/pallas_call | solution.py:1061
  408.4 11.2 %multiply_convert_fusion.2 = (bf16[2048,512]{1,0:T(8,128)(2,1)S(1)}, bf16[2048,512]{1,0:T(8,128)(2,1)S(1)}) fusion(f32[2048,1024]{1,0:T(8,128)} %copy-done.26, bf16[2048,2048]{1,0:T(8,128)(2,1)} %get-tuple-element.69.grad_mlp, bf16[512,2048]{1,0:T(8,128)(2,1)S(1)} %bitcast.228), kind=kOutput, calls=%fused_computation.9 | convolution fusion | flops 4308598784 | bytes 23068672 | tf_op jit(solution)/shard_map/rf,df->rd/dot_general | solution.py:26
  419.7 2.8 pad_maximum_fusion.grad_pair
  423.3 10.9 %convolution_convert_fusion.1.partial = bf16[2048,2048]{1,0:T(8,128)(2,1)} fusion(bf16[2048,1024]{1,0:T(8,128)(2,1)S(1)} %bitcast.256, bf16[2048,512]{1,0:T(8,128)(2,1)S(1)} %get-tuple-element.102, bf16[2048,512]{1,0:T(8,128)(2,1)S(1)} %get-tuple-element.101), kind=kOutput, calls=%fused_computation.2 | convolution fusion | flops 8602517504 | bytes 16777216 | tf_op jit(solution)/shard_map/rf,df->rd/dot_general | solution.py:26
  434.2 113.9 %branch_kernel.1 = (bf16[2048,2048]{1,0:T(8,128)(2,1)}, f32[128,2048]{1,0:T(8,128)S(1)}, f32[1,2048]{1,0:T(1,128)S(1)}, bf16[8,1,128,1024]{3,2,1,0:T(8,128)(2,1)}, bf16[8,256,256]{2,1,0:T(8,128)(2,1)}) custom-call(bf16[2048,2048]{1,0:T(8,128)(2,1)} %convolution_convert_fusion.1.partial, f32[128,2048]{1,0:T(8,128)S(1)} %get-tuple-element.70.branch, ...), custom_call_target="tpu_custom_call" | custom-call | bytes 300000000 | tf_op jit(solution)/shard_map/branch_kernel/pallas_call | solution.py:1061
  548.2 6.1 convolution_convert_fusion.6
  554.4 2.5 multiply_reduce_fusion
  556.9 10.0 %all-to-all-start.2 = ((bf16[8,128,1024]{2,1,0:T(8,128)(2,1)}), bf16[8,128,1024]{2,1,0:T(8,128)(2,1)}, u32[]{:S(2)}, u32[]{:S(2)}) async-start(bf16[8,128,1024]{2,1,0:T(8,128)(2,1)} %bitcast.39), calls=%async_computation.2 | async-start | bytes 4194304 | tf_op jit(solution)/shard_map/all_to_all | solution.py:1278
  566.9 3.9 multiply_convert_fusion
  570.9 1.3 copy-done.17
  573.1 1.4 copy-done.21
  575.3 1.3 collective-permute-start.1
  578.5 3.1 convolution_bitcast_fusion
  582.5 1.5 collective-permute-start.2
  584.1 4.7 convolution_convert_fusion.5
  589.0 5.4 fusion.33
  594.8 4.8 maximum_add_fusion
  600.0 4.1 maximum_add_fusion.1
  604.1 2.9 fusion.20
  607.3 1.5 fusion.10
  609.8 3.0 all-to-all-done.2
  612.8 1.1 slice.116.rest_0_
  613.9 2.7 slice.121
  616.6 15.8 %sum_kernel.3 = (f32[32,128]{1,0:T(8,128)S(1)}, bf16[8,32,1024]{2,1,0:T(8,128)(2,1)S(1)}) custom-call(f32[32,128]{1,0:T(8,128)S(1)} %reshape.530.value, bf16[8,32,1024]{2,1,0:T(8,128)(2,1)S(1)} %slice.116.rest_0_), custom_call_target="tpu_custom_call" | custom-call | bytes 30000000 | tf_op jit(solution)/shard_map/sum_kernel/pallas_call | solution.py:1061
  633.2 1.6 collective-permute-start.3
  634.9 6.1 all-to-all-start.3
  641.0 3.7 fusion.22
  644.8 6.9 convolution_convert_fusion.partial
  651.6 9.1 %convolution_convert_fusion.4 = bf16[2048,384]{1,0:T(8,128)(2,1)} fusion(bf16[2048,2048]{1,0:T(8,128)(2,1)} %get-tuple-element.56, bf16[2048,128]{1,0:T(8,128)(2,1)S(1)} %bitcast.235, bf16[2048,128]{1,0:T(8,128)(2,1)S(1)} %get-tuple-element.104, bf16[2048,128]{1,0:T(8,128)(2,1)S(1)} %get-tuple-element.103), kind=kOutput, calls=%fused_computation.14 | convolution fusion | flops 3226730496 | bytes 11534336 | tf_op jit(solution)/shard_map/rd,rf->df/dot_general | solution.py:22
  660.7 8.3 %collective-permute-done.3 = bf16[8,96,1024]{2,1,0:T(8,128)(2,1)} collective-permute-done((bf16[8,96,1024]{2,1,0:T(8,128)(2,1)}, bf16[8,96,1024]{2,1,0:T(8,128)(2,1)}, u32[]{:S(2)}, u32[]{:S(2)}) %collective-permute-start.3) | collective-permute-done | bytes 1572896 | tf_op jit(solution)/shard_map/ppermute | solution.py:1522
  669.0 1.2 copy-done.3
  670.3 92.5 %last_kernel.1 = (f32[256,2048]{1,0:T(8,128)}, bf16[8,2,128,384]{3,2,1,0:T(8,128)(2,1)S(1)}, bf16[8,2,64,256]{3,2,1,0:T(8,128)(2,1)S(1)}, f32[8,2,8,128]{3,2,1,0:T(8,128)S(1)}, bf16[8,2,256,256]{3,2,1,0:T(8,128)(2,1)}) custom-call(bf16[2048,2048]{1,0:T(8,128)(2,1)} %convolution_convert_fusion.partial, f32[128,2048]{1,0:T(8,128)S(1)} %copy-done.3, ...), custom_call_target="tpu_custom_call" | custom-call | bytes 240000000 | tf_op jit(solution)/shard_map/last_kernel/pallas_call | solution.py:1061
  764.0 1.1 copy_bitcast_fusion
  765.1 1.1 copy_bitcast_fusion.1
  766.2 1.1 copy_bitcast_fusion.2
  769.7 8.8 %unpack_kernel.1 = (f32[256,4096]{1,0:T(8,128)}, f32[256,4096]{1,0:T(8,128)}, f32[4096,256]{1,0:T(8,128)}) custom-call(s32[1]{0:T(128)} %bitcast.side, bf16[1,8,128,1024]{3,2,1,0:T(8,128)(2,1)} %bitcast.58.own, bf16[1,8,32,1024]{3,2,1,0:T(8,128)(2,1)} %bitcast.209, bf16[1,8,96,1024]{3,2,1,0:T(8,128)(2,1)} %bitcast.60.rest, bf16[1,8,512,256]{3,2,1,0:T(8,128)(2,1)} %bitcast.225), custom_call_target="tpu_custom_call" | custom-call | tf_op jit(solution)/shard_map/unpack_kernel/pallas_call | solution.py:1295
  779.5 3.1 copy.155
  (153 shorter events, 24.7 us)
Async XLA Ops:
  0.6 3.8 copy-start
  0.7 10.1 %copy-start.6 = (bf16[256,1024]{1,0:T(8,128)(2,1)S(1)}, bf16[256,1024]{1,0:T(8,128)(2,1)}, u32[]{:S(2)}) copy-start(bf16[256,1024]{1,0:T(8,128)(2,1)} %query.1) | copy-start | bytes 1572868
  0.7 10.1 %copy-start.7 = (bf16[256,1024]{1,0:T(8,128)(2,1)S(1)}, bf16[256,1024]{1,0:T(8,128)(2,1)}, u32[]{:S(2)}) copy-start(bf16[256,1024]{1,0:T(8,128)(2,1)} %key.1) | copy-start | bytes 1572868
  0.7 10.1 %copy-start.8 = (bf16[256,1024]{1,0:T(8,128)(2,1)S(1)}, bf16[256,1024]{1,0:T(8,128)(2,1)}, u32[]{:S(2)}) copy-start(bf16[256,1024]{1,0:T(8,128)(2,1)} %value.1) | copy-start | bytes 1572868
  4.5 6.3 copy-start.9
  76.7 1.2 copy-start.13
  77.9 50.1 %all-to-all-start.1 = ((bf16[8,256,256]{2,1,0:T(8,128)(2,1)}), bf16[8,256,256]{2,1,0:T(8,128)(2,1)S(1)}, u32[]{:S(2)}, u32[]{:S(2)}) async-start(bf16[8,256,256]{2,1,0:T(8,128)(2,1)} %get-tuple-element.63), calls=%async_computation.1 | async-start | bytes 2097152 | tf_op jit(solution)/shard_map/all_to_all | solution.py:1278
  125.3 1.0 copy-start.20
  128.0 51.3 %all-to-all-start = ((bf16[8,128,1024]{2,1,0:T(8,128)(2,1)}), bf16[8,128,1024]{2,1,0:T(8,128)(2,1)}, u32[]{:S(2)}, u32[]{:S(2)}) async-start(bf16[8,128,1024]{2,1,0:T(8,128)(2,1)} %get-tuple-element.62), calls=%async_computation | async-start | bytes 4194304 | tf_op jit(solution)/shard_map/all_to_all | solution.py:1278
  134.6 12.2 %copy-start.19 = (f32[2048,128]{1,0:T(8,128)S(1)}, f32[2048,128]{1,0:T(8,128)}, u32[]{:S(2)}) copy-start(f32[2048,128]{1,0:T(8,128)} %get-tuple-element.106) | copy-start | bytes 3145732
  135.9 1.0 copy-start.15
  143.1 16.1 %collective-permute-start = (bf16[8,256,1,128]{3,1,0,2:T(8,128)(2,1)}, bf16[8,256,1,128]{3,1,0,2:T(8,128)(2,1)}, u32[]{:S(2)}, u32[]{:S(2)}) collective-permute-start(bf16[8,256,1,128]{3,1,0,2:T(8,128)(2,1)} %fusion.15), channel_id=1, source_target_pairs={{0,2},{1,3},{4,6},{5,7},{8,10},{9,11},{12,14},{13,15},{16,18},{17,... | collective-permute-start | bytes 1572872 | tf_op jit(solution)/shard_map/ppermute | solution.py:1441
  159.2 5.3 copy-start.28
  294.6 3.3 copy-start.26
  297.9 1.9 copy-start.25
  408.4 11.3 %copy-start.4 = (bf16[256,2048]{1,0:T(8,128)(2,1)}, bf16[256,2048]{1,0:T(8,128)(2,1)S(1)}, u32[]{:S(2)}) copy-start(bf16[256,2048]{1,0:T(8,128)(2,1)S(1)} %get-tuple-element.155) | copy-start | bytes 3145732
  419.7 3.6 copy-start.35
  434.2 113.9 %copy-start.30 = (bf16[16,8,8,256]{3,1,2,0:T(8,128)(2,1)S(1)}, bf16[16,8,8,256]{3,1,2,0:T(8,128)(2,1)}, u32[]{:S(2)}) copy-start(bf16[16,8,8,256]{3,1,2,0:T(8,128)(2,1)} %copy.125) | copy-start | bytes 1572868
  548.2 6.2 copy-start.2
  548.2 6.2 copy-start.27
  548.2 6.2 copy-start.32
  548.2 6.2 copy-start.33
  554.4 2.5 copy-start.36
  556.9 55.9 %all-to-all-start.2 = ((bf16[8,128,1024]{2,1,0:T(8,128)(2,1)}), bf16[8,128,1024]{2,1,0:T(8,128)(2,1)}, u32[]{:S(2)}, u32[]{:S(2)}) async-start(bf16[8,128,1024]{2,1,0:T(8,128)(2,1)} %bitcast.39), calls=%async_computation.2 | async-start | bytes 4194304 | tf_op jit(solution)/shard_map/all_to_all | solution.py:1278
  566.9 5.2 copy-start.29
  570.9 1.3 copy-start.17
  573.0 1.4 copy-start.21
  575.3 19.5 %collective-permute-start.1 = (bf16[8,256,1,128]{3,1,0,2:T(8,128)(2,1)}, bf16[8,256,1,128]{3,1,0,2:T(8,128)(2,1)S(1)}, u32[]{:S(2)}, u32[]{:S(2)}) collective-permute-start(bf16[8,256,1,128]{3,1,0,2:T(8,128)(2,1)} %slice.178), channel_id=1, source_target_pairs={{2,0},{3,1},{6,4},{7,5},{10,8},{11,9},{14,12},{15,13},{18,16},{19,... | collective-permute-start | bytes 1572872 | tf_op jit(solution)/shard_map/ppermute | solution.py:1505
  581.6 7.2 copy-start.31
  582.5 6.5 copy-start.16
  582.5 6.5 copy-start.18
  582.5 24.8 %collective-permute-start.2 = (bf16[8,256,1,128]{1,3,0,2:T(8,128)(2,1)}, bf16[8,256,1,128]{1,3,0,2:T(8,128)(2,1)}, u32[]{:S(2)}, u32[]{:S(2)}) collective-permute-start(bf16[8,256,1,128]{1,3,0,2:T(8,128)(2,1)} %slice.177), channel_id=1, source_target_pairs={{2,0},{3,1},{6,4},{7,5},{10,8},{11,9},{14,12},{15,13},{18,16},{19,... | collective-permute-start | bytes 1572872 | tf_op jit(solution)/shard_map/ppermute | solution.py:1504
  589.0 5.8 copy-start.22
  599.6 4.5 copy-start.23
  604.1 2.9 copy-start.24
  616.6 28.2 %copy-start.14 = (bf16[8,2,128,384]{3,2,1,0:T(8,128)(2,1)S(1)}, bf16[8,2,128,384]{3,2,1,0:T(8,128)(2,1)}, u32[]{:S(2)}) copy-start(bf16[8,2,128,384]{3,2,1,0:T(8,128)(2,1)} %copy-done.13) | copy-start | bytes 4718596
  632.4 0.8 copy-start.10
  633.2 35.8 %collective-permute-start.3 = (bf16[8,96,1024]{2,1,0:T(8,128)(2,1)}, bf16[8,96,1024]{2,1,0:T(8,128)(2,1)}, u32[]{:S(2)}, u32[]{:S(2)}) collective-permute-start(bf16[8,96,1024]{2,1,0:T(8,128)(2,1)} %slice.121), channel_id=1, source_target_pairs={{0,2},{2,0},{1,3},{3,1},{4,6},{6,4},{5,7},{7,5},{8,10},{10,8},{9,1... | collective-permute-start | bytes 4718600 | tf_op jit(solution)/shard_map/ppermute | solution.py:1522
  634.9 34.2 %all-to-all-start.3 = ((bf16[8,256,256]{2,1,0:T(8,128)(2,1)}), bf16[8,256,256]{2,1,0:T(8,128)(2,1)S(1)}, u32[]{:S(2)}, u32[]{:S(2)}) async-start(bf16[8,256,256]{2,1,0:T(8,128)(2,1)} %get-tuple-element.82), calls=%async_computation.3 | async-start | bytes 2097152 | tf_op jit(solution)/shard_map/all_to_all | solution.py:1278
  641.0 3.8 copy-start.34
  669.0 1.2 copy-start.3
  762.8 0.8 copy-start.11
  763.6 3.7 copy-start.12
  767.3 11.2 %copy-start.5 = (bf16[256,2048]{1,0:T(8,128)(2,1)S(1)}, bf16[256,2048]{1,0:T(8,128)(2,1)}, u32[]{:S(2)}) copy-start(bf16[256,2048]{1,0:T(8,128)(2,1)} %copy-done.4) | copy-start | bytes 3145732
  769.7 12.9 %copy-start.1 = (bf16[256,2048]{1,0:T(8,128)(2,1)S(1)}, bf16[256,2048]{1,0:T(8,128)(2,1)}, u32[]{:S(2)}) copy-start(bf16[256,2048]{1,0:T(8,128)(2,1)} %param.14) | copy-start | bytes 3145732

commit v10 on v9

--- a/solution.py
+++ b/solution.py
@@ -667,8 +667,70 @@
 PIECES = 8
 
 
+class Pack:
+    def __init__(self, place, weights, outs, scratch):
+        gate, up, down = weights
+        pair, low = outs
+        held_gate, held_up, held_down, in_sem, out_sem = scratch
+        half, columns = held_gate.shape[0], pair.shape[2] // 2
+        down_half = held_down.shape[1]
+        rows = pl.ds(pl.multiple_of(place.side * half, half), half)
+        self.ins = [
+            pltpu.make_async_copy(gate.at[rows], held_gate, in_sem.at[0]),
+            pltpu.make_async_copy(up.at[rows], held_up, in_sem.at[1]),
+        ]
+        self.outs = []
+        for member in range(2 * LINE):
+            start = (2 * member + place.side) * down_half
+            down_rows = pl.ds(pl.multiple_of(start, down_half), down_half)
+            self.ins.append(
+                pltpu.make_async_copy(
+                    down.at[down_rows], held_down.at[member], in_sem.at[2 + member]
+                )
+            )
+            at = pl.ds(member * columns, columns)
+            for index, (source, target) in enumerate(
+                (
+                    (held_gate.at[:, at], pair.at[member, :, pl.ds(0, columns)]),
+                    (held_up.at[:, at], pair.at[member, :, pl.ds(columns, columns)]),
+                    (held_down.at[member], low.at[member]),
+                )
+            ):
+                sem = out_sem.at[index, member]
+                self.outs.append(pltpu.make_async_copy(source, target, sem))
+
+    def fetch(self):
+        for copy in self.ins:
+            copy.start()
+
+    def put(self):
+        for copy in self.ins:
+            copy.wait()
+        for copy in self.outs:
+            copy.start()
+
+    def finish(self):
+        for copy in self.outs:
+            copy.wait()
+
+
 def first_kernel(
-    own_ref, query, key, value, out, small, gathered, qkv_all, out_all, small_all, *scratch
+    own_ref,
+    query,
+    key,
+    value,
+    out,
+    small,
+    gate,
+    up,
+    down,
+    gathered,
+    qkv_all,
+    out_all,
+    small_all,
+    pair,
+    low,
+    *scratch,
 ):
     place = Place()
     sender = Sender()
@@ -703,9 +765,20 @@
         column_pair(value, 2),
         (out_source, lambda device, side: out_all.at[device, side]),
     ]
-    swap = Swap(place, pairs, scratch[GATHER:])
-    gather_phase(place, sender, gathered, scratch[:GATHER], swap.start, swap.pass_on)
+    swap = Swap(place, pairs, scratch[GATHER : GATHER + 3])
+    pack = Pack(place, (gate, up, down), (pair, low), scratch[GATHER + 3 :])
+
+    def begin():
+        swap.start()
+        pack.fetch()
+
+    def later():
+        pack.put()
+        swap.pass_on()
+
+    gather_phase(place, sender, gathered, scratch[:GATHER], begin, later)
     swap.finish()
+    pack.finish()
     sender.drain()
 
 
@@ -1036,21 +1109,19 @@
         side.wait()
 
 
-def pack_kernel(side, gate, up, down, pair_out, down_out):
-    columns = gate.shape[1]
-    pair_out[0, :, :columns] = gate[...]
-    pair_out[0, :, columns:] = up[...]
-    down_out[0] = down[...]
-
-
-def unpack_kernel(side, own, other, rest, down, gate_out, up_out, down_out):
-    half, columns = own.shape[2], gate_out.shape[1]
+def widen_own_kernel(side, own, gate_out, up_out):
+    columns = gate_out.shape[1]
+    value = jnp.sum(own[:, 0].astype(F32), axis=0)
+    gate_out[...] = value[:, :columns]
+    up_out[...] = value[:, columns:]
+
+
+def widen_other_kernel(side, gate, up, other, rest, down, gate_out, up_out, down_out):
+    columns = gate_out.shape[1]
     first = other.shape[2]
-    other_start = (1 - side[0]) * half
-    parts = ((own, side[0] * half), (other, other_start), (rest, other_start + first))
-    for part, start in parts:
+    for part, start in ((other, 0), (rest, first)):
         value = jnp.sum(part[:, 0].astype(F32), axis=0)
-        rows = pl.ds(pl.multiple_of(start, first), part.shape[2])
+        rows = pl.ds(start, part.shape[2])
         gate_out[rows] = value[:, :columns]
         up_out[rows] = value[:, columns:]
     down_out[...] = jnp.sum(down[:, 0].astype(F32), axis=0)
@@ -1103,11 +1174,13 @@
         shape = (pieces.shape[0], 2) + pieces.shape[1:]
         return jax.ShapeDtypeStruct(shape, pieces.dtype)
 
-    def first(self, own, weights, out, small):
+    def first(self, own, weights, out, small, gate, up, down):
         rows, columns = weights[0].shape
         rows, columns = rows // 2, columns // self.size
         out_rows = out.shape[0] // self.size // 2
-        return talk(
+        wide = gate.shape[1]
+        low = (self.size, down.shape[0] // self.size // 2, down.shape[1])
+        *results, pair, low = talk(
             first_kernel,
             0,
             (
@@ -1115,43 +1188,22 @@
                 jax.ShapeDtypeStruct((self.fsdp, 2, rows, 3 * columns), BF),
                 jax.ShapeDtypeStruct((self.fsdp, 2, out_rows, out.shape[1]), BF),
                 jax.ShapeDtypeStruct((self.fsdp, 2) + small.shape, F32),
+                jax.ShapeDtypeStruct((self.size, rows, 2 * wide // self.size), BF),
+                jax.ShapeDtypeStruct(low, BF),
             ),
-            ([VMEM] * 6, (HBM,) * 4),
-            self.gathers + swap_scratch(self.fsdp, 5),
+            ([VMEM] * 6 + [HBM] * 3, (HBM,) * 6),
+            self.gathers
+            + swap_scratch(self.fsdp, 5)
+            + [
+                pltpu.VMEM((rows, wide), BF),
+                pltpu.VMEM((rows, wide), BF),
+                pltpu.VMEM(low, BF),
+                DMA((2 + self.size,)),
+                DMA((3, self.size)),
+            ],
             80,
-        )(own, *weights, out, small)
-
-    def pack(self, gate, up, down):
-        rows, columns = gate.shape
-        rows, columns = rows // 2, columns // self.size
-        down_rows, down_columns = down.shape
-        down_rows = down_rows // self.size // 2
-
-        def column_spec():
-            return pl.BlockSpec((rows, columns), lambda d, side: (side[0], d))
-
-        def piece_spec(*shape):
-            return pl.BlockSpec((1,) + shape, lambda d, side: (d, 0, 0))
-
-        pair, low = pl.pallas_call(
-            pack_kernel,
-            grid_spec=pltpu.PrefetchScalarGridSpec(
-                num_scalar_prefetch=1,
-                grid=(self.size,),
-                in_specs=[
-                    column_spec(),
-                    column_spec(),
-                    pl.BlockSpec((down_rows, down_columns), lambda d, side: (2 * d + side[0], 0)),
-                ],
-                out_specs=[piece_spec(rows, 2 * columns), piece_spec(down_rows, down_columns)],
-            ),
-            out_shape=[
-                jax.ShapeDtypeStruct((self.size, rows, 2 * columns), BF),
-                jax.ShapeDtypeStruct((self.size, down_rows, down_columns), BF),
-            ],
-            name="pack_kernel",
-        )(self.context.reshape(1).astype(jnp.int32), gate, up, down)
-        return self.repeat(pair), self.repeat(low)
+        )(own, *weights, out, small, gate, up, down)
+        return *results, self.repeat(pair), self.repeat(low)
 
     def hidden(self, partial, tokens, gain, pair, down):
         return talk(
@@ -1280,44 +1332,47 @@
     def repeat(self, pieces):
         return jnp.concatenate([pieces] * self.teams, axis=0) if self.teams > 1 else pieces
 
-    def unpack(self, own, other, rest, down):
+    def pieces(self, array):
+        shape = (-1,) + array.shape[-2:] if array.ndim == 3 else (-1, 2 * array.shape[2], array.shape[3])
+        array = array.reshape(shape)
+        cut = array.reshape((self.teams, self.size) + array.shape[1:])
+        spec = pl.BlockSpec((self.teams, 1) + array.shape[1:], lambda d, side: (0, d, 0, 0))
+        return cut, spec
+
+    def widen_own(self, own):
         half, columns = own.shape[1], own.shape[2] // 2
-        rows, down_columns = 2 * down.shape[2], down.shape[3]
-
-        def cut(array, *shape):
-            return array.reshape((self.teams, self.size) + shape)
-
-        def piece_spec(*shape):
-            return pl.BlockSpec((self.teams, 1) + shape, lambda d, side: (0, d, 0, 0))
-
-        wide = pl.BlockSpec((2 * half, columns), lambda d, side: (0, d))
-        wide_shape = jax.ShapeDtypeStruct((2 * half, self.size * columns), F32)
+        cut, spec = self.pieces(own)
+        wide = pl.BlockSpec((half, columns), lambda d, side: (side[0], d))
         return pl.pallas_call(
-            unpack_kernel,
+            widen_own_kernel,
+            grid_spec=pltpu.PrefetchScalarGridSpec(
+                num_scalar_prefetch=1, grid=(self.size,), in_specs=[spec], out_specs=[wide] * 2
+            ),
+            out_shape=[jax.ShapeDtypeStruct((2 * half, self.size * columns), F32)] * 2,
+            name="widen_own_kernel",
+        )(self.context.reshape(1).astype(jnp.int32), cut)
+
+    def widen_other(self, gate, up, other, rest, down):
+        half, columns = other.shape[1] + rest.shape[1], other.shape[2] // 2
+        cuts, specs = zip(*[self.pieces(one) for one in (other, rest, down)])
+        rows, down_columns = cuts[2].shape[2:]
+        wide = pl.BlockSpec((half, columns), lambda d, side: (1 - side[0], d))
+        return pl.pallas_call(
+            widen_other_kernel,
             grid_spec=pltpu.PrefetchScalarGridSpec(
                 num_scalar_prefetch=1,
                 grid=(self.size,),
-                in_specs=[
-                    piece_spec(half, 2 * columns),
-                    piece_spec(other.shape[1], 2 * columns),
-                    piece_spec(rest.shape[1], 2 * columns),
-                    piece_spec(rows, down_columns),
-                ],
+                in_specs=[HBM, HBM] + list(specs),
                 out_specs=[wide, wide, pl.BlockSpec((rows, down_columns), lambda d, side: (d, 0))],
             ),
             out_shape=[
-                wide_shape,
-                wide_shape,
+                jax.ShapeDtypeStruct(gate.shape, F32),
+                jax.ShapeDtypeStruct(up.shape, F32),
                 jax.ShapeDtypeStruct((self.size * rows, down_columns), F32),
             ],
-            name="unpack_kernel",
-        )(
-            self.context.reshape(1).astype(jnp.int32),
-            cut(own, half, 2 * columns),
-            cut(other, other.shape[1], 2 * columns),
-            cut(rest, rest.shape[1], 2 * columns),
-            cut(down, rows, down_columns),
-        )
+            input_output_aliases={1: 0, 2: 1},
+            name="widen_other_kernel",
+        )(self.context.reshape(1).astype(jnp.int32), gate, up, *cuts)
 
     def columns_whole(self, came):
         return came.reshape(-1, came.shape[-1])
@@ -1390,8 +1445,8 @@
     small = [query_gain.reshape(-1), key_gain.reshape(-1), attn_gain, mlp_gain]
     small = jnp.concatenate([one.astype(F32) for one in small + [cont_lengths.reshape(-1)]])
     small = jnp.pad(small, (0, 8 * 128 - small.size)).reshape(8, 128)
-    tokens_all, qkv_came, output_came, small_came = team.first(
-        tokens_own, [w_query, w_key, w_value], w_output, small
+    tokens_all, qkv_came, output_came, small_came, pair_mine, down_mine = team.first(
+        tokens_own, [w_query, w_key, w_value], w_output, small, w_gate, w_up, w_down
     )
     qkv_w = team.columns_whole(qkv_came)
     output_w = team.rows_whole(output_came)
@@ -1417,9 +1472,6 @@
     cosine = cosine[:, :, None, :]
     sine = sine[:, :, None, :]
 
-    pair_mine, down_mine, tokens_all = lax.optimization_barrier(
-        team.pack(w_gate, w_up, w_down) + (tokens_all,)
-    )
     pair_came = team.swap(pair_mine)
     down_came = team.swap(down_mine)
 
@@ -1540,8 +1592,9 @@
     ]
     used = 2 * share + 2 * heads * head_share
     small = jnp.concatenate(small + [jnp.zeros((fsdp, 8 * 128 - used), F32)], axis=1)
-    partial, pair_rest = lax.optimization_barrier(
-        (product_right(grad_qkv, qkv_w).astype(BF), pair_rest)
+    gate_own, up_own = team.widen_own(pair_came)
+    partial, pair_rest, gate_own, up_own = lax.optimization_barrier(
+        (product_right(grad_qkv, qkv_w).astype(BF), pair_rest, gate_own, up_own)
     )
     input_grad, qkv_came, output_came, small_came, down_came = team.last(
         partial,
@@ -1552,8 +1605,8 @@
         down_came,
     )
     grad_w_query, grad_w_key, grad_w_value = team.columns_out(qkv_came, 3)
-    grad_w_gate, grad_w_up, grad_w_down = team.unpack(
-        pair_came, pair_other, pair_rest, down_came
+    grad_w_gate, grad_w_up, grad_w_down = team.widen_other(
+        gate_own, up_own, pair_other, pair_rest, down_came
     )
     grad_w_output = team.rows_out(output_came)
     came = jnp.sum(small_came, axis=1).reshape(fsdp, -1)

time: 791 us -> 788 us (level)
    unnamed x88 -> x92, local copies, waits for them, and re-layouts: 17.2 us -> 21.4 us
  transfers between devices with their start and end apart: 8 -> 8, of which waited for: 3 -> 3; matrix products, arithmetic and copies ran while one was open for 14% -> 15% of each run, Pallas kernels for 2% -> 3%
where the time goes in v10:
time: 788 us; the launch traced here: 780 us
  Pallas kernels  522 us (66%)
  matrix products  107 us (14%)
  other arithmetic  56.3 us (7%)
  starting transfers between devices  45.4 us (6%)
  local copies, waits for them, and re-layouts  39.8 us (5%)
  waiting for transfers between devices  8.14 us (1%)
    pallas_call x7, Pallas kernels, call(): pl.pallas_call(kernel, out_shape=shapes, in_specs=specs[0], out_specs=spe...  508 us
    all_to_all x4, starting transfers between devices, swap(): lax.all_to_all(pieces, 'fsdp', split_axis=0, concat_axis=0, tiled=True)  38 us
    dot_general x4, matrix products, product(): return jnp.dot(left, right, preferred_element_type=F32)  35.9 us
    dot_general x4, matrix products, product_right(): return jnp.einsum('rf,df->rd', left, right, preferred_element_type=F32)  35.2 us
    unnamed x92, local copies, waits for them, and re-layouts  21.4 us
  transfers between devices with their start and end apart: 8, of which 3 were waited for; matrix products, arithmetic and copies ran while one was open for 15% of the time, Pallas kernels for 3%

profile of v10, /device:TPU:16, one launch (start us, length us, event | category | flops | bytes accessed | tf_op | source)
XLA Modules:
  0.0 779.9 jit_solution(15720227468692967869)
XLA Ops:
  8.5 66.2 %first_kernel.1 = (bf16[2048,2048]{1,0:T(8,128)(2,1)}, bf16[8,2,128,384]{3,2,1,0:T(8,128)(2,1)S(1)}, bf16[8,2,64,256]{3,2,1,0:T(8,128)(2,1)S(1)}, f32[8,2,8,128]...) custom-call(bf16[128,2048]{1,0:T(8,128)(2,1)S(1)} %constant_dynamic-slice_fusion.3.own_ref.tokens, ...), custom_call_target="tpu_custom_call" | custom-call | bytes 240000000 | tf_op jit(solution)/shard_map/first_kernel/pallas_call | solution.py:1132
  74.8 1.2 copy-done.13
  75.9 15.3 %all-to-all-start.1 = ((bf16[8,256,256]{2,1,0:T(8,128)(2,1)}), bf16[8,256,256]{2,1,0:T(8,128)(2,1)S(1)}, u32[]{:S(2)}, u32[]{:S(2)}) async-start(bf16[8,256,256]{2,1,0:T(8,128)(2,1)} %get-tuple-element.61), calls=%async_computation.1 | async-start | bytes 2097152 | tf_op jit(solution)/shard_map/all_to_all | solution.py:1330
  91.3 10.0 %fusion.57 = f32[2048,384]{1,0:T(8,128)} fusion(bf16[2048,2048]{1,0:T(8,128)(2,1)} %get-tuple-element.54, bf16[2048,384]{1,0:T(8,128)(2,1)} %bitcast.216), kind=kOutput, calls=%fused_computation.152 | convolution fusion | flops 3221225472 | bytes 13107200 | tf_op jit(solution)/shard_map/dot_general | solution.py:18
  101.3 2.2 multiply_reduce_fusion.2
  103.7 1.3 split.54.rest_0_
  105.5 15.0 %sum_kernel.2 = (f32[32,128]{1,0:T(8,128)S(1)}, bf16[2048,128]{1,0:T(8,128)(2,1)S(1)}) custom-call(f32[32,128]{1,0:T(8,128)S(1)} %reshape.505.value, bf16[2048,128]{1,0:T(8,128)(2,1)S(1)} %split.54.rest_0_), custom_call_target="tpu_custom_call" | custom-call | bytes 30000000 | tf_op jit(solution)/shard_map/sum_kernel/pallas_call | solution.py:1132
  120.7 2.7 multiply_multiply_fusion
  124.4 1.7 slice_negate_fusion.2
  126.0 6.6 all-to-all-start
  132.6 1.3 fusion.35
  135.0 6.2 fusion.15
  141.2 3.4 collective-permute-start
  144.8 1.7 fusion.11
  150.8 6.4 fusion.13
  157.3 5.3 fusion.56
  162.5 4.2 fusion.9
  166.8 1.3 copy.97
  168.1 6.6 convolution_convert_fusion.3.partial
  174.7 2.6 all-to-all-done.pair
  177.3 102.9 %hidden_kernel.1 = (bf16[2048,2048]{1,0:T(8,128)(2,1)}, f32[128,2048]{1,0:T(8,128)S(1)}, f32[128,2048]{1,0:T(8,128)S(1)}, bf16[8,2,128,1024]{3,2,1,0:T(8,128)(2,1)}, bf16[8,2,256,256]{3,2,1,0:T(8,128)(2,1)S(1)}) custom-call(bf16[2048,2048]{1,0:T(8,128)(2,1)} %convolution_convert_fusion.3.partial, ...), custom_call_target="tpu_custom_call" | custom-call | bytes 300000000 | tf_op jit(solution)/shard_map/hidden_kernel/pallas_call | solution.py:1132
  280.2 12.5 %fusion.58 = f32[2048,1024]{1,0:T(8,128)S(1)} fusion(bf16[2048,2048]{1,0:T(8,128)(2,1)} %get-tuple-element.62.hidden_low, bf16[2048,1024]{1,0:T(8,128)(2,1)} %bitcast.255), kind=kOutput, calls=%fused_computation.153 | convolution fusion | flops 8589934592 | bytes 20971520 | tf_op jit(solution)/shard_map/dot_general | solution.py:18
  292.7 1.5 multiply_convert_fusion.3.inner_low
  294.2 1.8 copy-done.26
  296.0 1.2 copy.101
  297.9 6.8 convolution_convert_fusion.2.partial
  304.7 101.8 %turn_kernel.1 = (bf16[2048,2048]{1,0:T(8,128)(2,1)}, bf16[256,2048]{1,0:T(8,128)(2,1)S(1)}, f32[1,2048]{1,0:T(1,128)S(1)}) custom-call(bf16[2048,2048]{1,0:T(8,128)(2,1)} %convolution_convert_fusion.2.partial, f32[128,2048]{1,0:T(8,128)S(1)} %get-tuple-element.65.hidden, bf16[128,2048]{1,0:T(8,128)(2,1)S(1)} %constant_dynamic-slice_fusion.1.cotangent, ...), custom_call_target="tpu_custom_call" | custom-call | bytes 300000000 | tf_op jit(solution)/shard_map/turn_kernel/pallas_call | solution.py:1132
  406.5 11.2 %multiply_convert_fusion.2 = (bf16[2048,512]{1,0:T(8,128)(2,1)S(1)}, bf16[2048,512]{1,0:T(8,128)(2,1)S(1)}) fusion(f32[2048,1024]{1,0:T(8,128)} %copy-done.26, bf16[2048,2048]{1,0:T(8,128)(2,1)} %get-tuple-element.67.grad_mlp, bf16[512,2048]{1,0:T(8,128)(2,1)S(1)} %bitcast.228), kind=kOutput, calls=%fused_computation.9 | convolution fusion | flops 4308598784 | bytes 23068672 | tf_op jit(solution)/shard_map/rf,df->rd/dot_general | solution.py:26
  417.8 2.8 pad_maximum_fusion.grad_pair
  421.4 10.9 %convolution_convert_fusion.1.partial = bf16[2048,2048]{1,0:T(8,128)(2,1)} fusion(bf16[2048,1024]{1,0:T(8,128)(2,1)S(1)} %bitcast.256, bf16[2048,512]{1,0:T(8,128)(2,1)S(1)} %get-tuple-element.104, bf16[2048,512]{1,0:T(8,128)(2,1)S(1)} %get-tuple-element.103), kind=kOutput, calls=%fused_computation.2 | convolution fusion | flops 8602517504 | bytes 16777216 | tf_op jit(solution)/shard_map/rf,df->rd/dot_general | solution.py:26
  432.3 113.9 %branch_kernel.1 = (bf16[2048,2048]{1,0:T(8,128)(2,1)}, f32[128,2048]{1,0:T(8,128)S(1)}, f32[1,2048]{1,0:T(1,128)S(1)}, bf16[8,1,128,1024]{3,2,1,0:T(8,128)(2,1)}, bf16[8,256,256]{2,1,0:T(8,128)(2,1)}) custom-call(bf16[2048,2048]{1,0:T(8,128)(2,1)} %convolution_convert_fusion.1.partial, f32[128,2048]{1,0:T(8,128)S(1)} %get-tuple-element.68.branch, ...), custom_call_target="tpu_custom_call" | custom-call | bytes 300000000 | tf_op jit(solution)/shard_map/branch_kernel/pallas_call | solution.py:1132
  546.4 6.1 convolution_convert_fusion.6
  552.5 2.5 multiply_reduce_fusion
  555.0 10.0 %all-to-all-start.2 = ((bf16[8,128,1024]{2,1,0:T(8,128)(2,1)}), bf16[8,128,1024]{2,1,0:T(8,128)(2,1)}, u32[]{:S(2)}, u32[]{:S(2)}) async-start(bf16[8,128,1024]{2,1,0:T(8,128)(2,1)} %bitcast.38), calls=%async_computation.2 | async-start | bytes 4194304 | tf_op jit(solution)/shard_map/all_to_all | solution.py:1330
  565.0 3.9 multiply_convert_fusion
  568.9 1.3 copy-done.17
  571.1 1.4 copy-done.21
  573.4 1.3 collective-permute-start.1
  576.5 3.1 convolution_bitcast_fusion
  580.6 1.5 collective-permute-start.2
  582.1 4.7 convolution_convert_fusion.5
  587.1 5.4 fusion.33
  592.9 4.8 maximum_add_fusion
  598.1 4.1 maximum_add_fusion.1
  602.2 2.9 fusion.20
  605.4 1.5 fusion.10
  607.9 3.0 all-to-all-done.2
  610.9 1.1 slice.116.rest_0_
  612.0 2.7 slice.121
  614.7 16.3 %sum_kernel.3 = (f32[32,128]{1,0:T(8,128)S(1)}, bf16[8,32,1024]{2,1,0:T(8,128)(2,1)S(1)}) custom-call(f32[32,128]{1,0:T(8,128)S(1)} %reshape.526.value, bf16[8,32,1024]{2,1,0:T(8,128)(2,1)S(1)} %slice.116.rest_0_), custom_call_target="tpu_custom_call" | custom-call | bytes 30000000 | tf_op jit(solution)/shard_map/sum_kernel/pallas_call | solution.py:1132
  631.8 1.1 collective-permute-start.3
  632.9 6.1 all-to-all-start.3
  639.1 3.7 fusion.22
  642.9 6.9 convolution_convert_fusion.partial
  649.7 6.0 widen_own_kernel.1
  655.7 9.4 %convolution_convert_fusion.4 = bf16[2048,384]{1,0:T(8,128)(2,1)} fusion(bf16[2048,2048]{1,0:T(8,128)(2,1)} %get-tuple-element.54, bf16[2048,128]{1,0:T(8,128)(2,1)} %bitcast.234, bf16[2048,128]{1,0:T(8,128)(2,1)} %copy-done.33, bf16[2048,128]{1,0:T(8,128)(2,1)} %copy-done.32), kind=kOutput, calls=%fused_computation.14 | convolution fusion | flops 3226730496 | bytes 11534336 | tf_op jit(solution)/shard_map/rd,rf->df/dot_general | solution.py:22
  665.1 2.5 collective-permute-done.3
  667.6 1.2 copy-done.3
  668.9 92.0 %last_kernel.1 = (f32[256,2048]{1,0:T(8,128)}, bf16[8,2,128,384]{3,2,1,0:T(8,128)(2,1)S(1)}, bf16[8,2,64,256]{3,2,1,0:T(8,128)(2,1)S(1)}, f32[8,2,8,128]{3,2,1,0:T(8,128)S(1)}, bf16[8,2,256,256]{3,2,1,0:T(8,128)(2,1)}) custom-call(bf16[2048,2048]{1,0:T(8,128)(2,1)} %convolution_convert_fusion.partial, f32[128,2048]{1,0:T(8,128)S(1)} %copy-done.3, ...), custom_call_target="tpu_custom_call" | custom-call | bytes 240000000 | tf_op jit(solution)/shard_map/last_kernel/pallas_call | solution.py:1132
  762.0 1.1 copy_bitcast_fusion
  763.2 1.1 copy_bitcast_fusion.1
  764.3 1.1 copy_bitcast_fusion.2
  767.8 7.6 widen_other_kernel.1
  776.3 3.1 copy.159
  (157 shorter events, 28.8 us)
Async XLA Ops:
  0.6 3.7 copy-start
  4.4 1.0 copy-start.6
  5.4 1.0 copy-start.7
  6.5 1.0 copy-start.8
  7.5 1.0 copy-start.9
  74.8 1.2 copy-start.13
  75.9 50.1 %all-to-all-start.1 = ((bf16[8,256,256]{2,1,0:T(8,128)(2,1)}), bf16[8,256,256]{2,1,0:T(8,128)(2,1)S(1)}, u32[]{:S(2)}, u32[]{:S(2)}) async-start(bf16[8,256,256]{2,1,0:T(8,128)(2,1)} %get-tuple-element.61), calls=%async_computation.1 | async-start | bytes 2097152 | tf_op jit(solution)/shard_map/all_to_all | solution.py:1330
  123.4 1.0 copy-start.20
  126.0 51.3 %all-to-all-start = ((bf16[8,128,1024]{2,1,0:T(8,128)(2,1)}), bf16[8,128,1024]{2,1,0:T(8,128)(2,1)}, u32[]{:S(2)}, u32[]{:S(2)}) async-start(bf16[8,128,1024]{2,1,0:T(8,128)(2,1)} %get-tuple-element.60), calls=%async_computation | async-start | bytes 4194304 | tf_op jit(solution)/shard_map/all_to_all | solution.py:1330
  132.6 12.1 %copy-start.19 = (f32[2048,128]{1,0:T(8,128)S(1)}, f32[2048,128]{1,0:T(8,128)}, u32[]{:S(2)}) copy-start(f32[2048,128]{1,0:T(8,128)} %get-tuple-element.108) | copy-start | bytes 3145732
  134.0 1.0 copy-start.15
  141.2 16.0 %collective-permute-start = (bf16[8,256,1,128]{3,1,0,2:T(8,128)(2,1)}, bf16[8,256,1,128]{3,1,0,2:T(8,128)(2,1)}, u32[]{:S(2)}, u32[]{:S(2)}) collective-permute-start(bf16[8,256,1,128]{3,1,0,2:T(8,128)(2,1)} %fusion.15), channel_id=1, source_target_pairs={{0,2},{1,3},{4,6},{5,7},{8,10},{9,11},{12,14},{13,15},{16,18},{17,... | collective-permute-start | bytes 1572872 | tf_op jit(solution)/shard_map/ppermute | solution.py:1493
  157.2 5.3 copy-start.28
  292.7 3.3 copy-start.26
  296.0 1.9 copy-start.25
  406.5 11.3 %copy-start.4 = (bf16[256,2048]{1,0:T(8,128)(2,1)}, bf16[256,2048]{1,0:T(8,128)(2,1)S(1)}, u32[]{:S(2)}) copy-start(bf16[256,2048]{1,0:T(8,128)(2,1)S(1)} %get-tuple-element.157) | copy-start | bytes 3145732
  417.8 3.6 copy-start.37
  432.3 114.0 %copy-start.30 = (bf16[16,8,8,256]{3,1,2,0:T(8,128)(2,1)S(1)}, bf16[16,8,8,256]{3,1,2,0:T(8,128)(2,1)}, u32[]{:S(2)}) copy-start(bf16[16,8,8,256]{3,1,2,0:T(8,128)(2,1)} %copy.127) | copy-start | bytes 1572868
  546.3 6.2 copy-start.2
  546.3 6.2 copy-start.27
  546.3 6.2 copy-start.34
  546.3 6.2 copy-start.35
  552.5 2.5 copy-start.38
  555.0 55.9 %all-to-all-start.2 = ((bf16[8,128,1024]{2,1,0:T(8,128)(2,1)}), bf16[8,128,1024]{2,1,0:T(8,128)(2,1)}, u32[]{:S(2)}, u32[]{:S(2)}) async-start(bf16[8,128,1024]{2,1,0:T(8,128)(2,1)} %bitcast.38), calls=%async_computation.2 | async-start | bytes 4194304 | tf_op jit(solution)/shard_map/all_to_all | solution.py:1330
  565.0 5.2 copy-start.29
  568.9 1.3 copy-start.17
  571.1 1.4 copy-start.21
  573.4 19.5 %collective-permute-start.1 = (bf16[8,256,1,128]{3,1,0,2:T(8,128)(2,1)}, bf16[8,256,1,128]{3,1,0,2:T(8,128)(2,1)S(1)}, u32[]{:S(2)}, u32[]{:S(2)}) collective-permute-start(bf16[8,256,1,128]{3,1,0,2:T(8,128)(2,1)} %slice.178), channel_id=1, source_target_pairs={{2,0},{3,1},{6,4},{7,5},{10,8},{11,9},{14,12},{15,13},{18,16},{19,... | collective-permute-start | bytes 1572872 | tf_op jit(solution)/shard_map/ppermute | solution.py:1557
  579.6 7.2 copy-start.31
  580.6 6.5 copy-start.16
  580.6 6.5 copy-start.18
  580.6 24.8 %collective-permute-start.2 = (bf16[8,256,1,128]{1,3,0,2:T(8,128)(2,1)}, bf16[8,256,1,128]{1,3,0,2:T(8,128)(2,1)}, u32[]{:S(2)}, u32[]{:S(2)}) collective-permute-start(bf16[8,256,1,128]{1,3,0,2:T(8,128)(2,1)} %slice.177), channel_id=1, source_target_pairs={{2,0},{3,1},{6,4},{7,5},{10,8},{11,9},{14,12},{15,13},{18,16},{19,... | collective-permute-start | bytes 1572872 | tf_op jit(solution)/shard_map/ppermute | solution.py:1556
  587.1 5.8 copy-start.22
  597.7 4.5 copy-start.23
  602.2 2.9 copy-start.24
  614.7 28.2 %copy-start.14 = (bf16[8,2,128,384]{3,2,1,0:T(8,128)(2,1)S(1)}, bf16[8,2,128,384]{3,2,1,0:T(8,128)(2,1)}, u32[]{:S(2)}) copy-start(bf16[8,2,128,384]{3,2,1,0:T(8,128)(2,1)} %copy-done.13) | copy-start | bytes 4718596
  631.0 0.8 copy-start.10
  631.8 35.8 %collective-permute-start.3 = (bf16[8,96,1024]{2,1,0:T(8,128)(2,1)}, bf16[8,96,1024]{2,1,0:T(8,128)(2,1)}, u32[]{:S(2)}, u32[]{:S(2)}) collective-permute-start(bf16[8,96,1024]{2,1,0:T(8,128)(2,1)} %slice.121), channel_id=1, source_target_pairs={{0,2},{2,0},{1,3},{3,1},{4,6},{6,4},{5,7},{7,5},{8,10},{10,8},{9,1... | collective-permute-start | bytes 4718600 | tf_op jit(solution)/shard_map/ppermute | solution.py:1574
  632.9 34.7 %all-to-all-start.3 = ((bf16[8,256,256]{2,1,0:T(8,128)(2,1)}), bf16[8,256,256]{2,1,0:T(8,128)(2,1)S(1)}, u32[]{:S(2)}, u32[]{:S(2)}) async-start(bf16[8,256,256]{2,1,0:T(8,128)(2,1)} %get-tuple-element.82), calls=%async_computation.3 | async-start | bytes 2097152 | tf_op jit(solution)/shard_map/all_to_all | solution.py:1330
  639.1 3.8 copy-start.36
  642.8 6.9 copy-start.32
  642.8 6.9 copy-start.33
  667.6 1.2 copy-start.3
  760.9 0.8 copy-start.11
  761.7 3.7 copy-start.12
  767.7 7.6 copy-start.5
  767.7 11.7 %copy-start.1 = (bf16[256,2048]{1,0:T(8,128)(2,1)S(1)}, bf16[256,2048]{1,0:T(8,128)(2,1)}, u32[]{:S(2)}) copy-start(bf16[256,2048]{1,0:T(8,128)(2,1)} %param.14) | copy-start | bytes 3145732

commit v11 on v10

--- a/solution.py
+++ b/solution.py
@@ -1063,22 +1063,20 @@
     sender.drain()
 
 
-def sum_kernel(carried, value, *rest):
-    if carried:
-        moved, result, arrived, core_in, y_in, held, line_in, sem, side_sem = rest
-    else:
-        result, core_in, y_in, held, line_in, sem = rest
+def sum_kernel(value, moved, result, arrived, core_in, y_in, held, line_in, sem, side_sem):
     place = Place()
     z, y, core = place.z, place.y, place.core
     barrier = pltpu.get_barrier_semaphore()
     others = [place.at(z, y, 1 - core), place.at(z, 1 - y, core)]
     others += [place.at(lax.rem(z + k, LINE), y, core) for k in range(1, LINE)]
-    for device in others + [place.across()] * carried:
+    for device in others + [place.across()]:
         signal(barrier, device)
-    pl.semaphore_wait(barrier, len(others) + carried)
-    if carried:
-        side = remote(moved, arrived, side_sem.at[0], side_sem.at[1], place.across())
-        side.start()
+    pl.semaphore_wait(barrier, len(others) + 1)
+    source = moved
+    if moved.shape != arrived.shape:
+        source = moved.at[:, pl.ds(0, arrived.shape[1])]
+    side = remote(source, arrived, side_sem.at[0], side_sem.at[1], place.across())
+    side.start()
     first = remote(value, core_in, sem.at[0, 0], sem.at[1, 0], others[0])
     first.start()
     first.wait_recv()
@@ -1105,8 +1103,7 @@
     second.wait_send()
     for send in sends:
         send.wait_send()
-    if carried:
-        side.wait()
+    side.wait()
 
 
 def widen_own_kernel(side, own, gate_out, up_out):
@@ -1302,21 +1299,17 @@
             80,
         )(partial, grad_hidden, qkv, out, small, down)
 
-    def total(self, values, moved=None):
+    def total(self, values, moved, arrives):
         flat = values.reshape(-1, 128)
-        carried = int(moved is not None)
         shape = jax.ShapeDtypeStruct(flat.shape, F32)
         scratch = [pltpu.VMEM(flat.shape, F32)] * 2
         scratch += [pltpu.VMEM((2,) + flat.shape, F32), pltpu.VMEM((LINE,) + flat.shape, F32)]
-        scratch += [DMA((2, LINE + 1))] + [DMA((2,))] * carried
+        scratch += [DMA((2, LINE + 1)), DMA((2,))]
         which = 5 + self.sums
         self.sums += 1
-        kernel = functools.partial(sum_kernel, carried)
-        if not carried:
-            call = talk(kernel, which, shape, ([VMEM], VMEM), scratch, 10, "sum_kernel")
-            return call(flat).reshape(values.shape)
-        shapes = (shape, jax.ShapeDtypeStruct(moved.shape, moved.dtype))
-        call = talk(kernel, which, shapes, ([VMEM] * 2, (VMEM,) * 2), scratch, 10, "sum_kernel")
+        shapes = (shape, jax.ShapeDtypeStruct(arrives, moved.dtype))
+        spaces = ([VMEM, HBM], (VMEM, HBM))
+        call = talk(sum_kernel, which, shapes, spaces, scratch, 10, "sum_kernel")
         total, came = call(flat, moved)
         return total.reshape(values.shape), came
 
@@ -1482,6 +1475,7 @@
     sums, sent_value = team.total(
         jnp.stack([jnp.sum(query_raw * query_raw, axis=1), jnp.sum(key_raw * key_raw, axis=1)]),
         value_low,
+        value_low.shape,
     )
     value_low, sent_value = value_low.reshape(by_head), sent_value.reshape(by_head)
     scale_query = lax.rsqrt(sums[0] / width + EPS)[:, None]
@@ -1540,7 +1534,6 @@
         grad_pair,
     )
     pair_came = team.swap(pair_mine)
-    output_grad = team.of_rows(product_left(attended_low, grad_branch_all))
     grad_attended = product_right(grad_branch_all, output_w).astype(BF).reshape(by_head)
 
     grad_probs = jnp.einsum("gqhd,gkhd->ghqk", grad_attended, values_all, preferred_element_type=F32)
@@ -1572,7 +1565,12 @@
     inner_sums, pair_came = lax.optimization_barrier((inner_sums, pair_came))
     first = pair_came.shape[1] // 4
     pair_rest = lax.ppermute(pair_came[:, first:], "context", [(0, 1), (1, 0)])
-    totals, pair_other = team.total(inner_sums, pair_came[:, :first])
+    arrives = (pair_came.shape[0], first, pair_came.shape[2])
+    totals, pair_other = team.total(inner_sums, pair_came, arrives)
+    late_attended, late_grad, totals = lax.optimization_barrier(
+        (attended_low, grad_branch_all, totals)
+    )
+    output_grad = team.of_rows(product_left(late_attended, late_grad))
     down_mine, totals = lax.optimization_barrier((down_mine, totals))
     down_came = team.swap(down_mine)
     grad_query_low = norm_back(

time: 788 us -> 785 us (level)
    unnamed x92 -> x112, local copies, waits for them, and re-layouts: 21.4 us -> 21.3 us
  transfers between devices with their start and end apart: 8 -> 8, of which waited for: 3 -> 3; matrix products, arithmetic and copies ran while one was open for 15% -> 14% of each run, Pallas kernels for 3% -> 3%
where the time goes in v11:
time: 785 us; the launch traced here: 777 us
  Pallas kernels  520 us (66%)
  matrix products  103 us (13%)
  other arithmetic  59.6 us (8%)
  starting transfers between devices  44.8 us (6%)
  local copies, waits for them, and re-layouts  37.6 us (5%)
  waiting for transfers between devices  9.76 us (1%)
    pallas_call x7, Pallas kernels, call(): pl.pallas_call(kernel, out_shape=shapes, in_specs=specs[0], out_specs=spe...  507 us
    all_to_all x4, starting transfers between devices, swap(): lax.all_to_all(pieces, 'fsdp', split_axis=0, concat_axis=0, tiled=True)  37.6 us
    dot_general x4, matrix products, product_right(): return jnp.einsum('rf,df->rd', left, right, preferred_element_type=F32)  36.3 us
    dot_general x4, matrix products, product(): return jnp.dot(left, right, preferred_element_type=F32)  34.8 us
    unnamed x112, local copies, waits for them, and re-layouts  21.3 us
  transfers between devices with their start and end apart: 8, of which 3 were waited for; matrix products, arithmetic and copies ran while one was open for 14% of the time, Pallas kernels for 3%

profile of v11, /device:TPU:16, one launch (start us, length us, event | category | flops | bytes accessed | tf_op | source)
XLA Modules:
  0.0 777.0 jit_solution(1587159842596705582)
XLA Ops:
  8.5 66.2 %first_kernel.1 = (bf16[2048,2048]{1,0:T(8,128)(2,1)}, bf16[8,2,128,384]{3,2,1,0:T(8,128)(2,1)S(1)}, bf16[8,2,64,256]{3,2,1,0:T(8,128)(2,1)S(1)}, f32[8,2,8,128]...) custom-call(bf16[128,2048]{1,0:T(8,128)(2,1)S(1)} %constant_dynamic-slice_fusion.3.own_ref.tokens, ...), custom_call_target="tpu_custom_call" | custom-call | bytes 240000000 | tf_op jit(solution)/shard_map/first_kernel/pallas_call | solution.py:1129
  74.8 1.2 copy-done.16
  75.9 15.3 %all-to-all-start.1 = ((bf16[8,256,256]{2,1,0:T(8,128)(2,1)}), bf16[8,256,256]{2,1,0:T(8,128)(2,1)S(1)}, u32[]{:S(2)}, u32[]{:S(2)}) async-start(bf16[8,256,256]{2,1,0:T(8,128)(2,1)} %get-tuple-element.64), calls=%async_computation.1 | async-start | bytes 2097152 | tf_op jit(solution)/shard_map/all_to_all | solution.py:1323
  91.3 10.0 %fusion.57 = f32[2048,384]{1,0:T(8,128)} fusion(bf16[2048,2048]{1,0:T(8,128)(2,1)} %get-tuple-element.57, bf16[2048,384]{1,0:T(8,128)(2,1)} %bitcast.218), kind=kOutput, calls=%fused_computation.152 | convolution fusion | flops 3221225472 | bytes 13107200 | tf_op jit(solution)/shard_map/dot_general | solution.py:18
  101.3 2.2 multiply_reduce_fusion.2
  103.7 1.3 split.54.moved
  105.5 15.0 %sum_kernel.2 = (f32[32,128]{1,0:T(8,128)S(1)}, bf16[2048,128]{1,0:T(8,128)(2,1)S(1)}) custom-call(f32[32,128]{1,0:T(8,128)S(1)} %reshape.505.value, bf16[2048,128]{1,0:T(8,128)(2,1)S(1)} %split.54.moved), custom_call_target="tpu_custom_call" | custom-call | bytes 30000000 | tf_op jit(solution)/shard_map/sum_kernel/pallas_call | solution.py:1129
  120.7 2.7 multiply_multiply_fusion
  124.4 1.7 slice_negate_fusion.2
  126.0 6.6 all-to-all-start
  132.7 1.3 fusion.35
  135.0 6.2 fusion.15
  141.2 3.4 collective-permute-start
  144.8 1.7 fusion.11
  149.0 1.2 constant_dynamic-slice_fusion.1.cotangent
  150.2 6.4 fusion.13
  156.6 5.3 fusion.56
  161.9 4.2 fusion.9
  166.1 1.3 copy.97
  167.5 5.6 convolution_convert_fusion.3.partial
  173.1 4.3 all-to-all-done.pair
  177.4 102.9 %hidden_kernel.1 = (bf16[2048,2048]{1,0:T(8,128)(2,1)}, f32[128,2048]{1,0:T(8,128)S(1)}, f32[128,2048]{1,0:T(8,128)S(1)}, bf16[8,2,128,1024]{3,2,1,0:T(8,128)(2,1)}, bf16[8,2,256,256]{3,2,1,0:T(8,128)(2,1)S(1)}) custom-call(bf16[2048,2048]{1,0:T(8,128)(2,1)} %convolution_convert_fusion.3.partial, ...), custom_call_target="tpu_custom_call" | custom-call | bytes 300000000 | tf_op jit(solution)/shard_map/hidden_kernel/pallas_call | solution.py:1129
  280.3 12.5 %fusion.58 = f32[2048,1024]{1,0:T(8,128)S(1)} fusion(bf16[2048,2048]{1,0:T(8,128)(2,1)} %get-tuple-element.65.hidden_low, bf16[2048,1024]{1,0:T(8,128)(2,1)} %bitcast.259), kind=kOutput, calls=%fused_computation.153 | convolution fusion | flops 8589934592 | bytes 20971520 | tf_op jit(solution)/shard_map/dot_general | solution.py:18
  292.8 1.5 multiply_convert_fusion.3.inner_low
  294.3 1.7 copy-done.31
  296.0 1.2 copy.101
  297.9 6.8 convolution_convert_fusion.2.partial
  304.7 101.8 %turn_kernel.1 = (bf16[2048,2048]{1,0:T(8,128)(2,1)}, bf16[256,2048]{1,0:T(8,128)(2,1)S(1)}, f32[1,2048]{1,0:T(1,128)S(1)}) custom-call(bf16[2048,2048]{1,0:T(8,128)(2,1)} %convolution_convert_fusion.2.partial, f32[128,2048]{1,0:T(8,128)S(1)} %get-tuple-element.68.hidden, bf16[128,2048]{1,0:T(8,128)(2,1)S(1)} %constant_dynamic-slice_fusion.1.cotangent, ...), custom_call_target="tpu_custom_call" | custom-call | bytes 300000000 | tf_op jit(solution)/shard_map/turn_kernel/pallas_call | solution.py:1129
  406.5 11.2 %multiply_convert_fusion.2 = (bf16[2048,512]{1,0:T(8,128)(2,1)S(1)}, bf16[2048,512]{1,0:T(8,128)(2,1)S(1)}) fusion(f32[2048,1024]{1,0:T(8,128)} %copy-done.31, bf16[2048,2048]{1,0:T(8,128)(2,1)} %get-tuple-element.70.grad_mlp, bf16[512,2048]{1,0:T(8,128)(2,1)S(1)} %bitcast.232), kind=kOutput, calls=%fused_computation.9 | convolution fusion | flops 4308598784 | bytes 23068672 | tf_op jit(solution)/shard_map/rf,df->rd/dot_general | solution.py:26
  417.7 2.8 pad_maximum_fusion.grad_pair
  421.4 10.9 %convolution_convert_fusion.1.partial = bf16[2048,2048]{1,0:T(8,128)(2,1)} fusion(bf16[2048,1024]{1,0:T(8,128)(2,1)S(1)} %bitcast.260, bf16[2048,512]{1,0:T(8,128)(2,1)S(1)} %get-tuple-element.110, bf16[2048,512]{1,0:T(8,128)(2,1)S(1)} %get-tuple-element.109), kind=kOutput, calls=%fused_computation.2 | convolution fusion | flops 8602517504 | bytes 16777216 | tf_op jit(solution)/shard_map/rf,df->rd/dot_general | solution.py:26
  432.3 112.3 %branch_kernel.1 = (bf16[2048,2048]{1,0:T(8,128)(2,1)}, f32[128,2048]{1,0:T(8,128)S(1)}, f32[1,2048]{1,0:T(1,128)S(1)}, bf16[8,1,128,1024]{3,2,1,0:T(8,128)(2,1)S(1)}, bf16[8,256,256]{2,1,0:T(8,128)(2,1)S(1)}) custom-call(bf16[2048,2048]{1,0:T(8,128)(2,1)} %convolution_convert_fusion.1.partial, f32[128,2048]{1,0:T(8,128)S(1)} %get-tuple-element.71.branch, ...), custom_call_target="tpu_custom_call" | custom-call | bytes 300000000 | tf_op jit(solution)/shard_map/branch_kernel/pallas_call | solution.py:1129
  544.6 7.2 convolution_convert_fusion.6
  552.0 2.5 multiply_reduce_fusion
  554.4 9.5 %all-to-all-start.2 = ((bf16[8,128,1024]{2,1,0:T(8,128)(2,1)}), bf16[8,128,1024]{2,1,0:T(8,128)(2,1)S(1)}, u32[]{:S(2)}, u32[]{:S(2)}) async-start(bf16[8,128,1024]{2,1,0:T(8,128)(2,1)} %bitcast.209), calls=%async_computation.2 | async-start | bytes 4194304 | tf_op jit(solution)/shard_map/all_to_all | solution.py:1323
  563.9 3.9 multiply_convert_fusion
  567.9 1.3 copy-done.20
  570.0 1.3 copy-done.24
  572.2 1.3 collective-permute-start.1
  575.4 3.2 convolution_bitcast_fusion
  579.7 1.3 collective-permute-start.2
  581.0 5.4 fusion.33
  586.7 2.5 collective-permute-done.1
  589.2 6.4 maximum_add_fusion
  596.0 5.0 maximum_add_fusion.1
  601.1 2.9 fusion.20
  604.2 1.5 fusion.10
  606.7 2.9 all-to-all-done.2.moved
  609.7 1.5 slice.117
  611.2 16.1 %sum_kernel.3 = (f32[32,128]{1,0:T(8,128)S(1)}, bf16[8,32,1024]{2,1,0:T(8,128)(2,1)S(1)}) custom-call(f32[32,128]{1,0:T(8,128)S(1)} %reshape.526.value, bf16[8,128,1024]{2,1,0:T(8,128)(2,1)S(1)} %all-to-all-done.2.moved), custom_call_target="tpu_custom_call" | custom-call | bytes 30000000 | tf_op jit(solution)/shard_map/sum_kernel/pallas_call | solution.py:1129
  628.1 1.2 collective-permute-start.3
  629.3 6.1 all-to-all-start.3
  635.4 4.5 fusion.22
  640.8 6.9 convolution_convert_fusion.partial
  647.7 1.3 convolution_convert_fusion.5
  649.3 6.0 widen_own_kernel.1
  655.3 9.1 %convolution_convert_fusion.4 = bf16[2048,384]{1,0:T(8,128)(2,1)} fusion(bf16[2048,2048]{1,0:T(8,128)(2,1)} %get-tuple-element.57, bf16[2048,128]{1,0:T(8,128)(2,1)} %bitcast.238, bf16[2048,128]{1,0:T(8,128)(2,1)S(1)} %copy-done.41, bf16[2048,128]{1,0:T(8,128)(2,1)S(1)} %copy-done.39), kind=kOutput, calls=%fused_computation.14 | convolution fusion | flops 3226730496 | bytes 11534336 | tf_op jit(solution)/shard_map/rd,rf->df/dot_general | solution.py:22
  664.4 1.2 copy-done.5
  665.6 92.3 %last_kernel.1 = (f32[256,2048]{1,0:T(8,128)}, bf16[8,2,128,384]{3,2,1,0:T(8,128)(2,1)S(1)}, bf16[8,2,64,256]{3,2,1,0:T(8,128)(2,1)S(1)}, f32[8,2,8,128]{3,2,1,0:T(8,128)S(1)}, bf16[8,2,256,256]{3,2,1,0:T(8,128)(2,1)}) custom-call(bf16[2048,2048]{1,0:T(8,128)(2,1)} %convolution_convert_fusion.partial, f32[128,2048]{1,0:T(8,128)S(1)} %copy-done.5, ...), custom_call_target="tpu_custom_call" | custom-call | bytes 240000000 | tf_op jit(solution)/shard_map/last_kernel/pallas_call | solution.py:1129
  759.1 1.1 copy_bitcast_fusion
  760.2 1.1 copy_bitcast_fusion.1
  761.4 1.1 copy_bitcast_fusion.2
  764.8 7.6 widen_other_kernel.1
  773.4 3.1 copy.159
  (177 shorter events, 27.8 us)
Async XLA Ops:
  0.6 3.7 copy-start
  4.4 1.0 copy-start.9
  5.4 1.0 copy-start.10
  6.5 1.0 copy-start.11
  7.5 1.0 copy-start.12
  74.7 1.2 copy-start.16
  75.9 50.1 %all-to-all-start.1 = ((bf16[8,256,256]{2,1,0:T(8,128)(2,1)}), bf16[8,256,256]{2,1,0:T(8,128)(2,1)S(1)}, u32[]{:S(2)}, u32[]{:S(2)}) async-start(bf16[8,256,256]{2,1,0:T(8,128)(2,1)} %get-tuple-element.64), calls=%async_computation.1 | async-start | bytes 2097152 | tf_op jit(solution)/shard_map/all_to_all | solution.py:1323
  123.4 1.0 copy-start.23
  126.0 51.3 %all-to-all-start = ((bf16[8,128,1024]{2,1,0:T(8,128)(2,1)}), bf16[8,128,1024]{2,1,0:T(8,128)(2,1)}, u32[]{:S(2)}, u32[]{:S(2)}) async-start(bf16[8,128,1024]{2,1,0:T(8,128)(2,1)} %get-tuple-element.63), calls=%async_computation | async-start | bytes 4194304 | tf_op jit(solution)/shard_map/all_to_all | solution.py:1323
  132.7 12.1 %copy-start.22 = (f32[2048,128]{1,0:T(8,128)S(1)}, f32[2048,128]{1,0:T(8,128)}, u32[]{:S(2)}) copy-start(f32[2048,128]{1,0:T(8,128)} %get-tuple-element.114) | copy-start | bytes 3145732
  134.0 1.0 copy-start.18
  141.2 15.5 %collective-permute-start = (bf16[8,256,1,128]{3,1,0,2:T(8,128)(2,1)}, bf16[8,256,1,128]{3,1,0,2:T(8,128)(2,1)}, u32[]{:S(2)}, u32[]{:S(2)}) collective-permute-start(bf16[8,256,1,128]{3,1,0,2:T(8,128)(2,1)} %fusion.15), channel_id=1, source_target_pairs={{0,2},{1,3},{4,6},{5,7},{8,10},{9,11},{12,14},{13,15},{16,18},{17,... | collective-permute-start | bytes 1572872 | tf_op jit(solution)/shard_map/ppermute | solution.py:1487
  148.9 18.6 %copy-start.35 = (bf16[16,8,8,256]{3,1,2,0:T(8,128)(2,1)}, bf16[16,8,8,256]{3,1,2,0:T(8,128)(2,1)S(1)}, u32[]{:S(2)}) copy-start(bf16[16,8,8,256]{3,1,2,0:T(8,128)(2,1)S(1)} %copy.127) | copy-start | bytes 1572868
  156.6 5.3 copy-start.33
  167.5 5.6 copy-start.26
  292.8 3.2 copy-start.31
  296.0 1.9 copy-start.30
  406.5 11.3 %copy-start.6 = (bf16[256,2048]{1,0:T(8,128)(2,1)}, bf16[256,2048]{1,0:T(8,128)(2,1)S(1)}, u32[]{:S(2)}) copy-start(bf16[256,2048]{1,0:T(8,128)(2,1)S(1)} %get-tuple-element.163) | copy-start | bytes 3145732
  417.7 3.6 copy-start.45
  432.3 112.3 %copy-start.36 = (bf16[16,8,8,256]{3,1,2,0:T(8,128)(2,1)S(1)}, bf16[16,8,8,256]{3,1,2,0:T(8,128)(2,1)}, u32[]{:S(2)}) copy-start(bf16[16,8,8,256]{3,1,2,0:T(8,128)(2,1)} %copy-done.35) | copy-start | bytes 1572868
  544.6 7.3 copy-start.3
  544.6 7.3 copy-start.4
  544.6 7.3 copy-start.8
  544.6 7.3 copy-start.32
  544.6 7.3 copy-start.42
  544.6 7.3 copy-start.43
  551.9 2.5 copy-start.46
  554.4 55.2 %all-to-all-start.2 = ((bf16[8,128,1024]{2,1,0:T(8,128)(2,1)}), bf16[8,128,1024]{2,1,0:T(8,128)(2,1)S(1)}, u32[]{:S(2)}, u32[]{:S(2)}) async-start(bf16[8,128,1024]{2,1,0:T(8,128)(2,1)} %bitcast.209), calls=%async_computation.2 | async-start | bytes 4194304 | tf_op jit(solution)/shard_map/all_to_all | solution.py:1323
  563.9 5.2 copy-start.34
  567.8 1.3 copy-start.20
  570.0 1.3 copy-start.24
  572.2 17.0 %collective-permute-start.1 = (bf16[8,256,1,128]{3,1,0,2:T(8,128)(2,1)}, bf16[8,256,1,128]{3,1,0,2:T(8,128)(2,1)}, u32[]{:S(2)}, u32[]{:S(2)}) collective-permute-start(bf16[8,256,1,128]{3,1,0,2:T(8,128)(2,1)} %slice.174), channel_id=1, source_target_pairs={{2,0},{3,1},{6,4},{7,5},{10,8},{11,9},{14,12},{15,13},{18,16},{19,... | collective-permute-start | bytes 1572872 | tf_op jit(solution)/shard_map/ppermute | solution.py:1550
  575.4 5.5 copy-start.19
  575.4 5.5 copy-start.21
  578.7 2.3 copy-start.37
  579.7 24.6 %collective-permute-start.2 = (bf16[8,256,1,128]{1,3,0,2:T(8,128)(2,1)}, bf16[8,256,1,128]{1,3,0,2:T(8,128)(2,1)}, u32[]{:S(2)}, u32[]{:S(2)}) collective-permute-start(bf16[8,256,1,128]{1,3,0,2:T(8,128)(2,1)} %slice.173), channel_id=1, source_target_pairs={{2,0},{3,1},{6,4},{7,5},{10,8},{11,9},{14,12},{15,13},{18,16},{19,... | collective-permute-start | bytes 1572872 | tf_op jit(solution)/shard_map/ppermute | solution.py:1549
  581.0 8.3 %copy-start.25 = (f32[8,512,1,128]{3,1,0,2:T(8,128)S(1)}, f32[8,512,1,128]{3,1,0,2:T(8,128)}, u32[]{:S(2)}) copy-start(f32[8,512,1,128]{3,1,0,2:T(8,128)} %copy-done.24) | copy-start | bytes 6291460
  595.6 5.4 copy-start.28
  601.0 2.9 copy-start.29
  609.7 30.3 %copy-start.2 = (bf16[8,128,1024]{2,1,0:T(8,128)(2,1)}, bf16[8,128,1024]{2,1,0:T(8,128)(2,1)S(1)}, u32[]{:S(2)}) copy-start(bf16[8,128,1024]{2,1,0:T(8,128)(2,1)S(1)} %all-to-all-done.2.moved) | copy-start | bytes 6291460
  627.2 0.8 copy-start.13
  628.1 36.3 %collective-permute-start.3 = (bf16[8,96,1024]{2,1,0:T(8,128)(2,1)}, bf16[8,96,1024]{2,1,0:T(8,128)(2,1)}, u32[]{:S(2)}, u32[]{:S(2)}) collective-permute-start(bf16[8,96,1024]{2,1,0:T(8,128)(2,1)} %slice.117), channel_id=1, source_target_pairs={{0,2},{2,0},{1,3},{3,1},{4,6},{6,4},{5,7},{7,5},{8,10},{10,8},{9,1... | collective-permute-start | bytes 4718600 | tf_op jit(solution)/shard_map/ppermute | solution.py:1567
  629.3 35.1 %all-to-all-start.3 = ((bf16[8,256,256]{2,1,0:T(8,128)(2,1)}), bf16[8,256,256]{2,1,0:T(8,128)(2,1)S(1)}, u32[]{:S(2)}, u32[]{:S(2)}) async-start(bf16[8,256,256]{2,1,0:T(8,128)(2,1)} %copy-done.8), calls=%async_computation.3 | async-start | bytes 2097152 | tf_op jit(solution)/shard_map/all_to_all | solution.py:1323
  635.4 5.4 copy-start.17
  635.4 5.4 copy-start.44
  635.4 12.3 %slice-start = ((s8[8388608]{0:T(1024)(128)(4,1)}), s8[4194304]{0:T(1024)(128)(4,1)S(1)}, s32[]{:S(2)}) async-start(s8[8388608]{0:T(1024)(128)(4,1)} %bitcast.220), calls=%async_computation.4 | async-start | bytes 8388608
  640.0 0.8 copy-start.38
  640.0 7.7 copy-start.40
  640.8 6.9 slice-start.1
  640.8 6.9 copy-start.27
  649.0 6.3 copy-start.39
  649.0 6.3 copy-start.41
  664.4 1.2 copy-start.5
  758.0 0.8 copy-start.14
  758.8 3.7 copy-start.15
  764.8 7.6 copy-start.7
  764.8 11.7 %copy-start.1 = (bf16[256,2048]{1,0:T(8,128)(2,1)S(1)}, bf16[256,2048]{1,0:T(8,128)(2,1)}, u32[]{:S(2)}) copy-start(bf16[256,2048]{1,0:T(8,128)(2,1)} %param.14) | copy-start | bytes 3145732

commit v12 on v11

--- a/solution.py
+++ b/solution.py
@@ -303,7 +303,7 @@
     for number, block in enumerate(order[:-1]):
         if number == LINE - 2 and between is not None:
             between()
-        if number < 2 and idle is not None:
+        if idle is not None:
             idle(number)
         slot = 2 * block + y
         fetch(slot).wait()
@@ -902,9 +902,10 @@
             self.crossing(number, index).start()
         return carry
 
-    def some(self, which):
-        half = PIECES // 2
-        lax.fori_loop(which * half, which * half + half, self.one, 0)
+    def some(self, one):
+        slots = LINE - 1
+        first, end = (PIECES * one + slots - 1) // slots, (PIECES * (one + 1) + slots - 1) // slots
+        lax.fori_loop(first, end, self.one, 0)
 
     def add(self):
         def step(number, carry):

time: 785 us -> 787 us (level)
  no operation moved by 1% of the time
where the time goes in v12:
time: 787 us; the launch traced here: 778 us
  Pallas kernels  517 us (66%)
  matrix products  103 us (13%)
  other arithmetic  59.6 us (8%)
  starting transfers between devices  49.6 us (6%)
  local copies, waits for them, and re-layouts  37.6 us (5%)
  waiting for transfers between devices  9.89 us (1%)
    pallas_call x7, Pallas kernels, call(): pl.pallas_call(kernel, out_shape=shapes, in_specs=specs[0], out_specs=spe...  503 us
    all_to_all x4, starting transfers between devices, swap(): lax.all_to_all(pieces, 'fsdp', split_axis=0, concat_axis=0, tiled=True)  42.1 us
    dot_general x4, matrix products, product_right(): return jnp.einsum('rf,df->rd', left, right, preferred_element_type=F32)  36.3 us
    dot_general x4, matrix products, product(): return jnp.dot(left, right, preferred_element_type=F32)  34.8 us
    unnamed x112, local copies, waits for them, and re-layouts  21.3 us
  transfers between devices with their start and end apart: 8, of which 3 were waited for; matrix products, arithmetic and copies ran while one was open for 14% of the time, Pallas kernels for 3%

profile of v12, /device:TPU:16, one launch (start us, length us, event | category | flops | bytes accessed | tf_op | source)
XLA Modules:
  0.0 778.4 jit_solution(9490697676066987012)
XLA Ops:
  8.5 66.2 %first_kernel.1 = (bf16[2048,2048]{1,0:T(8,128)(2,1)}, bf16[8,2,128,384]{3,2,1,0:T(8,128)(2,1)S(1)}, bf16[8,2,64,256]{3,2,1,0:T(8,128)(2,1)S(1)}, f32[8,2,8,128]...) custom-call(bf16[128,2048]{1,0:T(8,128)(2,1)S(1)} %constant_dynamic-slice_fusion.3.own_ref.tokens, ...), custom_call_target="tpu_custom_call" | custom-call | bytes 240000000 | tf_op jit(solution)/shard_map/first_kernel/pallas_call | solution.py:1130
  74.8 1.2 copy-done.16
  75.9 15.3 %all-to-all-start.1 = ((bf16[8,256,256]{2,1,0:T(8,128)(2,1)}), bf16[8,256,256]{2,1,0:T(8,128)(2,1)S(1)}, u32[]{:S(2)}, u32[]{:S(2)}) async-start(bf16[8,256,256]{2,1,0:T(8,128)(2,1)} %get-tuple-element.64), calls=%async_computation.1 | async-start | bytes 2097152 | tf_op jit(solution)/shard_map/all_to_all | solution.py:1324
  91.3 10.0 %fusion.57 = f32[2048,384]{1,0:T(8,128)} fusion(bf16[2048,2048]{1,0:T(8,128)(2,1)} %get-tuple-element.57, bf16[2048,384]{1,0:T(8,128)(2,1)} %bitcast.218), kind=kOutput, calls=%fused_computation.152 | convolution fusion | flops 3221225472 | bytes 13107200 | tf_op jit(solution)/shard_map/dot_general | solution.py:18
  101.3 2.2 multiply_reduce_fusion.2
  103.7 1.3 split.54.moved
  105.5 15.0 %sum_kernel.2 = (f32[32,128]{1,0:T(8,128)S(1)}, bf16[2048,128]{1,0:T(8,128)(2,1)S(1)}) custom-call(f32[32,128]{1,0:T(8,128)S(1)} %reshape.505.value, bf16[2048,128]{1,0:T(8,128)(2,1)S(1)} %split.54.moved), custom_call_target="tpu_custom_call" | custom-call | bytes 30000000 | tf_op jit(solution)/shard_map/sum_kernel/pallas_call | solution.py:1130
  120.7 2.7 multiply_multiply_fusion
  124.4 1.7 slice_negate_fusion.2
  126.0 6.6 all-to-all-start
  132.7 1.3 fusion.35
  135.0 6.2 fusion.15
  141.2 3.4 collective-permute-start
  144.8 1.7 fusion.11
  149.0 1.2 constant_dynamic-slice_fusion.1.cotangent
  150.2 6.4 fusion.13
  156.6 5.3 fusion.56
  161.9 4.2 fusion.9
  166.1 1.3 copy.97
  167.5 5.6 convolution_convert_fusion.3.partial
  173.1 4.3 all-to-all-done.pair
  177.4 102.9 %hidden_kernel.1 = (bf16[2048,2048]{1,0:T(8,128)(2,1)}, f32[128,2048]{1,0:T(8,128)S(1)}, f32[128,2048]{1,0:T(8,128)S(1)}, bf16[8,2,128,1024]{3,2,1,0:T(8,128)(2,1)}, bf16[8,2,256,256]{3,2,1,0:T(8,128)(2,1)S(1)}) custom-call(bf16[2048,2048]{1,0:T(8,128)(2,1)} %convolution_convert_fusion.3.partial, ...), custom_call_target="tpu_custom_call" | custom-call | bytes 300000000 | tf_op jit(solution)/shard_map/hidden_kernel/pallas_call | solution.py:1130
  280.3 12.5 %fusion.58 = f32[2048,1024]{1,0:T(8,128)S(1)} fusion(bf16[2048,2048]{1,0:T(8,128)(2,1)} %get-tuple-element.65.hidden_low, bf16[2048,1024]{1,0:T(8,128)(2,1)} %bitcast.259), kind=kOutput, calls=%fused_computation.153 | convolution fusion | flops 8589934592 | bytes 20971520 | tf_op jit(solution)/shard_map/dot_general | solution.py:18
  292.8 1.5 multiply_convert_fusion.3.inner_low
  294.3 1.7 copy-done.31
  296.0 1.2 copy.101
  297.9 6.8 convolution_convert_fusion.2.partial
  304.7 101.8 %turn_kernel.1 = (bf16[2048,2048]{1,0:T(8,128)(2,1)}, bf16[256,2048]{1,0:T(8,128)(2,1)S(1)}, f32[1,2048]{1,0:T(1,128)S(1)}) custom-call(bf16[2048,2048]{1,0:T(8,128)(2,1)} %convolution_convert_fusion.2.partial, f32[128,2048]{1,0:T(8,128)S(1)} %get-tuple-element.68.hidden, bf16[128,2048]{1,0:T(8,128)(2,1)S(1)} %constant_dynamic-slice_fusion.1.cotangent, ...), custom_call_target="tpu_custom_call" | custom-call | bytes 300000000 | tf_op jit(solution)/shard_map/turn_kernel/pallas_call | solution.py:1130
  406.5 11.2 %multiply_convert_fusion.2 = (bf16[2048,512]{1,0:T(8,128)(2,1)S(1)}, bf16[2048,512]{1,0:T(8,128)(2,1)S(1)}) fusion(f32[2048,1024]{1,0:T(8,128)} %copy-done.31, bf16[2048,2048]{1,0:T(8,128)(2,1)} %get-tuple-element.70.grad_mlp, bf16[512,2048]{1,0:T(8,128)(2,1)S(1)} %bitcast.232), kind=kOutput, calls=%fused_computation.9 | convolution fusion | flops 4308598784 | bytes 23068672 | tf_op jit(solution)/shard_map/rf,df->rd/dot_general | solution.py:26
  417.7 2.8 pad_maximum_fusion.grad_pair
  421.4 10.9 %convolution_convert_fusion.1.partial = bf16[2048,2048]{1,0:T(8,128)(2,1)} fusion(bf16[2048,1024]{1,0:T(8,128)(2,1)S(1)} %bitcast.260, bf16[2048,512]{1,0:T(8,128)(2,1)S(1)} %get-tuple-element.110, bf16[2048,512]{1,0:T(8,128)(2,1)S(1)} %get-tuple-element.109), kind=kOutput, calls=%fused_computation.2 | convolution fusion | flops 8602517504 | bytes 16777216 | tf_op jit(solution)/shard_map/rf,df->rd/dot_general | solution.py:26
  432.3 109.4 %branch_kernel.1 = (bf16[2048,2048]{1,0:T(8,128)(2,1)}, f32[128,2048]{1,0:T(8,128)S(1)}, f32[1,2048]{1,0:T(1,128)S(1)}, bf16[8,1,128,1024]{3,2,1,0:T(8,128)(2,1)S(1)}, bf16[8,256,256]{2,1,0:T(8,128)(2,1)S(1)}) custom-call(bf16[2048,2048]{1,0:T(8,128)(2,1)} %convolution_convert_fusion.1.partial, f32[128,2048]{1,0:T(8,128)S(1)} %get-tuple-element.71.branch, ...), custom_call_target="tpu_custom_call" | custom-call | bytes 300000000 | tf_op jit(solution)/shard_map/branch_kernel/pallas_call | solution.py:1130
  541.8 7.2 convolution_convert_fusion.6
  549.1 2.5 multiply_reduce_fusion
  551.6 14.0 %all-to-all-start.2 = ((bf16[8,128,1024]{2,1,0:T(8,128)(2,1)}), bf16[8,128,1024]{2,1,0:T(8,128)(2,1)S(1)}, u32[]{:S(2)}, u32[]{:S(2)}) async-start(bf16[8,128,1024]{2,1,0:T(8,128)(2,1)} %bitcast.209), calls=%async_computation.2 | async-start | bytes 4194304 | tf_op jit(solution)/shard_map/all_to_all | solution.py:1324
  565.6 3.9 multiply_convert_fusion
  569.6 1.3 copy-done.20
  571.7 1.3 copy-done.24
  573.9 1.3 collective-permute-start.1
  577.1 3.3 convolution_bitcast_fusion
  581.4 1.3 collective-permute-start.2
  582.7 5.4 fusion.33
  588.4 2.5 collective-permute-done.1
  590.9 6.4 maximum_add_fusion
  597.7 5.0 maximum_add_fusion.1
  602.8 2.9 fusion.20
  605.9 1.5 fusion.10
  608.4 3.1 all-to-all-done.2.moved
  611.5 1.5 slice.117
  613.0 15.7 %sum_kernel.3 = (f32[32,128]{1,0:T(8,128)S(1)}, bf16[8,32,1024]{2,1,0:T(8,128)(2,1)S(1)}) custom-call(f32[32,128]{1,0:T(8,128)S(1)} %reshape.526.value, bf16[8,128,1024]{2,1,0:T(8,128)(2,1)S(1)} %all-to-all-done.2.moved), custom_call_target="tpu_custom_call" | custom-call | bytes 30000000 | tf_op jit(solution)/shard_map/sum_kernel/pallas_call | solution.py:1130
  629.6 1.5 collective-permute-start.3
  631.1 6.1 all-to-all-start.3
  637.3 4.5 fusion.22
  642.6 6.9 convolution_convert_fusion.partial
  649.6 1.3 convolution_convert_fusion.5
  651.1 6.0 widen_own_kernel.1
  657.1 9.1 %convolution_convert_fusion.4 = bf16[2048,384]{1,0:T(8,128)(2,1)} fusion(bf16[2048,2048]{1,0:T(8,128)(2,1)} %get-tuple-element.57, bf16[2048,128]{1,0:T(8,128)(2,1)} %bitcast.238, bf16[2048,128]{1,0:T(8,128)(2,1)S(1)} %copy-done.41, bf16[2048,128]{1,0:T(8,128)(2,1)S(1)} %copy-done.39), kind=kOutput, calls=%fused_computation.14 | convolution fusion | flops 3226730496 | bytes 11534336 | tf_op jit(solution)/shard_map/rd,rf->df/dot_general | solution.py:22
  666.3 1.2 copy-done.5
  667.5 91.9 %last_kernel.1 = (f32[256,2048]{1,0:T(8,128)}, bf16[8,2,128,384]{3,2,1,0:T(8,128)(2,1)S(1)}, bf16[8,2,64,256]{3,2,1,0:T(8,128)(2,1)S(1)}, f32[8,2,8,128]{3,2,1,0:T(8,128)S(1)}, bf16[8,2,256,256]{3,2,1,0:T(8,128)(2,1)}) custom-call(bf16[2048,2048]{1,0:T(8,128)(2,1)} %convolution_convert_fusion.partial, f32[128,2048]{1,0:T(8,128)S(1)} %copy-done.5, ...), custom_call_target="tpu_custom_call" | custom-call | bytes 240000000 | tf_op jit(solution)/shard_map/last_kernel/pallas_call | solution.py:1130
  760.6 1.1 copy_bitcast_fusion
  761.7 1.1 copy_bitcast_fusion.1
  762.8 1.1 copy_bitcast_fusion.2
  766.3 7.6 widen_other_kernel.1
  774.9 3.1 copy.159
  (177 shorter events, 27.8 us)
Async XLA Ops:
  0.6 3.7 copy-start
  4.4 1.0 copy-start.9
  5.4 1.0 copy-start.10
  6.5 1.0 copy-start.11
  7.5 1.0 copy-start.12
  74.7 1.2 copy-start.16
  75.9 50.1 %all-to-all-start.1 = ((bf16[8,256,256]{2,1,0:T(8,128)(2,1)}), bf16[8,256,256]{2,1,0:T(8,128)(2,1)S(1)}, u32[]{:S(2)}, u32[]{:S(2)}) async-start(bf16[8,256,256]{2,1,0:T(8,128)(2,1)} %get-tuple-element.64), calls=%async_computation.1 | async-start | bytes 2097152 | tf_op jit(solution)/shard_map/all_to_all | solution.py:1324
  123.4 1.0 copy-start.23
  126.0 51.3 %all-to-all-start = ((bf16[8,128,1024]{2,1,0:T(8,128)(2,1)}), bf16[8,128,1024]{2,1,0:T(8,128)(2,1)}, u32[]{:S(2)}, u32[]{:S(2)}) async-start(bf16[8,128,1024]{2,1,0:T(8,128)(2,1)} %get-tuple-element.63), calls=%async_computation | async-start | bytes 4194304 | tf_op jit(solution)/shard_map/all_to_all | solution.py:1324
  132.7 12.1 %copy-start.22 = (f32[2048,128]{1,0:T(8,128)S(1)}, f32[2048,128]{1,0:T(8,128)}, u32[]{:S(2)}) copy-start(f32[2048,128]{1,0:T(8,128)} %get-tuple-element.114) | copy-start | bytes 3145732
  134.0 1.0 copy-start.18
  141.2 15.5 %collective-permute-start = (bf16[8,256,1,128]{3,1,0,2:T(8,128)(2,1)}, bf16[8,256,1,128]{3,1,0,2:T(8,128)(2,1)}, u32[]{:S(2)}, u32[]{:S(2)}) collective-permute-start(bf16[8,256,1,128]{3,1,0,2:T(8,128)(2,1)} %fusion.15), channel_id=1, source_target_pairs={{0,2},{1,3},{4,6},{5,7},{8,10},{9,11},{12,14},{13,15},{16,18},{17,... | collective-permute-start | bytes 1572872 | tf_op jit(solution)/shard_map/ppermute | solution.py:1488
  148.9 18.6 %copy-start.35 = (bf16[16,8,8,256]{3,1,2,0:T(8,128)(2,1)}, bf16[16,8,8,256]{3,1,2,0:T(8,128)(2,1)S(1)}, u32[]{:S(2)}) copy-start(bf16[16,8,8,256]{3,1,2,0:T(8,128)(2,1)S(1)} %copy.127) | copy-start | bytes 1572868
  156.6 5.3 copy-start.33
  167.5 5.6 copy-start.26
  292.8 3.2 copy-start.31
  296.0 1.9 copy-start.30
  406.5 11.3 %copy-start.6 = (bf16[256,2048]{1,0:T(8,128)(2,1)}, bf16[256,2048]{1,0:T(8,128)(2,1)S(1)}, u32[]{:S(2)}) copy-start(bf16[256,2048]{1,0:T(8,128)(2,1)S(1)} %get-tuple-element.163) | copy-start | bytes 3145732
  417.7 3.6 copy-start.45
  432.3 109.5 %copy-start.36 = (bf16[16,8,8,256]{3,1,2,0:T(8,128)(2,1)S(1)}, bf16[16,8,8,256]{3,1,2,0:T(8,128)(2,1)}, u32[]{:S(2)}) copy-start(bf16[16,8,8,256]{3,1,2,0:T(8,128)(2,1)} %copy-done.35) | copy-start | bytes 1572868
  541.7 7.3 copy-start.3
  541.8 7.3 copy-start.4
  541.8 7.3 copy-start.8
  541.8 7.3 copy-start.32
  541.8 7.3 copy-start.42
  541.8 7.3 copy-start.43
  549.1 2.5 copy-start.46
  551.6 59.9 %all-to-all-start.2 = ((bf16[8,128,1024]{2,1,0:T(8,128)(2,1)}), bf16[8,128,1024]{2,1,0:T(8,128)(2,1)S(1)}, u32[]{:S(2)}, u32[]{:S(2)}) async-start(bf16[8,128,1024]{2,1,0:T(8,128)(2,1)} %bitcast.209), calls=%async_computation.2 | async-start | bytes 4194304 | tf_op jit(solution)/shard_map/all_to_all | solution.py:1324
  565.6 5.2 copy-start.34
  569.5 1.3 copy-start.20
  571.7 1.3 copy-start.24
  573.9 17.0 %collective-permute-start.1 = (bf16[8,256,1,128]{3,1,0,2:T(8,128)(2,1)}, bf16[8,256,1,128]{3,1,0,2:T(8,128)(2,1)}, u32[]{:S(2)}, u32[]{:S(2)}) collective-permute-start(bf16[8,256,1,128]{3,1,0,2:T(8,128)(2,1)} %slice.174), channel_id=1, source_target_pairs={{2,0},{3,1},{6,4},{7,5},{10,8},{11,9},{14,12},{15,13},{18,16},{19,... | collective-permute-start | bytes 1572872 | tf_op jit(solution)/shard_map/ppermute | solution.py:1551
  577.1 5.6 copy-start.19
  577.1 5.6 copy-start.21
  580.4 2.3 copy-start.37
  581.4 24.5 %collective-permute-start.2 = (bf16[8,256,1,128]{1,3,0,2:T(8,128)(2,1)}, bf16[8,256,1,128]{1,3,0,2:T(8,128)(2,1)}, u32[]{:S(2)}, u32[]{:S(2)}) collective-permute-start(bf16[8,256,1,128]{1,3,0,2:T(8,128)(2,1)} %slice.173), channel_id=1, source_target_pairs={{2,0},{3,1},{6,4},{7,5},{10,8},{11,9},{14,12},{15,13},{18,16},{19,... | collective-permute-start | bytes 1572872 | tf_op jit(solution)/shard_map/ppermute | solution.py:1550
  582.7 8.3 %copy-start.25 = (f32[8,512,1,128]{3,1,0,2:T(8,128)S(1)}, f32[8,512,1,128]{3,1,0,2:T(8,128)}, u32[]{:S(2)}) copy-start(f32[8,512,1,128]{3,1,0,2:T(8,128)} %copy-done.24) | copy-start | bytes 6291460
  597.3 5.4 copy-start.28
  602.7 2.9 copy-start.29
  611.5 30.3 %copy-start.2 = (bf16[8,128,1024]{2,1,0:T(8,128)(2,1)}, bf16[8,128,1024]{2,1,0:T(8,128)(2,1)S(1)}, u32[]{:S(2)}) copy-start(bf16[8,128,1024]{2,1,0:T(8,128)(2,1)S(1)} %all-to-all-done.2.moved) | copy-start | bytes 6291460
  628.7 0.8 copy-start.13
  629.6 36.7 %collective-permute-start.3 = (bf16[8,96,1024]{2,1,0:T(8,128)(2,1)}, bf16[8,96,1024]{2,1,0:T(8,128)(2,1)}, u32[]{:S(2)}, u32[]{:S(2)}) collective-permute-start(bf16[8,96,1024]{2,1,0:T(8,128)(2,1)} %slice.117), channel_id=1, source_target_pairs={{0,2},{2,0},{1,3},{3,1},{4,6},{6,4},{5,7},{7,5},{8,10},{10,8},{9,1... | collective-permute-start | bytes 4718600 | tf_op jit(solution)/shard_map/ppermute | solution.py:1568
  631.1 35.1 %all-to-all-start.3 = ((bf16[8,256,256]{2,1,0:T(8,128)(2,1)}), bf16[8,256,256]{2,1,0:T(8,128)(2,1)S(1)}, u32[]{:S(2)}, u32[]{:S(2)}) async-start(bf16[8,256,256]{2,1,0:T(8,128)(2,1)} %copy-done.8), calls=%async_computation.3 | async-start | bytes 2097152 | tf_op jit(solution)/shard_map/all_to_all | solution.py:1324
  637.2 5.4 copy-start.17
  637.2 5.4 copy-start.44
  637.3 12.3 %slice-start = ((s8[8388608]{0:T(1024)(128)(4,1)}), s8[4194304]{0:T(1024)(128)(4,1)S(1)}, s32[]{:S(2)}) async-start(s8[8388608]{0:T(1024)(128)(4,1)} %bitcast.220), calls=%async_computation.4 | async-start | bytes 8388608
  641.8 0.8 copy-start.38
  641.8 7.7 copy-start.40
  642.6 6.9 slice-start.1
  642.6 6.9 copy-start.27
  650.8 6.3 copy-start.39
  650.9 6.3 copy-start.41
  666.3 1.2 copy-start.5
  759.4 0.8 copy-start.14
  760.2 3.7 copy-start.15
  766.3 7.6 copy-start.7
  766.3 11.7 %copy-start.1 = (bf16[256,2048]{1,0:T(8,128)(2,1)S(1)}, bf16[256,2048]{1,0:T(8,128)(2,1)}, u32[]{:S(2)}) copy-start(bf16[256,2048]{1,0:T(8,128)(2,1)} %param.14) | copy-start | bytes 3145732
